TPU v7x, 8 devices: a whole 2x2x1 slice. The times are simulated.
8 devices in a mesh: dp: 2 (over z, y), sp: 4 (over x, core).
Axes of the slice: x: 2, y: 2, z: 1, core: 2. Of those that a mesh axis runs over, the one named last changes fastest.
Arguments:
- x: bfloat16 [8192, 3072], P(('dp', 'sp')), parts along dimension 0
- grad_out: bfloat16 [8192, 3072], P(('dp', 'sp')), parts along dimension 0
- positions: int32 [8192], P(('dp', 'sp')), parts along dimension 0
- gain: bfloat16 [3072], replicated
- w_q: bfloat16 [3072, 3072], replicated
- w_k: bfloat16 [3072, 1024], replicated
- w_v: bfloat16 [3072, 1024], replicated
- w_o: bfloat16 [3072, 3072], replicated
Outputs:
- output 1: bfloat16 [8192, 3072], P(('dp', 'sp')), parts along dimension 0
- output 2: bfloat16 [8192, 3072], P(('dp', 'sp')), parts along dimension 0
- output 3: float32 [6144, 3072], P('dp'), parts along dimension 0
- output 4: float32 [6144, 1024], P('dp'), parts along dimension 0
- output 5: float32 [6144, 1024], P('dp'), parts along dimension 0
- output 6: float32 [6144, 3072], P('dp'), parts along dimension 0
- output 7: float32 [6144], P('dp'), parts along dimension 0
There are 2 independent parts. A program takes and returns all parts, laid end to end along the dimension named above; an argument that names none is the same for every part.
All inputs are finite; a program needn't handle non-finite values.
Results may differ from a plain program's by a relative error of at most 0.0183931.
Values are sent between devices in bfloat16 or wider.
A program may use at most 1 GiB of HBM per device.

v0:
```python
import jax
import jax.numpy as jnp
from jax import lax
from jax.sharding import PartitionSpec as P

HEAD_DIM = 128
ROPE_THETA = 1000000.0
NORM_EPS = 1e-05
NEG_LARGE = -1e30
CONTRACT_ROWS = (((0,), (0,)), ((), ()))
CONTRACT_COLS = (((1,), (1,)), ((), ()))


def block_rows(seq_len, row_cost):
    row_count = seq_len
    while row_count > 8 and row_count * row_cost > 2 ** 24:
        row_count = row_count // 2
    return row_count


def rope_tables(positions):
    inv_freq = ROPE_THETA ** (-jnp.arange(0, HEAD_DIM, 2).astype(jnp.float32) / HEAD_DIM)
    angles = positions.astype(jnp.float32)[:, None] * inv_freq[None, :]
    return jnp.cos(angles)[:, None, :], jnp.sin(angles)[:, None, :]


def rotate(values, cos_t, sin_t):
    half_dim = values.shape[-1] // 2
    lower_half = values[..., :half_dim]
    upper_half = values[..., half_dim:]
    return jnp.concatenate([lower_half * cos_t - upper_half * sin_t, upper_half * cos_t + lower_half * sin_t], axis=-1)


def attn_forward(q_all, k_all, v_all):
    seq_len, kv_loc, group_size, head_dim = q_all.shape
    row_count = block_rows(seq_len, kv_loc * group_size * seq_len)
    n_blocks = seq_len // row_count
    qk_scale = head_dim ** -0.5
    key_index = jnp.arange(seq_len)
    q_blocks = q_all.reshape(n_blocks, row_count, kv_loc, group_size, head_dim)
    blk_starts = jnp.arange(n_blocks) * row_count

    def one_block(block_args):
        q_blk, blk_start = block_args
        scores = jnp.einsum('qhgd,khd->hgqk', q_blk, k_all, preferred_element_type=jnp.float32) * qk_scale
        causal = (blk_start + jnp.arange(row_count))[:, None] >= key_index[None, :]
        attn_prob = jax.nn.softmax(jnp.where(causal, scores, NEG_LARGE), axis=-1)
        blk_out = jnp.einsum('hgqk,khd->qhgd', attn_prob.astype(jnp.bfloat16), v_all, preferred_element_type=jnp.float32)
        return blk_out.astype(jnp.bfloat16)

    return lax.map(one_block, (q_blocks, blk_starts)).reshape(seq_len, kv_loc, group_size, head_dim)


def attn_backward(q_all, k_all, v_all, do_all):
    seq_len, kv_loc, group_size, head_dim = q_all.shape
    row_count = block_rows(seq_len, kv_loc * group_size * seq_len)
    n_blocks = seq_len // row_count
    qk_scale = head_dim ** -0.5
    key_index = jnp.arange(seq_len)
    q_blocks = q_all.reshape(n_blocks, row_count, kv_loc, group_size, head_dim)
    do_blocks = do_all.reshape(n_blocks, row_count, kv_loc, group_size, head_dim)
    blk_starts = jnp.arange(n_blocks) * row_count

    def one_block(acc_pair, block_args):
        dk_acc, dv_acc = acc_pair
        q_blk, do_blk, blk_start = block_args
        scores = jnp.einsum('qhgd,khd->hgqk', q_blk, k_all, preferred_element_type=jnp.float32) * qk_scale
        causal = (blk_start + jnp.arange(row_count))[:, None] >= key_index[None, :]
        attn_prob = jax.nn.softmax(jnp.where(causal, scores, NEG_LARGE), axis=-1)
        prob_bf = attn_prob.astype(jnp.bfloat16)
        dv_acc = dv_acc + jnp.einsum('hgqk,qhgd->khd', prob_bf, do_blk, preferred_element_type=jnp.float32)
        d_prob = jnp.einsum('qhgd,khd->hgqk', do_blk, v_all, preferred_element_type=jnp.float32)
        d_score = attn_prob * (d_prob - jnp.sum(attn_prob * d_prob, axis=-1, keepdims=True)) * qk_scale
        ds_bf = d_score.astype(jnp.bfloat16)
        dq_blk = jnp.einsum('hgqk,khd->qhgd', ds_bf, k_all, preferred_element_type=jnp.float32)
        dk_acc = dk_acc + jnp.einsum('hgqk,qhgd->khd', ds_bf, q_blk, preferred_element_type=jnp.float32)
        return (dk_acc, dv_acc), dq_blk.astype(jnp.bfloat16)

    zero_acc = jnp.zeros((seq_len, kv_loc, head_dim), jnp.float32)
    (dk_all, dv_all), dq_blocks = lax.scan(one_block, (zero_acc, zero_acc), (q_blocks, do_blocks, blk_starts))
    return dq_blocks.reshape(seq_len, kv_loc, group_size, head_dim), dk_all, dv_all


def solution(mesh):
    sp_size = mesh.shape['sp']
    seq_spec = P(('dp', 'sp'), None)
    pos_spec = P(('dp', 'sp'))
    replicated = P(None, None)
    part_rows = P('dp', None)

    def local_step(x, grad_out, positions, gain, w_q, w_k, w_v, w_o):
        tok_count = x.shape[0]
        n_heads = w_q.shape[1] // HEAD_DIM
        kv_heads = w_k.shape[1] // HEAD_DIM
        kv_copies = max(1, sp_size // kv_heads)
        q_loc = n_heads // sp_size
        kv_loc = max(kv_heads, sp_size) // sp_size
        group_size = q_loc // kv_loc
        seq_len = tok_count * sp_size
        x_f = x.astype(jnp.float32)
        inv_rms = lax.rsqrt(jnp.mean(x_f * x_f, axis=-1, keepdims=True) + NORM_EPS)
        normed = x_f * inv_rms
        gain_f = gain.astype(jnp.float32)
        hidden = (normed * gain_f).astype(jnp.bfloat16)
        cos_t, sin_t = rope_tables(positions)
        q_proj = jnp.dot(hidden, w_q, preferred_element_type=jnp.float32).reshape(tok_count, n_heads, HEAD_DIM)
        k_proj = jnp.dot(hidden, w_k, preferred_element_type=jnp.float32).reshape(tok_count, kv_heads, HEAD_DIM)
        v_send = jnp.dot(hidden, w_v, preferred_element_type=jnp.float32).astype(jnp.bfloat16).reshape(tok_count, kv_heads, HEAD_DIM)
        q_rot = rotate(q_proj, cos_t, sin_t).astype(jnp.bfloat16)
        k_send = rotate(k_proj, cos_t, sin_t).astype(jnp.bfloat16)
        if kv_copies > 1:
            k_send = jnp.repeat(k_send, kv_copies, axis=1)
            v_send = jnp.repeat(v_send, kv_copies, axis=1)
        q_all = lax.all_to_all(q_rot, 'sp', 1, 0, tiled=True).reshape(seq_len, kv_loc, group_size, HEAD_DIM)
        k_all = lax.all_to_all(k_send, 'sp', 1, 0, tiled=True)
        v_all = lax.all_to_all(v_send, 'sp', 1, 0, tiled=True)
        o_all = attn_forward(q_all, k_all, v_all)
        o_loc = lax.all_to_all(o_all.reshape(seq_len, q_loc, HEAD_DIM), 'sp', 0, 1, tiled=True).reshape(tok_count, n_heads * HEAD_DIM)
        mixed = jnp.dot(o_loc, w_o, preferred_element_type=jnp.float32)
        result = (x_f + mixed).astype(jnp.bfloat16)
        grad_wo = lax.psum(lax.dot_general(o_loc, grad_out, CONTRACT_ROWS, preferred_element_type=jnp.float32), 'sp')
        d_o = lax.dot_general(grad_out, w_o, CONTRACT_COLS, preferred_element_type=jnp.float32).astype(jnp.bfloat16)
        do_all = lax.all_to_all(d_o.reshape(tok_count, n_heads, HEAD_DIM), 'sp', 1, 0, tiled=True).reshape(seq_len, kv_loc, group_size, HEAD_DIM)
        dq_all, dk_all, dv_all = attn_backward(q_all, k_all, v_all, do_all)
        dq_loc = lax.all_to_all(dq_all.reshape(seq_len, q_loc, HEAD_DIM), 'sp', 0, 1, tiled=True)
        dk_loc = lax.all_to_all(dk_all.astype(jnp.bfloat16), 'sp', 0, 1, tiled=True)
        dv_loc = lax.all_to_all(dv_all.astype(jnp.bfloat16), 'sp', 0, 1, tiled=True)
        dk_sum = jnp.sum(dk_loc.reshape(tok_count, kv_heads, kv_copies, HEAD_DIM), axis=2, dtype=jnp.float32)
        dv_sum = jnp.sum(dv_loc.reshape(tok_count, kv_heads, kv_copies, HEAD_DIM), axis=2, dtype=jnp.float32)
        dq_pre = rotate(dq_loc.astype(jnp.float32), cos_t, -sin_t).astype(jnp.bfloat16).reshape(tok_count, n_heads * HEAD_DIM)
        dk_pre = rotate(dk_sum, cos_t, -sin_t).astype(jnp.bfloat16).reshape(tok_count, kv_heads * HEAD_DIM)
        dv_pre = dv_sum.astype(jnp.bfloat16).reshape(tok_count, kv_heads * HEAD_DIM)
        grad_wq = lax.psum(lax.dot_general(hidden, dq_pre, CONTRACT_ROWS, preferred_element_type=jnp.float32), 'sp')
        grad_wk = lax.psum(lax.dot_general(hidden, dk_pre, CONTRACT_ROWS, preferred_element_type=jnp.float32), 'sp')
        grad_wv = lax.psum(lax.dot_general(hidden, dv_pre, CONTRACT_ROWS, preferred_element_type=jnp.float32), 'sp')
        d_hidden = (lax.dot_general(dq_pre, w_q, CONTRACT_COLS, preferred_element_type=jnp.float32)
                    + lax.dot_general(dk_pre, w_k, CONTRACT_COLS, preferred_element_type=jnp.float32)
                    + lax.dot_general(dv_pre, w_v, CONTRACT_COLS, preferred_element_type=jnp.float32))
        grad_gain = lax.psum(jnp.sum(d_hidden * normed, axis=0), 'sp')
        d_normed = d_hidden * gain_f
        d_xnorm = inv_rms * (d_normed - normed * jnp.mean(d_normed * normed, axis=-1, keepdims=True))
        grad_x = (grad_out.astype(jnp.float32) + d_xnorm).astype(jnp.bfloat16)
        return result, grad_x, grad_wq, grad_wk, grad_wv, grad_wo, grad_gain

    return jax.shard_map(local_step, mesh=mesh,
                         in_specs=(seq_spec, seq_spec, pos_spec, P(None), replicated, replicated, replicated, replicated),
                         out_specs=(seq_spec, seq_spec, part_rows, part_rows, part_rows, part_rows, P('dp')),
                         check_vma=False)
```

profile of v0, /device:TPU:0, one launch (start us, length us, event | category | flops | bytes accessed | tf_op | source)
XLA Modules:
  0.0 4332.7 jit_solution(15610818156205032526)
XLA Ops:
  182.9 57.2 %all-to-all-done = bf16[1024,24,128]{2,0,1:T(8,128)(2,1)} async-done(((bf16[1024,24,128]{2,0,1:T(8,128)(2,1)}), bf16[1024,24,128]{2,0,1:T(8,128)(2,1)}, u32[]{:S(2)}, u32[]{:S(2)}) %all-to-all-start) | async-done | bytes 6291488 | tf_op jit(solution)/shard_map/all_to_all | solution.py:114
  250.7 1613.0 %while.27 = (s32[]{:T(128)}, f32[4096,2,128]{0,2,1:T(8,128)}, f32[4096,2,128]{0,2,1:T(8,128)}, bf16[8,512,2,3,128]{4,1,0,3,2:T(8,128)(2,1)}, bf16[8,512,2,3,128]...) while((s32[]{:T(128)}, f32[4096,2,128]{0,2,1:T(8,128)}, ...), condition=%wide.region_9.10_spmd.clone, body=%wide.region_5.9_spmd.clone.sunk | while | flops 16364489728 | bytes 584937984 | solution.py:80
  321.5 65.3 %fusion.218 = f32[4096,2,128]{0,2,1:T(8,128)} fusion(f32[2,512,3,4096]{3,1,2,0:T(8,128)} %fusion.216, f32[4096,2,128]{0,2,1:T(8,128)} %get-tuple-element.410, pred[]{:T(512)S(6)} %compare.3, bf16[8,512,2,3,128]{4,1,3,2,0:T(8,128)(2,1)} %get-tuple-element.424, s32[]{:T(128)S(6)} %copy.187, f32[2,3,512,4096]{3,2,1,0:T(8,128)} %get-tuple-element.375, ...), kind=kOutput, calls=%fused_computation.56.clone.2 | convolution fusion | flops 3311410176 | bytes 210534400 | tf_op jit(solution)/shard_map/while/body/eval_jaxpr/hgqk,qhgd->khd/dot_general | solution.py:76
  386.7 63.5 %fusion.220 = bf16[8,512,2,3,128]{4,1,0,3,2:T(8,128)(2,1)} fusion(bf16[8,512,2,3,128]{4,1,0,3,2:T(8,128)(2,1)} %get-tuple-element.412, s32[]{:T(128)S(6)} %copy.187, bf16[4096,2,128]{2,0,1:T(8,128)(2,1)} %get-tuple-element.426, f32[2,512,3,4096]{3,1,2,0:T(8,128)} %fusion.216, f32[2,3,512,4096]{3,2,1,0:T(8,128)} %get-tuple-element.375, ...), kind=kOutput, calls=%fused_computation.66.clone.1 | convolution fusion | flops 3309706240 | bytes 204242944 | tf_op jit(solution)/shard_map/while/body/eval_jaxpr/hgqk,khd->qhgd/dot_general | solution.py:75
  522.1 66.6 %fusion.218 = f32[4096,2,128]{0,2,1:T(8,128)} fusion(f32[2,512,3,4096]{3,1,2,0:T(8,128)} %fusion.216, f32[4096,2,128]{0,2,1:T(8,128)} %get-tuple-element.410, pred[]{:T(512)S(6)} %compare.3, bf16[8,512,2,3,128]{4,1,3,2,0:T(8,128)(2,1)} %get-tuple-element.424, s32[]{:T(128)S(6)} %copy.187, f32[2,3,512,4096]{3,2,1,0:T(8,128)} %get-tuple-element.375, ...), kind=kOutput, calls=%fused_computation.56.clone.2 | convolution fusion | flops 3311410176 | bytes 210534400 | tf_op jit(solution)/shard_map/while/body/eval_jaxpr/hgqk,qhgd->khd/dot_general | solution.py:76
  588.7 63.5 %fusion.220 = bf16[8,512,2,3,128]{4,1,0,3,2:T(8,128)(2,1)} fusion(bf16[8,512,2,3,128]{4,1,0,3,2:T(8,128)(2,1)} %get-tuple-element.412, s32[]{:T(128)S(6)} %copy.187, bf16[4096,2,128]{2,0,1:T(8,128)(2,1)} %get-tuple-element.426, f32[2,512,3,4096]{3,1,2,0:T(8,128)} %fusion.216, f32[2,3,512,4096]{3,2,1,0:T(8,128)} %get-tuple-element.375, ...), kind=kOutput, calls=%fused_computation.66.clone.1 | convolution fusion | flops 3309706240 | bytes 204242944 | tf_op jit(solution)/shard_map/while/body/eval_jaxpr/hgqk,khd->qhgd/dot_general | solution.py:75
  724.0 66.5 %fusion.218 = f32[4096,2,128]{0,2,1:T(8,128)} fusion(f32[2,512,3,4096]{3,1,2,0:T(8,128)} %fusion.216, f32[4096,2,128]{0,2,1:T(8,128)} %get-tuple-element.410, pred[]{:T(512)S(6)} %compare.3, bf16[8,512,2,3,128]{4,1,3,2,0:T(8,128)(2,1)} %get-tuple-element.424, s32[]{:T(128)S(6)} %copy.187, f32[2,3,512,4096]{3,2,1,0:T(8,128)} %get-tuple-element.375, ...), kind=kOutput, calls=%fused_computation.56.clone.2 | convolution fusion | flops 3311410176 | bytes 210534400 | tf_op jit(solution)/shard_map/while/body/eval_jaxpr/hgqk,qhgd->khd/dot_general | solution.py:76
  790.5 63.5 %fusion.220 = bf16[8,512,2,3,128]{4,1,0,3,2:T(8,128)(2,1)} fusion(bf16[8,512,2,3,128]{4,1,0,3,2:T(8,128)(2,1)} %get-tuple-element.412, s32[]{:T(128)S(6)} %copy.187, bf16[4096,2,128]{2,0,1:T(8,128)(2,1)} %get-tuple-element.426, f32[2,512,3,4096]{3,1,2,0:T(8,128)} %fusion.216, f32[2,3,512,4096]{3,2,1,0:T(8,128)} %get-tuple-element.375, ...), kind=kOutput, calls=%fused_computation.66.clone.1 | convolution fusion | flops 3309706240 | bytes 204242944 | tf_op jit(solution)/shard_map/while/body/eval_jaxpr/hgqk,khd->qhgd/dot_general | solution.py:75
  925.9 66.4 %fusion.218 = f32[4096,2,128]{0,2,1:T(8,128)} fusion(f32[2,512,3,4096]{3,1,2,0:T(8,128)} %fusion.216, f32[4096,2,128]{0,2,1:T(8,128)} %get-tuple-element.410, pred[]{:T(512)S(6)} %compare.3, bf16[8,512,2,3,128]{4,1,3,2,0:T(8,128)(2,1)} %get-tuple-element.424, s32[]{:T(128)S(6)} %copy.187, f32[2,3,512,4096]{3,2,1,0:T(8,128)} %get-tuple-element.375, ...), kind=kOutput, calls=%fused_computation.56.clone.2 | convolution fusion | flops 3311410176 | bytes 210534400 | tf_op jit(solution)/shard_map/while/body/eval_jaxpr/hgqk,qhgd->khd/dot_general | solution.py:76
  992.3 63.5 %fusion.220 = bf16[8,512,2,3,128]{4,1,0,3,2:T(8,128)(2,1)} fusion(bf16[8,512,2,3,128]{4,1,0,3,2:T(8,128)(2,1)} %get-tuple-element.412, s32[]{:T(128)S(6)} %copy.187, bf16[4096,2,128]{2,0,1:T(8,128)(2,1)} %get-tuple-element.426, f32[2,512,3,4096]{3,1,2,0:T(8,128)} %fusion.216, f32[2,3,512,4096]{3,2,1,0:T(8,128)} %get-tuple-element.375, ...), kind=kOutput, calls=%fused_computation.66.clone.1 | convolution fusion | flops 3309706240 | bytes 204242944 | tf_op jit(solution)/shard_map/while/body/eval_jaxpr/hgqk,khd->qhgd/dot_general | solution.py:75
  1127.7 66.4 %fusion.218 = f32[4096,2,128]{0,2,1:T(8,128)} fusion(f32[2,512,3,4096]{3,1,2,0:T(8,128)} %fusion.216, f32[4096,2,128]{0,2,1:T(8,128)} %get-tuple-element.410, pred[]{:T(512)S(6)} %compare.3, bf16[8,512,2,3,128]{4,1,3,2,0:T(8,128)(2,1)} %get-tuple-element.424, s32[]{:T(128)S(6)} %copy.187, f32[2,3,512,4096]{3,2,1,0:T(8,128)} %get-tuple-element.375, ...), kind=kOutput, calls=%fused_computation.56.clone.2 | convolution fusion | flops 3311410176 | bytes 210534400 | tf_op jit(solution)/shard_map/while/body/eval_jaxpr/hgqk,qhgd->khd/dot_general | solution.py:76
  1194.1 63.5 %fusion.220 = bf16[8,512,2,3,128]{4,1,0,3,2:T(8,128)(2,1)} fusion(bf16[8,512,2,3,128]{4,1,0,3,2:T(8,128)(2,1)} %get-tuple-element.412, s32[]{:T(128)S(6)} %copy.187, bf16[4096,2,128]{2,0,1:T(8,128)(2,1)} %get-tuple-element.426, f32[2,512,3,4096]{3,1,2,0:T(8,128)} %fusion.216, f32[2,3,512,4096]{3,2,1,0:T(8,128)} %get-tuple-element.375, ...), kind=kOutput, calls=%fused_computation.66.clone.1 | convolution fusion | flops 3309706240 | bytes 204242944 | tf_op jit(solution)/shard_map/while/body/eval_jaxpr/hgqk,khd->qhgd/dot_general | solution.py:75
  1329.5 66.5 %fusion.218 = f32[4096,2,128]{0,2,1:T(8,128)} fusion(f32[2,512,3,4096]{3,1,2,0:T(8,128)} %fusion.216, f32[4096,2,128]{0,2,1:T(8,128)} %get-tuple-element.410, pred[]{:T(512)S(6)} %compare.3, bf16[8,512,2,3,128]{4,1,3,2,0:T(8,128)(2,1)} %get-tuple-element.424, s32[]{:T(128)S(6)} %copy.187, f32[2,3,512,4096]{3,2,1,0:T(8,128)} %get-tuple-element.375, ...), kind=kOutput, calls=%fused_computation.56.clone.2 | convolution fusion | flops 3311410176 | bytes 210534400 | tf_op jit(solution)/shard_map/while/body/eval_jaxpr/hgqk,qhgd->khd/dot_general | solution.py:76
  1396.0 63.5 %fusion.220 = bf16[8,512,2,3,128]{4,1,0,3,2:T(8,128)(2,1)} fusion(bf16[8,512,2,3,128]{4,1,0,3,2:T(8,128)(2,1)} %get-tuple-element.412, s32[]{:T(128)S(6)} %copy.187, bf16[4096,2,128]{2,0,1:T(8,128)(2,1)} %get-tuple-element.426, f32[2,512,3,4096]{3,1,2,0:T(8,128)} %fusion.216, f32[2,3,512,4096]{3,2,1,0:T(8,128)} %get-tuple-element.375, ...), kind=kOutput, calls=%fused_computation.66.clone.1 | convolution fusion | flops 3309706240 | bytes 204242944 | tf_op jit(solution)/shard_map/while/body/eval_jaxpr/hgqk,khd->qhgd/dot_general | solution.py:75
  1531.4 66.5 %fusion.218 = f32[4096,2,128]{0,2,1:T(8,128)} fusion(f32[2,512,3,4096]{3,1,2,0:T(8,128)} %fusion.216, f32[4096,2,128]{0,2,1:T(8,128)} %get-tuple-element.410, pred[]{:T(512)S(6)} %compare.3, bf16[8,512,2,3,128]{4,1,3,2,0:T(8,128)(2,1)} %get-tuple-element.424, s32[]{:T(128)S(6)} %copy.187, f32[2,3,512,4096]{3,2,1,0:T(8,128)} %get-tuple-element.375, ...), kind=kOutput, calls=%fused_computation.56.clone.2 | convolution fusion | flops 3311410176 | bytes 210534400 | tf_op jit(solution)/shard_map/while/body/eval_jaxpr/hgqk,qhgd->khd/dot_general | solution.py:76
  1597.9 63.5 %fusion.220 = bf16[8,512,2,3,128]{4,1,0,3,2:T(8,128)(2,1)} fusion(bf16[8,512,2,3,128]{4,1,0,3,2:T(8,128)(2,1)} %get-tuple-element.412, s32[]{:T(128)S(6)} %copy.187, bf16[4096,2,128]{2,0,1:T(8,128)(2,1)} %get-tuple-element.426, f32[2,512,3,4096]{3,1,2,0:T(8,128)} %fusion.216, f32[2,3,512,4096]{3,2,1,0:T(8,128)} %get-tuple-element.375, ...), kind=kOutput, calls=%fused_computation.66.clone.1 | convolution fusion | flops 3309706240 | bytes 204242944 | tf_op jit(solution)/shard_map/while/body/eval_jaxpr/hgqk,khd->qhgd/dot_general | solution.py:75
  1733.2 66.5 %fusion.218 = f32[4096,2,128]{0,2,1:T(8,128)} fusion(f32[2,512,3,4096]{3,1,2,0:T(8,128)} %fusion.216, f32[4096,2,128]{0,2,1:T(8,128)} %get-tuple-element.410, pred[]{:T(512)S(6)} %compare.3, bf16[8,512,2,3,128]{4,1,3,2,0:T(8,128)(2,1)} %get-tuple-element.424, s32[]{:T(128)S(6)} %copy.187, f32[2,3,512,4096]{3,2,1,0:T(8,128)} %get-tuple-element.375, ...), kind=kOutput, calls=%fused_computation.56.clone.2 | convolution fusion | flops 3311410176 | bytes 210534400 | tf_op jit(solution)/shard_map/while/body/eval_jaxpr/hgqk,qhgd->khd/dot_general | solution.py:76
  1799.7 63.5 %fusion.220 = bf16[8,512,2,3,128]{4,1,0,3,2:T(8,128)(2,1)} fusion(bf16[8,512,2,3,128]{4,1,0,3,2:T(8,128)(2,1)} %get-tuple-element.412, s32[]{:T(128)S(6)} %copy.187, bf16[4096,2,128]{2,0,1:T(8,128)(2,1)} %get-tuple-element.426, f32[2,512,3,4096]{3,1,2,0:T(8,128)} %fusion.216, f32[2,3,512,4096]{3,2,1,0:T(8,128)} %get-tuple-element.375, ...), kind=kOutput, calls=%fused_computation.66.clone.1 | convolution fusion | flops 3309706240 | bytes 204242944 | tf_op jit(solution)/shard_map/while/body/eval_jaxpr/hgqk,khd->qhgd/dot_general | solution.py:75
  1909.0 392.9 %while.26 = (s32[]{:T(128)}, bf16[8,512,2,3,128]{4,1,0,3,2:T(8,128)(2,1)}, s32[8]{0:T(128)S(1)}, bf16[8,512,2,3,128]{4,1,3,2,0:T(8,128)(2,1)}, bf16[4096,2,128]{...) while((s32[]{:T(128)}, bf16[8,512,2,3,128]{4,1,0,3,2:T(8,128)(2,1)}, ...), condition=%wide.region_4.5_spmd.clone, body=%wide.region_1.4_spmd.clone.sunk | while | flops 6520443392 | bytes 110653552 | solution.py:51
  2326.3 83.5 %all-to-all-done.3 = bf16[4096,6,128]{2,1,0:T(8,128)(2,1)} async-done(((bf16[4096,6,128]{2,1,0:T(8,128)(2,1)}), bf16[4096,6,128]{2,1,0:T(8,128)(2,1)}, u32[]{:S(2)}, u32[]{:S(2)}) %all-to-all-start.3) | async-done | bytes 6291488 | tf_op jit(solution)/shard_map/all_to_all | solution.py:118
  2470.7 37.7 all-to-all-done.5
  2555.5 29.6 fusion.137
  2638.1 34.1 fusion.129
  2724.1 1521.5 %all-reduce.3.cloned.1.call-done = (f32[3072,3072]{1,0:T(8,128)}, f32[3072,1024]{1,0:T(8,128)}, f32[3072,1024]{1,0:T(8,128)}, f32[3072,3072]{1,0:T(8,128)}) async-done(((f32[3072,3072]{1,0:T(8,128)}, f32[3072,1024]{1,0:T(8,128)}, f32[3072,1024]{1,0:T(8,128)}, f32[3072,3072]{1,0:T(8,128)}), (f32[3072,3072]{1,0:T(8,128)}, f32[3072,1024]{1,0:T(8,128)}, f32[3072,1024]{1,0:T(8,128)}, ...) | async-done | bytes 100663312 | tf_op jit(solution)/shard_map/psum | solution.py:133
  (244 shorter events, 1514.6 us)
Async XLA Ops:
  11.4 80.1 %copy-start.13 = (f32[1024]{0:T(1024)}, f32[1024]{0:T(1024)S(1)}, u32[]{:S(2)}) copy-start(f32[1024]{0:T(1024)S(1)} %add_rsqrt_fusion) | copy-start | bytes 12292
  11.8 79.8 %copy-start.11 = (f32[3072]{0:T(1024)}, f32[3072]{0:T(1024)S(1)}, u32[]{:S(2)}) copy-start(f32[3072]{0:T(1024)S(1)} %convert_element_type.108) | copy-start | bytes 36868
  22.1 30.1 all-to-all-start.2
  28.5 89.4 %copy-start.4 = (f32[1024,64]{0,1:T(8,128)}, f32[1024,64]{0,1:T(8,128)S(1)}, u32[]{:S(2)}) copy-start(f32[1024,64]{0,1:T(8,128)S(1)} %get-tuple-element.275) | copy-start | bytes 786436
  52.2 33.7 all-to-all-start.1
  85.8 78.7 %all-to-all-start.4 = ((bf16[1024,24,128]{2,0,1:T(8,128)(2,1)}), bf16[1024,24,128]{2,0,1:T(8,128)(2,1)}, u32[]{:S(2)}, u32[]{:S(2)}) async-start(bf16[1024,24,128]{2,0,1:T(8,128)(2,1)} %bitcast.299), calls=%async_computation.4 | async-start | bytes 12582912 | tf_op jit(solution)/shard_map/all_to_all | solution.py:123
  164.6 75.6 %all-to-all-start = ((bf16[1024,24,128]{2,0,1:T(8,128)(2,1)}), bf16[1024,24,128]{2,0,1:T(8,128)(2,1)}, u32[]{:S(2)}, u32[]{:S(2)}) async-start(bf16[1024,24,128]{2,0,1:T(8,128)(2,1)} %pad_maximum_fusion), calls=%async_computation | async-start | bytes 12582912 | tf_op jit(solution)/shard_map/all_to_all | solution.py:114
  250.8 30.3 copy-start.17
  386.7 63.5 %copy-start.18 = (s32[8]{0:T(128)S(1)}, s32[8]{0:T(128)}, u32[]{:S(2)}) copy-start(s32[8]{0:T(128)} %copy-done.17) | copy-start | bytes 100 | tf_op jit(solution)/shard_map/while
  450.3 30.2 copy-start.17
  588.7 63.5 %copy-start.18 = (s32[8]{0:T(128)S(1)}, s32[8]{0:T(128)}, u32[]{:S(2)}) copy-start(s32[8]{0:T(128)} %copy-done.17) | copy-start | bytes 100 | tf_op jit(solution)/shard_map/while
  652.2 30.2 copy-start.17
  790.5 63.5 %copy-start.18 = (s32[8]{0:T(128)S(1)}, s32[8]{0:T(128)}, u32[]{:S(2)}) copy-start(s32[8]{0:T(128)} %copy-done.17) | copy-start | bytes 100 | tf_op jit(solution)/shard_map/while
  992.3 63.5 %copy-start.18 = (s32[8]{0:T(128)S(1)}, s32[8]{0:T(128)}, u32[]{:S(2)}) copy-start(s32[8]{0:T(128)} %copy-done.17) | copy-start | bytes 100 | tf_op jit(solution)/shard_map/while
  1194.1 63.5 %copy-start.18 = (s32[8]{0:T(128)S(1)}, s32[8]{0:T(128)}, u32[]{:S(2)}) copy-start(s32[8]{0:T(128)} %copy-done.17) | copy-start | bytes 100 | tf_op jit(solution)/shard_map/while
  1396.0 63.5 %copy-start.18 = (s32[8]{0:T(128)S(1)}, s32[8]{0:T(128)}, u32[]{:S(2)}) copy-start(s32[8]{0:T(128)} %copy-done.17) | copy-start | bytes 100 | tf_op jit(solution)/shard_map/while
  1597.9 63.5 %copy-start.18 = (s32[8]{0:T(128)S(1)}, s32[8]{0:T(128)}, u32[]{:S(2)}) copy-start(s32[8]{0:T(128)} %copy-done.17) | copy-start | bytes 100 | tf_op jit(solution)/shard_map/while
  1799.7 63.5 %copy-start.18 = (s32[8]{0:T(128)S(1)}, s32[8]{0:T(128)}, u32[]{:S(2)}) copy-start(s32[8]{0:T(128)} %copy-done.17) | copy-start | bytes 100 | tf_op jit(solution)/shard_map/while
  1870.5 29.9 all-to-all-start.6
  1900.4 410.7 %all-to-all-start.7 = ((bf16[4096,2,128]{2,1,0:T(2,128)(2,1)}), bf16[4096,2,128]{2,1,0:T(2,128)(2,1)}, u32[]{:S(2)}, u32[]{:S(2)}) async-start(bf16[4096,2,128]{2,1,0:T(2,128)(2,1)} %copy.148), calls=%async_computation.7 | async-start | bytes 4194304 | tf_op jit(solution)/shard_map/all_to_all | solution.py:127
  2311.0 98.8 %all-to-all-start.3 = ((bf16[4096,6,128]{2,1,0:T(8,128)(2,1)}), bf16[4096,6,128]{2,1,0:T(8,128)(2,1)}, u32[]{:S(2)}, u32[]{:S(2)}) async-start(bf16[4096,6,128]{2,1,0:T(8,128)(2,1)} %copy.133), calls=%async_computation.3 | async-start | bytes 16777216 | tf_op jit(solution)/shard_map/all_to_all | solution.py:118
  2409.8 98.5 %all-to-all-start.5 = ((bf16[4096,6,128]{2,1,0:T(8,128)(2,1)}), bf16[4096,6,128]{2,1,0:T(8,128)(2,1)}, u32[]{:S(2)}, u32[]{:S(2)}) async-start(bf16[4096,6,128]{2,1,0:T(8,128)(2,1)} %copy.141), calls=%async_computation.5 | async-start | bytes 16777216 | tf_op jit(solution)/shard_map/all_to_all | solution.py:125
  2415.5 1830.1 %all-reduce.3.cloned.1.call-start = ((), (), s32[]{:S(2)}) async-start(), calls=%async_computation.8 | async-start | bytes 201326592 | tf_op jit(solution)/shard_map/psum | solution.py:133
  2546.7 38.4 slice-start.4
  (24 other events, 370.6 us)
Sparse Core Ops, SparseCore 0:
  2611.2 1634.3 all-reduce.2
where the time goes:
time: 4340 us; the launch traced here: 4330 us
  matrix products  2170 us (50%)
  waiting for transfers between devices  1730 us (40%)
  local copies, waits for them, and re-layouts  234 us (5%)
  other arithmetic  129 us (3%)
    psum x1, waiting for transfers between devices, local_step(): lax.psum(lax.dot_general(hidden, dq_pre, CONTRACT_ROWS, preferred_element...  1520 us
    dot_general x8, matrix products, one_block(): jnp.einsum('hgqk,qhgd->khd', ds_bf, q_blk, preferred_element_type=jnp.flo...  531 us
    dot_general x8, matrix products, one_block(): jnp.einsum('hgqk,khd->qhgd', ds_bf, k_all, preferred_element_type=jnp.flo...  508 us
    sub x16, matrix products, one_block(): attn_prob = jax.nn.softmax(jnp.where(causal, scores, NEG_LARGE), axis=-1)  417 us
    dot_general x8, matrix products, one_block(): jnp.einsum('hgqk,qhgd->khd', prob_bf, do_blk, preferred_element_type=jnp....  168 us
    dot_general x8, matrix products, one_block(): jnp.einsum('qhgd,khd->hgqk', do_blk, v_all, preferred_element_type=jnp.fl...  164 us
    dot_general x8, matrix products, one_block(): jnp.einsum('hgqk,khd->qhgd', attn_prob.astype(jnp.bfloat16), v_all, prefe...  151 us
    unnamed x52, local copies, waits for them, and re-layouts  98.1 us
  transfers between devices with their start and end apart: 9, of which 6 were waited for; matrix products, arithmetic and copies ran while one was open for 16% of the time, Pallas kernels for 0%

commit v1 on v0

v1 whole, which is shorter than its diff:
```python
import functools
import math

import jax
import jax.numpy as jnp
from jax import lax
from jax.experimental import pallas as pl
from jax.experimental.pallas import tpu as pltpu
from jax.sharding import PartitionSpec as P

HEAD = 128
GROUP = 3
ROPE_THETA = 1000000.0
NORM_EPS = 1e-05
NEG_LARGE = -1e30
BF = jnp.bfloat16
F32 = jnp.float32
SCALE = HEAD ** -0.5
SCALE2 = SCALE * math.log2(math.e)
BLK = 512
VMEM_LIMIT = 62 * 1024 * 1024


def params(n_axes=1, limit=VMEM_LIMIT):
    return pltpu.CompilerParams(dimension_semantics=("arbitrary",) * n_axes, vmem_limit_bytes=limit)


def cost(flops, nbytes, trans=0):
    return pl.CostEstimate(flops=int(flops), bytes_accessed=int(nbytes), transcendentals=int(trans))


def mm(a, b):
    return jnp.dot(a, b, preferred_element_type=F32)


def mm_nt(a, b):
    return lax.dot_general(a, b, (((1,), (1,)), ((), ())), preferred_element_type=F32)


def rotate(val, cos_t, sin_t):
    return val * cos_t + pltpu.roll(val, HEAD // 2, 1) * sin_t


def proj_body(s_ref, x_ref, gain_ref, wq_ref, wk_ref, wv_ref, cos_ref, sin_ref, *rest):
    h_ref, q_ref, k_ref, v_ref = rest[-4:]
    xf = x_ref[...].astype(F32)
    inv = lax.rsqrt(jnp.mean(xf * xf, axis=-1, keepdims=True) + NORM_EPS)
    h_ref[...] = ((xf * inv) * gain_ref[...]).astype(BF)
    h = h_ref[...]
    cos_t, sin_t = cos_ref[...], sin_ref[...]
    for c in range(wq_ref.shape[1] // 256):
        out = mm(h, wq_ref[:, c * 256:(c + 1) * 256])
        for b in range(2):
            part = rotate(out[:, b * HEAD:(b + 1) * HEAD], cos_t, sin_t)
            q_ref[:, c * 256 + b * HEAD:c * 256 + (b + 1) * HEAD] = part.astype(BF)
    out = mm(h, wk_ref[...])
    for b in range(2):
        k_ref[:, b * HEAD:(b + 1) * HEAD] = rotate(out[:, b * HEAD:(b + 1) * HEAD], cos_t, sin_t).astype(BF)
    v_ref[...] = mm(h, wv_ref[...]).astype(BF)


def project(idx, x, gain, w_q, w_k, w_v, cos_t, sin_t, bufs, seq):
    rows, d = x.shape
    bm = min(512, rows)
    nb = rows // bm
    qc, kc = w_q.shape[1] // 4, w_k.shape[1] // 4
    row_map = lambda i, s: (s[0] * nb + i, 0)
    w_map = lambda i, s: (0, s[1])
    in_specs = [pl.BlockSpec((bm, d), lambda i, s: (i, 0)),
                pl.BlockSpec((1, d), lambda i, s: (0, 0)),
                pl.BlockSpec((d, qc), w_map), pl.BlockSpec((d, kc), w_map), pl.BlockSpec((d, kc), w_map),
                pl.BlockSpec((bm, HEAD), row_map), pl.BlockSpec((bm, HEAD), row_map)]
    args = [idx, x, gain, w_q, w_k, w_v, cos_t, sin_t]
    aliases = {}
    if bufs is not None:
        in_specs += [pl.BlockSpec(memory_space=pl.ANY)] * 4
        aliases = {len(args) + n: n for n in range(4)}
        args += list(bufs)
    widths = (d, qc, kc, kc)
    return pl.pallas_call(
        proj_body,
        grid_spec=pltpu.PrefetchScalarGridSpec(
            num_scalar_prefetch=1, grid=(nb,), in_specs=in_specs,
            out_specs=[pl.BlockSpec((bm, w), row_map) for w in widths]),
        out_shape=[jax.ShapeDtypeStruct((seq, w), BF) for w in widths],
        input_output_aliases=aliases,
        compiler_params=params(), name="proj",
        cost_estimate=cost(2 * rows * d * (qc + 2 * kc), rows * d * 4 + d * (qc + 2 * kc) * 2),
    )(*args)


def dout_body(s_ref, dy_ref, wo_ref, *rest):
    dy_out, do_out = rest[-2:]
    dy = dy_ref[...]
    dy_out[...] = dy
    for c in range(wo_ref.shape[0] // 256):
        do_out[:, c * 256:(c + 1) * 256] = mm_nt(dy, wo_ref[c * 256:(c + 1) * 256, :]).astype(BF)


def dout(idx, dy, w_o, bufs, seq):
    rows, d = dy.shape
    bm = min(512, rows)
    nb = rows // bm
    oc = w_o.shape[0] // 4
    row_map = lambda i, s: (s[0] * nb + i, 0)
    in_specs = [pl.BlockSpec((bm, d), lambda i, s: (i, 0)), pl.BlockSpec((oc, d), lambda i, s: (s[1], 0))]
    args = [idx, dy, w_o]
    aliases = {}
    if bufs is not None:
        in_specs += [pl.BlockSpec(memory_space=pl.ANY)] * 2
        aliases = {len(args) + n: n for n in range(2)}
        args += list(bufs)
    return pl.pallas_call(
        dout_body,
        grid_spec=pltpu.PrefetchScalarGridSpec(
            num_scalar_prefetch=1, grid=(nb,), in_specs=in_specs,
            out_specs=[pl.BlockSpec((bm, w), row_map) for w in (d, oc)]),
        out_shape=[jax.ShapeDtypeStruct((seq, w), BF) for w in (d, oc)],
        input_output_aliases=aliases,
        compiler_params=params(), name="dout",
        cost_estimate=cost(2 * rows * d * oc, rows * d * 4 + d * oc * 2),
    )(*args)


def fwd_body(q_ref, k_ref, v_ref, o_ref, lse_ref, qt, vt, s_scr, acc, stat):
    i = pl.program_id(1)
    seq = k_ref.shape[0]

    @pl.when(i == 0)
    def _():
        def tr(c, _):
            vt[:, pl.ds(c * BLK, BLK)] = v_ref[pl.ds(c * BLK, BLK), :].T
            return 0
        lax.fori_loop(0, seq // BLK, tr, 0)

    for h in range(GROUP):
        qt[h] = q_ref[:, h * HEAD:(h + 1) * HEAD].T
    acc[...] = jnp.zeros_like(acc)
    stat[0] = jnp.full(stat.shape[1:], NEG_LARGE, F32)
    stat[2] = jnp.zeros(stat.shape[1:], F32)

    def stage_a(h, j, masked):
        kj = k_ref[pl.ds(pl.multiple_of(j * BLK, BLK), BLK), :]
        s = mm(kj, qt[h])
        if masked:
            keep = lax.broadcasted_iota(jnp.int32, s.shape, 0) <= lax.broadcasted_iota(jnp.int32, s.shape, 1)
            s = jnp.where(keep, s, NEG_LARGE)
        s_scr[h] = s
        m_old = stat[0, h:h + 1]
        m_new = jnp.maximum(m_old, jnp.max(s, axis=0, keepdims=True))
        stat[1, h:h + 1] = jnp.exp2((m_old - m_new) * SCALE2)
        stat[0, h:h + 1] = m_new

    def stage_b(h, j):
        vj = vt[:, pl.ds(pl.multiple_of(j * BLK, BLK), BLK)]
        p = jnp.exp2(s_scr[h] * SCALE2 - stat[0, h:h + 1] * SCALE2)
        alpha = stat[1, h:h + 1]
        stat[2, h:h + 1] = stat[2, h:h + 1] * alpha + jnp.sum(p, axis=0, keepdims=True)
        acc[h] = acc[h] * alpha + mm(vj, p.astype(BF))

    @pl.when(i > 0)
    def _():
        for h in range(GROUP):
            stage_a(h, 0, False)

        def body(j, _):
            for h in range(GROUP):
                stage_b(h, j)
                stage_a(h, j + 1, False)
            return 0
        lax.fori_loop(0, i - 1, body, 0)
        for h in range(GROUP):
            stage_b(h, i - 1)
            stage_a(h, i, True)

    @pl.when(i == 0)
    def _():
        for h in range(GROUP):
            stage_a(h, 0, True)

    for h in range(GROUP):
        stage_b(h, i)
        den = stat[2, h:h + 1]
        o_ref[:, h * HEAD:(h + 1) * HEAD] = (acc[h] / den).T.astype(BF)
        lse_ref[0, h:h + 1, :] = stat[0, h:h + 1] * SCALE2 + jnp.log2(den)
    lse_ref[0, GROUP:, :] = jnp.zeros((8 - GROUP, BLK), F32)


def attn_fwd(q, k, v):
    seq = k.shape[0]
    nq = seq // BLK
    nkv = k.shape[1] // HEAD
    gw = GROUP * HEAD
    tiles = nkv * GROUP * nq * (nq + 1) // 2
    return pl.pallas_call(
        fwd_body, grid=(nkv, nq),
        in_specs=[pl.BlockSpec((BLK, gw), lambda g, i: (i, g)),
                  pl.BlockSpec((seq, HEAD), lambda g, i: (0, g)),
                  pl.BlockSpec((seq, HEAD), lambda g, i: (0, g))],
        out_specs=[pl.BlockSpec((BLK, gw), lambda g, i: (i, g)),
                   pl.BlockSpec((1, 8, BLK), lambda g, i: (g, 0, i))],
        out_shape=[jax.ShapeDtypeStruct(q.shape, BF), jax.ShapeDtypeStruct((nkv, 8, seq), F32)],
        scratch_shapes=[pltpu.VMEM((GROUP, HEAD, BLK), BF), pltpu.VMEM((HEAD, seq), BF),
                        pltpu.VMEM((GROUP, BLK, BLK), F32), pltpu.VMEM((GROUP, HEAD, BLK), F32),
                        pltpu.VMEM((3, 8, BLK), F32)],
        compiler_params=params(2), name="fwd",
        cost_estimate=cost(tiles * BLK * BLK * HEAD * 4, q.size * 4 + k.size * 4, tiles * BLK * BLK),
    )(q, k, v)


def bwd_body(q_ref, do_ref, o_ref, k_ref, v_ref, lse_ref, cos_ref, sin_ref, dq_ref, dk_ref, dv_ref,
             q3, do3, q3t, do3t, lse3, del3, dq3, dkt, dvt):
    i = pl.program_id(1)
    last = pl.num_programs(1) - 1
    seq = k_ref.shape[0]
    nc = BLK // HEAD

    @pl.when(i == 0)
    def _():
        dkt[...] = jnp.zeros_like(dkt)
        dvt[...] = jnp.zeros_like(dvt)

    for h in range(GROUP):
        cols = slice(h * HEAD, (h + 1) * HEAD)
        rows = slice(h * BLK, (h + 1) * BLK)
        qh, doh = q_ref[:, cols], do_ref[:, cols]
        q3[rows, :] = qh
        do3[rows, :] = doh
        q3t[:, rows] = qh.T
        do3t[:, rows] = doh.T
        delta = jnp.sum(doh.astype(F32) * o_ref[:, cols].astype(F32), axis=-1, keepdims=True)
        del3[rows, :] = jnp.broadcast_to(delta, (BLK, HEAD))
        for c in range(nc):
            row = lse_ref[0, h:h + 1, c * HEAD:(c + 1) * HEAD]
            lse3[h * BLK + c * HEAD:h * BLK + (c + 1) * HEAD, :] = jnp.broadcast_to(row, (HEAD, HEAD)).T
    dq3[...] = jnp.zeros_like(dq3)

    def step(j, masked):
        sl = pl.ds(pl.multiple_of(j * BLK, BLK), BLK)
        kj, vj = k_ref[sl, :], v_ref[sl, :]
        s = mm_nt(q3[...], kj)
        dp = mm_nt(do3[...], vj)
        p = jnp.exp2(s * SCALE2 - jnp.concatenate([lse3[...]] * nc, axis=1))
        if masked:
            keep = (lax.broadcasted_iota(jnp.int32, s.shape, 0) % BLK) >= lax.broadcasted_iota(jnp.int32, s.shape, 1)
            p = jnp.where(keep, p, 0.0)
        dvt[:, sl] += mm(do3t[...], p.astype(BF))
        ds = (p * (dp - jnp.concatenate([del3[...]] * nc, axis=1))).astype(BF)
        dkt[:, sl] += mm(q3t[...], ds)
        dq3[...] += mm(ds, kj)

    def body(j, _):
        step(j, False)
        return 0
    lax.fori_loop(0, i, body, 0)
    step(i, True)

    rsl = pl.ds(pl.multiple_of(i * BLK, BLK), BLK)
    for h in range(GROUP):
        val = dq3[h * BLK:(h + 1) * BLK, :] * SCALE
        dq_ref[:, h * HEAD:(h + 1) * HEAD] = rotate(val, cos_ref[rsl, :], -sin_ref[rsl, :]).astype(BF)

    @pl.when(i == last)
    def _():
        def fin(c, _):
            sl = pl.ds(pl.multiple_of(c * BLK, BLK), BLK)
            dk_ref[sl, :] = rotate(dkt[:, sl].T * SCALE, cos_ref[sl, :], -sin_ref[sl, :]).astype(BF)
            dv_ref[sl, :] = dvt[:, sl].T.astype(BF)
            return 0
        lax.fori_loop(0, seq // BLK, fin, 0)


def attn_bwd(q, do, o, k, v, lse, cos_t, sin_t):
    seq = k.shape[0]
    nq = seq // BLK
    nkv = k.shape[1] // HEAD
    gw = GROUP * HEAD
    tiles = nkv * GROUP * nq * (nq + 1) // 2
    qspec = pl.BlockSpec((BLK, gw), lambda g, i: (i, g))
    kspec = pl.BlockSpec((seq, HEAD), lambda g, i: (0, g))
    tspec = pl.BlockSpec((seq, HEAD), lambda g, i: (0, 0))
    m3 = GROUP * BLK
    return pl.pallas_call(
        bwd_body, grid=(nkv, nq),
        in_specs=[qspec, qspec, qspec, kspec, kspec, pl.BlockSpec((1, 8, BLK), lambda g, i: (g, 0, i)), tspec, tspec],
        out_specs=[qspec, kspec, kspec],
        out_shape=[jax.ShapeDtypeStruct(q.shape, BF), jax.ShapeDtypeStruct(k.shape, BF),
                   jax.ShapeDtypeStruct(k.shape, BF)],
        scratch_shapes=[pltpu.VMEM((m3, HEAD), BF), pltpu.VMEM((m3, HEAD), BF),
                        pltpu.VMEM((HEAD, m3), BF), pltpu.VMEM((HEAD, m3), BF),
                        pltpu.VMEM((m3, HEAD), F32), pltpu.VMEM((m3, HEAD), F32), pltpu.VMEM((m3, HEAD), F32),
                        pltpu.VMEM((HEAD, seq), F32), pltpu.VMEM((HEAD, seq), F32)],
        compiler_params=params(2), name="bwd",
        cost_estimate=cost(tiles * BLK * BLK * HEAD * 10, q.size * 8 + k.size * 8, tiles * BLK * BLK),
    )(q, do, o, k, v, lse, cos_t, sin_t)


def out_body(s_ref, x_ref, o0, o1, o2, o3, w_ref, out_ref):
    rows = o0.shape[1]
    acc = x_ref[...].astype(F32)
    for p, o_ref in enumerate((o0, o1, o2, o3)):
        start = pl.multiple_of(s_ref[1 + p] * rows, rows)
        acc = acc + mm(o_ref[...], w_ref[pl.ds(start, rows), :])
    out_ref[...] = acc.astype(BF)


def out_proj(idx, x, pieces, w_o):
    rows, d = x.shape
    hw = pieces[0].shape[1]
    bn = 512
    own = lambda n, s: (s[0], 0)
    loc = lambda n, s: (0, 0)
    return pl.pallas_call(
        out_body,
        grid_spec=pltpu.PrefetchScalarGridSpec(
            num_scalar_prefetch=1, grid=(d // bn,),
            in_specs=[pl.BlockSpec((rows, bn), lambda n, s: (0, n)),
                      pl.BlockSpec((rows, hw), own), pl.BlockSpec((rows, hw), loc),
                      pl.BlockSpec((rows, hw), own), pl.BlockSpec((rows, hw), loc),
                      pl.BlockSpec((w_o.shape[0], bn), lambda n, s: (0, n))],
            out_specs=pl.BlockSpec((rows, bn), lambda n, s: (0, n))),
        out_shape=jax.ShapeDtypeStruct((rows, d), BF),
        compiler_params=params(), name="outp",
        cost_estimate=cost(2 * rows * d * w_o.shape[0], rows * d * 6 + d * d * 2),
    )(idx, x, *pieces, w_o)


def dqkv_body(s_ref, h_ref, dq_ref, dk_ref, dv_ref, *rest):
    outs, ht = rest[-7:-1], rest[-1]
    ht[...] = h_ref[...].T
    for n, src in enumerate((dq_ref, dk_ref, dv_ref)):
        val = mm(ht[...], src[...])
        outs[n][...] = val
        outs[n + 3][...] = val


def dw_qkv(idx, h, dq, dk, dv, bufs):
    seq, d = h.shape
    bm = 256
    ws = (dq.shape[1], dk.shape[1], dv.shape[1])
    in_specs = [pl.BlockSpec((seq, bm), lambda i, s: (0, i))] + \
        [pl.BlockSpec((seq, w), lambda i, s: (0, 0)) for w in ws]
    args = [idx, h, dq, dk, dv]
    aliases = {}
    if bufs is not None:
        in_specs += [pl.BlockSpec(memory_space=pl.ANY)] * 3
        aliases = {len(args) + n: n for n in range(3)}
        args += list(bufs)
    return pl.pallas_call(
        dqkv_body,
        grid_spec=pltpu.PrefetchScalarGridSpec(
            num_scalar_prefetch=1, grid=(d // bm,), in_specs=in_specs,
            out_specs=[pl.BlockSpec((bm, w), lambda i, s: (i, s[0])) for w in ws]
            + [pl.BlockSpec((bm, w), lambda i, s: (i, 0)) for w in ws],
            scratch_shapes=[pltpu.VMEM((bm, seq), BF)]),
        out_shape=[jax.ShapeDtypeStruct((d, 4 * w), F32) for w in ws] + [jax.ShapeDtypeStruct((d, w), F32) for w in ws],
        input_output_aliases=aliases,
        compiler_params=params(), name="dwqkv",
        cost_estimate=cost(2 * seq * d * sum(ws), seq * (d + sum(ws)) * 2 + d * sum(ws) * 8),
    )(*args)


def dwo_body(s_ref, o_ref, dy_ref, *rest):
    fin, snd, ot = rest[-3:]

    @pl.when(pl.program_id(0) == 0)
    def _():
        def tr(c, _):
            sl = pl.ds(pl.multiple_of(c * BLK, BLK), BLK)
            ot[:, sl] = o_ref[sl, :].T
            return 0
        lax.fori_loop(0, o_ref.shape[0] // BLK, tr, 0)
    val = mm(ot[...], dy_ref[...])
    fin[...] = val
    snd[...] = val


def dw_o(idx, o, dy, buf):
    seq, d = dy.shape
    hw = o.shape[1]
    bn = 512
    in_specs = [pl.BlockSpec((seq, hw), lambda i, s: (0, 0)), pl.BlockSpec((seq, bn), lambda i, s: (0, i))]
    args = [idx, o, dy]
    aliases = {}
    if buf is not None:
        in_specs += [pl.BlockSpec(memory_space=pl.ANY)]
        aliases = {len(args): 0}
        args += [buf]
    return pl.pallas_call(
        dwo_body,
        grid_spec=pltpu.PrefetchScalarGridSpec(
            num_scalar_prefetch=1, grid=(d // bn,), in_specs=in_specs,
            out_specs=[pl.BlockSpec((hw, bn), lambda i, s: (s[0], i)), pl.BlockSpec((hw, bn), lambda i, s: (0, i))],
            scratch_shapes=[pltpu.VMEM((hw, seq), BF)]),
        out_shape=[jax.ShapeDtypeStruct((4 * hw, d), F32), jax.ShapeDtypeStruct((hw, d), F32)],
        input_output_aliases=aliases,
        compiler_params=params(), name="dwo",
        cost_estimate=cost(2 * seq * d * hw, seq * (d + hw) * 2 + d * hw * 8),
    )(*args)


def dx_body(s_ref, x_ref, dy_ref, gain_ref, *rest):
    pieces = rest[:12]
    wq_ref, wk_ref, wv_ref, dx_ref, dg_ref, acc = rest[12:]
    n = pl.program_id(0)
    bn = wq_ref.shape[0]
    val = None
    for p in range(4):
        dev = s_ref[1 + p]
        for src, w_ref in zip(pieces[3 * p:3 * p + 3], (wq_ref, wk_ref, wv_ref)):
            w = src.shape[1]
            part = mm_nt(src[...], w_ref[:, pl.ds(pl.multiple_of(dev * w, w), w)])
            val = part if val is None else val + part
    acc[:, pl.ds(pl.multiple_of(n * bn, bn), bn)] = val

    @pl.when(n == pl.num_programs(0) - 1)
    def _():
        step = 128
        gain = gain_ref[...]

        def epi(r, dg):
            sl = pl.ds(pl.multiple_of(r * step, step), step)
            xf = x_ref[sl, :].astype(F32)
            inv = lax.rsqrt(jnp.mean(xf * xf, axis=-1, keepdims=True) + NORM_EPS)
            normed = xf * inv
            dh = acc[sl, :]
            dn = dh * gain
            dxn = inv * (dn - normed * jnp.mean(dn * normed, axis=-1, keepdims=True))
            dx_ref[sl, :] = (dy_ref[sl, :].astype(F32) + dxn).astype(BF)
            return dg + jnp.sum(dh * normed, axis=0, keepdims=True)
        dg_ref[...] = lax.fori_loop(0, x_ref.shape[0] // step, epi, jnp.zeros(dg_ref.shape, F32))


def dx_call(idx, x, dy, gain, pieces, w_q, w_k, w_v):
    rows, d = x.shape
    bn = 512
    ws = (w_q.shape[1], w_k.shape[1], w_v.shape[1])
    own = lambda n, s: (s[0], 0)
    loc = lambda n, s: (0, 0)
    piece_specs = []
    for p in range(4):
        for w in ws:
            piece_specs.append(pl.BlockSpec((rows, w // 4), own if p % 2 == 0 else loc))
    return pl.pallas_call(
        dx_body,
        grid_spec=pltpu.PrefetchScalarGridSpec(
            num_scalar_prefetch=1, grid=(d // bn,),
            in_specs=[pl.BlockSpec((rows, d), loc), pl.BlockSpec((rows, d), loc), pl.BlockSpec((1, d), loc)]
            + piece_specs + [pl.BlockSpec((bn, w), lambda n, s: (n, 0)) for w in ws],
            out_specs=[pl.BlockSpec((rows, d), loc), pl.BlockSpec((1, d), loc)],
            scratch_shapes=[pltpu.VMEM((rows, d), F32)]),
        out_shape=[jax.ShapeDtypeStruct((rows, d), BF), jax.ShapeDtypeStruct((1, d), F32)],
        compiler_params=params(), name="dx",
        cost_estimate=cost(2 * rows * d * sum(ws), rows * d * 6 + d * sum(ws) * 2),
    )(idx, x, dy, gain, *[a for piece in pieces for a in piece], w_q, w_k, w_v)


def solution(mesh):
    sp = mesh.shape['sp']
    cross = [(a, a ^ 2) for a in range(sp)]
    pair = [(a, a ^ 1) for a in range(sp)]

    def over(val):
        return lax.ppermute(val, 'sp', cross)

    def near(val):
        return lax.ppermute(val, 'sp', pair)

    def after(val, *deps):
        return lax.optimization_barrier((val,) + deps)[0]

    def local_step(x, dy, positions, gain, w_q, w_k, w_v, w_o):
        j = lax.axis_index('sp').astype(jnp.int32)
        rows, d = x.shape
        seq = rows * sp
        dev = [j, j ^ 1, j ^ 2, j ^ 3]
        vec = lambda *vals: jnp.stack([jnp.asarray(v, jnp.int32) for v in vals])
        gain_f = gain.astype(F32).reshape(1, d)

        x2 = over(x)
        x1 = near(x)
        x3 = near(x2)
        dy2 = over(after(dy, x2))
        dy1 = near(after(dy, x1))
        dy3 = near(dy2)

        pos = lax.all_gather(positions, 'sp', tiled=True)
        inv_freq = ROPE_THETA ** (-jnp.arange(0, HEAD, 2).astype(F32) / HEAD)
        angles = pos.astype(F32)[:, None] * inv_freq[None, :]
        cos_h, sin_h = jnp.cos(angles), jnp.sin(angles)
        cos_t = jnp.concatenate([cos_h, cos_h], axis=1)
        sin_t = jnp.concatenate([-sin_h, sin_h], axis=1)

        bufs = None
        for p, xp in enumerate((x, x1, x2, x3)):
            bufs = project(vec(dev[p], j), xp, gain_f, w_q, w_k, w_v, cos_t, sin_t, bufs, seq)
        h_all, q, k, v = bufs
        o, lse = attn_fwd(q, k, v)

        dbufs = None
        for p, dyp in enumerate((dy, dy1, dy2, dy3)):
            dbufs = dout(vec(dev[p], j), dyp, w_o, dbufs, seq)
        dy_all, do = dbufs

        def rows_of(val, blk):
            return lax.dynamic_slice_in_dim(val, blk * rows, rows, 0)

        ox = over(after(o, dy2))
        o1 = near(rows_of(o, dev[1]))
        o3 = near(rows_of(ox, dev[1]))
        result = out_proj(vec(j, *dev), x, (o, o1, ox, o3), w_o)

        dq, dk, dv = attn_bwd(q, do, o, k, v, lse, cos_t, sin_t)
        grads = (dq, dk, dv)
        gx = tuple(over(g) for g in grads)
        g1 = tuple(near(rows_of(g, dev[1])) for g in grads)
        g3 = tuple(near(rows_of(g, dev[1])) for g in gx)

        wo_fin, wo_a = dw_o(vec(j), o, dy_all, None)
        wo_fin, wo_b = dw_o(vec(dev[2]), ox, dy_all, wo_fin)
        wo_1, wo_3 = near(wo_a), near(wo_b)
        wo_fin = lax.dynamic_update_slice(wo_fin, wo_1, (dev[1] * wo_1.shape[0], 0))
        wo_fin = lax.dynamic_update_slice(wo_fin, wo_3, (dev[3] * wo_3.shape[0], 0))

        res_a = dw_qkv(vec(j), h_all, *grads, None)
        res_b = dw_qkv(vec(dev[2]), h_all, *gx, res_a[:3])
        fins = []
        for n in range(3):
            fin = res_b[n]
            ra, rb = near(res_a[3 + n]), near(res_b[3 + n])
            fin = lax.dynamic_update_slice(fin, ra, (0, dev[1] * ra.shape[1]))
            fin = lax.dynamic_update_slice(fin, rb, (0, dev[3] * rb.shape[1]))
            fins.append(fin)

        grad_x, dg = dx_call(vec(j, *dev), x, dy, gain_f, (grads, g1, gx, g3), w_q, w_k, w_v)
        grad_gain = lax.psum(dg.reshape(d), 'sp')
        return result, grad_x, fins[0], fins[1], fins[2], wo_fin, grad_gain

    seq_spec = P(('dp', 'sp'), None)
    whole = P(None, None)
    part_rows = P('dp', None)
    return jax.shard_map(local_step, mesh=mesh,
                         in_specs=(seq_spec, seq_spec, P(('dp', 'sp')), P(None), whole, whole, whole, whole),
                         out_specs=(seq_spec, seq_spec, part_rows, part_rows, part_rows, part_rows, P('dp')),
                         check_vma=False)
```

time: 4340 us -> 1080 us (0.25)
  matrix products: 2170 us -> 0 us
  waiting for transfers between devices: 1730 us -> 252 us
  Pallas kernels: 0 us -> 579 us
  local copies, waits for them, and re-layouts: 234 us -> 64.7 us
  blocking collectives: 12.1 us -> 151 us
  other arithmetic: 129 us -> 13.6 us
    dot_general x52 -> x0, matrix products: 1750 us -> none  [the longest x8 531 us: one_block(): jnp.einsum('hgqk,qhgd->khd', ds_bf, q_blk, preferred_element_type=jnp.flo...]
    psum x1 -> x0, waiting for transfers between devices: 1520 us -> none  [local_step(): lax.psum(lax.dot_general(hidden, dq_pre, CONTRACT_ROWS, preferred_element...]
    pallas_call x0 -> x16, Pallas kernels: none -> 579 us  [the longest x1 162 us: attn_bwd(): pl.pallas_call(bwd_body, grid=(nkv, nq), in_specs=[qspec, qspec, qspec, k...]
    sub x16 -> x0, matrix products: 417 us -> none  [one_block(): attn_prob = jax.nn.softmax(jnp.where(causal, scores, NEG_LARGE), axis=-1)]
    ppermute x0 -> x26, waiting for transfers between devices: none -> 252 us  [the longest x6 247 us: over(): return lax.ppermute(val, 'sp', cross)]
    all_to_all x8 -> x0, waiting for transfers between devices: 207 us -> none  [the longest x1 83.5 us: local_step(): lax.all_to_all(o_all.reshape(seq_len, q_loc, HEAD_DIM), 'sp', 0, 1, tiled...]
    all_gather x0 -> x1, blocking collectives: none -> 138 us  [local_step(): pos = lax.all_gather(positions, 'sp', tiled=True)]
    unnamed x52 -> x2, local copies, waits for them, and re-layouts: 98.1 us -> 0.01 us
  transfers between devices with their start and end apart: 9 -> 26, of which waited for: 6 -> 4; matrix products, arithmetic and copies ran while one was open for 16% -> 7% of each run, Pallas kernels for 0% -> 54%
where the time goes in v1:
time: 1080 us; the launch traced here: 1070 us
  Pallas kernels  579 us (54%)
  waiting for transfers between devices  252 us (23%)
  blocking collectives  151 us (14%)
  local copies, waits for them, and re-layouts  64.7 us (6%)
  other arithmetic  13.6 us (1%)
  starting transfers between devices  13.3 us (1%)
    ppermute x6, waiting for transfers between devices, over(): return lax.ppermute(val, 'sp', cross)  247 us
    pallas_call x1, Pallas kernels, attn_bwd(): pl.pallas_call(bwd_body, grid=(nkv, nq), in_specs=[qspec, qspec, qspec, k...  162 us
    all_gather x1, blocking collectives, local_step(): pos = lax.all_gather(positions, 'sp', tiled=True)  138 us
    pallas_call x1, Pallas kernels, attn_fwd(): pl.pallas_call(fwd_body, grid=(nkv, nq), in_specs=[pl.BlockSpec((BLK, gw)...  83.8 us
    pallas_call x2, Pallas kernels, dw_qkv(): pl.pallas_call(dqkv_body, grid_spec=pltpu.PrefetchScalarGridSpec(num_scal...  82.1 us
    pallas_call x4, Pallas kernels, project(): pl.pallas_call(proj_body, grid_spec=pltpu.PrefetchScalarGridSpec(num_scal...  69.6 us
    pallas_call x2, Pallas kernels, dw_o(): pl.pallas_call(dwo_body, grid_spec=pltpu.PrefetchScalarGridSpec(num_scala...  57.6 us
    pallas_call x1, Pallas kernels, dx_call(): pl.pallas_call(dx_body, grid_spec=pltpu.PrefetchScalarGridSpec(num_scalar...  57.1 us
  transfers between devices with their start and end apart: 26, of which 4 were waited for; matrix products, arithmetic and copies ran while one was open for 7% of the time, Pallas kernels for 54%

profile of v1, /device:TPU:0, one launch (start us, length us, event | category | flops | bytes accessed | tf_op | source)
XLA Modules:
  0.0 1074.9 jit_solution(1869210743157236073)
XLA Ops:
  4.0 135.5 %collective-permute-done.x_ref = bf16[1024,3072]{1,0:T(8,128)(2,1)} collective-permute-done((bf16[1024,3072]{1,0:T(8,128)(2,1)}, bf16[1024,3072]{1,0:T(8,128)(2,1)}, u32[]{:S(2)}, u32[]{:S(2)}) %collective-permute-start) | collective-permute-done | bytes 6291488 | tf_op jit(solution)/shard_map/ppermute | solution.py:464
  141.3 138.4 %all_gather.3 = s32[4096]{0:T(1024)S(1)} all-gather(s32[1024]{0:T(1024)} %param.10), channel_id=1, replica_groups=mesh['dp'=2,'sp'=4] {'sp'}, dimensions={0}, use_global_device_ids=true | all-gather | bytes 20480 | tf_op jit(solution)/shard_map/all_gather | solution.py:487
  290.9 10.2 dout.4
  301.7 17.4 %proj.4 = (bf16[4096,3072]{1,0:T(8,128)(2,1)}, bf16[4096,768]{1,0:T(8,128)(2,1)}, bf16[4096,256]{1,0:T(8,128)(2,1)}, bf16[4096,256]{1,0:T(8,128)(2,1)}) custom-call(s32[2]{0:T(128)} %pad_add_fusion.3.s_ref, bf16[1024,3072]{1,0:T(8,128)(2,1)} %x_ref.5, f32[1,3072]{1,0:T(1,128)} %bitcast.6, bf16[3072,3072]{1,0:T(8,128)(2,1)} %rest_12_.1, ...), custom_call_target="tpu_custom_call" | custom-call | flops 8053063680 | bytes 20447232 | tf_op jit(solution)/shard_map/proj/pallas_call | solution.py:80
  321.4 17.5 %proj.5 = (bf16[4096,3072]{1,0:T(8,128)(2,1)}, bf16[4096,768]{1,0:T(8,128)(2,1)}, bf16[4096,256]{1,0:T(8,128)(2,1)}, bf16[4096,256]{1,0:T(8,128)(2,1)}) custom-call(s32[2]{0:T(128)} %pad_add_fusion.2.s_ref, bf16[1024,3072]{1,0:T(8,128)(2,1)} %collective-permute-done.2.x_ref, ...), custom_call_target="tpu_custom_call", output_to_operand_aliasing={{0}: (8, {}), {1}: (9, {}), {2}: (10, {}), {3}: (11, {})} | custom-call | flops 8053063680 | bytes 20447232 | tf_op jit(solution)/shard_map/proj/pallas_call | solution.py:80
  338.9 17.4 %proj.6 = (bf16[4096,3072]{1,0:T(8,128)(2,1)}, bf16[4096,768]{1,0:T(8,128)(2,1)}, bf16[4096,256]{1,0:T(8,128)(2,1)}, bf16[4096,256]{1,0:T(8,128)(2,1)}) custom-call(s32[2]{0:T(128)} %pad_add_fusion.1.s_ref, bf16[1024,3072]{1,0:T(8,128)(2,1)} %collective-permute-done.x_ref, ...), custom_call_target="tpu_custom_call", output_to_operand_aliasing={{0}: (8, {}), {1}: (9, {}), {2}: (10, {}), {3}: (11, {})} | custom-call | flops 8053063680 | bytes 20447232 | tf_op jit(solution)/shard_map/proj/pallas_call | solution.py:80
  356.2 17.4 %proj.7 = (bf16[4096,3072]{1,0:T(8,128)(2,1)}, bf16[4096,768]{1,0:T(8,128)(2,1)}, bf16[4096,256]{1,0:T(8,128)(2,1)}, bf16[4096,256]{1,0:T(8,128)(2,1)}) custom-call(s32[2]{0:T(128)} %pad_add_fusion.s_ref, bf16[1024,3072]{1,0:T(8,128)(2,1)} %collective-permute-done.1.x_ref, ...), custom_call_target="tpu_custom_call", output_to_operand_aliasing={{0}: (8, {}), {1}: (9, {}), {2}: (10, {}), {3}: (11, {})} | custom-call | flops 8053063680 | bytes 20447232 | tf_op jit(solution)/shard_map/proj/pallas_call | solution.py:80
  373.6 83.8 %fwd.1 = (bf16[4096,768]{1,0:T(8,128)(2,1)}, f32[2,8,4096]{2,1,0:T(8,128)}) custom-call(bf16[4096,768]{1,0:T(8,128)(2,1)} %get-tuple-element.69.q_ref, bf16[4096,256]{1,0:T(8,128)(2,1)} %get-tuple-element.70.k_ref, bf16[4096,256]{1,0:T(8,128)(2,1)} %get-tuple-element.71.v_ref), custom_call_target="tpu_custom_call" | custom-call | flops 28991029248 | bytes 16777216 | tf_op jit(solution)/shard_map/fwd/pallas_call | solution.py:195
  460.4 10.2 dout.5
  470.6 10.2 dout.6
  480.7 10.2 dout.7
  490.9 161.7 %bwd.1 = (bf16[4096,768]{1,0:T(8,128)(2,1)}, bf16[4096,256]{1,0:T(8,128)(2,1)}, bf16[4096,256]{1,0:T(8,128)(2,1)}) custom-call(bf16[4096,768]{1,0:T(8,128)(2,1)} %get-tuple-element.69.q_ref, bf16[4096,768]{1,0:T(8,128)(2,1)} %get-tuple-element.82.do_ref, bf16[4096,768]{1,0:T(8,128)(2,1)} %get-tuple-element.74.o0.o_ref, ...), custom_call_target="tpu_custom_call" | custom-call | flops 72477573120 | bytes 33554432 | tf_op jit(solution)/shard_map/bwd/pallas_call | solution.py:283
  661.8 41.0 %dwqkv.2 = (f32[3072,3072]{1,0:T(8,128)}, f32[3072,1024]{1,0:T(8,128)}, f32[3072,1024]{1,0:T(8,128)}, f32[3072,768]{1,0:T(8,128)}, f32[3072,256]{1,0:T(8,128)}, /*index=5*/f32[3072,256]{1,0:T(8,128)}) custom-call(s32[1]{0:T(128)} %bitcast.s_ref, bf16[4096,3072]{1,0:T(8,128)(2,1)} %get-tuple-element.88.h_ref, ...), custom_call_target="tpu_custom_call" | custom-call | flops 32212254720 | bytes 67108864 | tf_op jit(solution)/shard_map/dwqkv/pallas_call | solution.py:349
  703.4 42.8 %collective-permute-done.14.rest_8_.dv_ref = bf16[4096,256]{1,0:T(8,128)(2,1)} collective-permute-done((bf16[4096,256]{1,0:T(8,128)(2,1)}, bf16[4096,256]{1,0:T(8,128)(2,1)}, u32[]{:S(2)}, u32[]{:S(2)}) %collective-permute-start.14) | collective-permute-done | bytes 2097184 | tf_op jit(solution)/shard_map/ppermute | solution.py:464
  746.1 28.8 %dwo.2 = (f32[3072,3072]{1,0:T(8,128)}, f32[768,3072]{1,0:T(8,128)}) custom-call(s32[1]{0:T(128)} %bitcast.s_ref, bf16[4096,768]{1,0:T(8,128)(2,1)} %get-tuple-element.74.o0.o_ref, bf16[4096,3072]{1,0:T(8,128)(2,1)} %get-tuple-element.101.dy_ref), custom_call_target="tpu_custom_call" | custom-call | flops 19327352832 | bytes 50331648 | tf_op jit(solution)/shard_map/dwo/pallas_call | solution.py:389
  782.3 28.8 %dwo.3 = (f32[3072,3072]{1,0:T(8,128)}, f32[768,3072]{1,0:T(8,128)}) custom-call(s32[1]{0:T(128)} %bitcast.2.s_ref, bf16[4096,768]{1,0:T(8,128)(2,1)} %collective-permute-done.5.o2.o_ref, bf16[4096,3072]{1,0:T(8,128)(2,1)} %get-tuple-element.101.dy_ref, f32[3072,3072]{1,0:T(8,128)} %get-tuple-element.102.rest_0_), custom_call_target="tpu_custom_call", output_to_operand_aliasing={{0}: (3, {})} | custom-call | flops 19327352832 | bytes 50331648 | tf_op jit(solution)/shard_map/dwo/pallas_call | solution.py:389
  811.1 69.1 %collective-permute-done.12.rest_6_.dq_ref = bf16[4096,768]{1,0:T(8,128)(2,1)} collective-permute-done((bf16[4096,768]{1,0:T(8,128)(2,1)}, bf16[4096,768]{1,0:T(8,128)(2,1)}, u32[]{:S(2)}, u32[]{:S(2)}) %collective-permute-start.12) | collective-permute-done | bytes 6291488 | tf_op jit(solution)/shard_map/ppermute | solution.py:464
  882.9 41.1 %dwqkv.3 = (f32[3072,3072]{1,0:T(8,128)}, f32[3072,1024]{1,0:T(8,128)}, f32[3072,1024]{1,0:T(8,128)}, f32[3072,768]{1,0:T(8,128)}, f32[3072,256]{1,0:T(8,128)}, /*index=5*/f32[3072,256]{1,0:T(8,128)}) custom-call(s32[1]{0:T(128)} %bitcast.2.s_ref, ...), custom_call_target="tpu_custom_call", output_to_operand_aliasing={{0}: (5, {}), {1}: (6, {}), {2}: (7, {})} | custom-call | flops 32212254720 | bytes 67108864 | tf_op jit(solution)/shard_map/dwqkv/pallas_call | solution.py:349
  929.4 26.4 %outp.1 = bf16[1024,3072]{1,0:T(8,128)(2,1)} custom-call(s32[5]{0:T(128)} %stack.22.s_ref, bf16[1024,3072]{1,0:T(8,128)(2,1)} %x_ref.5, bf16[4096,768]{1,0:T(8,128)(2,1)} %get-tuple-element.74.o0.o_ref, bf16[1024,768]{1,0:T(8,128)(2,1)} %collective-permute-done.3.o1, bf16[4096,768]{1,0:T(8,128)(2,1)} %collective-permute-done.5.o2.o_ref, ...), custom_call_target="tpu_custom_call" | custom-call | flops 19327352832 | bytes 37748736 | tf_op jit(solution)/shard_map/outp/pallas_call | solution.py:313
  963.6 57.1 %dx.1 = (bf16[1024,3072]{1,0:T(8,128)(2,1)}, f32[1,3072]{1,0:T(1,128)}) custom-call(s32[5]{0:T(128)} %stack.22.s_ref, bf16[1024,3072]{1,0:T(8,128)(2,1)} %x_ref.5, bf16[1024,3072]{1,0:T(8,128)(2,1)} %dy_ref.3, f32[1,3072]{1,0:T(1,128)} %bitcast.10, bf16[4096,768]{1,0:T(8,128)(2,1)} %get-tuple-element.84.rest_0_.dq_ref, ...), custom_call_target="tpu_custom_call" | custom-call | flops 32212254720 | bytes 50331648 | tf_op jit(solution)/shard_map/dx/pallas_call | solution.py:444
  1020.6 13.1 %psum.7 = f32[3072]{0:T(1024)} all-reduce(f32[3072]{0:T(1024)} %bitcast.11), channel_id=1, replica_groups=mesh['dp'=2,'sp'=4] {'sp'}, use_global_device_ids=true, to_apply=%region_0.0 | all-reduce | flops 3072 | bytes 24576 | tf_op jit(solution)/shard_map/psum | solution.py:536
  1041.2 8.0 constant_dynamic-update-slice_fusion.7
  1049.3 8.6 constant_dynamic-update-slice_fusion.1
  1057.9 8.6 constant_dynamic-update-slice_fusion
  (74 shorter events, 70.6 us)
Async XLA Ops:
  0.6 138.9 %collective-permute-start = (bf16[1024,3072]{1,0:T(8,128)(2,1)}, bf16[1024,3072]{1,0:T(8,128)(2,1)}, u32[]{:S(2)}, u32[]{:S(2)}) collective-permute-start(bf16[1024,3072]{1,0:T(8,128)(2,1)} %x_ref.5), channel_id=1, source_target_pairs={{0,2},{1,3},{2,0},{3,1},{4,6},{5,7},{6,4},{7,5}} | collective-permute-start | bytes 18874376 | tf_op jit(solution)/shard_map/ppermute | solution.py:464
  4.0 286.9 %collective-permute-start.2 = (bf16[1024,3072]{1,0:T(8,128)(2,1)}, bf16[1024,3072]{1,0:T(8,128)(2,1)}, u32[]{:S(2)}, u32[]{:S(2)}) collective-permute-start(bf16[1024,3072]{1,0:T(8,128)(2,1)} %x_ref.5), channel_id=1, source_target_pairs={{0,1},{1,0},{2,3},{3,2},{4,5},{5,4},{6,7},{7,6}} | collective-permute-start | bytes 18874376 | tf_op jit(solution)/shard_map/ppermute | solution.py:467
  139.5 179.6 %collective-permute-start.4 = (bf16[1024,3072]{1,0:T(8,128)(2,1)}, bf16[1024,3072]{1,0:T(8,128)(2,1)}, u32[]{:S(2)}, u32[]{:S(2)}) collective-permute-start(bf16[1024,3072]{1,0:T(8,128)(2,1)} %dy_ref.3), channel_id=1, source_target_pairs={{0,2},{1,3},{2,0},{3,1},{4,6},{5,7},{6,4},{7,5}} | collective-permute-start | bytes 18874376 | tf_op jit(solution)/shard_map/ppermute | solution.py:464
  141.2 215.0 %collective-permute-start.1 = (bf16[1024,3072]{1,0:T(8,128)(2,1)}, bf16[1024,3072]{1,0:T(8,128)(2,1)}, u32[]{:S(2)}, u32[]{:S(2)}) collective-permute-start(bf16[1024,3072]{1,0:T(8,128)(2,1)} %collective-permute-done.x_ref), channel_id=1, source_target_pairs={{0,1},{1,0},{2,3},{3,2},{4,5},{5,4},{6,7},{7,6}} | collective-permute-start | bytes 18874376 | tf_op jit(solution)/shard_map/ppermute | solution.py:467
  290.9 169.5 %collective-permute-start.8 = (bf16[1024,3072]{1,0:T(8,128)(2,1)}, bf16[1024,3072]{1,0:T(8,128)(2,1)}, u32[]{:S(2)}, u32[]{:S(2)}) collective-permute-start(bf16[1024,3072]{1,0:T(8,128)(2,1)} %dy_ref.3), channel_id=1, source_target_pairs={{0,1},{1,0},{2,3},{3,2},{4,5},{5,4},{6,7},{7,6}} | collective-permute-start | bytes 18874376 | tf_op jit(solution)/shard_map/ppermute | solution.py:467
  319.1 161.6 %collective-permute-start.7 = (bf16[1024,3072]{1,0:T(8,128)(2,1)}, bf16[1024,3072]{1,0:T(8,128)(2,1)}, u32[]{:S(2)}, u32[]{:S(2)}) collective-permute-start(bf16[1024,3072]{1,0:T(8,128)(2,1)} %collective-permute-done.4.dy_ref), channel_id=1, source_target_pairs={{0,1},{1,0},{2,3},{3,2},{4,5},{5,4},{6,7},{7,6}} | collective-permute-start | bytes 18874376 | tf_op jit(solution)/shard_map/ppermute | solution.py:467
  460.1 242.7 %collective-permute-start.3 = (bf16[1024,768]{1,0:T(8,128)(2,1)}, bf16[1024,768]{1,0:T(8,128)(2,1)}, u32[]{:S(2)}, u32[]{:S(2)}) collective-permute-start(bf16[1024,768]{1,0:T(8,128)(2,1)} %constant_dynamic-slice_fusion.7), channel_id=1, source_target_pairs={{0,1},{1,0},{2,3},{3,2},{4,5},{5,4},{6,7},{7,6}} | collective-permute-start | bytes 4718600 | tf_op jit(solution)/shard_map/ppermute | solution.py:467
  460.1 198.3 %collective-permute-start.5 = (bf16[4096,768]{1,0:T(8,128)(2,1)}, bf16[4096,768]{1,0:T(8,128)(2,1)}, u32[]{:S(2)}, u32[]{:S(2)}) collective-permute-start(bf16[4096,768]{1,0:T(8,128)(2,1)} %get-tuple-element.74.o0.o_ref), channel_id=1, source_target_pairs={{0,2},{1,3},{2,0},{3,1},{4,6},{5,7},{6,4},{7,5}} | collective-permute-start | bytes 18874376 | tf_op jit(solution)/shard_map/ppermute | solution.py:464
  652.7 50.4 %collective-permute-start.13 = (bf16[4096,256]{1,0:T(8,128)(2,1)}, bf16[4096,256]{1,0:T(8,128)(2,1)}, u32[]{:S(2)}, u32[]{:S(2)}) collective-permute-start(bf16[4096,256]{1,0:T(8,128)(2,1)} %get-tuple-element.85.rest_1_.dk_ref), channel_id=1, source_target_pairs={{0,2},{1,3},{2,0},{3,1},{4,6},{5,7},{6,4},{7,5}} | collective-permute-start | bytes 6291464 | tf_op jit(solution)/shard_map/ppermute | solution.py:464
  654.5 91.7 %collective-permute-start.14 = (bf16[4096,256]{1,0:T(8,128)(2,1)}, bf16[4096,256]{1,0:T(8,128)(2,1)}, u32[]{:S(2)}, u32[]{:S(2)}) collective-permute-start(bf16[4096,256]{1,0:T(8,128)(2,1)} %get-tuple-element.86.rest_2_.dv_ref), channel_id=1, source_target_pairs={{0,2},{1,3},{2,0},{3,1},{4,6},{5,7},{6,4},{7,5}} | collective-permute-start | bytes 6291464 | tf_op jit(solution)/shard_map/ppermute | solution.py:464
  660.0 121.8 %collective-permute-start.6 = (bf16[1024,768]{1,0:T(8,128)(2,1)S(1)}, bf16[1024,768]{1,0:T(8,128)(2,1)}, u32[]{:S(2)}, u32[]{:S(2)}) collective-permute-start(bf16[1024,768]{1,0:T(8,128)(2,1)S(1)} %constant_dynamic-slice_fusion.6), channel_id=1, source_target_pairs={{0,1},{1,0},{2,3},{3,2},{4,5},{5,4},{6,7},{7,6}} | collective-permute-start | bytes 4718600 | tf_op jit(solution)/shard_map/ppermute | solution.py:467
  660.0 220.2 %collective-permute-start.12 = (bf16[4096,768]{1,0:T(8,128)(2,1)}, bf16[4096,768]{1,0:T(8,128)(2,1)}, u32[]{:S(2)}, u32[]{:S(2)}) collective-permute-start(bf16[4096,768]{1,0:T(8,128)(2,1)} %get-tuple-element.84.rest_0_.dq_ref), channel_id=1, source_target_pairs={{0,2},{1,3},{2,0},{3,1},{4,6},{5,7},{6,4},{7,5}} | collective-permute-start | bytes 18874376 | tf_op jit(solution)/shard_map/ppermute | solution.py:464
  702.8 78.5 %collective-permute-start.10 = (bf16[1024,256]{1,0:T(8,128)(2,1)}, bf16[1024,256]{1,0:T(8,128)(2,1)}, u32[]{:S(2)}, u32[]{:S(2)}) collective-permute-start(bf16[1024,256]{1,0:T(8,128)(2,1)} %constant_dynamic-slice_fusion.4), channel_id=1, source_target_pairs={{0,1},{1,0},{2,3},{3,2},{4,5},{5,4},{6,7},{7,6}} | collective-permute-start | bytes 1572872 | tf_op jit(solution)/shard_map/ppermute | solution.py:467
  703.0 78.7 %collective-permute-start.11 = (bf16[1024,256]{1,0:T(8,128)(2,1)}, bf16[1024,256]{1,0:T(8,128)(2,1)}, u32[]{:S(2)}, u32[]{:S(2)}) collective-permute-start(bf16[1024,256]{1,0:T(8,128)(2,1)} %constant_dynamic-slice_fusion.3), channel_id=1, source_target_pairs={{0,1},{1,0},{2,3},{3,2},{4,5},{5,4},{6,7},{7,6}} | collective-permute-start | bytes 1572872 | tf_op jit(solution)/shard_map/ppermute | solution.py:467
  746.1 136.7 %collective-permute-start.20 = (f32[3072,256]{1,0:T(8,128)}, f32[3072,256]{1,0:T(8,128)}, u32[]{:S(2)}, u32[]{:S(2)}) collective-permute-start(f32[3072,256]{1,0:T(8,128)} %get-tuple-element.96), channel_id=1, source_target_pairs={{0,1},{1,0},{2,3},{3,2},{4,5},{5,4},{6,7},{7,6}} | collective-permute-start | bytes 9437192 | tf_op jit(solution)/shard_map/ppermute | solution.py:467
  781.3 100.5 %collective-permute-start.9 = (bf16[1024,768]{1,0:T(8,128)(2,1)}, bf16[1024,768]{1,0:T(8,128)(2,1)}, u32[]{:S(2)}, u32[]{:S(2)}) collective-permute-start(bf16[1024,768]{1,0:T(8,128)(2,1)} %constant_dynamic-slice_fusion.5), channel_id=1, source_target_pairs={{0,1},{1,0},{2,3},{3,2},{4,5},{5,4},{6,7},{7,6}} | collective-permute-start | bytes 4718600 | tf_op jit(solution)/shard_map/ppermute | solution.py:467
  781.8 100.5 %collective-permute-start.16 = (bf16[1024,256]{1,0:T(8,128)(2,1)}, bf16[1024,256]{1,0:T(8,128)(2,1)}, u32[]{:S(2)}, u32[]{:S(2)}) collective-permute-start(bf16[1024,256]{1,0:T(8,128)(2,1)} %constant_dynamic-slice_fusion.1), channel_id=1, source_target_pairs={{0,1},{1,0},{2,3},{3,2},{4,5},{5,4},{6,7},{7,6}} | collective-permute-start | bytes 1572872 | tf_op jit(solution)/shard_map/ppermute | solution.py:467
  781.8 100.5 %collective-permute-start.17 = (bf16[1024,256]{1,0:T(8,128)(2,1)}, bf16[1024,256]{1,0:T(8,128)(2,1)}, u32[]{:S(2)}, u32[]{:S(2)}) collective-permute-start(bf16[1024,256]{1,0:T(8,128)(2,1)} %constant_dynamic-slice_fusion), channel_id=1, source_target_pairs={{0,1},{1,0},{2,3},{3,2},{4,5},{5,4},{6,7},{7,6}} | collective-permute-start | bytes 1572872 | tf_op jit(solution)/shard_map/ppermute | solution.py:467
  881.8 159.5 %collective-permute-start.18 = (f32[3072,768]{1,0:T(8,128)}, f32[3072,768]{1,0:T(8,128)}, u32[]{:S(2)}, u32[]{:S(2)}) collective-permute-start(f32[3072,768]{1,0:T(8,128)} %get-tuple-element.93), channel_id=1, source_target_pairs={{0,1},{1,0},{2,3},{3,2},{4,5},{5,4},{6,7},{7,6}} | collective-permute-start | bytes 28311560 | tf_op jit(solution)/shard_map/ppermute | solution.py:467
  882.3 167.0 %collective-permute-start.24 = (f32[768,3072]{1,0:T(8,128)}, f32[768,3072]{1,0:T(8,128)}, u32[]{:S(2)}, u32[]{:S(2)}) collective-permute-start(f32[768,3072]{1,0:T(8,128)} %get-tuple-element.104), channel_id=1, source_target_pairs={{0,1},{1,0},{2,3},{3,2},{4,5},{5,4},{6,7},{7,6}} | collective-permute-start | bytes 28311560 | tf_op jit(solution)/shard_map/ppermute | solution.py:467
  882.3 175.5 %collective-permute-start.25 = (f32[768,3072]{1,0:T(8,128)}, f32[768,3072]{1,0:T(8,128)}, u32[]{:S(2)}, u32[]{:S(2)}) collective-permute-start(f32[768,3072]{1,0:T(8,128)} %get-tuple-element.105), channel_id=1, source_target_pairs={{0,1},{1,0},{2,3},{3,2},{4,5},{5,4},{6,7},{7,6}} | collective-permute-start | bytes 28311560 | tf_op jit(solution)/shard_map/ppermute | solution.py:467
  882.8 45.8 %collective-permute-start.15 = (bf16[1024,768]{1,0:T(8,128)(2,1)S(1)}, bf16[1024,768]{1,0:T(8,128)(2,1)}, u32[]{:S(2)}, u32[]{:S(2)}) collective-permute-start(bf16[1024,768]{1,0:T(8,128)(2,1)S(1)} %constant_dynamic-slice_fusion.2), channel_id=1, source_target_pairs={{0,1},{1,0},{2,3},{3,2},{4,5},{5,4},{6,7},{7,6}} | collective-permute-start | bytes 4718600 | tf_op jit(solution)/shard_map/ppermute | solution.py:467
  924.0 142.5 %collective-permute-start.19 = (f32[3072,768]{1,0:T(8,128)}, f32[3072,768]{1,0:T(8,128)}, u32[]{:S(2)}, u32[]{:S(2)}) collective-permute-start(f32[3072,768]{1,0:T(8,128)} %get-tuple-element.94), channel_id=1, source_target_pairs={{0,1},{1,0},{2,3},{3,2},{4,5},{5,4},{6,7},{7,6}} | collective-permute-start | bytes 28311560 | tf_op jit(solution)/shard_map/ppermute | solution.py:467
  963.2 74.2 %collective-permute-start.23 = (f32[3072,256]{1,0:T(8,128)}, f32[3072,256]{1,0:T(8,128)}, u32[]{:S(2)}, u32[]{:S(2)}) collective-permute-start(f32[3072,256]{1,0:T(8,128)} %get-tuple-element.100), channel_id=1, source_target_pairs={{0,1},{1,0},{2,3},{3,2},{4,5},{5,4},{6,7},{7,6}} | collective-permute-start | bytes 9437192 | tf_op jit(solution)/shard_map/ppermute | solution.py:467
  (3 other events, 88.6 us)

commit v2 on v0

v2 whole, which is shorter than its diff:
```python
import math

import jax
import jax.numpy as jnp
from jax import lax
from jax.experimental import pallas as pl
from jax.experimental.pallas import tpu as pltpu
from jax.sharding import PartitionSpec as P


HEAD = 128
GROUP = 3
GW = GROUP * HEAD
QK = GW + HEAD
PW = QK + HEAD
PAIR = 2 * HEAD
ROPE_THETA = 1000000.0
NORM_EPS = 1e-05
NEG_LARGE = -1e30
BF = jnp.bfloat16
F32 = jnp.float32
SCALE = HEAD ** -0.5
SCALE2 = SCALE * math.log2(math.e)
BLK = 512
HB = BLK // 2
VMEM_LIMIT = 62 * 1024 * 1024
ANY = pl.BlockSpec(memory_space=pl.ANY)


def first_row(i, s):
    return (0, 0)


def row_map(i, s):
    return (i, 0)


def col_map(i, s):
    return (0, i)


def own_map(i, s):
    return (s[0], 0)


def sds(rows, cols, dtype=BF):
    return jax.ShapeDtypeStruct((rows, cols), dtype)


def call(body, grid, in_specs, out_specs, out_shape, args, flops, scratch=(), aliases=None):
    return pl.pallas_call(
        body,
        grid_spec=pltpu.PrefetchScalarGridSpec(
            num_scalar_prefetch=1, grid=grid, in_specs=in_specs, out_specs=out_specs, scratch_shapes=list(scratch)),
        out_shape=out_shape, input_output_aliases=aliases or {},
        compiler_params=pltpu.CompilerParams(dimension_semantics=("arbitrary",) * len(grid),
                                             vmem_limit_bytes=VMEM_LIMIT),
        cost_estimate=pl.CostEstimate(flops=int(flops), bytes_accessed=int(flops) // BLK,
                                      transcendentals=0))(*args)


def mm(a, b):
    return jnp.dot(a, b, preferred_element_type=F32)


def mm_nt(a, b):
    return lax.dot_general(a, b, (((1,), (1,)), ((), ())), preferred_element_type=F32)


def rotate(val, cos_t, sin_t):
    return val * cos_t + pltpu.roll(val, HEAD // 2, 1) * sin_t


def ds(start, size):
    return pl.ds(pl.multiple_of(start, size), size)


def split3(val):
    hi = val.astype(BF).astype(F32)
    mid = (val - hi).astype(BF).astype(F32)
    return hi, mid, val - hi - mid


def qkv_of(h, wq_ref, wk_ref, wv_ref, cos_ref, sin_ref, q_ref, k_ref, v_ref):
    cos_t, sin_t = cos_ref[...], sin_ref[...]
    out = mm(h, wq_ref[...])
    for c in range(wq_ref.shape[1] // HEAD):
        sl = slice(c * HEAD, c * HEAD + HEAD)
        q_ref[:, sl] = rotate(out[:, sl], cos_t, sin_t).astype(BF)
    out = mm(h, jnp.concatenate([wk_ref[...], wv_ref[...]], axis=1))
    for sl in (slice(0, HEAD), slice(HEAD, PAIR)):
        k_ref[:, sl] = rotate(out[:, sl], cos_t, sin_t).astype(BF)
    v_ref[...] = out[:, PAIR:].astype(BF)


def proj_body(s_ref, xa_ref, xb_ref, gain_ref, wq_ref, wk_ref, wv_ref, cos_ref, sin_ref, *rest):
    h_ref, q_ref, k_ref, v_ref, inv_scr = rest[-5:]
    half = pl.num_programs(0) // 2

    def norm(src):
        step = HEAD // 2

        def stats(c, _):
            sl = ds(c * step, step)
            xf = src[sl, :].astype(F32)
            inv = lax.rsqrt(jnp.mean(xf * xf, axis=-1, keepdims=True) + NORM_EPS)
            inv_scr[sl, :] = jnp.broadcast_to(inv, (step, HEAD))
            return 0

        def scale(c, _):
            sl = ds(c * step, step)
            inv, gain = inv_scr[sl, :], gain_ref[...]
            for n in range(src.shape[1] // HEAD):
                cols = slice(n * HEAD, n * HEAD + HEAD)
                h_ref[sl, cols] = (src[sl, cols].astype(F32) * inv * gain[:, cols]).astype(BF)
            return 0

        lax.fori_loop(0, src.shape[0] // step, stats, 0)
        lax.fori_loop(0, src.shape[0] // step, scale, 0)

    @pl.when(pl.program_id(0) < half)
    def _():
        norm(xa_ref)

    @pl.when(pl.program_id(0) >= half)
    def _():
        norm(xb_ref)

    qkv_of(h_ref[...], wq_ref, wk_ref, wv_ref, cos_ref, sin_ref, q_ref, k_ref, v_ref)


def two_source(rows):
    nb = rows // BLK

    def a_map(i, s):
        return (jnp.minimum(i, nb - 1), 0)

    def b_map(i, s):
        return (jnp.maximum(i - nb, 0), 0)

    def o_map(i, s):
        return (jnp.where(i < nb, s[0] + i, s[1] + i - nb), 0)

    return nb, a_map, b_map, o_map


def project(idx, xa, xb, gain, ws, tabs, bufs, seq):
    rows, d = xa.shape
    nb, a_map, b_map, o_map = two_source(rows)
    widths = [w.shape[1] // 4 for w in ws]
    in_specs = [pl.BlockSpec((BLK, d), a_map), pl.BlockSpec((BLK, d), b_map), pl.BlockSpec((1, d), first_row)]
    in_specs += [pl.BlockSpec((d, w), lambda i, s: (0, s[2])) for w in widths]
    in_specs += [pl.BlockSpec((BLK, HEAD), o_map)] * 2
    args = [idx, xa, xb, gain, *ws, *tabs]
    aliases = {}
    if bufs is not None:
        in_specs += [ANY] * 4
        aliases = {len(args) + n: n for n in range(4)}
        args += list(bufs)
    return call(proj_body, (2 * nb,), in_specs, [pl.BlockSpec((BLK, w), o_map) for w in (d, *widths)],
                [sds(seq, w) for w in (d, *widths)], args, 4 * rows * d * sum(widths),
                scratch=[pltpu.VMEM((BLK, HEAD), F32)], aliases=aliases)


def projc_body(s_ref, h_ref, *rest):
    qkv_of(h_ref[...], *rest)


def project_first(idx, h, ws, tabs, rows):
    d = h.shape[1]
    widths = [w.shape[1] // 4 for w in ws]
    return call(projc_body, (rows // BLK,),
                [pl.BlockSpec((BLK, d), row_map)] + [pl.BlockSpec((d, w), lambda i, s: (0, s[0])) for w in widths]
                + [pl.BlockSpec((BLK, HEAD), row_map)] * 2,
                [pl.BlockSpec((BLK, w), row_map) for w in widths], [sds(rows, w) for w in widths],
                [idx, h, *ws, *tabs], 2 * rows * d * sum(widths))


def dout_body(s_ref, da_ref, db_ref, wo_ref, *rest):
    dy_out, do_out = rest[-2:]
    half = pl.num_programs(0) // 2

    @pl.when(pl.program_id(0) < half)
    def _():
        dy_out[...] = da_ref[...]

    @pl.when(pl.program_id(0) >= half)
    def _():
        dy_out[...] = db_ref[...]

    do_out[...] = mm_nt(dy_out[...], wo_ref[...]).astype(BF)


def dout(idx, da, db, w_o, bufs, seq):
    rows, d = da.shape
    nb, a_map, b_map, o_map = two_source(rows)
    oc = w_o.shape[0] // 4
    in_specs = [pl.BlockSpec((BLK, d), a_map), pl.BlockSpec((BLK, d), b_map),
                pl.BlockSpec((oc, d), lambda i, s: (s[2], 0))]
    args = [idx, da, db, w_o]
    aliases = {}
    if bufs is not None:
        in_specs += [ANY] * 2
        aliases = {len(args) + n: n for n in range(2)}
        args += list(bufs)
    return call(dout_body, (2 * nb,), in_specs, [pl.BlockSpec((BLK, w), o_map) for w in (d, oc)],
                [sds(seq, w) for w in (d, oc)], args, 4 * rows * d * oc, aliases=aliases)


def fwd_body(s_ref, q_ref, k_ref, v_ref, o_ref, lse_ref, *rest):
    qt, kk, vt, s_scr, acc, stat = rest[-6:]
    seq = k_ref.shape[0]
    nq = seq // BLK

    def setup(c, _):
        sl = ds(c * BLK, BLK)
        vt[:, sl] = v_ref[sl, :].T
        kk[sl, :HEAD] = k_ref[sl, :]
        kk[sl, HEAD:] = k_ref[sl, :]
        for h in range(GROUP):
            qf = q_ref[sl, h * HEAD:(h + 1) * HEAD].astype(F32) * SCALE2
            hi = qf.astype(BF)
            qt[h, :HEAD, sl] = hi.T
            qt[h, HEAD:, sl] = (qf - hi.astype(F32)).astype(BF).T
        return 0

    lax.fori_loop(0, nq, setup, 0)
    acc[...] = jnp.zeros_like(acc)
    stat[...] = jnp.zeros_like(stat)
    cur, old, den_row = 0, 1, 2

    def stage_a(h, i, j, masked, first):
        row = slice(h, h + 1)
        s = mm(kk[ds(j * BLK, BLK), :], qt[h, :, ds(i * BLK, BLK)])
        if masked:
            keep = lax.broadcasted_iota(jnp.int32, s.shape, 0) <= lax.broadcasted_iota(jnp.int32, s.shape, 1)
            s = jnp.where(keep, s, NEG_LARGE)
        s_scr[h] = s
        m_new = jnp.max(s, axis=0, keepdims=True)
        if first:
            stat[old, row] = jnp.zeros((1, BLK), F32)
        else:
            m_old = stat[cur, row]
            m_new = jnp.maximum(m_old, m_new)
            stat[old, row] = jnp.exp2(m_old - m_new)
        stat[cur, row] = m_new

    def stage_b(h, j):
        row = slice(h, h + 1)
        p = jnp.exp2(s_scr[h] - stat[cur, row])
        alpha = stat[old, row]
        stat[den_row, row] = stat[den_row, row] * alpha + jnp.sum(p, axis=0, keepdims=True)
        acc[h] = acc[h] * alpha + mm(vt[:, ds(j * BLK, BLK)], p.astype(BF))

    def finish(h, i):
        row = slice(h, h + 1)
        den = stat[den_row, row]
        o_ref[ds(i * BLK, BLK), h * HEAD:(h + 1) * HEAD] = (acc[h] / den).T.astype(BF)
        lse_ref[0, row, ds(i * BLK, BLK)] = stat[cur, row] + jnp.log2(den)

    for h in range(GROUP):
        stage_a(h, 0, 0, True, True)

    def row(i, _):
        def inner(j, _):
            for h in range(GROUP):
                stage_b(h, j)
                stage_a(h, i, j + 1, False, False)
            return 0

        lax.fori_loop(0, i - 1, inner, 0)

        @pl.when(i > 0)
        def _():
            for h in range(GROUP):
                stage_b(h, i - 1)
                stage_a(h, i, i, True, False)

        nxt = jnp.minimum(i + 1, nq - 1)
        for h in range(GROUP):
            stage_b(h, i)
            finish(h, i)
            stage_a(h, nxt, 0, False, True)
        return 0

    lax.fori_loop(0, nq, row, 0)
    lse_ref[0, GROUP:, :] = jnp.zeros((8 - GROUP, seq), F32)
    if len(rest) > 6:
        hi_ref, pair_ref = rest[:2]
        hi_ref[...] = o_ref[seq // 2:, :]
        pair_ref[...] = o_ref[ds(s_ref[0] * pair_ref.shape[0], pair_ref.shape[0]), :]


def attn_fwd(idx, q, k, v, out_rows, rows):
    seq = k.shape[0]
    nq = seq // BLK
    nkv = k.shape[1] // HEAD
    extra = (seq // 2, rows) if rows else ()
    tiles = nkv * GROUP * nq * (nq + 1)
    qspec, kspec = pl.BlockSpec((seq, GW), col_map), pl.BlockSpec((seq, HEAD), col_map)
    return call(fwd_body, (nkv,), [qspec, kspec, kspec],
                [qspec, pl.BlockSpec((1, 8, seq), lambda g, s: (g, 0, 0))] + [pl.BlockSpec((r, GW), col_map) for r in extra],
                [sds(out_rows, q.shape[1]), jax.ShapeDtypeStruct((nkv, 8, seq), F32)] + [sds(r, q.shape[1]) for r in extra],
                [idx, q, k, v], tiles * BLK * BLK * PAIR,
                scratch=[pltpu.VMEM((GROUP, PAIR, seq), BF), pltpu.VMEM((seq, PAIR), BF),
                         pltpu.VMEM((HEAD, seq), BF), pltpu.VMEM((GROUP, BLK, BLK), F32),
                         pltpu.VMEM((GROUP, HEAD, BLK), F32), pltpu.VMEM((GROUP, 8, BLK), F32)])


def bwd_body(s_ref, q_ref, do_ref, o_ref, k_ref, v_ref, lse_ref, cos_ref, sin_ref, out_ref, pair_ref,
             qa, da, ka, va, q3t, do3t, dq3, dkt, dvt):
    i = pl.program_id(0)
    last = pl.num_programs(0) - 1
    seq = k_ref.shape[0]
    m3 = GROUP * HB

    @pl.when(i == 0)
    def _():
        dkt[...] = jnp.zeros_like(dkt)
        dvt[...] = jnp.zeros_like(dvt)

        def setup(c, _):
            sl = ds(c * BLK, BLK)
            minus = jnp.where(lax.broadcasted_iota(jnp.int32, (BLK, HEAD), 1) < 3, -1.0, 0.0).astype(BF)
            for src, dst in ((k_ref, ka), (v_ref, va)):
                dst[sl, :HEAD] = src[sl, :]
                dst[sl, HEAD:] = minus
            return 0

        lax.fori_loop(0, seq // BLK, setup, 0)

    srow = lax.broadcasted_iota(jnp.int32, (16, HB), 0)

    def augment(dst, rows, row):
        hi, mid, low = split3(row)
        parts = jnp.where(srow == 0, hi, jnp.where(srow == 1, mid, jnp.where(srow == 2, low, 0.0))).astype(BF)
        dst[rows, HEAD:] = jnp.concatenate([parts, jnp.zeros((HEAD - 16, HB), BF)], axis=0).T

    def spots():
        for b in range(2):
            for h in range(GROUP):
                start = (b * GROUP + h) * HB
                yield h, slice(b * HB, (b + 1) * HB), slice(h * HEAD, (h + 1) * HEAD), slice(start, start + HB)

    for h, src, cols, rows in spots():
        qh, doh = q_ref[src, cols], do_ref[src, cols]
        qa[rows, :HEAD] = qh
        da[rows, :HEAD] = doh
        q3t[:, rows] = qh.T
        dt = doh.T
        do3t[:, rows] = dt
        augment(da, rows, jnp.sum(dt.astype(F32) * o_ref[src, cols].T.astype(F32), axis=0, keepdims=True))
        augment(qa, rows, lse_ref[0, h:h + 1, src] * (1.0 / SCALE2))
    dq3[...] = jnp.zeros_like(dq3)

    def step(rows, start, width, masked):
        sl = pl.ds(pl.multiple_of(start, BLK), width)
        s = mm_nt(qa[rows, :], ka[sl, :])
        dp = mm_nt(da[rows, :], va[sl, :])
        p = jnp.exp2(s * SCALE2)
        if masked:
            off = width - HB
            tail = p[:, off:]
            keep = lax.broadcasted_iota(jnp.int32, tail.shape, 0) % HB >= lax.broadcasted_iota(jnp.int32, tail.shape, 1)
            tail = jnp.where(keep, tail, 0.0)
            p = jnp.concatenate([p[:, :off], tail], axis=1) if off else tail
        dvt[:, sl] += mm(do3t[:, rows], p.astype(BF))
        dsv = (p * dp).astype(BF)
        dkt[:, sl] += mm(q3t[:, rows], dsv)
        dq3[rows, :] += mm(dsv, ka[sl, :HEAD])

    def body(t, _):
        step(slice(0, 2 * m3), t * 2 * BLK, 2 * BLK, False)
        return 0

    lax.fori_loop(0, i // 2, body, 0)

    def tail_steps(start, width):
        step(slice(0, m3), start, width - HB, True)
        step(slice(m3, 2 * m3), start, width, True)

    @pl.when(i % 2 == 1)
    def _():
        tail_steps((i - 1) * BLK, 2 * BLK)

    @pl.when(i % 2 == 0)
    def _():
        tail_steps(i * BLK, BLK)

    for h, src, cols, rows in spots():
        rsl = ds(i * BLK + src.start, HB)
        out_ref[rsl, cols] = rotate(dq3[rows, :] * SCALE, cos_ref[rsl, :], -sin_ref[rsl, :]).astype(BF)

    @pl.when(i == last)
    def _():
        def fin(c, _):
            sl = ds(c * BLK, BLK)
            out_ref[sl, GW:QK] = rotate(dkt[:, sl].T * SCALE, cos_ref[sl, :], -sin_ref[sl, :]).astype(BF)
            out_ref[sl, QK:] = dvt[:, sl].T.astype(BF)
            return 0

        lax.fori_loop(0, seq // BLK, fin, 0)
        pair_ref[...] = out_ref[ds(s_ref[0] * pair_ref.shape[0], pair_ref.shape[0]), :]


def attn_bwd(idx, q, do, o, k, v, lse, tabs, rows):
    seq = k.shape[0]
    nq = seq // BLK
    qspec = pl.BlockSpec((BLK, GW), lambda i, s: (i, s[1]))
    kspec = pl.BlockSpec((seq, HEAD), lambda i, s: (0, s[1]))
    m3 = GROUP * BLK
    return call(bwd_body, (nq,),
                [qspec] * 3 + [kspec] * 2 + [pl.BlockSpec((1, 8, BLK), lambda i, s: (s[1], 0, i))]
                + [pl.BlockSpec((seq, HEAD), first_row)] * 2,
                [pl.BlockSpec((r, PW), first_row) for r in (seq, rows)], [sds(r, PW) for r in (seq, rows)],
                [idx, q, do, o, k, v, lse, *tabs], GROUP * nq * (nq + 1) * BLK * BLK * PW,
                scratch=[pltpu.VMEM((m3, PAIR), BF)] * 2 + [pltpu.VMEM((seq, PAIR), BF)] * 2
                + [pltpu.VMEM((HEAD, m3), BF)] * 2 + [pltpu.VMEM((m3, HEAD), F32)] + [pltpu.VMEM((HEAD, seq), F32)] * 2)


def out_body(s_ref, x_ref, *rest):
    ops, weights, out_ref = rest[:4], rest[4:8], rest[8]
    lhs = jnp.concatenate([r[...] for r in ops], axis=1)
    rhs = jnp.concatenate([r[...] for r in weights], axis=0)
    out_ref[...] = (x_ref[...].astype(F32) + mm(lhs, rhs)).astype(BF)


def out_proj(idx, x, pieces, w_o):
    rows, d = x.shape
    hw = pieces[0].shape[1]
    return call(out_body, (d // BLK,),
                [pl.BlockSpec((rows, BLK), col_map)]
                + [pl.BlockSpec((rows, hw), m) for m in (own_map, first_row, own_map, first_row)]
                + [pl.BlockSpec((hw, BLK), lambda n, s, p=p: (s[p], n)) for p in range(4)],
                pl.BlockSpec((rows, BLK), col_map), sds(rows, d), [idx, x, *pieces] + [w_o] * 4,
                2 * rows * d * d)


def dwo_body(s_ref, oa_ref, ob_ref, dy_ref, fin, snd, ot):
    hw = oa_ref.shape[1]

    @pl.when(jnp.logical_and(pl.program_id(0) == 0, pl.program_id(1) == 0))
    def _():
        def tr(c, _):
            sl = ds(c * BLK, BLK)
            ot[:hw, sl] = oa_ref[sl, :].T
            ot[hw:, sl] = ob_ref[sl, :].T
            return 0

        lax.fori_loop(0, oa_ref.shape[0] // BLK, tr, 0)

    val = mm(ot[ds(pl.program_id(1) * hw, hw), :], dy_ref[...])
    fin[...] = val
    snd[...] = val


def dw_o(idx, oa, ob, dy):
    seq, d = dy.shape
    hw = oa.shape[1]
    once = pl.BlockSpec((seq, hw), lambda i, p, s: (0, 0), pipeline_mode=pl.Buffered(1))
    return call(dwo_body, (d // BLK, 2),
                [once, once, pl.BlockSpec((seq, BLK), lambda i, p, s: (0, i))],
                [pl.BlockSpec((hw, BLK), lambda i, p, s: (s[p], i)), pl.BlockSpec((hw, BLK), lambda i, p, s: (p, i))],
                [sds(4 * hw, d, F32), sds(2 * hw, d, F32)], [idx, oa, ob, dy], 4 * seq * d * hw,
                scratch=[pltpu.VMEM((2 * hw, seq), BF)])


def dwown_body(s_ref, h_ref, ga_ref, gb_ref, wo_ref, _, fq, fk, fv, snd, wo_fin, ht, sem):
    i, rows = pl.program_id(0), wo_ref.shape[0]
    per = pl.num_programs(0) // 2
    start = jnp.where(i < per, s_ref[1] * per + i, s_ref[2] * per + i - per)
    copy = pltpu.make_async_copy(wo_ref, wo_fin.at[ds(start * rows, rows), :], sem)
    copy.start()
    ht[...] = h_ref[...].T
    lhs = ht[...]
    for n, g in enumerate((ga_ref, gb_ref)):
        val = mm(lhs, g[:, :QK])
        for ref, base in ((fq, 0), (snd, 0)):
            ref[:, base + n * GW:base + (n + 1) * GW] = val[:, :GW]
        fk[:, n * HEAD:(n + 1) * HEAD] = val[:, GW:]
        snd[:, 2 * GW + n * HEAD:2 * GW + (n + 1) * HEAD] = val[:, GW:]
    val = mm(lhs, jnp.concatenate([ga_ref[:, QK:], gb_ref[:, QK:]], axis=1))
    fv[...] = val
    snd[:, 2 * QK:] = val
    copy.wait()


def dw_own(idx, h, ga, gb, wo_rcv, wo_fin):
    seq, d = h.shape
    steps = d // HB
    gspec = pl.BlockSpec((seq, PW), first_row)
    widths = (2 * GW, PAIR, PAIR)
    return call(dwown_body, (steps,),
                [pl.BlockSpec((seq, HB), col_map), gspec, gspec, pl.BlockSpec((wo_rcv.shape[0] // steps, d), row_map), ANY],
                [pl.BlockSpec((HB, w), lambda i, s: (i, s[0])) for w in widths]
                + [pl.BlockSpec((HB, 2 * PW), row_map), ANY],
                [sds(d, 4 * w, F32) for w in widths] + [sds(d, 2 * PW, F32), sds(*wo_fin.shape, F32)],
                [idx, h, ga, gb, wo_rcv, wo_fin], 4 * seq * d * PW,
                scratch=[pltpu.VMEM((HB, seq), BF), pltpu.SemaphoreType.DMA], aliases={5: 4})


def dwgrp_body(with_v, s_ref, h_ref, ga_ref, gb_ref, *rest):
    ht, snd = rest[-1], rest[-2]
    outs = rest[-2 - (3 if with_v else 2):-2]
    ht[...] = h_ref[...].T
    lhs = ht[...]
    val = mm(lhs, (gb_ref if with_v else ga_ref)[:, :QK])
    outs[0][...] = val[:, :GW]
    outs[1][...] = val[:, GW:]
    snd[:, :QK] = val
    if with_v:
        val = mm(lhs, jnp.concatenate([ga_ref[:, QK:], gb_ref[:, QK:]], axis=1))
        outs[2][...] = val
        snd[:, QK:] = val


def group_specs(with_v):
    specs = [pl.BlockSpec((HB, w), lambda i, s: (i, 2 * s[0] + int(with_v))) for w in (GW, HEAD)]
    return specs + ([pl.BlockSpec((HB, PAIR), lambda i, s: (i, s[0]))] if with_v else [])


def dw_group(with_v, idx, h, ga, gb, bufs):
    seq, d = h.shape
    gspec = pl.BlockSpec((seq, PW), first_row)
    specs = group_specs(with_v)
    bufs = bufs[:len(specs)]
    sw = QK + (PAIR if with_v else 0)
    return call(lambda *refs: dwgrp_body(with_v, *refs), (d // HB,),
                [pl.BlockSpec((seq, HB), col_map), gspec, gspec] + [ANY] * len(specs),
                specs + [pl.BlockSpec((HB, sw), row_map)], [sds(*b.shape, F32) for b in bufs] + [sds(d, sw, F32)],
                [idx, h, ga, gb, *bufs], 2 * seq * d * sw, scratch=[pltpu.VMEM((HB, seq), BF)],
                aliases={4 + n: n for n in range(len(specs))})


def place_body(s_ref, rcv, *rest):
    q_out, k_out, v_out = rest[-3:]
    q_out[...] = rcv[:, :GW]
    k_out[...] = rcv[:, GW:QK]
    v_out[...] = rcv[:, QK:]


def place(idx, rcv, bufs):
    d, w = rcv.shape
    return call(place_body, (d // HB,), [pl.BlockSpec((HB, w), row_map)] + [ANY] * 3, group_specs(True),
                [sds(*b.shape, F32) for b in bufs], [idx, rcv, *bufs], d * w, aliases={2 + n: n for n in range(3)})


def pack_body(s_ref, q_ref, k_ref, v_ref, out_ref):
    out_ref[:, :GW] = q_ref[...]
    out_ref[:, GW:QK] = k_ref[...]
    out_ref[:, QK:] = v_ref[...]


def pack_weights(idx, ws):
    d, groups = ws[1].shape[0], ws[1].shape[1] // HEAD
    return call(pack_body, (groups,), [pl.BlockSpec((d, w), col_map) for w in (GW, HEAD, HEAD)],
                pl.BlockSpec((d, PW), col_map), sds(d, groups * PW), [idx, *ws], d * groups * PW)


def puts(rcv, outs, cols, widths, sem):
    rows, src, copies = ds(pl.program_id(0) * rcv.shape[0], rcv.shape[0]), 0, []
    for n, (out, col, w) in enumerate(zip(outs, cols, widths)):
        copies.append(pltpu.make_async_copy(rcv.at[:, src:src + w], out.at[rows, ds(col * w, w)], sem.at[n]))
        src += w
    for copy in copies:
        copy.start()
    return copies


def dxa_body(s_ref, *rest):
    pieces, weights, rcv = rest[:6], rest[6:10], rest[10]
    out_ref, fq, fk, fv, sem = rest[-5:]
    copies = puts(rcv, (fq, fk, fv), [s_ref[1]] * 3, (2 * GW, PAIR, PAIR), sem)
    lhs = jnp.concatenate([r[...] for r in pieces], axis=1)
    rhs = jnp.concatenate([r[...] for r in weights], axis=1)
    out_ref[...] = mm_nt(lhs, rhs)
    for copy in copies:
        copy.wait()


def dx_early(idx, pieces, w_p, rows, rcv, bufs):
    d = w_p.shape[0]
    maps = (own_map, own_map, first_row, first_row, own_map, first_row)
    wspecs = [pl.BlockSpec((BLK, 2 * PW), lambda n, s, p=p: (n, s[p])) for p in range(2)]
    wspecs += [pl.BlockSpec((BLK, PW), lambda n, s, p=p: (n, 2 * s[p])) for p in (2, 3)]
    return call(dxa_body, (d // BLK,),
                [pl.BlockSpec((rows, PW), m) for m in maps] + wspecs + [pl.BlockSpec((BLK, 2 * PW), row_map)] + [ANY] * 3,
                [pl.BlockSpec((rows, BLK), col_map)] + [ANY] * 3, [sds(rows, d, F32)] + [sds(*b.shape, F32) for b in bufs],
                [idx, *pieces] + [w_p] * 4 + [rcv, *bufs], 12 * rows * d * PW,
                scratch=[pltpu.SemaphoreType.DMA((3,))], aliases={12 + n: 1 + n for n in range(3)})


def dxb_body(s_ref, x_ref, dy_ref, gain_ref, early_ref, b2, b3, w2, w3, rcv, *rest):
    dx_ref, dg_ref, fq, fk, acc, inv_scr, sem = rest[-7:]
    n = pl.program_id(0)
    copies = puts(rcv, (fq, fk), [2 * s_ref[3]] * 2, (GW, HEAD), sem)
    lhs = jnp.concatenate([b2[...], b3[...]], axis=1)
    rhs = jnp.concatenate([w2[...], w3[...]], axis=1)
    acc[:, ds(n * BLK, BLK)] = early_ref[...] + mm_nt(lhs, rhs)

    @pl.when(n == pl.num_programs(0) - 1)
    def _():
        step = HEAD // 2
        rows, d = x_ref.shape
        tiles = [slice(c * HEAD, c * HEAD + HEAD) for c in range(d // HEAD)]

        def stats(r, _):
            sl = ds(r * step, step)
            sq = jnp.zeros((step, HEAD), F32)
            dot = jnp.zeros((step, HEAD), F32)
            for c in tiles:
                xf = x_ref[sl, c].astype(F32)
                sq += xf * xf
                dot += xf * acc[sl, c] * gain_ref[:, c]
            inv = lax.rsqrt(jnp.sum(sq, axis=-1, keepdims=True) / d + NORM_EPS)
            inv_scr[0, sl, :] = jnp.broadcast_to(inv, (step, HEAD))
            inv_scr[1, sl, :] = jnp.broadcast_to(jnp.sum(dot, axis=-1, keepdims=True) * inv * inv / d, (step, HEAD))
            return 0

        lax.fori_loop(0, rows // step, stats, 0)
        dg_ref[...] = jnp.zeros_like(dg_ref)

        def epi(r, _):
            sl = ds(r * step, step)
            inv, coef = inv_scr[0, sl, :], inv_scr[1, sl, :]
            for c in tiles:
                xf = x_ref[sl, c].astype(F32)
                dh = acc[sl, c]
                part = dh * (xf * inv)
                dx_ref[sl, c] = (dy_ref[sl, c].astype(F32) + inv * (dh * gain_ref[:, c] - xf * coef)).astype(BF)
                dg_ref[:, c] += jnp.sum(part.reshape(step // 8, 8, HEAD), axis=0)
            return 0

        lax.fori_loop(0, rows // step, epi, 0)

    for copy in copies:
        copy.wait()


def dx_late(idx, x, dy, gain, early, b2, b3, w_p, rcv, bufs):
    rows, d = x.shape
    wspecs = [pl.BlockSpec((BLK, PW), lambda n, s, p=p: (n, 2 * s[p] + 1)) for p in (2, 3)]
    whole = pl.BlockSpec((rows, d), first_row)
    return call(dxb_body, (d // BLK,),
                [whole, whole, pl.BlockSpec((1, d), first_row), pl.BlockSpec((rows, BLK), col_map),
                 pl.BlockSpec((rows, PW), own_map), pl.BlockSpec((rows, PW), first_row)] + wspecs
                + [pl.BlockSpec((BLK, QK), row_map)] + [ANY] * 2,
                [whole, pl.BlockSpec((8, d), first_row)] + [ANY] * 2,
                [sds(rows, d), sds(8, d, F32)] + [sds(*b.shape, F32) for b in bufs],
                [idx, x, dy, gain, early, b2, b3, w_p, w_p, rcv, *bufs], 4 * rows * d * PW,
                scratch=[pltpu.VMEM((rows, d), F32), pltpu.VMEM((2, rows, HEAD), F32), pltpu.SemaphoreType.DMA((2,))],
                aliases={10: 2, 11: 3})


def solution(mesh):
    sp = mesh.shape['sp']
    cross = [(a, a ^ 2) for a in range(sp)]
    pair = [(a, a ^ 1) for a in range(sp)]

    def over(val):
        return lax.ppermute(val, 'sp', cross)

    def near(val):
        return lax.ppermute(val, 'sp', pair)

    def after(val, *deps):
        return lax.optimization_barrier((val,) + deps)[0]

    def vec(*vals, dep=()):
        out = jnp.stack([jnp.asarray(v, jnp.int32) for v in vals])
        return after(out, *dep) if dep else out

    def step(x, dy, positions, gain, w_q, w_k, w_v, w_o):
        j = lax.axis_index('sp').astype(jnp.int32)
        rows, d = x.shape
        seq = rows * sp
        half = rows // 2
        j1, j2, j3 = [j ^ n for n in (1, 2, 3)]
        dev = (j, j1, j2, j3)
        bpr = rows // BLK
        ws = (w_q, w_k, w_v)

        def rows_of(val, blk):
            return lax.dynamic_slice_in_dim(val, blk * rows, rows, 0)

        gain_f = gain.astype(F32).reshape(1, d)

        xa, xb = after((x[:half], x[half:]), positions)
        pos2 = over(positions)
        pos1 = near(positions)
        x2a = over(after(xa, pos2))
        x2b = over(after(xb, pos2))
        x1 = near(x)
        pos3 = near(pos2)
        dy1 = near(after(dy, x1))

        pos = jnp.zeros((seq,), jnp.int32)
        for blk, val in zip(dev, (positions, pos1, pos2, pos3)):
            pos = lax.dynamic_update_slice(pos, val, (blk * rows,))
        inv_freq = ROPE_THETA ** (-jnp.arange(0, HEAD, 2).astype(F32) / HEAD)
        angles = pos.astype(F32)[:, None] * inv_freq[None, :]
        cos_h, sin_h = jnp.cos(angles), jnp.sin(angles)
        tabs = (jnp.concatenate([cos_h, cos_h], axis=1), jnp.concatenate([-sin_h, sin_h], axis=1))

        bufs = project(vec(j * bpr, j1 * bpr, j), x, x1, gain_f, ws, tabs, None, seq)
        dbufs = dout(vec(j * bpr, j1 * bpr, j, dep=(bufs[1],)), dy, dy1, w_o, None, seq)
        w_p = pack_weights(vec(j, dep=(dbufs[1],)), ws)

        x2a = after(x2a, w_p)
        dy2a = over(after(dy, x2a)[:half])
        x3a = near(x2a)
        bufs = project(vec(j2 * bpr, j3 * bpr, j), x2a, x3a, gain_f, ws, tabs, bufs, seq)
        x2b = after(x2b, bufs[1])
        dy2b = over(after(dy, x2b)[half:])
        x3b = near(x2b)
        bufs = project(vec(j2 * bpr + 1, j3 * bpr + 1, j), x2b, x3b, gain_f, ws, tabs, bufs, seq)
        h_all, q, k, v = bufs
        o, lse, o_hi, o_pair = attn_fwd(vec(j1), q, k, v, seq, rows)
        orv = over(o_hi)
        o1 = near(o_pair)
        qc, kc, vc = project_first(vec(j2, dep=(o,)), h_all, ws, tabs, seq // 2)
        oc = attn_fwd(vec(j), qc, kc, vc, seq, 0)[0]

        dy2a = after(dy2a, oc)
        dy3a = near(dy2a)
        dbufs = dout(vec(j2 * bpr, j3 * bpr, j), dy2a, dy3a, w_o, dbufs, seq)
        dy2b = after(dy2b, dbufs[1])
        dy3b = near(dy2b)
        dbufs = dout(vec(j2 * bpr + 1, j3 * bpr + 1, j), dy2b, dy3b, w_o, dbufs, seq)
        dy_all, do = dbufs

        ga, ga_pair = attn_bwd(vec(j1, 0), q, do, o, k, v, lse, tabs, rows)
        ga2 = over(ga)
        ga1 = near(ga_pair)
        gb, gb_pair = attn_bwd(vec(j1, 1, dep=(ga,)), q, do, o, k, v, lse, tabs, rows)
        gb2 = over(gb)
        gb1 = near(gb_pair)

        ox = lax.dynamic_update_slice(oc, after(orv, gb), (seq // 2, 0))
        o3 = near(rows_of(ox, j1))
        wo_fin, wo_snd = dw_o(vec(j, j2, dep=(gb,)), o, ox, dy_all)
        wo_rcv = near(wo_snd)
        result = out_proj(vec(*dev, dep=(wo_snd,)), x, (o, o1, ox, o3), w_o)
        fq, fk, fv, snd, wo_fin = dw_own(vec(j, j1, j3, dep=(result,)), h_all, ga, gb, wo_rcv, wo_fin)
        rcv = near(snd)

        ga2 = after(ga2, snd)
        ga3 = near(rows_of(ga2, j1))
        fq, fk, snd_a = dw_group(False, vec(j2), h_all, ga2, ga2, (fq, fk))
        rcv_a = near(snd_a)
        early, fq, fk, fv = dx_early(vec(*dev, dep=(snd_a,)), (ga, gb, ga1, gb1, ga2, ga3), w_p, rows,
                                     rcv, (fq, fk, fv))

        gb2 = after(gb2, early)
        gb3 = near(rows_of(gb2, j1))
        fq, fk, fv, snd_b = dw_group(True, vec(j2), h_all, ga2, gb2, (fq, fk, fv))
        rcv_b = near(snd_b)
        grad_x, dg, fq, fk = dx_late(vec(*dev, dep=(snd_b,)), x, dy, gain_f, early, gb2, gb3, w_p, rcv_a, (fq, fk))
        dg = jnp.sum(dg, axis=0)
        dg = dg + near(dg)
        dg = dg + over(dg)
        fq, fk, fv = place(vec(j3), rcv_b, (fq, fk, fv))
        return result, grad_x, fq, fk, fv, wo_fin, dg

    seq_spec = P(('dp', 'sp'), None)
    whole = P(None, None)
    part_rows = P('dp', None)
    return jax.shard_map(step, mesh=mesh,
                         in_specs=(seq_spec, seq_spec, P(('dp', 'sp')), P(None), whole, whole, whole, whole),
                         out_specs=(seq_spec, seq_spec, part_rows, part_rows, part_rows, part_rows, P('dp')),
                         check_vma=False)
```

time: 4340 us -> 1110 us (0.26)
  matrix products: 2170 us -> 0 us
  waiting for transfers between devices: 1730 us -> 333 us
  Pallas kernels: 0 us -> 698 us
  local copies, waits for them, and re-layouts: 234 us -> 29.1 us
  other arithmetic: 129 us -> 17.7 us
    dot_general x52 -> x0, matrix products: 1750 us -> none  [the longest x8 531 us: one_block(): jnp.einsum('hgqk,qhgd->khd', ds_bf, q_blk, preferred_element_type=jnp.flo...]
    psum x1 -> x0, waiting for transfers between devices: 1520 us -> none  [local_step(): lax.psum(lax.dot_general(hidden, dq_pre, CONTRACT_ROWS, preferred_element...]
    pallas_call x0 -> x20, Pallas kernels: none -> 698 us  [call(): pl.pallas_call(body, grid_spec=pltpu.PrefetchScalarGridSpec(num_scalar_pr...]
    sub x16 -> x0, matrix products: 417 us -> none  [one_block(): attn_prob = jax.nn.softmax(jnp.where(causal, scores, NEG_LARGE), axis=-1)]
    ppermute x0 -> x28, waiting for transfers between devices: none -> 333 us  [the longest x9 262 us: over(): return lax.ppermute(val, 'sp', cross)]
    all_to_all x8 -> x0, waiting for transfers between devices: 207 us -> none  [the longest x1 83.5 us: local_step(): lax.all_to_all(o_all.reshape(seq_len, q_loc, HEAD_DIM), 'sp', 0, 1, tiled...]
    unnamed x52 -> x14, local copies, waits for them, and re-layouts: 98.1 us -> 6.87 us
    ge x16 -> x0, other arithmetic: 47.1 us -> none  [one_block(): causal = (blk_start + jnp.arange(row_count))[:, None] >= key_index[None, :]]
  transfers between devices with their start and end apart: 9 -> 28, of which waited for: 6 -> 14; matrix products, arithmetic and copies ran while one was open for 16% -> 3% of each run, Pallas kernels for 0% -> 51%
where the time goes in v2:
time: 1110 us; the launch traced here: 1100 us
  Pallas kernels  698 us (63%)
  waiting for transfers between devices  333 us (30%)
  local copies, waits for them, and re-layouts  29.1 us (3%)
  other arithmetic  17.7 us (2%)
  starting transfers between devices  17.4 us (2%)
    pallas_call x20, Pallas kernels, call(): pl.pallas_call(body, grid_spec=pltpu.PrefetchScalarGridSpec(num_scalar_pr...  698 us
    ppermute x9, waiting for transfers between devices, over(): return lax.ppermute(val, 'sp', cross)  262 us
    ppermute x19, waiting for transfers between devices, near(): return lax.ppermute(val, 'sp', pair)  71.1 us
  transfers between devices with their start and end apart: 28, of which 14 were waited for; matrix products, arithmetic and copies ran while one was open for 3% of the time, Pallas kernels for 51%

profile of v2, /device:TPU:0, one launch (start us, length us, event | category | flops | bytes accessed | tf_op | source)
XLA Modules:
  0.0 1095.7 jit_solution(16094705387493163696)
XLA Ops:
  36.4 34.5 %shard_map.135 = (bf16[4096,3072]{1,0:T(8,128)(2,1)}, bf16[4096,768]{1,0:T(8,128)(2,1)}, bf16[4096,256]{1,0:T(8,128)(2,1)}, bf16[4096,256]{1,0:T(8,128)(2,1)}) custom-call(s32[3]{0:T(128)} %add_add_fusion.2.s_ref, bf16[1024,3072]{1,0:T(8,128)(2,1)} %x_ref.3, bf16[1024,3072]{1,0:T(8,128)(2,1)} %copy-done.6, f32[1,3072]{1,0:T(1,128)} %bitcast.11, ...), custom_call_target="tpu_custom_call" | custom-call | flops 16106127360 | bytes 31457280 | tf_op jit(solution)/shard_map/pallas_call | solution.py:51
  71.0 17.7 %shard_map.136 = (bf16[4096,3072]{1,0:T(8,128)(2,1)}, bf16[4096,768]{1,0:T(8,128)(2,1)}) custom-call(s32[3]{0:T(128)} %add_add_fusion.2.s_ref, bf16[1024,3072]{1,0:T(8,128)(2,1)} %dy_ref.1, bf16[1024,3072]{1,0:T(8,128)(2,1)} %collective-permute-done.6.db_ref, bf16[3072,3072]{1,0:T(8,128)(2,1)} %rest_7_.1), custom_call_target="tpu_custom_call" | custom-call | flops 9663676416 | bytes 18874368 | tf_op jit(solution)/shard_map/pallas_call | solution.py:51
  88.7 22.8 %shard_map.137.rest_6_.rest_7_.rest_8_.rest_9_.w2.w3 = bf16[3072,5120]{1,0:T(8,128)(2,1)} custom-call(s32[1]{0:T(128)} %bitcast.s_ref, bf16[3072,3072]{1,0:T(8,128)(2,1)} %rest_0_.1, bf16[3072,1024]{1,0:T(8,128)(2,1)} %rest_1_.1, bf16[3072,1024]{1,0:T(8,128)(2,1)} %rest_2_.1), custom_call_target="tpu_custom_call" | custom-call | flops 15728640 | bytes 30720 | tf_op jit(solution)/shard_map/pallas_call | solution.py:51
  117.6 21.2 %shard_map.138 = (bf16[4096,3072]{1,0:T(8,128)(2,1)}, bf16[4096,768]{1,0:T(8,128)(2,1)}, bf16[4096,256]{1,0:T(8,128)(2,1)}, bf16[4096,256]{1,0:T(8,128)(2,1)}) custom-call(s32[3]{0:T(128)} %add_add_fusion.1.s_ref, bf16[512,3072]{1,0:T(8,128)(2,1)} %collective-permute-done.2.xa_ref, ...), custom_call_target="tpu_custom_call", output_to_operand_aliasing={{0}: (9, {}), {1}: (10, {}), {2}: (11, {}), {3}: (12, {})} | custom-call | flops 8053063680 | bytes 15728640 | tf_op jit(solution)/shard_map/pallas_call | solution.py:51
  138.8 43.6 %collective-permute-done.1.xa_ref = bf16[512,3072]{1,0:T(8,128)(2,1)} collective-permute-done((bf16[512,3072]{1,0:T(8,128)(2,1)}, bf16[512,3072]{1,0:T(8,128)(2,1)}, u32[]{:S(2)}, u32[]{:S(2)}) %collective-permute-start.1) | collective-permute-done | bytes 3145760 | tf_op jit(solution)/shard_map/ppermute | solution.py:661
  188.4 21.2 %shard_map.139 = (bf16[4096,3072]{1,0:T(8,128)(2,1)}, bf16[4096,768]{1,0:T(8,128)(2,1)}, bf16[4096,256]{1,0:T(8,128)(2,1)}, bf16[4096,256]{1,0:T(8,128)(2,1)}) custom-call(s32[3]{0:T(128)} %add_add_fusion.s_ref, bf16[512,3072]{1,0:T(8,128)(2,1)} %collective-permute-done.1.xa_ref, ...), custom_call_target="tpu_custom_call", output_to_operand_aliasing={{0}: (9, {}), {1}: (10, {}), {2}: (11, {}), {3}: (12, {})} | custom-call | flops 8053063680 | bytes 15728640 | tf_op jit(solution)/shard_map/pallas_call | solution.py:51
  209.7 81.1 %shard_map.140 = (bf16[4096,768]{1,0:T(8,128)(2,1)}, f32[2,8,4096]{2,1,0:T(8,128)}, bf16[2048,768]{1,0:T(8,128)(2,1)}, bf16[1024,768]{1,0:T(8,128)(2,1)}) custom-call(s32[1]{0:T(128)} %bitcast.1.s_ref, bf16[4096,768]{1,0:T(8,128)(2,1)} %get-tuple-element.103.q_ref, bf16[4096,256]{1,0:T(8,128)(2,1)} %get-tuple-element.106.k_ref, ...), custom_call_target="tpu_custom_call" | custom-call | flops 28991029248 | bytes 56623104 | tf_op jit(solution)/shard_map/pallas_call | solution.py:51
  290.8 23.0 %shard_map.141 = (bf16[2048,768]{1,0:T(8,128)(2,1)}, bf16[2048,256]{1,0:T(8,128)(2,1)}, bf16[2048,256]{1,0:T(8,128)(2,1)}) custom-call(s32[1]{0:T(128)} %bitcast.2.s_ref.refs_0_, bf16[4096,3072]{1,0:T(8,128)(2,1)} %get-tuple-element.110.h_ref.refs_1_, bf16[3072,3072]{1,0:T(8,128)(2,1)} %rest_0_.1, bf16[3072,1024]{1,0:T(8,128)(2,1)} %rest_1_.1, ...), custom_call_target="tpu_custom_call" | custom-call | flops 16106127360 | bytes 31457280 | tf_op jit(solution)/shard_map/pallas_call | solution.py:51
  313.7 26.2 %shard_map.142 = (bf16[4096,768]{1,0:T(8,128)(2,1)}, f32[2,8,2048]{2,1,0:T(8,128)}) custom-call(s32[1]{0:T(128)} %bitcast.s_ref, bf16[2048,768]{1,0:T(8,128)(2,1)} %get-tuple-element.111.q_ref, bf16[2048,256]{1,0:T(8,128)(2,1)} %get-tuple-element.112.k_ref, bf16[2048,256]{1,0:T(8,128)(2,1)} %get-tuple-element.113.v_ref), custom_call_target="tpu_custom_call" | custom-call | flops 8053063680 | bytes 15728640 | tf_op jit(solution)/shard_map/pallas_call | solution.py:51
  346.0 11.5 %shard_map.143 = (bf16[4096,3072]{1,0:T(8,128)(2,1)}, bf16[4096,768]{1,0:T(8,128)(2,1)}) custom-call(s32[3]{0:T(128)} %add_add_fusion.1.s_ref, bf16[512,3072]{1,0:T(8,128)(2,1)} %collective-permute-done.10.da_ref, bf16[512,3072]{1,0:T(8,128)(2,1)} %collective-permute-done.11.db_ref, ...), custom_call_target="tpu_custom_call", output_to_operand_aliasing={{0}: (4, {}), {1}: (5, {})} | custom-call | flops 4831838208 | bytes 9437184 | tf_op jit(solution)/shard_map/pallas_call | solution.py:51
  357.5 57.0 %collective-permute-done.9.da_ref = bf16[512,3072]{1,0:T(8,128)(2,1)} collective-permute-done((bf16[512,3072]{1,0:T(8,128)(2,1)}, bf16[512,3072]{1,0:T(8,128)(2,1)}, u32[]{:S(2)}, u32[]{:S(2)}) %collective-permute-start.9) | collective-permute-done | bytes 3145760 | tf_op jit(solution)/shard_map/ppermute | solution.py:661
  432.1 82.4 %shard_map.145 = (bf16[4096,640]{1,0:T(8,128)(2,1)}, bf16[1024,640]{1,0:T(8,128)(2,1)}) custom-call(s32[2]{0:T(128)} %pad_add_fusion.3.s_ref, bf16[4096,768]{1,0:T(8,128)(2,1)} %get-tuple-element.103.q_ref, bf16[4096,768]{1,0:T(8,128)(2,1)} %get-tuple-element.120.do_ref, bf16[4096,768]{1,0:T(8,128)(2,1)} %get-tuple-element.108.o_ref.oa_ref.rest_0_, ...), custom_call_target="tpu_custom_call" | custom-call | flops 36238786560 | bytes 70778880 | tf_op jit(solution)/shard_map/pallas_call | solution.py:51
  514.5 82.5 %shard_map.146 = (bf16[4096,640]{1,0:T(8,128)(2,1)}, bf16[1024,640]{1,0:T(8,128)(2,1)}) custom-call(s32[2]{0:T(128)} %pad_add_fusion.2.s_ref, bf16[4096,768]{1,0:T(8,128)(2,1)} %get-tuple-element.103.q_ref, bf16[4096,768]{1,0:T(8,128)(2,1)} %get-tuple-element.120.do_ref, bf16[4096,768]{1,0:T(8,128)(2,1)} %get-tuple-element.108.o_ref.oa_ref.rest_0_, ...), custom_call_target="tpu_custom_call" | custom-call | flops 36238786560 | bytes 70778880 | tf_op jit(solution)/shard_map/pallas_call | solution.py:51
  600.8 53.9 %shard_map.147 = (f32[3072,3072]{1,0:T(8,128)}, f32[1536,3072]{1,0:T(8,128)}) custom-call(s32[2]{0:T(128)} %pad_add_fusion.1.s_ref, bf16[4096,768]{1,0:T(8,128)(2,1)} %get-tuple-element.108.o_ref.oa_ref.rest_0_, bf16[4096,768]{1,0:T(8,128)(2,1)} %constant_dynamic-update-slice_fusion.ob_ref.rest_2_, bf16[4096,3072]{1,0:T(8,128)(2,1)} %get-tuple-element.128.dy_ref), custom_call_target="tpu_custom_call" | custom-call | flops 38654705664 | bytes 75497472 | tf_op jit(solution)/shard_map/pallas_call | solution.py:51
  658.1 27.2 %collective-permute-done.14.rest_1_ = bf16[1024,768]{1,0:T(8,128)(2,1)S(1)} collective-permute-done((bf16[1024,768]{1,0:T(8,128)(2,1)}, bf16[1024,768]{1,0:T(8,128)(2,1)S(1)}, u32[]{:S(2)}, u32[]{:S(2)}) %collective-permute-start.14) | collective-permute-done | bytes 1572896 | tf_op jit(solution)/shard_map/ppermute | solution.py:664
  687.7 27.1 %shard_map.148 = bf16[1024,3072]{1,0:T(8,128)(2,1)} custom-call(s32[4]{0:T(128)} %pad_add_fusion.s_ref, bf16[1024,3072]{1,0:T(8,128)(2,1)} %x_ref.3, bf16[4096,768]{1,0:T(8,128)(2,1)} %get-tuple-element.108.o_ref.oa_ref.rest_0_, bf16[1024,768]{1,0:T(8,128)(2,1)} %copy-done.1, bf16[4096,768]{1,0:T(8,128)(2,1)} %constant_dynamic-update-slice_fusion.ob_ref.rest_2_, ...), custom_call_target="tpu_custom_call" | custom-call | flops 19327352832 | bytes 37748736 | tf_op jit(solution)/shard_map/pallas_call | solution.py:51
  714.8 46.3 %shard_map.149 = (f32[3072,3072]{1,0:T(8,128)}, f32[3072,1024]{1,0:T(8,128)}, f32[3072,1024]{1,0:T(8,128)}, f32[3072,1280]{1,0:T(8,128)}, f32[3072,3072]{1,0:T(8,128)}) custom-call(s32[3]{0:T(128)} %pad_add_fusion.4.s_ref, bf16[4096,3072]{1,0:T(8,128)(2,1)} %get-tuple-element.110.h_ref.refs_1_, ...), custom_call_target="tpu_custom_call", output_to_operand_aliasing={{4}: (5, {})} | custom-call | flops 32212254720 | bytes 62914560 | tf_op jit(solution)/shard_map/pallas_call | solution.py:51
  763.9 113.6 %collective-permute-done.16.refs_2_.refs_3_.rest_4_ = bf16[4096,640]{1,0:T(8,128)(2,1)S(1)} collective-permute-done((bf16[4096,640]{1,0:T(8,128)(2,1)}, bf16[4096,640]{1,0:T(8,128)(2,1)S(1)}, u32[]{:S(2)}, u32[]{:S(2)}) %collective-permute-start.16) | collective-permute-done | bytes 5242912 | tf_op jit(solution)/shard_map/ppermute | solution.py:661
  881.0 25.9 %shard_map.150 = (f32[3072,3072]{1,0:T(8,128)}, f32[3072,1024]{1,0:T(8,128)}, f32[3072,512]{1,0:T(8,128)}) custom-call(s32[1]{0:T(128)} %bitcast.2.s_ref.refs_0_, bf16[4096,3072]{1,0:T(8,128)(2,1)} %get-tuple-element.110.h_ref.refs_1_, bf16[4096,640]{1,0:T(8,128)(2,1)} %copy-done, ...), custom_call_target="tpu_custom_call", output_to_operand_aliasing={{0}: (4, {}), {1}: (5, {})} | custom-call | flops 12884901888 | bytes 25165824 | tf_op jit(solution)/shard_map/pallas_call | solution.py:51
  908.0 36.1 %shard_map.151 = (f32[1024,3072]{1,0:T(8,128)}, f32[3072,3072]{1,0:T(8,128)}, f32[3072,1024]{1,0:T(8,128)}, f32[3072,1024]{1,0:T(8,128)}) custom-call(s32[4]{0:T(128)} %pad_add_fusion.s_ref, bf16[4096,640]{1,0:T(8,128)(2,1)} %get-tuple-element.122.ga_ref.rest_0_, ...), custom_call_target="tpu_custom_call", output_to_operand_aliasing={{1}: (12, {}), {2}: (13, {}), {3}: (14, {})} | custom-call | flops 24159191040 | bytes 47185920 | tf_op jit(solution)/shard_map/pallas_call | solution.py:51
  944.0 45.3 %collective-permute-done.18.refs_3_.b2 = bf16[4096,640]{1,0:T(8,128)(2,1)} collective-permute-done((bf16[4096,640]{1,0:T(8,128)(2,1)}, bf16[4096,640]{1,0:T(8,128)(2,1)}, u32[]{:S(2)}, u32[]{:S(2)}) %collective-permute-start.18) | collective-permute-done | bytes 5242912 | tf_op jit(solution)/shard_map/ppermute | solution.py:661
  989.3 29.6 %shard_map.152 = (f32[3072,3072]{1,0:T(8,128)}, f32[3072,1024]{1,0:T(8,128)}, f32[3072,1024]{1,0:T(8,128)}, f32[3072,768]{1,0:T(8,128)}) custom-call(s32[1]{0:T(128)} %bitcast.2.s_ref.refs_0_, bf16[4096,3072]{1,0:T(8,128)(2,1)} %get-tuple-element.110.h_ref.refs_1_, ...), custom_call_target="tpu_custom_call", output_to_operand_aliasing={{0}: (4, {}), {1}: (5, {}), {2}: (6, {})} | custom-call | flops 19327352832 | bytes 37748736 | tf_op jit(solution)/shard_map/pallas_call | solution.py:51
  1020.9 22.0 %collective-permute-done.24.rcv = f32[3072,512]{1,0:T(8,128)} collective-permute-done((f32[3072,512]{1,0:T(8,128)}, f32[3072,512]{1,0:T(8,128)}, u32[]{:S(2)}, u32[]{:S(2)}) %collective-permute-start.24) | collective-permute-done | bytes 6291488 | tf_op jit(solution)/shard_map/ppermute | solution.py:664
  1045.8 31.6 %shard_map.153 = (bf16[1024,3072]{1,0:T(8,128)(2,1)}, f32[8,3072]{1,0:T(8,128)}, f32[3072,3072]{1,0:T(8,128)}, f32[3072,1024]{1,0:T(8,128)}) custom-call(s32[4]{0:T(128)} %pad_add_fusion.s_ref, bf16[1024,3072]{1,0:T(8,128)(2,1)} %x_ref.3, bf16[1024,3072]{1,0:T(8,128)(2,1)} %dy_ref.1, ...), custom_call_target="tpu_custom_call", output_to_operand_aliasing={{2}: (10, {}), {3}: (11, {})} | custom-call | flops 8053063680 | bytes 15728640 | tf_op jit(solution)/shard_map/pallas_call | solution.py:51
  (94 shorter events, 111.1 us)
Async XLA Ops:
  0.7 10.9 collective-permute-start.3
  11.5 59.4 %collective-permute-start.6 = (bf16[1024,3072]{1,0:T(8,128)(2,1)}, bf16[1024,3072]{1,0:T(8,128)(2,1)}, u32[]{:S(2)}, u32[]{:S(2)}) collective-permute-start(bf16[1024,3072]{1,0:T(8,128)(2,1)} %dy_ref.1), channel_id=1, source_target_pairs={{0,1},{1,0},{2,3},{3,2},{4,5},{5,4},{6,7},{7,6}} | collective-permute-start | bytes 18874376 | tf_op jit(solution)/shard_map/ppermute | solution.py:664
  14.2 10.8 collective-permute-start.4
  14.6 8.6 collective-permute-start
  24.7 86.8 %collective-permute-start.2 = (bf16[512,3072]{1,0:T(8,128)(2,1)}, bf16[512,3072]{1,0:T(8,128)(2,1)}, u32[]{:S(2)}, u32[]{:S(2)}) collective-permute-start(bf16[512,3072]{1,0:T(8,128)(2,1)} %get-tuple-element.88), channel_id=1, source_target_pairs={{0,2},{1,3},{2,0},{3,1},{4,6},{5,7},{6,4},{7,5}} | collective-permute-start | bytes 9437192 | tf_op jit(solution)/shard_map/ppermute | solution.py:661
  111.5 6.1 collective-permute-start.7
  112.0 70.4 %collective-permute-start.1 = (bf16[512,3072]{1,0:T(8,128)(2,1)}, bf16[512,3072]{1,0:T(8,128)(2,1)}, u32[]{:S(2)}, u32[]{:S(2)}) collective-permute-start(bf16[512,3072]{1,0:T(8,128)(2,1)} %get-tuple-element.86), channel_id=1, source_target_pairs={{0,2},{1,3},{2,0},{3,1},{4,6},{5,7},{6,4},{7,5}} | collective-permute-start | bytes 9437192 | tf_op jit(solution)/shard_map/ppermute | solution.py:661
  182.3 6.1 collective-permute-start.8
  186.7 153.3 %collective-permute-start.10 = (bf16[512,3072]{1,0:T(8,128)(2,1)}, bf16[512,3072]{1,0:T(8,128)(2,1)}, u32[]{:S(2)}, u32[]{:S(2)}) collective-permute-start(bf16[512,3072]{1,0:T(8,128)(2,1)} %slice.15), channel_id=1, source_target_pairs={{0,2},{1,3},{2,0},{3,1},{4,6},{5,7},{6,4},{7,5}} | collective-permute-start | bytes 9437192 | tf_op jit(solution)/shard_map/ppermute | solution.py:661
  340.0 6.0 collective-permute-start.11
  343.9 70.6 %collective-permute-start.9 = (bf16[512,3072]{1,0:T(8,128)(2,1)}, bf16[512,3072]{1,0:T(8,128)(2,1)}, u32[]{:S(2)}, u32[]{:S(2)}) collective-permute-start(bf16[512,3072]{1,0:T(8,128)(2,1)} %slice.14), channel_id=1, source_target_pairs={{0,2},{1,3},{2,0},{3,1},{4,6},{5,7},{6,4},{7,5}} | collective-permute-start | bytes 9437192 | tf_op jit(solution)/shard_map/ppermute | solution.py:661
  416.4 180.6 %collective-permute-start.13 = (bf16[2048,768]{1,0:T(8,128)(2,1)}, bf16[2048,768]{1,0:T(8,128)(2,1)}, u32[]{:S(2)}, u32[]{:S(2)}) collective-permute-start(bf16[2048,768]{1,0:T(8,128)(2,1)} %get-tuple-element.126), channel_id=1, source_target_pairs={{0,2},{1,3},{2,0},{3,1},{4,6},{5,7},{6,4},{7,5}} | collective-permute-start | bytes 9437192 | tf_op jit(solution)/shard_map/ppermute | solution.py:661
  654.7 60.1 %collective-permute-start.17 = (f32[1536,3072]{1,0:T(8,128)}, f32[1536,3072]{1,0:T(8,128)}, u32[]{:S(2)}, u32[]{:S(2)}) collective-permute-start(f32[1536,3072]{1,0:T(8,128)} %get-tuple-element.129), channel_id=1, source_target_pairs={{0,1},{1,0},{2,3},{3,2},{4,5},{5,4},{6,7},{7,6}} | collective-permute-start | bytes 56623112 | tf_op jit(solution)/shard_map/ppermute | solution.py:664
  654.9 30.5 %collective-permute-start.14 = (bf16[1024,768]{1,0:T(8,128)(2,1)}, bf16[1024,768]{1,0:T(8,128)(2,1)S(1)}, u32[]{:S(2)}, u32[]{:S(2)}) collective-permute-start(bf16[1024,768]{1,0:T(8,128)(2,1)} %get-tuple-element.131), channel_id=1, source_target_pairs={{0,1},{1,0},{2,3},{3,2},{4,5},{5,4},{6,7},{7,6}} | collective-permute-start | bytes 4718600 | tf_op jit(solution)/shard_map/ppermute | solution.py:664
  656.7 31.0 %collective-permute-start.15 = (bf16[1024,768]{1,0:T(8,128)(2,1)S(1)}, bf16[1024,768]{1,0:T(8,128)(2,1)}, u32[]{:S(2)}, u32[]{:S(2)}) collective-permute-start(bf16[1024,768]{1,0:T(8,128)(2,1)S(1)} %constant_dynamic-slice_fusion.2), channel_id=1, source_target_pairs={{0,1},{1,0},{2,3},{3,2},{4,5},{5,4},{6,7},{7,6}} | collective-permute-start | bytes 4718600 | tf_op jit(solution)/shard_map/ppermute | solution.py:664
  761.2 145.7 %collective-permute-start.22 = (f32[3072,1280]{1,0:T(8,128)}, f32[3072,1280]{1,0:T(8,128)}, u32[]{:S(2)}, u32[]{:S(2)}) collective-permute-start(f32[3072,1280]{1,0:T(8,128)} %get-tuple-element.134), channel_id=1, source_target_pairs={{0,1},{1,0},{2,3},{3,2},{4,5},{5,4},{6,7},{7,6}} | collective-permute-start | bytes 47185928 | tf_op jit(solution)/shard_map/ppermute | solution.py:664
  761.3 116.1 %collective-permute-start.16 = (bf16[4096,640]{1,0:T(8,128)(2,1)}, bf16[4096,640]{1,0:T(8,128)(2,1)S(1)}, u32[]{:S(2)}, u32[]{:S(2)}) collective-permute-start(bf16[4096,640]{1,0:T(8,128)(2,1)} %get-tuple-element.122.ga_ref.rest_0_), channel_id=1, source_target_pairs={{0,2},{1,3},{2,0},{3,1},{4,6},{5,7},{6,4},{7,5}} | collective-permute-start | bytes 15728648 | tf_op jit(solution)/shard_map/ppermute | solution.py:661
  762.9 226.4 %collective-permute-start.18 = (bf16[4096,640]{1,0:T(8,128)(2,1)}, bf16[4096,640]{1,0:T(8,128)(2,1)}, u32[]{:S(2)}, u32[]{:S(2)}) collective-permute-start(bf16[4096,640]{1,0:T(8,128)(2,1)} %get-tuple-element.124.gb_ref.rest_1_), channel_id=1, source_target_pairs={{0,2},{1,3},{2,0},{3,1},{4,6},{5,7},{6,4},{7,5}} | collective-permute-start | bytes 15728648 | tf_op jit(solution)/shard_map/ppermute | solution.py:661
  763.3 143.5 %collective-permute-start.20 = (bf16[1024,640]{1,0:T(8,128)(2,1)}, bf16[1024,640]{1,0:T(8,128)(2,1)S(1)}, u32[]{:S(2)}, u32[]{:S(2)}) collective-permute-start(bf16[1024,640]{1,0:T(8,128)(2,1)} %get-tuple-element.141), channel_id=1, source_target_pairs={{0,1},{1,0},{2,3},{3,2},{4,5},{5,4},{6,7},{7,6}} | collective-permute-start | bytes 3932168 | tf_op jit(solution)/shard_map/ppermute | solution.py:664
  763.3 143.5 %collective-permute-start.19 = (bf16[1024,640]{1,0:T(8,128)(2,1)}, bf16[1024,640]{1,0:T(8,128)(2,1)}, u32[]{:S(2)}, u32[]{:S(2)}) collective-permute-start(bf16[1024,640]{1,0:T(8,128)(2,1)} %get-tuple-element.140), channel_id=1, source_target_pairs={{0,1},{1,0},{2,3},{3,2},{4,5},{5,4},{6,7},{7,6}} | collective-permute-start | bytes 3932168 | tf_op jit(solution)/shard_map/ppermute | solution.py:664
  881.0 25.9 %collective-permute-start.21 = (bf16[1024,640]{1,0:T(8,128)(2,1)}, bf16[1024,640]{1,0:T(8,128)(2,1)}, u32[]{:S(2)}, u32[]{:S(2)}) collective-permute-start(bf16[1024,640]{1,0:T(8,128)(2,1)} %constant_dynamic-slice_fusion.1), channel_id=1, source_target_pairs={{0,1},{1,0},{2,3},{3,2},{4,5},{5,4},{6,7},{7,6}} | collective-permute-start | bytes 3932168 | tf_op jit(solution)/shard_map/ppermute | solution.py:664
  1018.9 64.9 %collective-permute-start.25 = (f32[3072,768]{1,0:T(8,128)}, f32[3072,768]{1,0:T(8,128)}, u32[]{:S(2)}, u32[]{:S(2)}) collective-permute-start(f32[3072,768]{1,0:T(8,128)} %get-tuple-element.150), channel_id=1, source_target_pairs={{0,1},{1,0},{2,3},{3,2},{4,5},{5,4},{6,7},{7,6}} | collective-permute-start | bytes 28311560 | tf_op jit(solution)/shard_map/ppermute | solution.py:664
  1018.9 24.0 %collective-permute-start.24 = (f32[3072,512]{1,0:T(8,128)}, f32[3072,512]{1,0:T(8,128)}, u32[]{:S(2)}, u32[]{:S(2)}) collective-permute-start(f32[3072,512]{1,0:T(8,128)} %get-tuple-element.138), channel_id=1, source_target_pairs={{0,1},{1,0},{2,3},{3,2},{4,5},{5,4},{6,7},{7,6}} | collective-permute-start | bytes 18874376 | tf_op jit(solution)/shard_map/ppermute | solution.py:664
  1020.9 23.8 %collective-permute-start.23 = (bf16[1024,640]{1,0:T(8,128)(2,1)S(1)}, bf16[1024,640]{1,0:T(8,128)(2,1)S(1)}, u32[]{:S(2)}, u32[]{:S(2)}) collective-permute-start(bf16[1024,640]{1,0:T(8,128)(2,1)S(1)} %constant_dynamic-slice_fusion), channel_id=1, source_target_pairs={{0,1},{1,0},{2,3},{3,2},{4,5},{5,4},{6,7},{7,6}} | collective-permute-start | bytes 3932168 | tf_op jit(solution)/shard_map/ppermute | solution.py:664
  (11 other events, 70.0 us)

commit v3 on v2

--- a/solution.py
+++ b/solution.py
@@ -94,7 +94,7 @@
 
 
 def proj_body(s_ref, xa_ref, xb_ref, gain_ref, wq_ref, wk_ref, wv_ref, cos_ref, sin_ref, *rest):
-    h_ref, q_ref, k_ref, v_ref, inv_scr = rest[-5:]
+    h_ref, q_ref, k_ref, v_ref, inv_ref = rest[-5:]
     half = pl.num_programs(0) // 2
 
     def norm(src):
@@ -104,12 +104,12 @@
             sl = ds(c * step, step)
             xf = src[sl, :].astype(F32)
             inv = lax.rsqrt(jnp.mean(xf * xf, axis=-1, keepdims=True) + NORM_EPS)
-            inv_scr[sl, :] = jnp.broadcast_to(inv, (step, HEAD))
+            inv_ref[sl, :] = jnp.broadcast_to(inv, (step, HEAD))
             return 0
 
         def scale(c, _):
             sl = ds(c * step, step)
-            inv, gain = inv_scr[sl, :], gain_ref[...]
+            inv, gain = inv_ref[sl, :], gain_ref[...]
             for n in range(src.shape[1] // HEAD):
                 cols = slice(n * HEAD, n * HEAD + HEAD)
                 h_ref[sl, cols] = (src[sl, cols].astype(F32) * inv * gain[:, cols]).astype(BF)
@@ -130,7 +130,8 @@
 
 
 def two_source(rows):
-    nb = rows // BLK
+    bm = HB if rows % BLK else BLK
+    nb = rows // bm
 
     def a_map(i, s):
         return (jnp.minimum(i, nb - 1), 0)
@@ -141,25 +142,25 @@
     def o_map(i, s):
         return (jnp.where(i < nb, s[0] + i, s[1] + i - nb), 0)
 
-    return nb, a_map, b_map, o_map
+    return bm, nb, a_map, b_map, o_map
 
 
 def project(idx, xa, xb, gain, ws, tabs, bufs, seq):
     rows, d = xa.shape
-    nb, a_map, b_map, o_map = two_source(rows)
+    bm, nb, a_map, b_map, o_map = two_source(rows)
     widths = [w.shape[1] // 4 for w in ws]
-    in_specs = [pl.BlockSpec((BLK, d), a_map), pl.BlockSpec((BLK, d), b_map), pl.BlockSpec((1, d), first_row)]
+    in_specs = [pl.BlockSpec((bm, d), a_map), pl.BlockSpec((bm, d), b_map), pl.BlockSpec((1, d), first_row)]
     in_specs += [pl.BlockSpec((d, w), lambda i, s: (0, s[2])) for w in widths]
-    in_specs += [pl.BlockSpec((BLK, HEAD), o_map)] * 2
+    in_specs += [pl.BlockSpec((bm, HEAD), o_map)] * 2
     args = [idx, xa, xb, gain, *ws, *tabs]
     aliases = {}
     if bufs is not None:
-        in_specs += [ANY] * 4
-        aliases = {len(args) + n: n for n in range(4)}
+        in_specs += [ANY] * len(bufs)
+        aliases = {len(args) + n: n for n in range(len(bufs))}
         args += list(bufs)
-    return call(proj_body, (2 * nb,), in_specs, [pl.BlockSpec((BLK, w), o_map) for w in (d, *widths)],
-                [sds(seq, w) for w in (d, *widths)], args, 4 * rows * d * sum(widths),
-                scratch=[pltpu.VMEM((BLK, HEAD), F32)], aliases=aliases)
+    return call(proj_body, (2 * nb,), in_specs, [pl.BlockSpec((bm, w), o_map) for w in (d, *widths, HEAD)],
+                [sds(seq, w) for w in (d, *widths)] + [sds(seq, HEAD, F32)], args, 4 * rows * d * sum(widths),
+                aliases=aliases)
 
 
 def projc_body(s_ref, h_ref, *rest):
@@ -193,9 +194,9 @@
 
 def dout(idx, da, db, w_o, bufs, seq):
     rows, d = da.shape
-    nb, a_map, b_map, o_map = two_source(rows)
+    bm, nb, a_map, b_map, o_map = two_source(rows)
     oc = w_o.shape[0] // 4
-    in_specs = [pl.BlockSpec((BLK, d), a_map), pl.BlockSpec((BLK, d), b_map),
+    in_specs = [pl.BlockSpec((bm, d), a_map), pl.BlockSpec((bm, d), b_map),
                 pl.BlockSpec((oc, d), lambda i, s: (s[2], 0))]
     args = [idx, da, db, w_o]
     aliases = {}
@@ -203,7 +204,7 @@
         in_specs += [ANY] * 2
         aliases = {len(args) + n: n for n in range(2)}
         args += list(bufs)
-    return call(dout_body, (2 * nb,), in_specs, [pl.BlockSpec((BLK, w), o_map) for w in (d, oc)],
+    return call(dout_body, (2 * nb,), in_specs, [pl.BlockSpec((bm, w), o_map) for w in (d, oc)],
                 [sds(seq, w) for w in (d, oc)], args, 4 * rows * d * oc, aliases=aliases)
 
 
@@ -245,18 +246,20 @@
             stat[old, row] = jnp.exp2(m_old - m_new)
         stat[cur, row] = m_new
 
-    def stage_b(h, j):
+    def stage_p(h):
         row = slice(h, h + 1)
         p = jnp.exp2(s_scr[h] - stat[cur, row])
         alpha = stat[old, row]
         stat[den_row, row] = stat[den_row, row] * alpha + jnp.sum(p, axis=0, keepdims=True)
-        acc[h] = acc[h] * alpha + mm(vt[:, ds(j * BLK, BLK)], p.astype(BF))
-
-    def finish(h, i):
+        return p.astype(BF), alpha
+
+    def stage_v(h, j, held):
+        acc[h] = acc[h] * held[1] + mm(vt[:, ds(j * BLK, BLK)], held[0])
+
+    def finish(h, i, den, top):
         row = slice(h, h + 1)
-        den = stat[den_row, row]
         o_ref[ds(i * BLK, BLK), h * HEAD:(h + 1) * HEAD] = (acc[h] / den).T.astype(BF)
-        lse_ref[0, row, ds(i * BLK, BLK)] = stat[cur, row] + jnp.log2(den)
+        lse_ref[0, row, ds(i * BLK, BLK)] = top + jnp.log2(den)
 
     for h in range(GROUP):
         stage_a(h, 0, 0, True, True)
@@ -264,8 +267,9 @@
     def row(i, _):
         def inner(j, _):
             for h in range(GROUP):
-                stage_b(h, j)
+                held = stage_p(h)
                 stage_a(h, i, j + 1, False, False)
+                stage_v(h, j, held)
             return 0
 
         lax.fori_loop(0, i - 1, inner, 0)
@@ -273,14 +277,17 @@
         @pl.when(i > 0)
         def _():
             for h in range(GROUP):
-                stage_b(h, i - 1)
+                held = stage_p(h)
                 stage_a(h, i, i, True, False)
+                stage_v(h, i - 1, held)
 
         nxt = jnp.minimum(i + 1, nq - 1)
         for h in range(GROUP):
-            stage_b(h, i)
-            finish(h, i)
+            held = stage_p(h)
+            final = (stat[den_row, h:h + 1], stat[cur, h:h + 1])
             stage_a(h, nxt, 0, False, True)
+            stage_v(h, i, held)
+            finish(h, i, *final)
         return 0
 
     lax.fori_loop(0, nq, row, 0)
@@ -321,20 +328,24 @@
 
         def setup(c, _):
             sl = ds(c * BLK, BLK)
-            minus = jnp.where(lax.broadcasted_iota(jnp.int32, (BLK, HEAD), 1) < 3, -1.0, 0.0).astype(BF)
-            for src, dst in ((k_ref, ka), (v_ref, va)):
+            third = lax.broadcasted_iota(jnp.int32, (BLK, HEAD), 1) // 3
+            for n, (src, dst) in enumerate(((k_ref, ka), (v_ref, va))):
                 dst[sl, :HEAD] = src[sl, :]
-                dst[sl, HEAD:] = minus
+                dst[sl, HEAD:] = jnp.where(third == n, -1.0, 0.0).astype(BF)
             return 0
 
         lax.fori_loop(0, seq // BLK, setup, 0)
 
     srow = lax.broadcasted_iota(jnp.int32, (16, HB), 0)
-
-    def augment(dst, rows, row):
-        hi, mid, low = split3(row)
-        parts = jnp.where(srow == 0, hi, jnp.where(srow == 1, mid, jnp.where(srow == 2, low, 0.0))).astype(BF)
-        dst[rows, HEAD:] = jnp.concatenate([parts, jnp.zeros((HEAD - 16, HB), BF)], axis=0).T
+    blank = jnp.zeros((HEAD - 16, HB), BF)
+
+    def augment(rows, *vals):
+        parts = jnp.zeros((16, HB), F32)
+        for n, part in enumerate(split3(vals[0]) + split3(vals[1])):
+            parts = jnp.where(srow == n, part, parts)
+        block = jnp.concatenate([parts.astype(BF), blank], axis=0).T
+        qa[rows, HEAD:] = block
+        da[rows, HEAD:] = block
 
     def spots():
         for b in range(2):
@@ -349,8 +360,8 @@
         q3t[:, rows] = qh.T
         dt = doh.T
         do3t[:, rows] = dt
-        augment(da, rows, jnp.sum(dt.astype(F32) * o_ref[src, cols].T.astype(F32), axis=0, keepdims=True))
-        augment(qa, rows, lse_ref[0, h:h + 1, src] * (1.0 / SCALE2))
+        delta = jnp.sum(dt.astype(F32) * o_ref[src, cols].T.astype(F32), axis=0, keepdims=True)
+        augment(rows, lse_ref[0, h:h + 1, src] * (1.0 / SCALE2), delta)
     dq3[...] = jnp.zeros_like(dq3)
 
     def step(rows, start, width, masked):
@@ -465,71 +476,90 @@
                 scratch=[pltpu.VMEM((2 * hw, seq), BF)])
 
 
-def dwown_body(s_ref, h_ref, ga_ref, gb_ref, wo_ref, _, fq, fk, fv, snd, wo_fin, ht, sem):
-    i, rows = pl.program_id(0), wo_ref.shape[0]
-    per = pl.num_programs(0) // 2
-    start = jnp.where(i < per, s_ref[1] * per + i, s_ref[2] * per + i - per)
-    copy = pltpu.make_async_copy(wo_ref, wo_fin.at[ds(start * rows, rows), :], sem)
-    copy.start()
+def dwown_body(s_ref, h_ref, ga_ref, gb_ref, gc_ref, wo_ref, _, fq, fk, fv, snd, wo_fin, ht, sem, wsem):
+    i, steps = pl.program_id(0), pl.num_programs(0)
+    rows, per = wo_ref.shape[0], steps // 2
+    start = jnp.where(i < per, s_ref[1] * per + i, s_ref[3] * per + i - per)
+    wcopy = pltpu.make_async_copy(wo_ref, wo_fin.at[ds(start * rows, rows), :], wsem)
+    wcopy.start()
+
+    @pl.when(i > 0)
+    def _():
+        for copy in scatter(snd, (fq, fk, fv), s_ref[0], s_ref[2], sem):
+            copy.wait()
+
     ht[...] = h_ref[...].T
     lhs = ht[...]
-    for n, g in enumerate((ga_ref, gb_ref)):
+    for g, q_at, k_at in ((ga_ref, 0, 2 * GW), (gb_ref, GW, 2 * GW + HEAD), (gc_ref, 2 * PW, 2 * PW + GW)):
         val = mm(lhs, g[:, :QK])
-        for ref, base in ((fq, 0), (snd, 0)):
-            ref[:, base + n * GW:base + (n + 1) * GW] = val[:, :GW]
-        fk[:, n * HEAD:(n + 1) * HEAD] = val[:, GW:]
-        snd[:, 2 * GW + n * HEAD:2 * GW + (n + 1) * HEAD] = val[:, GW:]
+        snd[:, q_at:q_at + GW] = val[:, :GW]
+        snd[:, k_at:k_at + HEAD] = val[:, GW:]
+    snd[:, 2 * QK:2 * PW] = mm(lhs, jnp.concatenate([ga_ref[:, QK:], gb_ref[:, QK:]], axis=1))
+    copies = scatter(snd, (fq, fk, fv), s_ref[0], s_ref[2], sem)
+    for copy in copies:
+        copy.start()
+
+    @pl.when(i == steps - 1)
+    def _():
+        for copy in copies:
+            copy.wait()
+
+    wcopy.wait()
+
+
+def scatter(rcv, outs, whole_dev, part_dev, sem):
+    rows, src, copies = ds(pl.program_id(0) * rcv.shape[0], rcv.shape[0]), 0, []
+    fq, fk, fv = outs
+    for n, (out, col, w) in enumerate(((fq, whole_dev, 2 * GW), (fk, whole_dev, PAIR), (fv, whole_dev, PAIR),
+                                       (fq, 2 * part_dev, GW), (fk, 2 * part_dev, HEAD))):
+        copies.append(pltpu.make_async_copy(rcv.at[:, src:src + w], out.at[rows, ds(col * w, w)], sem.at[n]))
+        src += w
+    return copies
+
+
+def dw_own(idx, h, ga, gb, gc, wo_rcv, wo_fin):
+    seq, d = h.shape
+    steps = d // HB
+    gspec = pl.BlockSpec((seq, PW), first_row, pipeline_mode=pl.Buffered(1))
+    widths = (2 * GW, PAIR, PAIR)
+    sw = 2 * PW + QK
+    return call(dwown_body, (steps,),
+                [pl.BlockSpec((seq, HB), col_map)] + [gspec] * 3
+                + [pl.BlockSpec((wo_rcv.shape[0] // steps, d), row_map), ANY],
+                [ANY] * 3 + [pl.BlockSpec((HB, sw), row_map), ANY],
+                [sds(d, 4 * w, F32) for w in widths] + [sds(d, sw, F32), sds(*wo_fin.shape, F32)],
+                [idx, h, ga, gb, gc, wo_rcv, wo_fin], 2 * seq * d * sw,
+                scratch=[pltpu.VMEM((HB, seq), BF), pltpu.SemaphoreType.DMA((5,)), pltpu.SemaphoreType.DMA],
+                aliases={6: 4})
+
+
+def dwgrp_body(s_ref, h_ref, ga_ref, gb_ref, *rest):
+    fq, fk, fv, snd, ht = rest[-5:]
+    ht[...] = h_ref[...].T
+    lhs = ht[...]
+    val = mm(lhs, gb_ref[:, :QK])
+    fq[...] = val[:, :GW]
+    fk[...] = val[:, GW:]
+    snd[:, :QK] = val
     val = mm(lhs, jnp.concatenate([ga_ref[:, QK:], gb_ref[:, QK:]], axis=1))
     fv[...] = val
-    snd[:, 2 * QK:] = val
-    copy.wait()
-
-
-def dw_own(idx, h, ga, gb, wo_rcv, wo_fin):
+    snd[:, QK:] = val
+
+
+def group_specs():
+    return [pl.BlockSpec((HB, w), lambda i, s: (i, 2 * s[0] + 1)) for w in (GW, HEAD)] + \
+        [pl.BlockSpec((HB, PAIR), lambda i, s: (i, s[0]))]
+
+
+def dw_group(idx, h, ga, gb, bufs):
     seq, d = h.shape
-    steps = d // HB
-    gspec = pl.BlockSpec((seq, PW), first_row)
-    widths = (2 * GW, PAIR, PAIR)
-    return call(dwown_body, (steps,),
-                [pl.BlockSpec((seq, HB), col_map), gspec, gspec, pl.BlockSpec((wo_rcv.shape[0] // steps, d), row_map), ANY],
-                [pl.BlockSpec((HB, w), lambda i, s: (i, s[0])) for w in widths]
-                + [pl.BlockSpec((HB, 2 * PW), row_map), ANY],
-                [sds(d, 4 * w, F32) for w in widths] + [sds(d, 2 * PW, F32), sds(*wo_fin.shape, F32)],
-                [idx, h, ga, gb, wo_rcv, wo_fin], 4 * seq * d * PW,
-                scratch=[pltpu.VMEM((HB, seq), BF), pltpu.SemaphoreType.DMA], aliases={5: 4})
-
-
-def dwgrp_body(with_v, s_ref, h_ref, ga_ref, gb_ref, *rest):
-    ht, snd = rest[-1], rest[-2]
-    outs = rest[-2 - (3 if with_v else 2):-2]
-    ht[...] = h_ref[...].T
-    lhs = ht[...]
-    val = mm(lhs, (gb_ref if with_v else ga_ref)[:, :QK])
-    outs[0][...] = val[:, :GW]
-    outs[1][...] = val[:, GW:]
-    snd[:, :QK] = val
-    if with_v:
-        val = mm(lhs, jnp.concatenate([ga_ref[:, QK:], gb_ref[:, QK:]], axis=1))
-        outs[2][...] = val
-        snd[:, QK:] = val
-
-
-def group_specs(with_v):
-    specs = [pl.BlockSpec((HB, w), lambda i, s: (i, 2 * s[0] + int(with_v))) for w in (GW, HEAD)]
-    return specs + ([pl.BlockSpec((HB, PAIR), lambda i, s: (i, s[0]))] if with_v else [])
-
-
-def dw_group(with_v, idx, h, ga, gb, bufs):
-    seq, d = h.shape
-    gspec = pl.BlockSpec((seq, PW), first_row)
-    specs = group_specs(with_v)
-    bufs = bufs[:len(specs)]
-    sw = QK + (PAIR if with_v else 0)
-    return call(lambda *refs: dwgrp_body(with_v, *refs), (d // HB,),
-                [pl.BlockSpec((seq, HB), col_map), gspec, gspec] + [ANY] * len(specs),
-                specs + [pl.BlockSpec((HB, sw), row_map)], [sds(*b.shape, F32) for b in bufs] + [sds(d, sw, F32)],
+    gspec = pl.BlockSpec((seq, PW), first_row, pipeline_mode=pl.Buffered(1))
+    sw = QK + PAIR
+    return call(dwgrp_body, (d // HB,),
+                [pl.BlockSpec((seq, HB), col_map), gspec, gspec] + [ANY] * 3,
+                group_specs() + [pl.BlockSpec((HB, sw), row_map)], [sds(*b.shape, F32) for b in bufs] + [sds(d, sw, F32)],
                 [idx, h, ga, gb, *bufs], 2 * seq * d * sw, scratch=[pltpu.VMEM((HB, seq), BF)],
-                aliases={4 + n: n for n in range(len(specs))})
+                aliases={4 + n: n for n in range(3)})
 
 
 def place_body(s_ref, rcv, *rest):
@@ -541,7 +571,7 @@
 
 def place(idx, rcv, bufs):
     d, w = rcv.shape
-    return call(place_body, (d // HB,), [pl.BlockSpec((HB, w), row_map)] + [ANY] * 3, group_specs(True),
+    return call(place_body, (d // HB,), [pl.BlockSpec((HB, w), row_map)] + [ANY] * 3, group_specs(),
                 [sds(*b.shape, F32) for b in bufs], [idx, rcv, *bufs], d * w, aliases={2 + n: n for n in range(3)})
 
 
@@ -557,99 +587,76 @@
                 pl.BlockSpec((d, PW), col_map), sds(d, groups * PW), [idx, *ws], d * groups * PW)
 
 
-def puts(rcv, outs, cols, widths, sem):
-    rows, src, copies = ds(pl.program_id(0) * rcv.shape[0], rcv.shape[0]), 0, []
-    for n, (out, col, w) in enumerate(zip(outs, cols, widths)):
-        copies.append(pltpu.make_async_copy(rcv.at[:, src:src + w], out.at[rows, ds(col * w, w)], sem.at[n]))
-        src += w
+def dx_body(s_ref, x_ref, dy_ref, gain_ref, inv_ref, *rest):
+    pieces, weights, rcv = rest[:8], rest[8:12], rest[12]
+    dx_ref, dg_ref, fq, fk, fv, acc, xs, tot, sem = rest[-9:]
+    n = pl.program_id(0)
+    bn = x_ref.shape[1]
+    rows, d = acc.shape
+    copies = scatter(rcv, (fq, fk, fv), s_ref[1], s_ref[3], sem)
     for copy in copies:
         copy.start()
-    return copies
-
-
-def dxa_body(s_ref, *rest):
-    pieces, weights, rcv = rest[:6], rest[6:10], rest[10]
-    out_ref, fq, fk, fv, sem = rest[-5:]
-    copies = puts(rcv, (fq, fk, fv), [s_ref[1]] * 3, (2 * GW, PAIR, PAIR), sem)
+
+    @pl.when(n == 0)
+    def _():
+        tot[...] = jnp.zeros_like(tot)
+
     lhs = jnp.concatenate([r[...] for r in pieces], axis=1)
     rhs = jnp.concatenate([r[...] for r in weights], axis=1)
-    out_ref[...] = mm_nt(lhs, rhs)
+    dh = mm_nt(lhs, rhs)
+    inv = inv_ref[...]
+    for c in range(bn // HEAD):
+        cols = slice(c * HEAD, c * HEAD + HEAD)
+        xb = x_ref[:, cols]
+        xs[:, ds(n * bn + cols.start, HEAD)] = xb
+        part, xf = dh[:, cols], xb.astype(F32)
+        scaled = part * gain_ref[:, cols]
+        tot[...] += scaled * xf
+        acc[:, ds(n * bn + cols.start, HEAD)] = dy_ref[:, cols].astype(F32) + inv * scaled
+        dg_ref[:, cols] = jnp.sum((part * (xf * inv)).reshape(rows // 8, 8, HEAD), axis=0)
+
+    @pl.when(n == pl.num_programs(0) - 1)
+    def _():
+        step = HEAD // 2
+
+        def stats(r, _):
+            sl = ds(r * step, step)
+            inv = inv_ref[sl, :]
+            tot[sl, :] = jnp.broadcast_to(jnp.sum(tot[sl, :], axis=-1, keepdims=True) / d, (step, HEAD)) * inv * inv * inv
+            return 0
+
+        lax.fori_loop(0, rows // step, stats, 0)
+
+        def epi(r, _):
+            sl = ds(r * step, step)
+            coef = tot[sl, :]
+            for c in range(d // HEAD):
+                cols = slice(c * HEAD, c * HEAD + HEAD)
+                dx_ref[sl, cols] = (acc[sl, cols] - xs[sl, cols].astype(F32) * coef).astype(BF)
+            return 0
+
+        lax.fori_loop(0, rows // step, epi, 0)
+
     for copy in copies:
         copy.wait()
 
 
-def dx_early(idx, pieces, w_p, rows, rcv, bufs):
-    d = w_p.shape[0]
-    maps = (own_map, own_map, first_row, first_row, own_map, first_row)
-    wspecs = [pl.BlockSpec((BLK, 2 * PW), lambda n, s, p=p: (n, s[p])) for p in range(2)]
-    wspecs += [pl.BlockSpec((BLK, PW), lambda n, s, p=p: (n, 2 * s[p])) for p in (2, 3)]
-    return call(dxa_body, (d // BLK,),
-                [pl.BlockSpec((rows, PW), m) for m in maps] + wspecs + [pl.BlockSpec((BLK, 2 * PW), row_map)] + [ANY] * 3,
-                [pl.BlockSpec((rows, BLK), col_map)] + [ANY] * 3, [sds(rows, d, F32)] + [sds(*b.shape, F32) for b in bufs],
-                [idx, *pieces] + [w_p] * 4 + [rcv, *bufs], 12 * rows * d * PW,
-                scratch=[pltpu.SemaphoreType.DMA((3,))], aliases={12 + n: 1 + n for n in range(3)})
-
-
-def dxb_body(s_ref, x_ref, dy_ref, gain_ref, early_ref, b2, b3, w2, w3, rcv, *rest):
-    dx_ref, dg_ref, fq, fk, acc, inv_scr, sem = rest[-7:]
-    n = pl.program_id(0)
-    copies = puts(rcv, (fq, fk), [2 * s_ref[3]] * 2, (GW, HEAD), sem)
-    lhs = jnp.concatenate([b2[...], b3[...]], axis=1)
-    rhs = jnp.concatenate([w2[...], w3[...]], axis=1)
-    acc[:, ds(n * BLK, BLK)] = early_ref[...] + mm_nt(lhs, rhs)
-
-    @pl.when(n == pl.num_programs(0) - 1)
-    def _():
-        step = HEAD // 2
-        rows, d = x_ref.shape
-        tiles = [slice(c * HEAD, c * HEAD + HEAD) for c in range(d // HEAD)]
-
-        def stats(r, _):
-            sl = ds(r * step, step)
-            sq = jnp.zeros((step, HEAD), F32)
-            dot = jnp.zeros((step, HEAD), F32)
-            for c in tiles:
-                xf = x_ref[sl, c].astype(F32)
-                sq += xf * xf
-                dot += xf * acc[sl, c] * gain_ref[:, c]
-            inv = lax.rsqrt(jnp.sum(sq, axis=-1, keepdims=True) / d + NORM_EPS)
-            inv_scr[0, sl, :] = jnp.broadcast_to(inv, (step, HEAD))
-            inv_scr[1, sl, :] = jnp.broadcast_to(jnp.sum(dot, axis=-1, keepdims=True) * inv * inv / d, (step, HEAD))
-            return 0
-
-        lax.fori_loop(0, rows // step, stats, 0)
-        dg_ref[...] = jnp.zeros_like(dg_ref)
-
-        def epi(r, _):
-            sl = ds(r * step, step)
-            inv, coef = inv_scr[0, sl, :], inv_scr[1, sl, :]
-            for c in tiles:
-                xf = x_ref[sl, c].astype(F32)
-                dh = acc[sl, c]
-                part = dh * (xf * inv)
-                dx_ref[sl, c] = (dy_ref[sl, c].astype(F32) + inv * (dh * gain_ref[:, c] - xf * coef)).astype(BF)
-                dg_ref[:, c] += jnp.sum(part.reshape(step // 8, 8, HEAD), axis=0)
-            return 0
-
-        lax.fori_loop(0, rows // step, epi, 0)
-
-    for copy in copies:
-        copy.wait()
-
-
-def dx_late(idx, x, dy, gain, early, b2, b3, w_p, rcv, bufs):
+def dx_call(idx, x, dy, gain, inv, pieces, w_p, rcv, bufs):
     rows, d = x.shape
-    wspecs = [pl.BlockSpec((BLK, PW), lambda n, s, p=p: (n, 2 * s[p] + 1)) for p in (2, 3)]
-    whole = pl.BlockSpec((rows, d), first_row)
-    return call(dxb_body, (d // BLK,),
-                [whole, whole, pl.BlockSpec((1, d), first_row), pl.BlockSpec((rows, BLK), col_map),
-                 pl.BlockSpec((rows, PW), own_map), pl.BlockSpec((rows, PW), first_row)] + wspecs
-                + [pl.BlockSpec((BLK, QK), row_map)] + [ANY] * 2,
-                [whole, pl.BlockSpec((8, d), first_row)] + [ANY] * 2,
+    bn = HB
+    once = pl.Buffered(1)
+    maps = (own_map, own_map, first_row, first_row) * 2
+    return call(dx_body, (d // bn,),
+                [pl.BlockSpec((rows, bn), col_map)] * 2 + [pl.BlockSpec((1, bn), col_map), pl.BlockSpec((rows, HEAD), own_map)]
+                + [pl.BlockSpec((rows, PW), m, pipeline_mode=once) for m in maps]
+                + [pl.BlockSpec((bn, 2 * PW), lambda n, s, p=p: (n, s[p])) for p in range(4)]
+                + [pl.BlockSpec((bn, rcv.shape[1]), row_map)] + [ANY] * 3,
+                [pl.BlockSpec((rows, d), first_row, pipeline_mode=once), pl.BlockSpec((8, bn), col_map)] + [ANY] * 3,
                 [sds(rows, d), sds(8, d, F32)] + [sds(*b.shape, F32) for b in bufs],
-                [idx, x, dy, gain, early, b2, b3, w_p, w_p, rcv, *bufs], 4 * rows * d * PW,
-                scratch=[pltpu.VMEM((rows, d), F32), pltpu.VMEM((2, rows, HEAD), F32), pltpu.SemaphoreType.DMA((2,))],
-                aliases={10: 2, 11: 3})
+                [idx, x, dy, gain, inv, *pieces] + [w_p] * 4 + [rcv, *bufs], 16 * rows * d * PW,
+                scratch=[pltpu.VMEM((rows, d), F32), pltpu.VMEM((rows, d), BF), pltpu.VMEM((rows, HEAD), F32),
+                         pltpu.SemaphoreType.DMA((5,))],
+                aliases={18 + n: 2 + n for n in range(3)})
 
 
 def solution(mesh):
@@ -677,7 +684,7 @@
         half = rows // 2
         j1, j2, j3 = [j ^ n for n in (1, 2, 3)]
         dev = (j, j1, j2, j3)
-        bpr = rows // BLK
+        bpr, hpr = rows // BLK, rows // HB
         ws = (w_q, w_k, w_v)
 
         def rows_of(val, blk):
@@ -685,11 +692,12 @@
 
         gain_f = gain.astype(F32).reshape(1, d)
 
-        xa, xb = after((x[:half], x[half:]), positions)
+        cut = rows - HB
+        xa = x[:cut]
         pos2 = over(positions)
         pos1 = near(positions)
-        x2a = over(after(xa, pos2))
-        x2b = over(after(xb, pos2))
+        x2a = over(xa)
+        x2b = over(after(x, xa)[cut:])
         x1 = near(x)
         pos3 = near(pos2)
         dy1 = near(after(dy, x1))
@@ -709,12 +717,12 @@
         x2a = after(x2a, w_p)
         dy2a = over(after(dy, x2a)[:half])
         x3a = near(x2a)
-        bufs = project(vec(j2 * bpr, j3 * bpr, j), x2a, x3a, gain_f, ws, tabs, bufs, seq)
+        bufs = project(vec(j2 * hpr, j3 * hpr, j), x2a, x3a, gain_f, ws, tabs, bufs, seq)
         x2b = after(x2b, bufs[1])
         dy2b = over(after(dy, x2b)[half:])
         x3b = near(x2b)
-        bufs = project(vec(j2 * bpr + 1, j3 * bpr + 1, j), x2b, x3b, gain_f, ws, tabs, bufs, seq)
-        h_all, q, k, v = bufs
+        bufs = project(vec((j2 + 1) * hpr - 1, (j3 + 1) * hpr - 1, j), x2b, x3b, gain_f, ws, tabs, bufs, seq)
+        h_all, q, k, v, inv = bufs
         o, lse, o_hi, o_pair = attn_fwd(vec(j1), q, k, v, seq, rows)
         orv = over(o_hi)
         o1 = near(o_pair)
@@ -741,21 +749,17 @@
         wo_fin, wo_snd = dw_o(vec(j, j2, dep=(gb,)), o, ox, dy_all)
         wo_rcv = near(wo_snd)
         result = out_proj(vec(*dev, dep=(wo_snd,)), x, (o, o1, ox, o3), w_o)
-        fq, fk, fv, snd, wo_fin = dw_own(vec(j, j1, j3, dep=(result,)), h_all, ga, gb, wo_rcv, wo_fin)
+        ga2 = after(ga2, wo_snd)
+        ga3 = near(rows_of(ga2, j1))
+        fq, fk, fv, snd, wo_fin = dw_own(vec(*dev, dep=(result,)), h_all, ga, gb, ga2, wo_rcv, wo_fin)
         rcv = near(snd)
 
-        ga2 = after(ga2, snd)
-        ga3 = near(rows_of(ga2, j1))
-        fq, fk, snd_a = dw_group(False, vec(j2), h_all, ga2, ga2, (fq, fk))
-        rcv_a = near(snd_a)
-        early, fq, fk, fv = dx_early(vec(*dev, dep=(snd_a,)), (ga, gb, ga1, gb1, ga2, ga3), w_p, rows,
-                                     rcv, (fq, fk, fv))
-
-        gb2 = after(gb2, early)
+        gb2 = after(gb2, snd)
         gb3 = near(rows_of(gb2, j1))
-        fq, fk, fv, snd_b = dw_group(True, vec(j2), h_all, ga2, gb2, (fq, fk, fv))
+        fq, fk, fv, snd_b = dw_group(vec(j2), h_all, ga2, gb2, (fq, fk, fv))
         rcv_b = near(snd_b)
-        grad_x, dg, fq, fk = dx_late(vec(*dev, dep=(snd_b,)), x, dy, gain_f, early, gb2, gb3, w_p, rcv_a, (fq, fk))
+        grad_x, dg, fq, fk, fv = dx_call(vec(*dev, dep=(snd_b,)), x, dy, gain_f, inv,
+                                         (ga, gb, ga1, gb1, ga2, gb2, ga3, gb3), w_p, rcv, (fq, fk, fv))
         dg = jnp.sum(dg, axis=0)
         dg = dg + near(dg)
         dg = dg + over(dg)

time: 1110 us -> 1140 us (1.027)
  waiting for transfers between devices: 333 us -> 401 us
  Pallas kernels: 698 us -> 672 us
    ppermute x9, waiting for transfers between devices: 262 us -> 333 us  [over(): return lax.ppermute(val, 'sp', cross)]
    pallas_call x20 -> x18, Pallas kernels: 698 us -> 672 us  [call(): pl.pallas_call(body, grid_spec=pltpu.PrefetchScalarGridSpec(num_scalar_pr...]
    ppermute x19 -> x18, waiting for transfers between devices: 71.1 us -> 67.9 us  [near(): return lax.ppermute(val, 'sp', pair)]
  transfers between devices with their start and end apart: 28 -> 27, of which waited for: 14 -> 16; matrix products, arithmetic and copies ran while one was open for 3% -> 3% of each run, Pallas kernels for 51% -> 48%
where the time goes in v3:
time: 1140 us; the launch traced here: 1130 us
  Pallas kernels  672 us (59%)
  waiting for transfers between devices  401 us (35%)
  local copies, waits for them, and re-layouts  24.1 us (2%)
  other arithmetic  18.2 us (2%)
  starting transfers between devices  12.5 us (1%)
    pallas_call x18, Pallas kernels, call(): pl.pallas_call(body, grid_spec=pltpu.PrefetchScalarGridSpec(num_scalar_pr...  672 us
    ppermute x9, waiting for transfers between devices, over(): return lax.ppermute(val, 'sp', cross)  333 us
    ppermute x18, waiting for transfers between devices, near(): return lax.ppermute(val, 'sp', pair)  67.9 us
  transfers between devices with their start and end apart: 27, of which 16 were waited for; matrix products, arithmetic and copies ran while one was open for 3% of the time, Pallas kernels for 48%

profile of v3, /device:TPU:0, one launch (start us, length us, event | category | flops | bytes accessed | tf_op | source)
XLA Modules:
  0.0 1128.7 jit_solution(11014359113831524407)
XLA Ops:
  19.9 102.3 %collective-permute-done.4 = s32[1024]{0:T(1024)S(1)} collective-permute-done((s32[1024]{0:T(1024)S(1)}, s32[1024]{0:T(1024)S(1)}, u32[]{:S(2)}, u32[]{:S(2)}) %collective-permute-start.4) | collective-permute-done | bytes 4128 | tf_op jit(solution)/shard_map/ppermute | solution.py:668
  135.1 34.4 %shard_map.135 = (bf16[4096,3072]{1,0:T(8,128)(2,1)}, bf16[4096,768]{1,0:T(8,128)(2,1)}, bf16[4096,256]{1,0:T(8,128)(2,1)}, bf16[4096,256]{1,0:T(8,128)(2,1)}, f32[4096,128]{1,0:T(8,128)}) custom-call(s32[3]{0:T(128)} %add_add_fusion.2.s_ref, bf16[1024,3072]{1,0:T(8,128)(2,1)} %x_ref.3, bf16[1024,3072]{1,0:T(8,128)(2,1)} %collective-permute-done.2.xb_ref, ...), custom_call_target="tpu_custom_call" | custom-call | flops 16106127360 | bytes 31457280 | tf_op jit(solution)/shard_map/pallas_call | solution.py:51
  169.5 17.7 %shard_map.136 = (bf16[4096,3072]{1,0:T(8,128)(2,1)}, bf16[4096,768]{1,0:T(8,128)(2,1)}) custom-call(s32[3]{0:T(128)} %add_add_fusion.2.s_ref, bf16[1024,3072]{1,0:T(8,128)(2,1)} %dy_ref.1, bf16[1024,3072]{1,0:T(8,128)(2,1)} %collective-permute-done.6.db_ref, bf16[3072,3072]{1,0:T(8,128)(2,1)} %rest_7_.1), custom_call_target="tpu_custom_call" | custom-call | flops 9663676416 | bytes 18874368 | tf_op jit(solution)/shard_map/pallas_call | solution.py:51
  187.2 22.9 %shard_map.137.rest_8_.rest_9_.rest_10_.rest_11_ = bf16[3072,5120]{1,0:T(8,128)(2,1)} custom-call(s32[1]{0:T(128)} %bitcast.s_ref, bf16[3072,3072]{1,0:T(8,128)(2,1)} %rest_0_.1, bf16[3072,1024]{1,0:T(8,128)(2,1)} %rest_1_.1, bf16[3072,1024]{1,0:T(8,128)(2,1)} %rest_2_.1), custom_call_target="tpu_custom_call" | custom-call | flops 15728640 | bytes 30720 | tf_op jit(solution)/shard_map/pallas_call | solution.py:51
  218.6 27.2 %shard_map.138 = (bf16[4096,3072]{1,0:T(8,128)(2,1)}, bf16[4096,768]{1,0:T(8,128)(2,1)}, bf16[4096,256]{1,0:T(8,128)(2,1)}, bf16[4096,256]{1,0:T(8,128)(2,1)}, f32[4096,128]{1,0:T(8,128)}) custom-call(s32[3]{0:T(128)} %add_add_fusion.1.s_ref, ...), custom_call_target="tpu_custom_call", output_to_operand_aliasing={{0}: (9, {}), {1}: (10, {}), {2}: (11, {}), {3}: (12, {}), ... | custom-call | flops 12079595520 | bytes 23592960 | tf_op jit(solution)/shard_map/pallas_call | solution.py:51
  255.9 13.1 %shard_map.139 = (bf16[4096,3072]{1,0:T(8,128)(2,1)}, bf16[4096,768]{1,0:T(8,128)(2,1)}, bf16[4096,256]{1,0:T(8,128)(2,1)}, bf16[4096,256]{1,0:T(8,128)(2,1)}, f32[4096,128]{1,0:T(8,128)}) custom-call(s32[3]{0:T(128)} %add_add_fusion.s_ref, ...), custom_call_target="tpu_custom_call", output_to_operand_aliasing={{0}: (9, {}), {1}: (10, {}), {2}: (11, {}), {3}: (12, {}), ... | custom-call | flops 4026531840 | bytes 7864320 | tf_op jit(solution)/shard_map/pallas_call | solution.py:51
  269.0 76.9 %shard_map.140 = (bf16[4096,768]{1,0:T(8,128)(2,1)}, f32[2,8,4096]{2,1,0:T(8,128)}, bf16[2048,768]{1,0:T(8,128)(2,1)}, bf16[1024,768]{1,0:T(8,128)(2,1)}) custom-call(s32[1]{0:T(128)} %bitcast.1.s_ref, bf16[4096,768]{1,0:T(8,128)(2,1)} %get-tuple-element.95.q_ref, bf16[4096,256]{1,0:T(8,128)(2,1)} %get-tuple-element.98.k_ref, ...), custom_call_target="tpu_custom_call" | custom-call | flops 28991029248 | bytes 56623104 | tf_op jit(solution)/shard_map/pallas_call | solution.py:51
  345.9 23.0 %shard_map.141 = (bf16[2048,768]{1,0:T(8,128)(2,1)}, bf16[2048,256]{1,0:T(8,128)(2,1)}, bf16[2048,256]{1,0:T(8,128)(2,1)}) custom-call(s32[1]{0:T(128)} %bitcast.2.s_ref, bf16[4096,3072]{1,0:T(8,128)(2,1)} %get-tuple-element.102.h_ref, bf16[3072,3072]{1,0:T(8,128)(2,1)} %rest_0_.1, bf16[3072,1024]{1,0:T(8,128)(2,1)} %rest_1_.1, bf16[3072,1024]{1,0:T(8,128)(2,1)} %rest_2_.1, ...), custom_call_target="tpu_custom_call" | custom-call | flops 16106127360 | bytes 31457280 | tf_op jit(solution)/shard_map/pallas_call | solution.py:51
  368.9 25.5 %shard_map.142 = (bf16[4096,768]{1,0:T(8,128)(2,1)}, f32[2,8,2048]{2,1,0:T(8,128)}) custom-call(s32[1]{0:T(128)} %bitcast.s_ref, bf16[2048,768]{1,0:T(8,128)(2,1)} %get-tuple-element.103.q_ref, bf16[2048,256]{1,0:T(8,128)(2,1)} %get-tuple-element.104.k_ref, bf16[2048,256]{1,0:T(8,128)(2,1)} %get-tuple-element.105.v_ref), custom_call_target="tpu_custom_call" | custom-call | flops 8053063680 | bytes 15728640 | tf_op jit(solution)/shard_map/pallas_call | solution.py:51
  400.4 11.5 %shard_map.143 = (bf16[4096,3072]{1,0:T(8,128)(2,1)}, bf16[4096,768]{1,0:T(8,128)(2,1)}) custom-call(s32[3]{0:T(128)} %add_add_fusion.4.s_ref, bf16[512,3072]{1,0:T(8,128)(2,1)} %collective-permute-done.10.da_ref, bf16[512,3072]{1,0:T(8,128)(2,1)} %collective-permute-done.11.db_ref, ...), custom_call_target="tpu_custom_call", output_to_operand_aliasing={{0}: (4, {}), {1}: (5, {})} | custom-call | flops 4831838208 | bytes 9437184 | tf_op jit(solution)/shard_map/pallas_call | solution.py:51
  411.9 57.0 %collective-permute-done.9.da_ref = bf16[512,3072]{1,0:T(8,128)(2,1)} collective-permute-done((bf16[512,3072]{1,0:T(8,128)(2,1)}, bf16[512,3072]{1,0:T(8,128)(2,1)}, u32[]{:S(2)}, u32[]{:S(2)}) %collective-permute-start.9) | collective-permute-done | bytes 3145760 | tf_op jit(solution)/shard_map/ppermute | solution.py:668
  474.9 11.5 %shard_map.144 = (bf16[4096,3072]{1,0:T(8,128)(2,1)}, bf16[4096,768]{1,0:T(8,128)(2,1)}) custom-call(s32[3]{0:T(128)} %add_add_fusion.3.s_ref, bf16[512,3072]{1,0:T(8,128)(2,1)} %collective-permute-done.9.da_ref, bf16[512,3072]{1,0:T(8,128)(2,1)} %collective-permute-done.12.db_ref, ...), custom_call_target="tpu_custom_call", output_to_operand_aliasing={{0}: (4, {}), {1}: (5, {})} | custom-call | flops 4831838208 | bytes 9437184 | tf_op jit(solution)/shard_map/pallas_call | solution.py:51
  486.4 80.9 %shard_map.145 = (bf16[4096,640]{1,0:T(8,128)(2,1)}, bf16[1024,640]{1,0:T(8,128)(2,1)}) custom-call(s32[2]{0:T(128)} %pad_add_fusion.3.s_ref, bf16[4096,768]{1,0:T(8,128)(2,1)} %get-tuple-element.95.q_ref, bf16[4096,768]{1,0:T(8,128)(2,1)} %get-tuple-element.112.do_ref, bf16[4096,768]{1,0:T(8,128)(2,1)} %get-tuple-element.100.o_ref.oa_ref.rest_0_, ...), custom_call_target="tpu_custom_call" | custom-call | flops 36238786560 | bytes 70778880 | tf_op jit(solution)/shard_map/pallas_call | solution.py:51
  567.4 80.9 %shard_map.146 = (bf16[4096,640]{1,0:T(8,128)(2,1)}, bf16[1024,640]{1,0:T(8,128)(2,1)}) custom-call(s32[2]{0:T(128)} %pad_add_fusion.2.s_ref, bf16[4096,768]{1,0:T(8,128)(2,1)} %get-tuple-element.95.q_ref, bf16[4096,768]{1,0:T(8,128)(2,1)} %get-tuple-element.112.do_ref, bf16[4096,768]{1,0:T(8,128)(2,1)} %get-tuple-element.100.o_ref.oa_ref.rest_0_, ...), custom_call_target="tpu_custom_call" | custom-call | flops 36238786560 | bytes 70778880 | tf_op jit(solution)/shard_map/pallas_call | solution.py:51
  652.0 54.1 %shard_map.147 = (f32[3072,3072]{1,0:T(8,128)}, f32[1536,3072]{1,0:T(8,128)}) custom-call(s32[2]{0:T(128)} %pad_add_fusion.1.s_ref, bf16[4096,768]{1,0:T(8,128)(2,1)} %get-tuple-element.100.o_ref.oa_ref.rest_0_, bf16[4096,768]{1,0:T(8,128)(2,1)} %constant_dynamic-update-slice_fusion.ob_ref.rest_2_, bf16[4096,3072]{1,0:T(8,128)(2,1)} %get-tuple-element.120.dy_ref), custom_call_target="tpu_custom_call" | custom-call | flops 38654705664 | bytes 75497472 | tf_op jit(solution)/shard_map/pallas_call | solution.py:51
  709.3 27.4 %collective-permute-done.14.rest_1_ = bf16[1024,768]{1,0:T(8,128)(2,1)S(1)} collective-permute-done((bf16[1024,768]{1,0:T(8,128)(2,1)}, bf16[1024,768]{1,0:T(8,128)(2,1)S(1)}, u32[]{:S(2)}, u32[]{:S(2)}) %collective-permute-start.14) | collective-permute-done | bytes 1572896 | tf_op jit(solution)/shard_map/ppermute | solution.py:671
  739.1 27.1 %shard_map.148 = bf16[1024,3072]{1,0:T(8,128)(2,1)} custom-call(s32[4]{0:T(128)} %pad_add_fusion.s_ref, bf16[1024,3072]{1,0:T(8,128)(2,1)} %x_ref.3, bf16[4096,768]{1,0:T(8,128)(2,1)} %get-tuple-element.100.o_ref.oa_ref.rest_0_, bf16[1024,768]{1,0:T(8,128)(2,1)} %copy-done.1, bf16[4096,768]{1,0:T(8,128)(2,1)} %constant_dynamic-update-slice_fusion.ob_ref.rest_2_, ...), custom_call_target="tpu_custom_call" | custom-call | flops 19327352832 | bytes 37748736 | tf_op jit(solution)/shard_map/pallas_call | solution.py:51
  766.2 55.7 %collective-permute-done.16.gc_ref.ga_ref.rest_4_ = bf16[4096,640]{1,0:T(8,128)(2,1)} collective-permute-done((bf16[4096,640]{1,0:T(8,128)(2,1)}, bf16[4096,640]{1,0:T(8,128)(2,1)}, u32[]{:S(2)}, u32[]{:S(2)}) %collective-permute-start.16) | collective-permute-done | bytes 5242912 | tf_op jit(solution)/shard_map/ppermute | solution.py:668
  821.9 71.1 %shard_map.149 = (f32[3072,3072]{1,0:T(8,128)}, f32[3072,1024]{1,0:T(8,128)}, f32[3072,1024]{1,0:T(8,128)}, f32[3072,1792]{1,0:T(8,128)}, f32[3072,3072]{1,0:T(8,128)}) custom-call(s32[4]{0:T(128)} %pad_add_fusion.s_ref, bf16[4096,3072]{1,0:T(8,128)(2,1)} %get-tuple-element.102.h_ref, ...), custom_call_target="tpu_custom_call", output_to_operand_aliasing={{4}: (6, {})} | custom-call | flops 45097156608 | bytes 88080384 | tf_op jit(solution)/shard_map/pallas_call | solution.py:51
  893.4 115.4 %collective-permute-done.17.gb_ref.rest_5_ = bf16[4096,640]{1,0:T(8,128)(2,1)} collective-permute-done((bf16[4096,640]{1,0:T(8,128)(2,1)}, bf16[4096,640]{1,0:T(8,128)(2,1)}, u32[]{:S(2)}, u32[]{:S(2)}) %collective-permute-start.17) | collective-permute-done | bytes 5242912 | tf_op jit(solution)/shard_map/ppermute | solution.py:668
  1008.8 29.7 %shard_map.150 = (f32[3072,3072]{1,0:T(8,128)}, f32[3072,1024]{1,0:T(8,128)}, f32[3072,1024]{1,0:T(8,128)}, f32[3072,768]{1,0:T(8,128)}) custom-call(s32[1]{0:T(128)} %bitcast.2.s_ref, bf16[4096,3072]{1,0:T(8,128)(2,1)} %get-tuple-element.102.h_ref, ...), custom_call_target="tpu_custom_call", output_to_operand_aliasing={{0}: (4, {}), {1}: (5, {}), {2}: (6, {})} | custom-call | flops 19327352832 | bytes 37748736 | tf_op jit(solution)/shard_map/pallas_call | solution.py:51
  1042.4 12.8 %collective-permute-done.20.rest_3_ = bf16[1024,640]{1,0:T(8,128)(2,1)S(1)} collective-permute-done((bf16[1024,640]{1,0:T(8,128)(2,1)}, bf16[1024,640]{1,0:T(8,128)(2,1)S(1)}, u32[]{:S(2)}, u32[]{:S(2)}) %collective-permute-start.20) | collective-permute-done | bytes 1310752 | tf_op jit(solution)/shard_map/ppermute | solution.py:671
  1061.0 52.6 %shard_map.151 = (bf16[1024,3072]{1,0:T(8,128)(2,1)}, f32[8,3072]{1,0:T(8,128)}, f32[3072,3072]{1,0:T(8,128)}, f32[3072,1024]{1,0:T(8,128)}, f32[3072,1024]{1,0:T(8,128)}) custom-call(s32[4]{0:T(128)} %pad_add_fusion.s_ref, bf16[1024,3072]{1,0:T(8,128)(2,1)} %x_ref.3, ...), custom_call_target="tpu_custom_call", output_to_operand_aliasing={{2}: (18, {}), {3}: (19, {}), {4}: (20, {})} | custom-call | flops 32212254720 | bytes 62914560 | tf_op jit(solution)/shard_map/pallas_call | solution.py:51
  1116.2 11.4 %shard_map.152 = (f32[3072,3072]{1,0:T(8,128)}, f32[3072,1024]{1,0:T(8,128)}, f32[3072,1024]{1,0:T(8,128)}) custom-call(s32[1]{0:T(128)} %bitcast.3.s_ref, f32[3072,768]{1,0:T(8,128)} %collective-permute-done.24.rcv, f32[3072,3072]{1,0:T(8,128)} %get-tuple-element.141.rest_0_, ...), custom_call_target="tpu_custom_call", output_to_operand_aliasing={{0}: (2, {}), {1}: (3, {}), {2}: (4, {})} | custom-call | flops 2359296 | bytes 4608 | tf_op jit(solution)/shard_map/pallas_call | solution.py:51
  (88 shorter events, 85.3 us)
Async XLA Ops:
  0.7 11.0 collective-permute-start.2
  11.6 157.8 %collective-permute-start.6 = (bf16[1024,3072]{1,0:T(8,128)(2,1)}, bf16[1024,3072]{1,0:T(8,128)(2,1)}, u32[]{:S(2)}, u32[]{:S(2)}) collective-permute-start(bf16[1024,3072]{1,0:T(8,128)(2,1)} %dy_ref.1), channel_id=1, source_target_pairs={{0,1},{1,0},{2,3},{3,2},{4,5},{5,4},{6,7},{7,6}} | collective-permute-start | bytes 18874376 | tf_op jit(solution)/shard_map/ppermute | solution.py:671
  16.9 193.2 %collective-permute-start.1 = (bf16[768,3072]{1,0:T(8,128)(2,1)}, bf16[768,3072]{1,0:T(8,128)(2,1)}, u32[]{:S(2)}, u32[]{:S(2)}) collective-permute-start(bf16[768,3072]{1,0:T(8,128)(2,1)} %slice.12), channel_id=1, source_target_pairs={{0,2},{1,3},{2,0},{3,1},{4,6},{5,7},{6,4},{7,5}} | collective-permute-start | bytes 14155784 | tf_op jit(solution)/shard_map/ppermute | solution.py:668
  19.5 104.1 %collective-permute-start.3 = (s32[1024]{0:T(1024)S(1)}, s32[1024]{0:T(1024)S(1)}, u32[]{:S(2)}, u32[]{:S(2)}) collective-permute-start(s32[1024]{0:T(1024)S(1)} %copy-done.4), channel_id=1, source_target_pairs={{0,1},{1,0},{2,3},{3,2},{4,5},{5,4},{6,7},{7,6}} | collective-permute-start | bytes 12296 | tf_op jit(solution)/shard_map/ppermute | solution.py:671
  19.6 102.6 %collective-permute-start.4 = (s32[1024]{0:T(1024)S(1)}, s32[1024]{0:T(1024)S(1)}, u32[]{:S(2)}, u32[]{:S(2)}) collective-permute-start(s32[1024]{0:T(1024)S(1)} %copy-done.4), channel_id=1, source_target_pairs={{0,2},{1,3},{2,0},{3,1},{4,6},{5,7},{6,4},{7,5}} | collective-permute-start | bytes 12296 | tf_op jit(solution)/shard_map/ppermute | solution.py:668
  210.1 8.5 collective-permute-start.7
  212.2 36.4 %collective-permute-start = (bf16[256,3072]{1,0:T(8,128)(2,1)S(1)}, bf16[256,3072]{1,0:T(8,128)(2,1)}, u32[]{:S(2)}, u32[]{:S(2)}) collective-permute-start(bf16[256,3072]{1,0:T(8,128)(2,1)S(1)} %slice.13), channel_id=1, source_target_pairs={{0,2},{1,3},{2,0},{3,1},{4,6},{5,7},{6,4},{7,5}} | collective-permute-start | bytes 4718600 | tf_op jit(solution)/shard_map/ppermute | solution.py:668
  248.7 6.1 collective-permute-start.8
  253.0 141.3 %collective-permute-start.10 = (bf16[512,3072]{1,0:T(8,128)(2,1)}, bf16[512,3072]{1,0:T(8,128)(2,1)}, u32[]{:S(2)}, u32[]{:S(2)}) collective-permute-start(bf16[512,3072]{1,0:T(8,128)(2,1)} %slice.15), channel_id=1, source_target_pairs={{0,2},{1,3},{2,0},{3,1},{4,6},{5,7},{6,4},{7,5}} | collective-permute-start | bytes 9437192 | tf_op jit(solution)/shard_map/ppermute | solution.py:668
  394.3 6.0 collective-permute-start.11
  398.4 70.5 %collective-permute-start.9 = (bf16[512,3072]{1,0:T(8,128)(2,1)}, bf16[512,3072]{1,0:T(8,128)(2,1)}, u32[]{:S(2)}, u32[]{:S(2)}) collective-permute-start(bf16[512,3072]{1,0:T(8,128)(2,1)} %slice.14), channel_id=1, source_target_pairs={{0,2},{1,3},{2,0},{3,1},{4,6},{5,7},{6,4},{7,5}} | collective-permute-start | bytes 9437192 | tf_op jit(solution)/shard_map/ppermute | solution.py:668
  468.9 6.0 collective-permute-start.12
  471.3 176.9 %collective-permute-start.13 = (bf16[2048,768]{1,0:T(8,128)(2,1)}, bf16[2048,768]{1,0:T(8,128)(2,1)}, u32[]{:S(2)}, u32[]{:S(2)}) collective-permute-start(bf16[2048,768]{1,0:T(8,128)(2,1)} %get-tuple-element.118), channel_id=1, source_target_pairs={{0,2},{1,3},{2,0},{3,1},{4,6},{5,7},{6,4},{7,5}} | collective-permute-start | bytes 9437192 | tf_op jit(solution)/shard_map/ppermute | solution.py:668
  706.1 115.8 %collective-permute-start.18 = (f32[1536,3072]{1,0:T(8,128)}, f32[1536,3072]{1,0:T(8,128)}, u32[]{:S(2)}, u32[]{:S(2)}) collective-permute-start(f32[1536,3072]{1,0:T(8,128)} %get-tuple-element.121), channel_id=1, source_target_pairs={{0,1},{1,0},{2,3},{3,2},{4,5},{5,4},{6,7},{7,6}} | collective-permute-start | bytes 56623112 | tf_op jit(solution)/shard_map/ppermute | solution.py:671
  706.3 115.6 %collective-permute-start.16 = (bf16[4096,640]{1,0:T(8,128)(2,1)}, bf16[4096,640]{1,0:T(8,128)(2,1)}, u32[]{:S(2)}, u32[]{:S(2)}) collective-permute-start(bf16[4096,640]{1,0:T(8,128)(2,1)} %get-tuple-element.114.ga_ref.rest_0_), channel_id=1, source_target_pairs={{0,2},{1,3},{2,0},{3,1},{4,6},{5,7},{6,4},{7,5}} | collective-permute-start | bytes 15728648 | tf_op jit(solution)/shard_map/ppermute | solution.py:668
  706.7 30.1 %collective-permute-start.14 = (bf16[1024,768]{1,0:T(8,128)(2,1)}, bf16[1024,768]{1,0:T(8,128)(2,1)S(1)}, u32[]{:S(2)}, u32[]{:S(2)}) collective-permute-start(bf16[1024,768]{1,0:T(8,128)(2,1)} %get-tuple-element.123), channel_id=1, source_target_pairs={{0,1},{1,0},{2,3},{3,2},{4,5},{5,4},{6,7},{7,6}} | collective-permute-start | bytes 4718600 | tf_op jit(solution)/shard_map/ppermute | solution.py:671
  708.3 30.9 %collective-permute-start.15 = (bf16[1024,768]{1,0:T(8,128)(2,1)S(1)}, bf16[1024,768]{1,0:T(8,128)(2,1)}, u32[]{:S(2)}, u32[]{:S(2)}) collective-permute-start(bf16[1024,768]{1,0:T(8,128)(2,1)S(1)} %constant_dynamic-slice_fusion.2), channel_id=1, source_target_pairs={{0,1},{1,0},{2,3},{3,2},{4,5},{5,4},{6,7},{7,6}} | collective-permute-start | bytes 4718600 | tf_op jit(solution)/shard_map/ppermute | solution.py:671
  893.0 168.0 %collective-permute-start.23 = (f32[3072,1792]{1,0:T(8,128)}, f32[3072,1792]{1,0:T(8,128)}, u32[]{:S(2)}, u32[]{:S(2)}) collective-permute-start(f32[3072,1792]{1,0:T(8,128)} %get-tuple-element.127), channel_id=1, source_target_pairs={{0,1},{1,0},{2,3},{3,2},{4,5},{5,4},{6,7},{7,6}} | collective-permute-start | bytes 66060296 | tf_op jit(solution)/shard_map/ppermute | solution.py:671
  893.0 115.8 %collective-permute-start.17 = (bf16[4096,640]{1,0:T(8,128)(2,1)}, bf16[4096,640]{1,0:T(8,128)(2,1)}, u32[]{:S(2)}, u32[]{:S(2)}) collective-permute-start(bf16[4096,640]{1,0:T(8,128)(2,1)} %get-tuple-element.116.gb_ref.rest_1_), channel_id=1, source_target_pairs={{0,2},{1,3},{2,0},{3,1},{4,6},{5,7},{6,4},{7,5}} | collective-permute-start | bytes 15728648 | tf_op jit(solution)/shard_map/ppermute | solution.py:668
  1038.5 77.7 %collective-permute-start.24 = (f32[3072,768]{1,0:T(8,128)}, f32[3072,768]{1,0:T(8,128)}, u32[]{:S(2)}, u32[]{:S(2)}) collective-permute-start(f32[3072,768]{1,0:T(8,128)} %get-tuple-element.132), channel_id=1, source_target_pairs={{0,1},{1,0},{2,3},{3,2},{4,5},{5,4},{6,7},{7,6}} | collective-permute-start | bytes 28311560 | tf_op jit(solution)/shard_map/ppermute | solution.py:671
  1038.5 16.7 %collective-permute-start.20 = (bf16[1024,640]{1,0:T(8,128)(2,1)}, bf16[1024,640]{1,0:T(8,128)(2,1)S(1)}, u32[]{:S(2)}, u32[]{:S(2)}) collective-permute-start(bf16[1024,640]{1,0:T(8,128)(2,1)} %get-tuple-element.136), channel_id=1, source_target_pairs={{0,1},{1,0},{2,3},{3,2},{4,5},{5,4},{6,7},{7,6}} | collective-permute-start | bytes 3932168 | tf_op jit(solution)/shard_map/ppermute | solution.py:671
  1039.0 18.2 %collective-permute-start.19 = (bf16[1024,640]{1,0:T(8,128)(2,1)}, bf16[1024,640]{1,0:T(8,128)(2,1)}, u32[]{:S(2)}, u32[]{:S(2)}) collective-permute-start(bf16[1024,640]{1,0:T(8,128)(2,1)} %get-tuple-element.135), channel_id=1, source_target_pairs={{0,1},{1,0},{2,3},{3,2},{4,5},{5,4},{6,7},{7,6}} | collective-permute-start | bytes 3932168 | tf_op jit(solution)/shard_map/ppermute | solution.py:671
  1040.5 18.7 %collective-permute-start.21 = (bf16[1024,640]{1,0:T(8,128)(2,1)S(1)}, bf16[1024,640]{1,0:T(8,128)(2,1)}, u32[]{:S(2)}, u32[]{:S(2)}) collective-permute-start(bf16[1024,640]{1,0:T(8,128)(2,1)S(1)} %constant_dynamic-slice_fusion.1), channel_id=1, source_target_pairs={{0,1},{1,0},{2,3},{3,2},{4,5},{5,4},{6,7},{7,6}} | collective-permute-start | bytes 3932168 | tf_op jit(solution)/shard_map/ppermute | solution.py:671
  1115.7 11.9 %collective-permute-start.26 = (f32[3072]{0:T(1024)S(1)}, f32[3072]{0:T(1024)S(1)}, u32[]{:S(2)}, u32[]{:S(2)}) collective-permute-start(f32[3072]{0:T(1024)S(1)} %add.43), channel_id=1, source_target_pairs={{0,2},{1,3},{2,0},{3,1},{4,6},{5,7},{6,4},{7,5}} | collective-permute-start | bytes 36872 | tf_op jit(solution)/shard_map/ppermute | solution.py:668
  (8 other events, 159.1 us)

commit v4 on v3

--- a/solution.py
+++ b/solution.py
@@ -208,10 +208,21 @@
                 [sds(seq, w) for w in (d, oc)], args, 4 * rows * d * oc, aliases=aliases)
 
 
-def fwd_body(s_ref, q_ref, k_ref, v_ref, o_ref, lse_ref, *rest):
+TASK = 4
+HEADER = 3
+
+
+def row_tasks(first, last):
+    return [(i, i + 1, 1, -1) for i in range(first, last)]
+
+
+def fwd_body(kind, s_ref, q_ref, k_ref, v_ref, *rest):
     qt, kk, vt, s_scr, acc, stat = rest[-6:]
+    if kind == "rest":
+        o1_ref, lse1_ref, st_ref, o_ref, lse_ref, hi_ref, pair_ref = rest[:7]
+    else:
+        o_ref, lse_ref = rest[:2]
     seq = k_ref.shape[0]
-    nq = seq // BLK
 
     def setup(c, _):
         sl = ds(c * BLK, BLK)
@@ -225,25 +236,35 @@
             qt[h, HEAD:, sl] = (qf - hi.astype(F32)).astype(BF).T
         return 0
 
-    lax.fori_loop(0, nq, setup, 0)
+    lax.fori_loop(0, seq // BLK, setup, 0)
     acc[...] = jnp.zeros_like(acc)
     stat[...] = jnp.zeros_like(stat)
     cur, old, den_row = 0, 1, 2
-
-    def stage_a(h, i, j, masked, first):
+    if kind == "rest":
+        @pl.when(s_ref[1] == 0)
+        def _():
+            o_ref[:seq // 2, :] = o1_ref[...]
+            lse_ref[0, :, :seq // 2] = lse1_ref[0]
+
+    def task(t):
+        return [s_ref[HEADER + t * TASK + n] for n in range(TASK)]
+
+    def stage_a(h, i, j, masked, init=None):
         row = slice(h, h + 1)
         s = mm(kk[ds(j * BLK, BLK), :], qt[h, :, ds(i * BLK, BLK)])
-        if masked:
+        if masked is not False:
             keep = lax.broadcasted_iota(jnp.int32, s.shape, 0) <= lax.broadcasted_iota(jnp.int32, s.shape, 1)
-            s = jnp.where(keep, s, NEG_LARGE)
+            s = jnp.where(keep if masked is True else jnp.logical_or(keep, jnp.logical_not(masked)), s, NEG_LARGE)
         s_scr[h] = s
         m_new = jnp.max(s, axis=0, keepdims=True)
-        if first:
-            stat[old, row] = jnp.zeros((1, BLK), F32)
+        if init is None:
+            m_old = stat[cur, row]
+        elif kind == "rest":
+            m_old = jnp.where(init >= 0, lse1_ref[0, row, ds(jnp.maximum(init, 0) * BLK, BLK)], NEG_LARGE)
         else:
-            m_old = stat[cur, row]
-            m_new = jnp.maximum(m_old, m_new)
-            stat[old, row] = jnp.exp2(m_old - m_new)
+            m_old = jnp.full(m_new.shape, NEG_LARGE, F32)
+        m_new = jnp.maximum(m_old, m_new)
+        stat[old, row] = jnp.exp2(m_old - m_new)
         stat[cur, row] = m_new
 
     def stage_p(h):
@@ -258,57 +279,91 @@
 
     def finish(h, i, den, top):
         row = slice(h, h + 1)
-        o_ref[ds(i * BLK, BLK), h * HEAD:(h + 1) * HEAD] = (acc[h] / den).T.astype(BF)
+        out = acc[h] / den
+        o_ref[ds(i * BLK, BLK), h * HEAD:(h + 1) * HEAD] = out.T.astype(BF)
         lse_ref[0, row, ds(i * BLK, BLK)] = top + jnp.log2(den)
-
+        if kind == "local":
+            rest[2][0, h, :, ds(i * BLK, BLK)] = out
+
+    def pipeline(i, j, masked):
+        for h in range(GROUP):
+            held = stage_p(h)
+            stage_a(h, i, j + 1, masked)
+            stage_v(h, j, held)
+
+    count = s_ref[HEADER - 1]
+    i, steps, diag, init = task(0)
     for h in range(GROUP):
-        stage_a(h, 0, 0, True, True)
-
-    def row(i, _):
+        stage_a(h, i, 0, jnp.logical_and(steps == 1, diag == 1), init)
+
+    def row(t, _):
+        i, steps, diag, _ = task(t)
+
         def inner(j, _):
-            for h in range(GROUP):
-                held = stage_p(h)
-                stage_a(h, i, j + 1, False, False)
-                stage_v(h, j, held)
+            pipeline(i, j, False)
             return 0
 
-        lax.fori_loop(0, i - 1, inner, 0)
-
-        @pl.when(i > 0)
+        lax.fori_loop(0, steps - 2, inner, 0)
+
+        @pl.when(jnp.logical_and(steps > 1, diag == 1))
         def _():
-            for h in range(GROUP):
-                held = stage_p(h)
-                stage_a(h, i, i, True, False)
-                stage_v(h, i - 1, held)
-
-        nxt = jnp.minimum(i + 1, nq - 1)
+            pipeline(i, steps - 2, True)
+
+        if kind == "rest":
+            @pl.when(diag == 0)
+            def _():
+                pipeline(i, steps - 2, False)
+        i2, _, _, init2 = task(jnp.minimum(t + 1, count - 1))
         for h in range(GROUP):
             held = stage_p(h)
             final = (stat[den_row, h:h + 1], stat[cur, h:h + 1])
-            stage_a(h, nxt, 0, False, True)
-            stage_v(h, i, held)
+            stage_a(h, i2, 0, False, init2)
+            stage_v(h, steps - 1, held)
             finish(h, i, *final)
+        if kind == "rest":
+            @pl.when(init2 >= 0)
+            def _():
+                stat[den_row] = jnp.ones(stat.shape[1:], F32)
+                for h in range(GROUP):
+                    acc[h] = st_ref[0, h, :, ds(init2 * BLK, BLK)]
         return 0
 
-    lax.fori_loop(0, nq, row, 0)
+    lax.fori_loop(0, count, row, 0)
     lse_ref[0, GROUP:, :] = jnp.zeros((8 - GROUP, seq), F32)
-    if len(rest) > 6:
-        hi_ref, pair_ref = rest[:2]
+    if kind == "rest":
         hi_ref[...] = o_ref[seq // 2:, :]
         pair_ref[...] = o_ref[ds(s_ref[0] * pair_ref.shape[0], pair_ref.shape[0]), :]
 
 
-def attn_fwd(idx, q, k, v, out_rows, rows):
-    seq = k.shape[0]
-    nq = seq // BLK
+def attn_fwd(kind, idx, q, k, v, rows=0, local=()):
+    whole = q.shape[0]
+    seq = whole if kind == "rest" else whole // (2 if kind == "local" else 1)
     nkv = k.shape[1] // HEAD
-    extra = (seq // 2, rows) if rows else ()
-    tiles = nkv * GROUP * nq * (nq + 1)
-    qspec, kspec = pl.BlockSpec((seq, GW), col_map), pl.BlockSpec((seq, HEAD), col_map)
-    return call(fwd_body, (nkv,), [qspec, kspec, kspec],
-                [qspec, pl.BlockSpec((1, 8, seq), lambda g, s: (g, 0, 0))] + [pl.BlockSpec((r, GW), col_map) for r in extra],
-                [sds(out_rows, q.shape[1]), jax.ShapeDtypeStruct((nkv, 8, seq), F32)] + [sds(r, q.shape[1]) for r in extra],
-                [idx, q, k, v], tiles * BLK * BLK * PAIR,
+
+    def half_map(g, s):
+        return (s[1], g)
+
+    def head_map(g, s):
+        return (g, 0, 0)
+
+    def state_map(g, s):
+        return (g, 0, 0, 0)
+
+    at = half_map if kind == "local" else col_map
+    lse_spec = pl.BlockSpec((1, 8, seq), head_map)
+    outs, specs = [sds(seq * 2 if kind == "first" else seq, q.shape[1]), jax.ShapeDtypeStruct((nkv, 8, seq), F32)], []
+    out_specs = [pl.BlockSpec((seq, GW), col_map), lse_spec]
+    state = pl.BlockSpec((1, GROUP, HEAD, whole // 2), state_map)
+    if kind == "local":
+        outs.append(jax.ShapeDtypeStruct((nkv, GROUP, HEAD, seq), F32))
+        out_specs.append(state)
+    if kind == "rest":
+        specs = [pl.BlockSpec((seq // 2, GW), col_map), pl.BlockSpec((1, 8, seq // 2), head_map), state]
+        outs += [sds(r, q.shape[1]) for r in (seq // 2, rows)]
+        out_specs += [pl.BlockSpec((r, GW), col_map) for r in (seq // 2, rows)]
+    kspec = pl.BlockSpec((seq, HEAD), at)
+    return call(lambda *refs: fwd_body(kind, *refs), (nkv,), [pl.BlockSpec((seq, GW), at), kspec, kspec] + specs,
+                out_specs, outs, [idx, q, k, v, *local], nkv * GROUP * seq * seq * PAIR,
                 scratch=[pltpu.VMEM((GROUP, PAIR, seq), BF), pltpu.VMEM((seq, PAIR), BF),
                          pltpu.VMEM((HEAD, seq), BF), pltpu.VMEM((GROUP, BLK, BLK), F32),
                          pltpu.VMEM((GROUP, HEAD, BLK), F32), pltpu.VMEM((GROUP, 8, BLK), F32)])
@@ -483,9 +538,9 @@
     wcopy = pltpu.make_async_copy(wo_ref, wo_fin.at[ds(start * rows, rows), :], wsem)
     wcopy.start()
 
-    @pl.when(i > 0)
-    def _():
-        for copy in scatter(snd, (fq, fk, fv), s_ref[0], s_ref[2], sem):
+    @pl.when(i > 1)
+    def _():
+        for copy in scatter(snd, (fq, fk, fv), s_ref[0], s_ref[2], sem.at[i % 2]):
             copy.wait()
 
     ht[...] = h_ref[...].T
@@ -495,14 +550,14 @@
         snd[:, q_at:q_at + GW] = val[:, :GW]
         snd[:, k_at:k_at + HEAD] = val[:, GW:]
     snd[:, 2 * QK:2 * PW] = mm(lhs, jnp.concatenate([ga_ref[:, QK:], gb_ref[:, QK:]], axis=1))
-    copies = scatter(snd, (fq, fk, fv), s_ref[0], s_ref[2], sem)
-    for copy in copies:
+    for copy in scatter(snd, (fq, fk, fv), s_ref[0], s_ref[2], sem.at[i % 2]):
         copy.start()
 
     @pl.when(i == steps - 1)
     def _():
-        for copy in copies:
-            copy.wait()
+        for slot in range(2):
+            for copy in scatter(snd, (fq, fk, fv), s_ref[0], s_ref[2], sem.at[slot]):
+                copy.wait()
 
     wcopy.wait()
 
@@ -529,7 +584,7 @@
                 [ANY] * 3 + [pl.BlockSpec((HB, sw), row_map), ANY],
                 [sds(d, 4 * w, F32) for w in widths] + [sds(d, sw, F32), sds(*wo_fin.shape, F32)],
                 [idx, h, ga, gb, gc, wo_rcv, wo_fin], 2 * seq * d * sw,
-                scratch=[pltpu.VMEM((HB, seq), BF), pltpu.SemaphoreType.DMA((5,)), pltpu.SemaphoreType.DMA],
+                scratch=[pltpu.VMEM((HB, seq), BF), pltpu.SemaphoreType.DMA((2, 5)), pltpu.SemaphoreType.DMA],
                 aliases={6: 4})
 
 
@@ -575,20 +630,8 @@
                 [sds(*b.shape, F32) for b in bufs], [idx, rcv, *bufs], d * w, aliases={2 + n: n for n in range(3)})
 
 
-def pack_body(s_ref, q_ref, k_ref, v_ref, out_ref):
-    out_ref[:, :GW] = q_ref[...]
-    out_ref[:, GW:QK] = k_ref[...]
-    out_ref[:, QK:] = v_ref[...]
-
-
-def pack_weights(idx, ws):
-    d, groups = ws[1].shape[0], ws[1].shape[1] // HEAD
-    return call(pack_body, (groups,), [pl.BlockSpec((d, w), col_map) for w in (GW, HEAD, HEAD)],
-                pl.BlockSpec((d, PW), col_map), sds(d, groups * PW), [idx, *ws], d * groups * PW)
-
-
 def dx_body(s_ref, x_ref, dy_ref, gain_ref, inv_ref, *rest):
-    pieces, weights, rcv = rest[:8], rest[8:12], rest[12]
+    pieces, weights, rcv = rest[:8], rest[8:20], rest[20]
     dx_ref, dg_ref, fq, fk, fv, acc, xs, tot, sem = rest[-9:]
     n = pl.program_id(0)
     bn = x_ref.shape[1]
@@ -601,7 +644,8 @@
     def _():
         tot[...] = jnp.zeros_like(tot)
 
-    lhs = jnp.concatenate([r[...] for r in pieces], axis=1)
+    cuts = (slice(0, GW), slice(GW, QK), slice(QK, PW))
+    lhs = jnp.concatenate([pieces[2 * p + g][:, c] for p in range(4) for c in cuts for g in range(2)], axis=1)
     rhs = jnp.concatenate([r[...] for r in weights], axis=1)
     dh = mm_nt(lhs, rhs)
     inv = inv_ref[...]
@@ -641,7 +685,7 @@
         copy.wait()
 
 
-def dx_call(idx, x, dy, gain, inv, pieces, w_p, rcv, bufs):
+def dx_call(idx, x, dy, gain, inv, pieces, ws, rcv, bufs):
     rows, d = x.shape
     bn = HB
     once = pl.Buffered(1)
@@ -649,14 +693,14 @@
     return call(dx_body, (d // bn,),
                 [pl.BlockSpec((rows, bn), col_map)] * 2 + [pl.BlockSpec((1, bn), col_map), pl.BlockSpec((rows, HEAD), own_map)]
                 + [pl.BlockSpec((rows, PW), m, pipeline_mode=once) for m in maps]
-                + [pl.BlockSpec((bn, 2 * PW), lambda n, s, p=p: (n, s[p])) for p in range(4)]
+                + [pl.BlockSpec((bn, w.shape[1] // 4), lambda n, s, p=p: (n, s[p])) for p in range(4) for w in ws]
                 + [pl.BlockSpec((bn, rcv.shape[1]), row_map)] + [ANY] * 3,
                 [pl.BlockSpec((rows, d), first_row, pipeline_mode=once), pl.BlockSpec((8, bn), col_map)] + [ANY] * 3,
                 [sds(rows, d), sds(8, d, F32)] + [sds(*b.shape, F32) for b in bufs],
-                [idx, x, dy, gain, inv, *pieces] + [w_p] * 4 + [rcv, *bufs], 16 * rows * d * PW,
+                [idx, x, dy, gain, inv, *pieces] + list(ws) * 4 + [rcv, *bufs], 16 * rows * d * PW,
                 scratch=[pltpu.VMEM((rows, d), F32), pltpu.VMEM((rows, d), BF), pltpu.VMEM((rows, HEAD), F32),
                          pltpu.SemaphoreType.DMA((5,))],
-                aliases={18 + n: 2 + n for n in range(3)})
+                aliases={26 + n: 2 + n for n in range(3)})
 
 
 def solution(mesh):
@@ -710,30 +754,41 @@
         cos_h, sin_h = jnp.cos(angles), jnp.sin(angles)
         tabs = (jnp.concatenate([cos_h, cos_h], axis=1), jnp.concatenate([-sin_h, sin_h], axis=1))
 
-        bufs = project(vec(j * bpr, j1 * bpr, j), x, x1, gain_f, ws, tabs, None, seq)
+        dya, dyb = dy[:half], dy[half:]
+        bufs = project(vec(j * bpr, j1 * bpr, j, dep=(dya, dyb)), x, x1, gain_f, ws, tabs, None, seq)
         dbufs = dout(vec(j * bpr, j1 * bpr, j, dep=(bufs[1],)), dy, dy1, w_o, None, seq)
-        w_p = pack_weights(vec(j, dep=(dbufs[1],)), ws)
-
-        x2a = after(x2a, w_p)
-        dy2a = over(after(dy, x2a)[:half])
+
+        chip, nh = j // 2, seq // BLK // 2
+        tri = row_tasks(0, nh)
+        square = [(i + nh, nh, 0, i) for i in range(nh)]
+
+        def table(head, tasks):
+            return jnp.concatenate([vec(*head, len(tasks)), jnp.asarray(tasks, jnp.int32).reshape(-1)])
+
+        local = attn_fwd("local", after(table((j1, chip), tri), dbufs[1]), *bufs[1:4])
+        rest_tasks = jnp.where(chip == 0, table((j1, 0), row_tasks(nh, 2 * nh) * 2).at[HEADER - 1].set(nh),
+                               table((j1, 1), tri + square))
+
+        x2a = after(x2a, local[0])
+        dy2a = over(after(dya, x2a))
         x3a = near(x2a)
         bufs = project(vec(j2 * hpr, j3 * hpr, j), x2a, x3a, gain_f, ws, tabs, bufs, seq)
         x2b = after(x2b, bufs[1])
-        dy2b = over(after(dy, x2b)[half:])
+        dy2b = over(after(dyb, x2b))
         x3b = near(x2b)
         bufs = project(vec((j2 + 1) * hpr - 1, (j3 + 1) * hpr - 1, j), x2b, x3b, gain_f, ws, tabs, bufs, seq)
         h_all, q, k, v, inv = bufs
-        o, lse, o_hi, o_pair = attn_fwd(vec(j1), q, k, v, seq, rows)
+        o, lse, o_hi, o_pair = attn_fwd("rest", rest_tasks, q, k, v, rows, local)
         orv = over(o_hi)
         o1 = near(o_pair)
+        dy2a = after(dy2a, o)
+        dy3a = near(dy2a)
         qc, kc, vc = project_first(vec(j2, dep=(o,)), h_all, ws, tabs, seq // 2)
-        oc = attn_fwd(vec(j), qc, kc, vc, seq, 0)[0]
-
-        dy2a = after(dy2a, oc)
-        dy3a = near(dy2a)
-        dbufs = dout(vec(j2 * bpr, j3 * bpr, j), dy2a, dy3a, w_o, dbufs, seq)
-        dy2b = after(dy2b, dbufs[1])
+        oc = attn_fwd("first", table((j1, 0), tri), qc, kc, vc)[0]
+
+        dy2b = after(dy2b, oc)
         dy3b = near(dy2b)
+        dbufs = dout(vec(j2 * bpr, j3 * bpr, j, dep=(oc,)), dy2a, dy3a, w_o, dbufs, seq)
         dbufs = dout(vec(j2 * bpr + 1, j3 * bpr + 1, j), dy2b, dy3b, w_o, dbufs, seq)
         dy_all, do = dbufs
 
@@ -759,7 +814,7 @@
         fq, fk, fv, snd_b = dw_group(vec(j2), h_all, ga2, gb2, (fq, fk, fv))
         rcv_b = near(snd_b)
         grad_x, dg, fq, fk, fv = dx_call(vec(*dev, dep=(snd_b,)), x, dy, gain_f, inv,
-                                         (ga, gb, ga1, gb1, ga2, gb2, ga3, gb3), w_p, rcv, (fq, fk, fv))
+                                         (ga, gb, ga1, gb1, ga2, gb2, ga3, gb3), ws, rcv, (fq, fk, fv))
         dg = jnp.sum(dg, axis=0)
         dg = dg + near(dg)
         dg = dg + over(dg)

time: 1140 us -> 971 us (0.85)
  waiting for transfers between devices: 401 us -> 251 us
  Pallas kernels: 672 us -> 650 us
    ppermute x9, waiting for transfers between devices: 333 us -> 187 us  [over(): return lax.ppermute(val, 'sp', cross)]
    pallas_call x18, Pallas kernels: 672 us -> 650 us  [call(): pl.pallas_call(body, grid_spec=pltpu.PrefetchScalarGridSpec(num_scalar_pr...]
  transfers between devices with their start and end apart: 27 -> 27, of which waited for: 16 -> 15; matrix products, arithmetic and copies ran while one was open for 3% -> 4% of each run, Pallas kernels for 48% -> 56%
where the time goes in v4:
time: 971 us; the launch traced here: 961 us
  Pallas kernels  650 us (67%)
  waiting for transfers between devices  251 us (26%)
  local copies, waits for them, and re-layouts  25 us (3%)
  other arithmetic  18.9 us (2%)
  starting transfers between devices  14.6 us (2%)
    pallas_call x18, Pallas kernels, call(): pl.pallas_call(body, grid_spec=pltpu.PrefetchScalarGridSpec(num_scalar_pr...  650 us
    ppermute x9, waiting for transfers between devices, over(): return lax.ppermute(val, 'sp', cross)  187 us
    ppermute x18, waiting for transfers between devices, near(): return lax.ppermute(val, 'sp', pair)  64 us
  transfers between devices with their start and end apart: 27, of which 15 were waited for; matrix products, arithmetic and copies ran while one was open for 4% of the time, Pallas kernels for 56%

profile of v4, /device:TPU:0, one launch (start us, length us, event | category | flops | bytes accessed | tf_op | source)
XLA Modules:
  0.0 960.8 jit_solution(17524838801654207017)
XLA Ops:
  1.5 10.0 %collective-permute-done.2.xb_ref = bf16[1024,3072]{1,0:T(8,128)(2,1)S(1)} collective-permute-done((bf16[1024,3072]{1,0:T(8,128)(2,1)}, bf16[1024,3072]{1,0:T(8,128)(2,1)S(1)}, u32[]{:S(2)}, u32[]{:S(2)}) %collective-permute-start.2) | collective-permute-done | bytes 6291488 | tf_op jit(solution)/shard_map/ppermute | solution.py:715
  41.5 34.5 %shard_map.171 = (bf16[4096,3072]{1,0:T(8,128)(2,1)}, bf16[4096,768]{1,0:T(8,128)(2,1)}, bf16[4096,256]{1,0:T(8,128)(2,1)}, bf16[4096,256]{1,0:T(8,128)(2,1)}, f32[4096,128]{1,0:T(8,128)}) custom-call(s32[3]{0:T(128)} %add_add_fusion.2.s_ref, bf16[1024,3072]{1,0:T(8,128)(2,1)} %x_ref.3, bf16[1024,3072]{1,0:T(8,128)(2,1)} %copy-done.8, f32[1,3072]{1,0:T(1,128)} %bitcast.16, ...), custom_call_target="tpu_custom_call" | custom-call | flops 16106127360 | bytes 31457280 | tf_op jit(solution)/shard_map/pallas_call | solution.py:51
  76.1 17.7 %shard_map.172 = (bf16[4096,3072]{1,0:T(8,128)(2,1)}, bf16[4096,768]{1,0:T(8,128)(2,1)}) custom-call(s32[3]{0:T(128)} %add_add_fusion.2.s_ref, bf16[1024,3072]{1,0:T(8,128)(2,1)} %dy_ref.1, bf16[1024,3072]{1,0:T(8,128)(2,1)} %collective-permute-done.6.db_ref, bf16[3072,3072]{1,0:T(8,128)(2,1)} %rest_7_.1), custom_call_target="tpu_custom_call" | custom-call | flops 9663676416 | bytes 18874368 | tf_op jit(solution)/shard_map/pallas_call | solution.py:51
  93.8 27.7 %shard_map.173 = (bf16[2048,768]{1,0:T(8,128)(2,1)}, f32[2,8,2048]{2,1,0:T(8,128)}, f32[2,3,128,2048]{3,2,1,0:T(8,128)}) custom-call(s32[19]{0:T(128)} %get-tuple-element.101.refs_0_, bf16[4096,768]{1,0:T(8,128)(2,1)} %get-tuple-element.97.refs_1_.rest_1_, bf16[4096,256]{1,0:T(8,128)(2,1)} %get-tuple-element.102.refs_2_.rest_2_, ...), custom_call_target="tpu_custom_call" | custom-call | flops 6442450944 | bytes 12582912 | tf_op jit(solution)/shard_map/pallas_call | solution.py:51
  134.4 27.4 %shard_map.174 = (bf16[4096,3072]{1,0:T(8,128)(2,1)}, bf16[4096,768]{1,0:T(8,128)(2,1)}, bf16[4096,256]{1,0:T(8,128)(2,1)}, bf16[4096,256]{1,0:T(8,128)(2,1)}, f32[4096,128]{1,0:T(8,128)}) custom-call(s32[3]{0:T(128)} %add_add_fusion.1.s_ref, ...), custom_call_target="tpu_custom_call", output_to_operand_aliasing={{0}: (9, {}), {1}: (10, {}), {2}: (11, {}), {3}: (12, {}), ... | custom-call | flops 12079595520 | bytes 23592960 | tf_op jit(solution)/shard_map/pallas_call | solution.py:51
  169.4 13.1 %shard_map.175 = (bf16[4096,3072]{1,0:T(8,128)(2,1)}, bf16[4096,768]{1,0:T(8,128)(2,1)}, bf16[4096,256]{1,0:T(8,128)(2,1)}, bf16[4096,256]{1,0:T(8,128)(2,1)}, f32[4096,128]{1,0:T(8,128)}) custom-call(s32[3]{0:T(128)} %add_add_fusion.s_ref, ...), custom_call_target="tpu_custom_call", output_to_operand_aliasing={{0}: (9, {}), {1}: (10, {}), {2}: (11, {}), {3}: (12, {}), ... | custom-call | flops 4026531840 | bytes 7864320 | tf_op jit(solution)/shard_map/pallas_call | solution.py:51
  182.5 61.3 %shard_map.176 = (bf16[4096,768]{1,0:T(8,128)(2,1)}, f32[2,8,4096]{2,1,0:T(8,128)}, bf16[2048,768]{1,0:T(8,128)(2,1)}, bf16[1024,768]{1,0:T(8,128)(2,1)}) custom-call(s32[35]{0:T(128)} %broadcast_select_fusion.refs_0_, bf16[4096,768]{1,0:T(8,128)(2,1)} %get-tuple-element.114.refs_1_.q_ref, bf16[4096,256]{1,0:T(8,128)(2,1)} %get-tuple-element.116.refs_2_.k_ref, ...), custom_call_target="tpu_custom_call" | custom-call | flops 25769803776 | bytes 50331648 | tf_op jit(solution)/shard_map/pallas_call | solution.py:51
  244.1 22.6 %shard_map.177 = (bf16[2048,768]{1,0:T(8,128)(2,1)}, bf16[2048,256]{1,0:T(8,128)(2,1)}, bf16[2048,256]{1,0:T(8,128)(2,1)}) custom-call(s32[1]{0:T(128)} %bitcast.2.s_ref, bf16[4096,3072]{1,0:T(8,128)(2,1)} %get-tuple-element.122.h_ref, bf16[3072,3072]{1,0:T(8,128)(2,1)} %rest_17_.1, bf16[3072,1024]{1,0:T(8,128)(2,1)} %rest_18_.1, ...), custom_call_target="tpu_custom_call" | custom-call | flops 16106127360 | bytes 31457280 | tf_op jit(solution)/shard_map/pallas_call | solution.py:51
  266.6 26.3 %shard_map.178 = (bf16[4096,768]{1,0:T(8,128)(2,1)}, f32[2,8,2048]{2,1,0:T(8,128)}) custom-call(s32[19]{0:T(128)} %get-tuple-element.176.refs_0_, bf16[2048,768]{1,0:T(8,128)(2,1)} %get-tuple-element.123.refs_1_, bf16[2048,256]{1,0:T(8,128)(2,1)} %get-tuple-element.124.refs_2_, bf16[2048,256]{1,0:T(8,128)(2,1)} %get-tuple-element.125.refs_3_), custom_call_target="tpu_custom_call" | custom-call | flops 6442450944 | bytes 12582912 | tf_op jit(solution)/shard_map/pallas_call | solution.py:51
  292.9 9.9 %collective-permute-done.9.da_ref = bf16[512,3072]{1,0:T(8,128)(2,1)} collective-permute-done((bf16[512,3072]{1,0:T(8,128)(2,1)}, bf16[512,3072]{1,0:T(8,128)(2,1)}, u32[]{:S(2)}, u32[]{:S(2)}) %collective-permute-start.9) | collective-permute-done | bytes 3145760 | tf_op jit(solution)/shard_map/ppermute | solution.py:712
  305.6 11.7 %shard_map.179 = (bf16[4096,3072]{1,0:T(8,128)(2,1)}, bf16[4096,768]{1,0:T(8,128)(2,1)}) custom-call(s32[3]{0:T(128)} %add_add_fusion.4.s_ref, bf16[512,3072]{1,0:T(8,128)(2,1)} %collective-permute-done.11.da_ref, bf16[512,3072]{1,0:T(8,128)(2,1)} %collective-permute-done.12.db_ref, ...), custom_call_target="tpu_custom_call", output_to_operand_aliasing={{0}: (4, {}), {1}: (5, {})} | custom-call | flops 4831838208 | bytes 9437184 | tf_op jit(solution)/shard_map/pallas_call | solution.py:51
  317.3 11.5 %shard_map.180 = (bf16[4096,3072]{1,0:T(8,128)(2,1)}, bf16[4096,768]{1,0:T(8,128)(2,1)}) custom-call(s32[3]{0:T(128)} %add_add_fusion.3.s_ref, bf16[512,3072]{1,0:T(8,128)(2,1)} %collective-permute-done.9.da_ref, bf16[512,3072]{1,0:T(8,128)(2,1)} %collective-permute-done.10.db_ref, ...), custom_call_target="tpu_custom_call", output_to_operand_aliasing={{0}: (4, {}), {1}: (5, {})} | custom-call | flops 4831838208 | bytes 9437184 | tf_op jit(solution)/shard_map/pallas_call | solution.py:51
  328.8 80.7 %shard_map.181 = (bf16[4096,640]{1,0:T(8,128)(2,1)}, bf16[1024,640]{1,0:T(8,128)(2,1)}) custom-call(s32[2]{0:T(128)} %pad_add_fusion.9.s_ref, bf16[4096,768]{1,0:T(8,128)(2,1)} %get-tuple-element.114.refs_1_.q_ref, bf16[4096,768]{1,0:T(8,128)(2,1)} %get-tuple-element.134.do_ref, bf16[4096,768]{1,0:T(8,128)(2,1)} %get-tuple-element.120.o_ref.oa_ref.rest_0_, ...), custom_call_target="tpu_custom_call" | custom-call | flops 36238786560 | bytes 70778880 | tf_op jit(solution)/shard_map/pallas_call | solution.py:51
  409.5 81.2 %shard_map.182 = (bf16[4096,640]{1,0:T(8,128)(2,1)}, bf16[1024,640]{1,0:T(8,128)(2,1)}) custom-call(s32[2]{0:T(128)} %get-tuple-element.137.s_ref, bf16[4096,768]{1,0:T(8,128)(2,1)} %get-tuple-element.114.refs_1_.q_ref, bf16[4096,768]{1,0:T(8,128)(2,1)} %get-tuple-element.134.do_ref, bf16[4096,768]{1,0:T(8,128)(2,1)} %get-tuple-element.120.o_ref.oa_ref.rest_0_, ...), custom_call_target="tpu_custom_call" | custom-call | flops 36238786560 | bytes 70778880 | tf_op jit(solution)/shard_map/pallas_call | solution.py:51
  494.4 53.9 %shard_map.183 = (f32[3072,3072]{1,0:T(8,128)}, f32[1536,3072]{1,0:T(8,128)}) custom-call(s32[2]{0:T(128)} %get-tuple-element.139.s_ref, bf16[4096,768]{1,0:T(8,128)(2,1)} %get-tuple-element.120.o_ref.oa_ref.rest_0_, bf16[4096,768]{1,0:T(8,128)(2,1)} %constant_dynamic-update-slice_fusion.ob_ref.rest_2_, bf16[4096,3072]{1,0:T(8,128)(2,1)} %get-tuple-element.142.dy_ref), custom_call_target="tpu_custom_call" | custom-call | flops 38654705664 | bytes 75497472 | tf_op jit(solution)/shard_map/pallas_call | solution.py:51
  553.0 26.0 %collective-permute-done.14.rest_1_ = bf16[1024,768]{1,0:T(8,128)(2,1)S(1)} collective-permute-done((bf16[1024,768]{1,0:T(8,128)(2,1)}, bf16[1024,768]{1,0:T(8,128)(2,1)S(1)}, u32[]{:S(2)}, u32[]{:S(2)}) %collective-permute-start.14) | collective-permute-done | bytes 1572896 | tf_op jit(solution)/shard_map/ppermute | solution.py:715
  581.3 27.1 %shard_map.184 = bf16[1024,3072]{1,0:T(8,128)(2,1)} custom-call(s32[4]{0:T(128)} %pad_add_fusion.6.s_ref, bf16[1024,3072]{1,0:T(8,128)(2,1)} %x_ref.3, bf16[4096,768]{1,0:T(8,128)(2,1)} %get-tuple-element.120.o_ref.oa_ref.rest_0_, bf16[1024,768]{1,0:T(8,128)(2,1)} %copy-done.1, bf16[4096,768]{1,0:T(8,128)(2,1)} %constant_dynamic-update-slice_fusion.ob_ref.rest_2_, ...), custom_call_target="tpu_custom_call" | custom-call | flops 19327352832 | bytes 37748736 | tf_op jit(solution)/shard_map/pallas_call | solution.py:51
  608.4 55.7 %collective-permute-done.16.gc_ref.ga_ref.rest_4_ = bf16[4096,640]{1,0:T(8,128)(2,1)} collective-permute-done((bf16[4096,640]{1,0:T(8,128)(2,1)}, bf16[4096,640]{1,0:T(8,128)(2,1)}, u32[]{:S(2)}, u32[]{:S(2)}) %collective-permute-start.16) | collective-permute-done | bytes 5242912 | tf_op jit(solution)/shard_map/ppermute | solution.py:712
  664.1 58.5 %shard_map.185 = (f32[3072,3072]{1,0:T(8,128)}, f32[3072,1024]{1,0:T(8,128)}, f32[3072,1024]{1,0:T(8,128)}, f32[3072,1792]{1,0:T(8,128)}, f32[3072,3072]{1,0:T(8,128)}) custom-call(s32[4]{0:T(128)} %pad_add_fusion.6.s_ref, bf16[4096,3072]{1,0:T(8,128)(2,1)} %get-tuple-element.122.h_ref, ...), custom_call_target="tpu_custom_call", output_to_operand_aliasing={{4}: (6, {})} | custom-call | flops 45097156608 | bytes 88080384 | tf_op jit(solution)/shard_map/pallas_call | solution.py:51
  724.5 114.0 %collective-permute-done.17.gb_ref.rest_5_ = bf16[4096,640]{1,0:T(8,128)(2,1)} collective-permute-done((bf16[4096,640]{1,0:T(8,128)(2,1)}, bf16[4096,640]{1,0:T(8,128)(2,1)}, u32[]{:S(2)}, u32[]{:S(2)}) %collective-permute-start.17) | collective-permute-done | bytes 5242912 | tf_op jit(solution)/shard_map/ppermute | solution.py:712
  838.5 29.6 %shard_map.186 = (f32[3072,3072]{1,0:T(8,128)}, f32[3072,1024]{1,0:T(8,128)}, f32[3072,1024]{1,0:T(8,128)}, f32[3072,768]{1,0:T(8,128)}) custom-call(s32[1]{0:T(128)} %bitcast.2.s_ref, bf16[4096,3072]{1,0:T(8,128)(2,1)} %get-tuple-element.122.h_ref, ...), custom_call_target="tpu_custom_call", output_to_operand_aliasing={{0}: (4, {}), {1}: (5, {}), {2}: (6, {})} | custom-call | flops 19327352832 | bytes 37748736 | tf_op jit(solution)/shard_map/pallas_call | solution.py:51
  872.0 12.8 %collective-permute-done.20.rest_3_ = bf16[1024,640]{1,0:T(8,128)(2,1)S(1)} collective-permute-done((bf16[1024,640]{1,0:T(8,128)(2,1)}, bf16[1024,640]{1,0:T(8,128)(2,1)S(1)}, u32[]{:S(2)}, u32[]{:S(2)}) %collective-permute-start.20) | collective-permute-done | bytes 1310752 | tf_op jit(solution)/shard_map/ppermute | solution.py:715
  890.6 53.8 %shard_map.187 = (bf16[1024,3072]{1,0:T(8,128)(2,1)}, f32[8,3072]{1,0:T(8,128)}, f32[3072,3072]{1,0:T(8,128)}, f32[3072,1024]{1,0:T(8,128)}, f32[3072,1024]{1,0:T(8,128)}) custom-call(s32[4]{0:T(128)} %pad_add_fusion.6.s_ref, bf16[1024,3072]{1,0:T(8,128)(2,1)} %x_ref.3, ...), custom_call_target="tpu_custom_call", output_to_operand_aliasing={{2}: (26, {}), {3}: (27, {}), {4}: (28, {})} | custom-call | flops 32212254720 | bytes 62914560 | tf_op jit(solution)/shard_map/pallas_call | solution.py:51
  948.3 11.4 %shard_map.188 = (f32[3072,3072]{1,0:T(8,128)}, f32[3072,1024]{1,0:T(8,128)}, f32[3072,1024]{1,0:T(8,128)}) custom-call(s32[1]{0:T(128)} %bitcast.3.s_ref, f32[3072,768]{1,0:T(8,128)} %collective-permute-done.24.rcv, f32[3072,3072]{1,0:T(8,128)} %get-tuple-element.163.rest_0_, ...), custom_call_target="tpu_custom_call", output_to_operand_aliasing={{0}: (2, {}), {1}: (3, {}), {2}: (4, {})} | custom-call | flops 2359296 | bytes 4608 | tf_op jit(solution)/shard_map/pallas_call | solution.py:51
  (98 shorter events, 81.2 us)
Async XLA Ops:
  0.6 10.9 %collective-permute-start.2 = (bf16[1024,3072]{1,0:T(8,128)(2,1)}, bf16[1024,3072]{1,0:T(8,128)(2,1)S(1)}, u32[]{:S(2)}, u32[]{:S(2)}) collective-permute-start(bf16[1024,3072]{1,0:T(8,128)(2,1)} %x_ref.3), channel_id=1, source_target_pairs={{0,1},{1,0},{2,3},{3,2},{4,5},{5,4},{6,7},{7,6}} | collective-permute-start | bytes 18874376 | tf_op jit(solution)/shard_map/ppermute | solution.py:715
  11.5 64.5 %collective-permute-start.6 = (bf16[1024,3072]{1,0:T(8,128)(2,1)}, bf16[1024,3072]{1,0:T(8,128)(2,1)}, u32[]{:S(2)}, u32[]{:S(2)}) collective-permute-start(bf16[1024,3072]{1,0:T(8,128)(2,1)} %dy_ref.1), channel_id=1, source_target_pairs={{0,1},{1,0},{2,3},{3,2},{4,5},{5,4},{6,7},{7,6}} | collective-permute-start | bytes 18874376 | tf_op jit(solution)/shard_map/ppermute | solution.py:715
  14.2 15.9 %collective-permute-start.3 = (s32[1024]{0:T(1024)}, s32[1024]{0:T(1024)S(1)}, u32[]{:S(2)}, u32[]{:S(2)}) collective-permute-start(s32[1024]{0:T(1024)} %param.16), channel_id=1, source_target_pairs={{0,1},{1,0},{2,3},{3,2},{4,5},{5,4},{6,7},{7,6}} | collective-permute-start | bytes 12296 | tf_op jit(solution)/shard_map/ppermute | solution.py:715
  14.6 14.0 %collective-permute-start.4 = (s32[1024]{0:T(1024)}, s32[1024]{0:T(1024)S(1)}, u32[]{:S(2)}, u32[]{:S(2)}) collective-permute-start(s32[1024]{0:T(1024)} %param.16), channel_id=1, source_target_pairs={{0,2},{1,3},{2,0},{3,1},{4,6},{5,7},{6,4},{7,5}} | collective-permute-start | bytes 12296 | tf_op jit(solution)/shard_map/ppermute | solution.py:712
  22.0 104.1 %collective-permute-start.1 = (bf16[768,3072]{1,0:T(8,128)(2,1)}, bf16[768,3072]{1,0:T(8,128)(2,1)}, u32[]{:S(2)}, u32[]{:S(2)}) collective-permute-start(bf16[768,3072]{1,0:T(8,128)(2,1)} %slice.22), channel_id=1, source_target_pairs={{0,2},{1,3},{2,0},{3,1},{4,6},{5,7},{6,4},{7,5}} | collective-permute-start | bytes 14155784 | tf_op jit(solution)/shard_map/ppermute | solution.py:712
  126.1 8.3 collective-permute-start.7
  127.7 36.9 %collective-permute-start = (bf16[256,3072]{1,0:T(8,128)(2,1)S(1)}, bf16[256,3072]{1,0:T(8,128)(2,1)}, u32[]{:S(2)}, u32[]{:S(2)}) collective-permute-start(bf16[256,3072]{1,0:T(8,128)(2,1)S(1)} %slice.23), channel_id=1, source_target_pairs={{0,2},{1,3},{2,0},{3,1},{4,6},{5,7},{6,4},{7,5}} | collective-permute-start | bytes 4718600 | tf_op jit(solution)/shard_map/ppermute | solution.py:712
  164.6 79.2 %collective-permute-start.11 = (bf16[512,3072]{1,0:T(8,128)(2,1)}, bf16[512,3072]{1,0:T(8,128)(2,1)}, u32[]{:S(2)}, u32[]{:S(2)}) collective-permute-start(bf16[512,3072]{1,0:T(8,128)(2,1)} %get-tuple-element.129), channel_id=1, source_target_pairs={{0,2},{1,3},{2,0},{3,1},{4,6},{5,7},{6,4},{7,5}} | collective-permute-start | bytes 9437192 | tf_op jit(solution)/shard_map/ppermute | solution.py:712
  166.2 136.6 %collective-permute-start.9 = (bf16[512,3072]{1,0:T(8,128)(2,1)}, bf16[512,3072]{1,0:T(8,128)(2,1)}, u32[]{:S(2)}, u32[]{:S(2)}) collective-permute-start(bf16[512,3072]{1,0:T(8,128)(2,1)} %get-tuple-element.115), channel_id=1, source_target_pairs={{0,2},{1,3},{2,0},{3,1},{4,6},{5,7},{6,4},{7,5}} | collective-permute-start | bytes 9437192 | tf_op jit(solution)/shard_map/ppermute | solution.py:712
  243.8 61.8 %collective-permute-start.12 = (bf16[512,3072]{1,0:T(8,128)(2,1)}, bf16[512,3072]{1,0:T(8,128)(2,1)}, u32[]{:S(2)}, u32[]{:S(2)}) collective-permute-start(bf16[512,3072]{1,0:T(8,128)(2,1)} %collective-permute-done.11.da_ref), channel_id=1, source_target_pairs={{0,1},{1,0},{2,3},{3,2},{4,5},{5,4},{6,7},{7,6}} | collective-permute-start | bytes 9437192 | tf_op jit(solution)/shard_map/ppermute | solution.py:715
  302.8 14.4 %collective-permute-start.10 = (bf16[512,3072]{1,0:T(8,128)(2,1)}, bf16[512,3072]{1,0:T(8,128)(2,1)}, u32[]{:S(2)}, u32[]{:S(2)}) collective-permute-start(bf16[512,3072]{1,0:T(8,128)(2,1)} %collective-permute-done.9.da_ref), channel_id=1, source_target_pairs={{0,1},{1,0},{2,3},{3,2},{4,5},{5,4},{6,7},{7,6}} | collective-permute-start | bytes 9437192 | tf_op jit(solution)/shard_map/ppermute | solution.py:715
  305.3 185.4 %collective-permute-start.13 = (bf16[2048,768]{1,0:T(8,128)(2,1)}, bf16[2048,768]{1,0:T(8,128)(2,1)}, u32[]{:S(2)}, u32[]{:S(2)}) collective-permute-start(bf16[2048,768]{1,0:T(8,128)(2,1)} %get-tuple-element.140), channel_id=1, source_target_pairs={{0,2},{1,3},{2,0},{3,1},{4,6},{5,7},{6,4},{7,5}} | collective-permute-start | bytes 9437192 | tf_op jit(solution)/shard_map/ppermute | solution.py:712
  548.3 115.8 %collective-permute-start.18 = (f32[1536,3072]{1,0:T(8,128)}, f32[1536,3072]{1,0:T(8,128)}, u32[]{:S(2)}, u32[]{:S(2)}) collective-permute-start(f32[1536,3072]{1,0:T(8,128)} %get-tuple-element.143), channel_id=1, source_target_pairs={{0,1},{1,0},{2,3},{3,2},{4,5},{5,4},{6,7},{7,6}} | collective-permute-start | bytes 56623112 | tf_op jit(solution)/shard_map/ppermute | solution.py:715
  548.6 115.5 %collective-permute-start.16 = (bf16[4096,640]{1,0:T(8,128)(2,1)}, bf16[4096,640]{1,0:T(8,128)(2,1)}, u32[]{:S(2)}, u32[]{:S(2)}) collective-permute-start(bf16[4096,640]{1,0:T(8,128)(2,1)} %get-tuple-element.136.ga_ref.rest_0_), channel_id=1, source_target_pairs={{0,2},{1,3},{2,0},{3,1},{4,6},{5,7},{6,4},{7,5}} | collective-permute-start | bytes 15728648 | tf_op jit(solution)/shard_map/ppermute | solution.py:712
  550.3 28.6 %collective-permute-start.14 = (bf16[1024,768]{1,0:T(8,128)(2,1)}, bf16[1024,768]{1,0:T(8,128)(2,1)S(1)}, u32[]{:S(2)}, u32[]{:S(2)}) collective-permute-start(bf16[1024,768]{1,0:T(8,128)(2,1)} %get-tuple-element.145), channel_id=1, source_target_pairs={{0,1},{1,0},{2,3},{3,2},{4,5},{5,4},{6,7},{7,6}} | collective-permute-start | bytes 4718600 | tf_op jit(solution)/shard_map/ppermute | solution.py:715
  551.8 29.5 %collective-permute-start.15 = (bf16[1024,768]{1,0:T(8,128)(2,1)S(1)}, bf16[1024,768]{1,0:T(8,128)(2,1)}, u32[]{:S(2)}, u32[]{:S(2)}) collective-permute-start(bf16[1024,768]{1,0:T(8,128)(2,1)S(1)} %constant_dynamic-slice_fusion.2), channel_id=1, source_target_pairs={{0,1},{1,0},{2,3},{3,2},{4,5},{5,4},{6,7},{7,6}} | collective-permute-start | bytes 4718600 | tf_op jit(solution)/shard_map/ppermute | solution.py:715
  722.7 167.9 %collective-permute-start.23 = (f32[3072,1792]{1,0:T(8,128)}, f32[3072,1792]{1,0:T(8,128)}, u32[]{:S(2)}, u32[]{:S(2)}) collective-permute-start(f32[3072,1792]{1,0:T(8,128)} %get-tuple-element.149), channel_id=1, source_target_pairs={{0,1},{1,0},{2,3},{3,2},{4,5},{5,4},{6,7},{7,6}} | collective-permute-start | bytes 66060296 | tf_op jit(solution)/shard_map/ppermute | solution.py:715
  722.7 115.8 %collective-permute-start.17 = (bf16[4096,640]{1,0:T(8,128)(2,1)}, bf16[4096,640]{1,0:T(8,128)(2,1)}, u32[]{:S(2)}, u32[]{:S(2)}) collective-permute-start(bf16[4096,640]{1,0:T(8,128)(2,1)} %get-tuple-element.138.gb_ref.rest_1_), channel_id=1, source_target_pairs={{0,2},{1,3},{2,0},{3,1},{4,6},{5,7},{6,4},{7,5}} | collective-permute-start | bytes 15728648 | tf_op jit(solution)/shard_map/ppermute | solution.py:712
  868.1 80.2 %collective-permute-start.24 = (f32[3072,768]{1,0:T(8,128)}, f32[3072,768]{1,0:T(8,128)}, u32[]{:S(2)}, u32[]{:S(2)}) collective-permute-start(f32[3072,768]{1,0:T(8,128)} %get-tuple-element.154), channel_id=1, source_target_pairs={{0,1},{1,0},{2,3},{3,2},{4,5},{5,4},{6,7},{7,6}} | collective-permute-start | bytes 28311560 | tf_op jit(solution)/shard_map/ppermute | solution.py:715
  868.1 16.7 %collective-permute-start.20 = (bf16[1024,640]{1,0:T(8,128)(2,1)}, bf16[1024,640]{1,0:T(8,128)(2,1)S(1)}, u32[]{:S(2)}, u32[]{:S(2)}) collective-permute-start(bf16[1024,640]{1,0:T(8,128)(2,1)} %get-tuple-element.158), channel_id=1, source_target_pairs={{0,1},{1,0},{2,3},{3,2},{4,5},{5,4},{6,7},{7,6}} | collective-permute-start | bytes 3932168 | tf_op jit(solution)/shard_map/ppermute | solution.py:715
  868.6 18.2 %collective-permute-start.19 = (bf16[1024,640]{1,0:T(8,128)(2,1)}, bf16[1024,640]{1,0:T(8,128)(2,1)}, u32[]{:S(2)}, u32[]{:S(2)}) collective-permute-start(bf16[1024,640]{1,0:T(8,128)(2,1)} %get-tuple-element.157), channel_id=1, source_target_pairs={{0,1},{1,0},{2,3},{3,2},{4,5},{5,4},{6,7},{7,6}} | collective-permute-start | bytes 3932168 | tf_op jit(solution)/shard_map/ppermute | solution.py:715
  870.1 18.7 %collective-permute-start.21 = (bf16[1024,640]{1,0:T(8,128)(2,1)S(1)}, bf16[1024,640]{1,0:T(8,128)(2,1)}, u32[]{:S(2)}, u32[]{:S(2)}) collective-permute-start(bf16[1024,640]{1,0:T(8,128)(2,1)S(1)} %constant_dynamic-slice_fusion.1), channel_id=1, source_target_pairs={{0,1},{1,0},{2,3},{3,2},{4,5},{5,4},{6,7},{7,6}} | collective-permute-start | bytes 3932168 | tf_op jit(solution)/shard_map/ppermute | solution.py:715
  884.8 5.8 collective-permute-start.22
  946.6 13.2 %collective-permute-start.26 = (f32[3072]{0:T(1024)S(1)}, f32[3072]{0:T(1024)S(1)}, u32[]{:S(2)}, u32[]{:S(2)}) collective-permute-start(f32[3072]{0:T(1024)S(1)} %add.46), channel_id=1, source_target_pairs={{0,2},{1,3},{2,0},{3,1},{4,6},{5,7},{6,4},{7,5}} | collective-permute-start | bytes 36872 | tf_op jit(solution)/shard_map/ppermute | solution.py:712
  (12 other events, 115.9 us)

commit v5 on v4

--- a/solution.py
+++ b/solution.py
@@ -59,6 +59,22 @@
                                       transcendentals=0))(*args)
 
 
+def down(shape):
+    return lax.broadcasted_iota(jnp.int32, shape, 0)
+
+
+def across(shape):
+    return lax.broadcasted_iota(jnp.int32, shape, 1)
+
+
+def one(h):
+    return slice(h, h + 1)
+
+
+def head_cols(h):
+    return slice(h * HEAD, h * HEAD + HEAD)
+
+
 def mm(a, b):
     return jnp.dot(a, b, preferred_element_type=F32)
 
@@ -85,7 +101,7 @@
     cos_t, sin_t = cos_ref[...], sin_ref[...]
     out = mm(h, wq_ref[...])
     for c in range(wq_ref.shape[1] // HEAD):
-        sl = slice(c * HEAD, c * HEAD + HEAD)
+        sl = head_cols(c)
         q_ref[:, sl] = rotate(out[:, sl], cos_t, sin_t).astype(BF)
     out = mm(h, jnp.concatenate([wk_ref[...], wv_ref[...]], axis=1))
     for sl in (slice(0, HEAD), slice(HEAD, PAIR)):
@@ -111,7 +127,7 @@
             sl = ds(c * step, step)
             inv, gain = inv_ref[sl, :], gain_ref[...]
             for n in range(src.shape[1] // HEAD):
-                cols = slice(n * HEAD, n * HEAD + HEAD)
+                cols = head_cols(n)
                 h_ref[sl, cols] = (src[sl, cols].astype(F32) * inv * gain[:, cols]).astype(BF)
             return 0
 
@@ -230,7 +246,7 @@
         kk[sl, :HEAD] = k_ref[sl, :]
         kk[sl, HEAD:] = k_ref[sl, :]
         for h in range(GROUP):
-            qf = q_ref[sl, h * HEAD:(h + 1) * HEAD].astype(F32) * SCALE2
+            qf = q_ref[sl, head_cols(h)].astype(F32) * SCALE2
             hi = qf.astype(BF)
             qt[h, :HEAD, sl] = hi.T
             qt[h, HEAD:, sl] = (qf - hi.astype(F32)).astype(BF).T
@@ -250,10 +266,10 @@
         return [s_ref[HEADER + t * TASK + n] for n in range(TASK)]
 
     def stage_a(h, i, j, masked, init=None):
-        row = slice(h, h + 1)
+        row = one(h)
         s = mm(kk[ds(j * BLK, BLK), :], qt[h, :, ds(i * BLK, BLK)])
         if masked is not False:
-            keep = lax.broadcasted_iota(jnp.int32, s.shape, 0) <= lax.broadcasted_iota(jnp.int32, s.shape, 1)
+            keep = down(s.shape) <= across(s.shape)
             s = jnp.where(keep if masked is True else jnp.logical_or(keep, jnp.logical_not(masked)), s, NEG_LARGE)
         s_scr[h] = s
         m_new = jnp.max(s, axis=0, keepdims=True)
@@ -268,19 +284,20 @@
         stat[cur, row] = m_new
 
     def stage_p(h):
-        row = slice(h, h + 1)
+        row = one(h)
         p = jnp.exp2(s_scr[h] - stat[cur, row])
         alpha = stat[old, row]
         stat[den_row, row] = stat[den_row, row] * alpha + jnp.sum(p, axis=0, keepdims=True)
         return p.astype(BF), alpha
 
     def stage_v(h, j, held):
-        acc[h] = acc[h] * held[1] + mm(vt[:, ds(j * BLK, BLK)], held[0])
+        p, alpha = held
+        acc[h] = acc[h] * alpha + mm(vt[:, ds(j * BLK, BLK)], p)
 
     def finish(h, i, den, top):
-        row = slice(h, h + 1)
+        row = one(h)
         out = acc[h] / den
-        o_ref[ds(i * BLK, BLK), h * HEAD:(h + 1) * HEAD] = out.T.astype(BF)
+        o_ref[ds(i * BLK, BLK), head_cols(h)] = out.T.astype(BF)
         lse_ref[0, row, ds(i * BLK, BLK)] = top + jnp.log2(den)
         if kind == "local":
             rest[2][0, h, :, ds(i * BLK, BLK)] = out
@@ -316,7 +333,7 @@
         i2, _, _, init2 = task(jnp.minimum(t + 1, count - 1))
         for h in range(GROUP):
             held = stage_p(h)
-            final = (stat[den_row, h:h + 1], stat[cur, h:h + 1])
+            final = (stat[den_row, one(h)], stat[cur, one(h)])
             stage_a(h, i2, 0, False, init2)
             stage_v(h, steps - 1, held)
             finish(h, i, *final)
@@ -351,7 +368,7 @@
 
     at = half_map if kind == "local" else col_map
     lse_spec = pl.BlockSpec((1, 8, seq), head_map)
-    outs, specs = [sds(seq * 2 if kind == "first" else seq, q.shape[1]), jax.ShapeDtypeStruct((nkv, 8, seq), F32)], []
+    outs, specs = [sds(seq, q.shape[1]), jax.ShapeDtypeStruct((nkv, 8, seq), F32)], []
     out_specs = [pl.BlockSpec((seq, GW), col_map), lse_spec]
     state = pl.BlockSpec((1, GROUP, HEAD, whole // 2), state_map)
     if kind == "local":
@@ -369,12 +386,39 @@
                          pltpu.VMEM((GROUP, HEAD, BLK), F32), pltpu.VMEM((GROUP, 8, BLK), F32)])
 
 
-def bwd_body(s_ref, q_ref, do_ref, o_ref, k_ref, v_ref, lse_ref, cos_ref, sin_ref, out_ref, pair_ref,
-             qa, da, ka, va, q3t, do3t, dq3, dkt, dvt):
+def bwd_body(s_ref, q_ref, do_ref, o_ref, lse_ref, qn_ref, don_ref, on_ref, lsen_ref, k_ref, v_ref, cos_ref, sin_ref,
+             out_ref, pair_ref, ka, va, dkt, dvt, *sets):
     i = pl.program_id(0)
     last = pl.num_programs(0) - 1
     seq = k_ref.shape[0]
     m3 = GROUP * HB
+    sets = (sets[:5], sets[5:])
+
+    def spots():
+        for b in range(2):
+            for h in range(GROUP):
+                start = (b * GROUP + h) * HB
+                yield h, slice(b * HB, (b + 1) * HB), head_cols(h), slice(start, start + HB)
+
+    def prepare(q_src, do_src, o_src, lse_src, dst):
+        qa, da, q3t, do3t, dq3 = dst
+        srow = down((16, HB))
+        blank = jnp.zeros((HEAD - 16, HB), BF)
+        for h, src, cols, rows in spots():
+            qh, doh = q_src[src, cols], do_src[src, cols]
+            qa[rows, :HEAD] = qh
+            da[rows, :HEAD] = doh
+            q3t[:, rows] = qh.T
+            dt = doh.T
+            do3t[:, rows] = dt
+            delta = jnp.sum(dt.astype(F32) * o_src[src, cols].T.astype(F32), axis=0, keepdims=True)
+            parts = jnp.zeros((16, HB), F32)
+            for n, part in enumerate(split3(lse_src[0, one(h), src] * (1.0 / SCALE2)) + split3(delta)):
+                parts = jnp.where(srow == n, part, parts)
+            block = jnp.concatenate([parts.astype(BF), blank], axis=0).T
+            qa[rows, HEAD:] = block
+            da[rows, HEAD:] = block
+        dq3[...] = jnp.zeros_like(dq3)
 
     @pl.when(i == 0)
     def _():
@@ -383,79 +427,54 @@
 
         def setup(c, _):
             sl = ds(c * BLK, BLK)
-            third = lax.broadcasted_iota(jnp.int32, (BLK, HEAD), 1) // 3
+            third = across((BLK, HEAD)) // 3
             for n, (src, dst) in enumerate(((k_ref, ka), (v_ref, va))):
                 dst[sl, :HEAD] = src[sl, :]
                 dst[sl, HEAD:] = jnp.where(third == n, -1.0, 0.0).astype(BF)
             return 0
 
         lax.fori_loop(0, seq // BLK, setup, 0)
-
-    srow = lax.broadcasted_iota(jnp.int32, (16, HB), 0)
-    blank = jnp.zeros((HEAD - 16, HB), BF)
-
-    def augment(rows, *vals):
-        parts = jnp.zeros((16, HB), F32)
-        for n, part in enumerate(split3(vals[0]) + split3(vals[1])):
-            parts = jnp.where(srow == n, part, parts)
-        block = jnp.concatenate([parts.astype(BF), blank], axis=0).T
-        qa[rows, HEAD:] = block
-        da[rows, HEAD:] = block
-
-    def spots():
-        for b in range(2):
-            for h in range(GROUP):
-                start = (b * GROUP + h) * HB
-                yield h, slice(b * HB, (b + 1) * HB), slice(h * HEAD, (h + 1) * HEAD), slice(start, start + HB)
-
-    for h, src, cols, rows in spots():
-        qh, doh = q_ref[src, cols], do_ref[src, cols]
-        qa[rows, :HEAD] = qh
-        da[rows, :HEAD] = doh
-        q3t[:, rows] = qh.T
-        dt = doh.T
-        do3t[:, rows] = dt
-        delta = jnp.sum(dt.astype(F32) * o_ref[src, cols].T.astype(F32), axis=0, keepdims=True)
-        augment(rows, lse_ref[0, h:h + 1, src] * (1.0 / SCALE2), delta)
-    dq3[...] = jnp.zeros_like(dq3)
-
-    def step(rows, start, width, masked):
-        sl = pl.ds(pl.multiple_of(start, BLK), width)
-        s = mm_nt(qa[rows, :], ka[sl, :])
-        dp = mm_nt(da[rows, :], va[sl, :])
-        p = jnp.exp2(s * SCALE2)
-        if masked:
-            off = width - HB
-            tail = p[:, off:]
-            keep = lax.broadcasted_iota(jnp.int32, tail.shape, 0) % HB >= lax.broadcasted_iota(jnp.int32, tail.shape, 1)
-            tail = jnp.where(keep, tail, 0.0)
-            p = jnp.concatenate([p[:, :off], tail], axis=1) if off else tail
-        dvt[:, sl] += mm(do3t[:, rows], p.astype(BF))
-        dsv = (p * dp).astype(BF)
-        dkt[:, sl] += mm(q3t[:, rows], dsv)
-        dq3[rows, :] += mm(dsv, ka[sl, :HEAD])
-
-    def body(t, _):
-        step(slice(0, 2 * m3), t * 2 * BLK, 2 * BLK, False)
-        return 0
-
-    lax.fori_loop(0, i // 2, body, 0)
-
-    def tail_steps(start, width):
-        step(slice(0, m3), start, width - HB, True)
-        step(slice(m3, 2 * m3), start, width, True)
+        prepare(q_ref, do_ref, o_ref, lse_ref, sets[0])
+
+    def run(mine, other, tail_width):
+        qa, da, q3t, do3t, dq3 = mine
+
+        def step(rows, start, width, masked):
+            sl = pl.ds(pl.multiple_of(start, BLK), width)
+            s = mm_nt(qa[rows, :], ka[sl, :])
+            dp = mm_nt(da[rows, :], va[sl, :])
+            p = jnp.exp2(s * SCALE2)
+            if masked:
+                off = width - HB
+                tail = p[:, off:]
+                keep = down(tail.shape) % HB >= across(tail.shape)
+                tail = jnp.where(keep, tail, 0.0)
+                p = jnp.concatenate([p[:, :off], tail], axis=1) if off else tail
+            dvt[:, sl] += mm(do3t[:, rows], p.astype(BF))
+            dsv = (p * dp).astype(BF)
+            dkt[:, sl] += mm(q3t[:, rows], dsv)
+            dq3[rows, :] += mm(dsv, ka[sl, :HEAD])
+
+        def body(t, _):
+            step(slice(0, 2 * m3), t * 2 * BLK, 2 * BLK, False)
+            return 0
+
+        lax.fori_loop(0, i // 2, body, 0)
+        start = (i // 2) * 2 * BLK
+        step(slice(0, m3), start, tail_width - HB, True)
+        prepare(qn_ref, don_ref, on_ref, lsen_ref, other)
+        step(slice(m3, 2 * m3), start, tail_width, True)
+        for h, src, cols, rows in spots():
+            rsl = ds(i * BLK + src.start, HB)
+            out_ref[rsl, cols] = rotate(dq3[rows, :] * SCALE, cos_ref[rsl, :], -sin_ref[rsl, :]).astype(BF)
+
+    @pl.when(i % 2 == 0)
+    def _():
+        run(*sets, BLK)
 
     @pl.when(i % 2 == 1)
     def _():
-        tail_steps((i - 1) * BLK, 2 * BLK)
-
-    @pl.when(i % 2 == 0)
-    def _():
-        tail_steps(i * BLK, BLK)
-
-    for h, src, cols, rows in spots():
-        rsl = ds(i * BLK + src.start, HB)
-        out_ref[rsl, cols] = rotate(dq3[rows, :] * SCALE, cos_ref[rsl, :], -sin_ref[rsl, :]).astype(BF)
+        run(*sets[::-1], 2 * BLK)
 
     @pl.when(i == last)
     def _():
@@ -472,66 +491,74 @@
 def attn_bwd(idx, q, do, o, k, v, lse, tabs, rows):
     seq = k.shape[0]
     nq = seq // BLK
-    qspec = pl.BlockSpec((BLK, GW), lambda i, s: (i, s[1]))
+    m3 = GROUP * BLK
     kspec = pl.BlockSpec((seq, HEAD), lambda i, s: (0, s[1]))
-    m3 = GROUP * BLK
+    row_specs = []
+    for ahead in range(2):
+        row_specs += [pl.BlockSpec((BLK, GW), lambda i, s, a=ahead: (jnp.minimum(i + a, nq - 1), s[1]))] * 3
+        row_specs += [pl.BlockSpec((1, 8, BLK), lambda i, s, a=ahead: (s[1], 0, jnp.minimum(i + a, nq - 1)))]
+    one_set = [pltpu.VMEM((m3, PAIR), BF)] * 2 + [pltpu.VMEM((HEAD, m3), BF)] * 2 + [pltpu.VMEM((m3, HEAD), F32)]
     return call(bwd_body, (nq,),
-                [qspec] * 3 + [kspec] * 2 + [pl.BlockSpec((1, 8, BLK), lambda i, s: (s[1], 0, i))]
-                + [pl.BlockSpec((seq, HEAD), first_row)] * 2,
+                row_specs + [kspec] * 2 + [pl.BlockSpec((seq, HEAD), first_row)] * 2,
                 [pl.BlockSpec((r, PW), first_row) for r in (seq, rows)], [sds(r, PW) for r in (seq, rows)],
-                [idx, q, do, o, k, v, lse, *tabs], GROUP * nq * (nq + 1) * BLK * BLK * PW,
-                scratch=[pltpu.VMEM((m3, PAIR), BF)] * 2 + [pltpu.VMEM((seq, PAIR), BF)] * 2
-                + [pltpu.VMEM((HEAD, m3), BF)] * 2 + [pltpu.VMEM((m3, HEAD), F32)] + [pltpu.VMEM((HEAD, seq), F32)] * 2)
+                [idx] + [q, do, o, lse] * 2 + [k, v, *tabs], GROUP * nq * (nq + 1) * BLK * BLK * PW,
+                scratch=[pltpu.VMEM((seq, PAIR), BF)] * 2 + [pltpu.VMEM((HEAD, seq), F32)] * 2 + one_set * 2)
 
 
 def out_body(s_ref, x_ref, *rest):
-    ops, weights, out_ref = rest[:4], rest[4:8], rest[8]
-    lhs = jnp.concatenate([r[...] for r in ops], axis=1)
+    ops, weights, out_ref = rest[:5], rest[5:9], rest[9]
+    o0, o1, oc, orv, o3 = [r[...] for r in ops]
+    lhs = jnp.concatenate([o0, o1, jnp.where(s_ref[4] == 0, oc, orv), o3], axis=1)
     rhs = jnp.concatenate([r[...] for r in weights], axis=0)
     out_ref[...] = (x_ref[...].astype(F32) + mm(lhs, rhs)).astype(BF)
 
 
 def out_proj(idx, x, pieces, w_o):
+    def first_map(n, s):
+        return (s[0] % 2, 0)
+
     rows, d = x.shape
     hw = pieces[0].shape[1]
     return call(out_body, (d // BLK,),
                 [pl.BlockSpec((rows, BLK), col_map)]
-                + [pl.BlockSpec((rows, hw), m) for m in (own_map, first_row, own_map, first_row)]
+                + [pl.BlockSpec((rows, hw), m) for m in (own_map, first_row, first_map, first_map, first_row)]
                 + [pl.BlockSpec((hw, BLK), lambda n, s, p=p: (s[p], n)) for p in range(4)],
                 pl.BlockSpec((rows, BLK), col_map), sds(rows, d), [idx, x, *pieces] + [w_o] * 4,
                 2 * rows * d * d)
 
 
-def dwo_body(s_ref, oa_ref, ob_ref, dy_ref, fin, snd, ot):
-    hw = oa_ref.shape[1]
+def dwo_body(s_ref, oa_ref, ob_ref, oc_ref, dy_ref, fin, snd, ot):
+    half, hw = ob_ref.shape
 
     @pl.when(jnp.logical_and(pl.program_id(0) == 0, pl.program_id(1) == 0))
     def _():
         def tr(c, _):
-            sl = ds(c * BLK, BLK)
+            sl, up = ds(c * BLK, BLK), ds(c * BLK + half, BLK)
             ot[:hw, sl] = oa_ref[sl, :].T
+            ot[:hw, up] = oa_ref[up, :].T
             ot[hw:, sl] = ob_ref[sl, :].T
+            ot[hw:, up] = oc_ref[sl, :].T
             return 0
 
-        lax.fori_loop(0, oa_ref.shape[0] // BLK, tr, 0)
+        lax.fori_loop(0, half // BLK, tr, 0)
 
     val = mm(ot[ds(pl.program_id(1) * hw, hw), :], dy_ref[...])
     fin[...] = val
     snd[...] = val
 
 
-def dw_o(idx, oa, ob, dy):
+def dw_o(idx, oa, ob, oc, dy):
     seq, d = dy.shape
     hw = oa.shape[1]
-    once = pl.BlockSpec((seq, hw), lambda i, p, s: (0, 0), pipeline_mode=pl.Buffered(1))
+    o_specs = [pl.BlockSpec(o.shape, lambda i, p, s: (0, 0), pipeline_mode=pl.Buffered(1)) for o in (oa, ob, oc)]
     return call(dwo_body, (d // BLK, 2),
-                [once, once, pl.BlockSpec((seq, BLK), lambda i, p, s: (0, i))],
+                o_specs + [pl.BlockSpec((seq, BLK), lambda i, p, s: (0, i))],
                 [pl.BlockSpec((hw, BLK), lambda i, p, s: (s[p], i)), pl.BlockSpec((hw, BLK), lambda i, p, s: (p, i))],
-                [sds(4 * hw, d, F32), sds(2 * hw, d, F32)], [idx, oa, ob, dy], 4 * seq * d * hw,
+                [sds(4 * hw, d, F32), sds(2 * hw, d, F32)], [idx, oa, ob, oc, dy], 4 * seq * d * hw,
                 scratch=[pltpu.VMEM((2 * hw, seq), BF)])
 
 
-def dwown_body(s_ref, h_ref, ga_ref, gb_ref, gc_ref, wo_ref, _, fq, fk, fv, snd, wo_fin, ht, sem, wsem):
+def dwown_body(s_ref, h_ref, ga_ref, gb_ref, gc_ref, wo_ref, _, fq, fk, fv, snd, wo_fin, g3, ht, sem, wsem):
     i, steps = pl.program_id(0), pl.num_programs(0)
     rows, per = wo_ref.shape[0], steps // 2
     start = jnp.where(i < per, s_ref[1] * per + i, s_ref[3] * per + i - per)
@@ -555,6 +582,7 @@
 
     @pl.when(i == steps - 1)
     def _():
+        g3[...] = gc_ref[ds(s_ref[1] * g3.shape[0], g3.shape[0]), :]
         for slot in range(2):
             for copy in scatter(snd, (fq, fk, fv), s_ref[0], s_ref[2], sem.at[slot]):
                 copy.wait()
@@ -581,8 +609,8 @@
     return call(dwown_body, (steps,),
                 [pl.BlockSpec((seq, HB), col_map)] + [gspec] * 3
                 + [pl.BlockSpec((wo_rcv.shape[0] // steps, d), row_map), ANY],
-                [ANY] * 3 + [pl.BlockSpec((HB, sw), row_map), ANY],
-                [sds(d, 4 * w, F32) for w in widths] + [sds(d, sw, F32), sds(*wo_fin.shape, F32)],
+                [ANY] * 3 + [pl.BlockSpec((HB, sw), row_map), ANY, pl.BlockSpec((seq // 4, PW), first_row)],
+                [sds(d, 4 * w, F32) for w in widths] + [sds(d, sw, F32), sds(*wo_fin.shape, F32), sds(seq // 4, PW)],
                 [idx, h, ga, gb, gc, wo_rcv, wo_fin], 2 * seq * d * sw,
                 scratch=[pltpu.VMEM((HB, seq), BF), pltpu.SemaphoreType.DMA((2, 5)), pltpu.SemaphoreType.DMA],
                 aliases={6: 4})
@@ -596,14 +624,14 @@
     fq[...] = val[:, :GW]
     fk[...] = val[:, GW:]
     snd[:, :QK] = val
-    val = mm(lhs, jnp.concatenate([ga_ref[:, QK:], gb_ref[:, QK:]], axis=1))
+    val = mm(lhs, jnp.concatenate([ga_ref[...], gb_ref[:, QK:]], axis=1))
     fv[...] = val
     snd[:, QK:] = val
 
 
-def group_specs():
-    return [pl.BlockSpec((HB, w), lambda i, s: (i, 2 * s[0] + 1)) for w in (GW, HEAD)] + \
-        [pl.BlockSpec((HB, PAIR), lambda i, s: (i, s[0]))]
+def group_specs(bm):
+    return [pl.BlockSpec((bm, w), lambda i, s: (i, 2 * s[0] + 1)) for w in (GW, HEAD)] + \
+        [pl.BlockSpec((bm, PAIR), lambda i, s: (i, s[0]))]
 
 
 def dw_group(idx, h, ga, gb, bufs):
@@ -611,8 +639,9 @@
     gspec = pl.BlockSpec((seq, PW), first_row, pipeline_mode=pl.Buffered(1))
     sw = QK + PAIR
     return call(dwgrp_body, (d // HB,),
-                [pl.BlockSpec((seq, HB), col_map), gspec, gspec] + [ANY] * 3,
-                group_specs() + [pl.BlockSpec((HB, sw), row_map)], [sds(*b.shape, F32) for b in bufs] + [sds(d, sw, F32)],
+                [pl.BlockSpec((seq, HB), col_map),
+                 pl.BlockSpec((seq, HEAD), lambda i, s: (0, QK // HEAD), pipeline_mode=pl.Buffered(1)), gspec] + [ANY] * 3,
+                group_specs(HB) + [pl.BlockSpec((HB, sw), row_map)], [sds(*b.shape, F32) for b in bufs] + [sds(d, sw, F32)],
                 [idx, h, ga, gb, *bufs], 2 * seq * d * sw, scratch=[pltpu.VMEM((HB, seq), BF)],
                 aliases={4 + n: n for n in range(3)})
 
@@ -626,7 +655,8 @@
 
 def place(idx, rcv, bufs):
     d, w = rcv.shape
-    return call(place_body, (d // HB,), [pl.BlockSpec((HB, w), row_map)] + [ANY] * 3, group_specs(),
+    bm = 2 * BLK
+    return call(place_body, (d // bm,), [pl.BlockSpec((bm, w), row_map)] + [ANY] * 3, group_specs(bm),
                 [sds(*b.shape, F32) for b in bufs], [idx, rcv, *bufs], d * w, aliases={2 + n: n for n in range(3)})
 
 
@@ -650,7 +680,7 @@
     dh = mm_nt(lhs, rhs)
     inv = inv_ref[...]
     for c in range(bn // HEAD):
-        cols = slice(c * HEAD, c * HEAD + HEAD)
+        cols = head_cols(c)
         xb = x_ref[:, cols]
         xs[:, ds(n * bn + cols.start, HEAD)] = xb
         part, xf = dh[:, cols], xb.astype(F32)
@@ -675,7 +705,7 @@
             sl = ds(r * step, step)
             coef = tot[sl, :]
             for c in range(d // HEAD):
-                cols = slice(c * HEAD, c * HEAD + HEAD)
+                cols = head_cols(c)
                 dx_ref[sl, cols] = (acc[sl, cols] - xs[sl, cols].astype(F32) * coef).astype(BF)
             return 0
 
@@ -725,7 +755,6 @@
         j = lax.axis_index('sp').astype(jnp.int32)
         rows, d = x.shape
         seq = rows * sp
-        half = rows // 2
         j1, j2, j3 = [j ^ n for n in (1, 2, 3)]
         dev = (j, j1, j2, j3)
         bpr, hpr = rows // BLK, rows // HB
@@ -738,6 +767,7 @@
 
         cut = rows - HB
         xa = x[:cut]
+        positions = after(positions, xa)
         pos2 = over(positions)
         pos1 = near(positions)
         x2a = over(xa)
@@ -754,7 +784,7 @@
         cos_h, sin_h = jnp.cos(angles), jnp.sin(angles)
         tabs = (jnp.concatenate([cos_h, cos_h], axis=1), jnp.concatenate([-sin_h, sin_h], axis=1))
 
-        dya, dyb = dy[:half], dy[half:]
+        dya, dyb = dy[:cut], dy[cut:]
         bufs = project(vec(j * bpr, j1 * bpr, j, dep=(dya, dyb)), x, x1, gain_f, ws, tabs, None, seq)
         dbufs = dout(vec(j * bpr, j1 * bpr, j, dep=(bufs[1],)), dy, dy1, w_o, None, seq)
 
@@ -781,15 +811,15 @@
         o, lse, o_hi, o_pair = attn_fwd("rest", rest_tasks, q, k, v, rows, local)
         orv = over(o_hi)
         o1 = near(o_pair)
-        dy2a = after(dy2a, o)
+        qc, kc, vc = project_first(vec(j2, dep=(o,)), h_all, ws, tabs, seq // 2)
+        dy2a = after(dy2a, qc)
         dy3a = near(dy2a)
-        qc, kc, vc = project_first(vec(j2, dep=(o,)), h_all, ws, tabs, seq // 2)
         oc = attn_fwd("first", table((j1, 0), tri), qc, kc, vc)[0]
 
         dy2b = after(dy2b, oc)
         dy3b = near(dy2b)
-        dbufs = dout(vec(j2 * bpr, j3 * bpr, j, dep=(oc,)), dy2a, dy3a, w_o, dbufs, seq)
-        dbufs = dout(vec(j2 * bpr + 1, j3 * bpr + 1, j), dy2b, dy3b, w_o, dbufs, seq)
+        dbufs = dout(vec(j2 * hpr, j3 * hpr, j, dep=(oc,)), dy2a, dy3a, w_o, dbufs, seq)
+        dbufs = dout(vec((j2 + 1) * hpr - 1, (j3 + 1) * hpr - 1, j), dy2b, dy3b, w_o, dbufs, seq)
         dy_all, do = dbufs
 
         ga, ga_pair = attn_bwd(vec(j1, 0), q, do, o, k, v, lse, tabs, rows)
@@ -799,15 +829,15 @@
         gb2 = over(gb)
         gb1 = near(gb_pair)
 
-        ox = lax.dynamic_update_slice(oc, after(orv, gb), (seq // 2, 0))
-        o3 = near(rows_of(ox, j1))
-        wo_fin, wo_snd = dw_o(vec(j, j2, dep=(gb,)), o, ox, dy_all)
+        orv = after(orv, gb)
+        o3 = near(jnp.where(chip == 0, rows_of(oc, j1 % 2), rows_of(orv, j1 % 2)))
+        wo_fin, wo_snd = dw_o(vec(j, j2, dep=(gb,)), o, oc, orv, dy_all)
         wo_rcv = near(wo_snd)
-        result = out_proj(vec(*dev, dep=(wo_snd,)), x, (o, o1, ox, o3), w_o)
+        result = out_proj(vec(*dev, chip, dep=(wo_snd,)), x, (o, o1, oc, orv, o3), w_o)
         ga2 = after(ga2, wo_snd)
-        ga3 = near(rows_of(ga2, j1))
-        fq, fk, fv, snd, wo_fin = dw_own(vec(*dev, dep=(result,)), h_all, ga, gb, ga2, wo_rcv, wo_fin)
+        fq, fk, fv, snd, wo_fin, g3 = dw_own(vec(*dev, dep=(result,)), h_all, ga, gb, ga2, wo_rcv, wo_fin)
         rcv = near(snd)
+        ga3 = near(g3)
 
         gb2 = after(gb2, snd)
         gb3 = near(rows_of(gb2, j1))

time: 971 us -> 955 us (0.984)
  Pallas kernels: 650 us -> 639 us
    pallas_call x18, Pallas kernels: 650 us -> 639 us  [call(): pl.pallas_call(body, grid_spec=pltpu.PrefetchScalarGridSpec(num_scalar_pr...]
  transfers between devices with their start and end apart: 27 -> 27, of which waited for: 15 -> 17; matrix products, arithmetic and copies ran while one was open for 4% -> 4% of each run, Pallas kernels for 56% -> 56%
where the time goes in v5:
time: 955 us; the launch traced here: 945 us
  Pallas kernels  639 us (67%)
  waiting for transfers between devices  254 us (27%)
  other arithmetic  20.1 us (2%)
  local copies, waits for them, and re-layouts  18.1 us (2%)
  starting transfers between devices  12.7 us (1%)
    pallas_call x18, Pallas kernels, call(): pl.pallas_call(body, grid_spec=pltpu.PrefetchScalarGridSpec(num_scalar_pr...  639 us
    ppermute x9, waiting for transfers between devices, over(): return lax.ppermute(val, 'sp', cross)  188 us
    ppermute x18, waiting for transfers between devices, near(): return lax.ppermute(val, 'sp', pair)  66 us
  transfers between devices with their start and end apart: 27, of which 17 were waited for; matrix products, arithmetic and copies ran while one was open for 4% of the time, Pallas kernels for 56%

profile of v5, /device:TPU:0, one launch (start us, length us, event | category | flops | bytes accessed | tf_op | source)
XLA Modules:
  0.0 945.0 jit_solution(16633317060336553235)
XLA Ops:
  1.5 10.1 %collective-permute-done.2.xb_ref = bf16[1024,3072]{1,0:T(8,128)(2,1)} collective-permute-done((bf16[1024,3072]{1,0:T(8,128)(2,1)}, bf16[1024,3072]{1,0:T(8,128)(2,1)}, u32[]{:S(2)}, u32[]{:S(2)}) %collective-permute-start.2) | collective-permute-done | bytes 6291488 | tf_op jit(solution)/shard_map/ppermute | solution.py:745
  41.5 34.5 %shard_map.171 = (bf16[4096,3072]{1,0:T(8,128)(2,1)}, bf16[4096,768]{1,0:T(8,128)(2,1)}, bf16[4096,256]{1,0:T(8,128)(2,1)}, bf16[4096,256]{1,0:T(8,128)(2,1)}, f32[4096,128]{1,0:T(8,128)}) custom-call(s32[3]{0:T(128)} %add_add_fusion.2.s_ref, bf16[1024,3072]{1,0:T(8,128)(2,1)} %x_ref.3, bf16[1024,3072]{1,0:T(8,128)(2,1)} %collective-permute-done.2.xb_ref, ...), custom_call_target="tpu_custom_call" | custom-call | flops 16106127360 | bytes 31457280 | tf_op jit(solution)/shard_map/pallas_call | solution.py:51
  76.0 17.7 %shard_map.172 = (bf16[4096,3072]{1,0:T(8,128)(2,1)}, bf16[4096,768]{1,0:T(8,128)(2,1)}) custom-call(s32[3]{0:T(128)} %add_add_fusion.2.s_ref, bf16[1024,3072]{1,0:T(8,128)(2,1)} %dy_ref.1, bf16[1024,3072]{1,0:T(8,128)(2,1)} %collective-permute-done.6.db_ref, bf16[3072,3072]{1,0:T(8,128)(2,1)} %rest_8_.2), custom_call_target="tpu_custom_call" | custom-call | flops 9663676416 | bytes 18874368 | tf_op jit(solution)/shard_map/pallas_call | solution.py:51
  93.7 28.0 %shard_map.173 = (bf16[2048,768]{1,0:T(8,128)(2,1)}, f32[2,8,2048]{2,1,0:T(8,128)}, f32[2,3,128,2048]{3,2,1,0:T(8,128)}) custom-call(s32[19]{0:T(128)} %get-tuple-element.104.refs_0_, bf16[4096,768]{1,0:T(8,128)(2,1)} %get-tuple-element.100.refs_1_.rest_1_, bf16[4096,256]{1,0:T(8,128)(2,1)} %get-tuple-element.105.refs_2_.rest_2_, ...), custom_call_target="tpu_custom_call" | custom-call | flops 6442450944 | bytes 12582912 | tf_op jit(solution)/shard_map/pallas_call | solution.py:51
  132.3 27.4 %shard_map.174 = (bf16[4096,3072]{1,0:T(8,128)(2,1)}, bf16[4096,768]{1,0:T(8,128)(2,1)}, bf16[4096,256]{1,0:T(8,128)(2,1)}, bf16[4096,256]{1,0:T(8,128)(2,1)}, f32[4096,128]{1,0:T(8,128)}) custom-call(s32[3]{0:T(128)} %add_add_fusion.1.s_ref, ...), custom_call_target="tpu_custom_call", output_to_operand_aliasing={{0}: (9, {}), {1}: (10, {}), {2}: (11, {}), {3}: (12, {}), ... | custom-call | flops 12079595520 | bytes 23592960 | tf_op jit(solution)/shard_map/pallas_call | solution.py:51
  167.2 13.1 %shard_map.175 = (bf16[4096,3072]{1,0:T(8,128)(2,1)}, bf16[4096,768]{1,0:T(8,128)(2,1)}, bf16[4096,256]{1,0:T(8,128)(2,1)}, bf16[4096,256]{1,0:T(8,128)(2,1)}, f32[4096,128]{1,0:T(8,128)}) custom-call(s32[3]{0:T(128)} %add_add_fusion.s_ref, ...), custom_call_target="tpu_custom_call", output_to_operand_aliasing={{0}: (9, {}), {1}: (10, {}), {2}: (11, {}), {3}: (12, {}), ... | custom-call | flops 4026531840 | bytes 7864320 | tf_op jit(solution)/shard_map/pallas_call | solution.py:51
  180.4 61.0 %shard_map.176 = (bf16[4096,768]{1,0:T(8,128)(2,1)}, f32[2,8,4096]{2,1,0:T(8,128)}, bf16[2048,768]{1,0:T(8,128)(2,1)}, bf16[1024,768]{1,0:T(8,128)(2,1)}) custom-call(s32[35]{0:T(128)} %broadcast_select_fusion.refs_0_, bf16[4096,768]{1,0:T(8,128)(2,1)} %get-tuple-element.117.refs_1_.q_ref.qn_ref, bf16[4096,256]{1,0:T(8,128)(2,1)} %get-tuple-element.119.refs_2_.k_ref, ...), custom_call_target="tpu_custom_call" | custom-call | flops 25769803776 | bytes 50331648 | tf_op jit(solution)/shard_map/pallas_call | solution.py:51
  241.4 22.7 %shard_map.177 = (bf16[2048,768]{1,0:T(8,128)(2,1)}, bf16[2048,256]{1,0:T(8,128)(2,1)}, bf16[2048,256]{1,0:T(8,128)(2,1)}) custom-call(s32[1]{0:T(128)} %bitcast.2.s_ref, bf16[4096,3072]{1,0:T(8,128)(2,1)} %get-tuple-element.125.h_ref, bf16[3072,3072]{1,0:T(8,128)(2,1)} %rest_17_.1, bf16[3072,1024]{1,0:T(8,128)(2,1)} %rest_18_.1, ...), custom_call_target="tpu_custom_call" | custom-call | flops 16106127360 | bytes 31457280 | tf_op jit(solution)/shard_map/pallas_call | solution.py:51
  267.3 26.4 %shard_map.178 = (bf16[2048,768]{1,0:T(8,128)(2,1)}, f32[2,8,2048]{2,1,0:T(8,128)}) custom-call(s32[19]{0:T(128)} %get-tuple-element.178.refs_0_, bf16[2048,768]{1,0:T(8,128)(2,1)} %get-tuple-element.126.refs_1_, bf16[2048,256]{1,0:T(8,128)(2,1)} %get-tuple-element.127.refs_2_, bf16[2048,256]{1,0:T(8,128)(2,1)} %get-tuple-element.128.refs_3_), custom_call_target="tpu_custom_call" | custom-call | flops 6442450944 | bytes 12582912 | tf_op jit(solution)/shard_map/pallas_call | solution.py:51
  293.7 10.3 %collective-permute-done.9.da_ref = bf16[256,3072]{1,0:T(8,128)(2,1)S(1)} collective-permute-done((bf16[256,3072]{1,0:T(8,128)(2,1)}, bf16[256,3072]{1,0:T(8,128)(2,1)S(1)}, u32[]{:S(2)}, u32[]{:S(2)}) %collective-permute-start.9) | collective-permute-done | bytes 1572896 | tf_op jit(solution)/shard_map/ppermute | solution.py:742
  305.6 15.2 %shard_map.179 = (bf16[4096,3072]{1,0:T(8,128)(2,1)}, bf16[4096,768]{1,0:T(8,128)(2,1)}) custom-call(s32[3]{0:T(128)} %add_add_fusion.1.s_ref, bf16[768,3072]{1,0:T(8,128)(2,1)} %collective-permute-done.11.da_ref, bf16[768,3072]{1,0:T(8,128)(2,1)} %collective-permute-done.12.db_ref, ...), custom_call_target="tpu_custom_call", output_to_operand_aliasing={{0}: (4, {}), {1}: (5, {})} | custom-call | flops 7247757312 | bytes 14155776 | tf_op jit(solution)/shard_map/pallas_call | solution.py:51
  320.8 7.8 shard_map.180
  328.6 76.8 %shard_map.181 = (bf16[4096,640]{1,0:T(8,128)(2,1)}, bf16[1024,640]{1,0:T(8,128)(2,1)}) custom-call(s32[2]{0:T(128)} %pad_add_fusion.8.s_ref, bf16[4096,768]{1,0:T(8,128)(2,1)} %get-tuple-element.117.refs_1_.q_ref.qn_ref, bf16[4096,768]{1,0:T(8,128)(2,1)} %get-tuple-element.137.do_ref.don_ref, ...), custom_call_target="tpu_custom_call" | custom-call | flops 36238786560 | bytes 70778880 | tf_op jit(solution)/shard_map/pallas_call | solution.py:51
  405.5 77.1 %shard_map.182 = (bf16[4096,640]{1,0:T(8,128)(2,1)}, bf16[1024,640]{1,0:T(8,128)(2,1)}) custom-call(s32[2]{0:T(128)} %get-tuple-element.140.s_ref, bf16[4096,768]{1,0:T(8,128)(2,1)} %get-tuple-element.117.refs_1_.q_ref.qn_ref, bf16[4096,768]{1,0:T(8,128)(2,1)} %get-tuple-element.137.do_ref.don_ref, ...), custom_call_target="tpu_custom_call" | custom-call | flops 36238786560 | bytes 70778880 | tf_op jit(solution)/shard_map/pallas_call | solution.py:51
  482.6 53.8 %shard_map.183 = (f32[3072,3072]{1,0:T(8,128)}, f32[1536,3072]{1,0:T(8,128)}) custom-call(s32[2]{0:T(128)} %get-tuple-element.142.s_ref, bf16[4096,768]{1,0:T(8,128)(2,1)} %get-tuple-element.123.o_ref.on_ref.oa_ref.rest_0_, bf16[2048,768]{1,0:T(8,128)(2,1)} %get-tuple-element.129.ob_ref.rest_2_, bf16[2048,768]{1,0:T(8,128)(2,1)} %collective-permute-done.13.oc_ref.rest_3_, ...), custom_call_target="tpu_custom_call" | custom-call | flops 38654705664 | bytes 75497472 | tf_op jit(solution)/shard_map/pallas_call | solution.py:51
  542.2 24.8 %collective-permute-done.14.rest_1_ = bf16[1024,768]{1,0:T(8,128)(2,1)S(1)} collective-permute-done((bf16[1024,768]{1,0:T(8,128)(2,1)}, bf16[1024,768]{1,0:T(8,128)(2,1)S(1)}, u32[]{:S(2)}, u32[]{:S(2)}) %collective-permute-start.14) | collective-permute-done | bytes 1572896 | tf_op jit(solution)/shard_map/ppermute | solution.py:745
  569.4 27.6 %shard_map.184 = bf16[1024,3072]{1,0:T(8,128)(2,1)} custom-call(s32[5]{0:T(128)} %stack.43.s_ref, bf16[1024,3072]{1,0:T(8,128)(2,1)} %x_ref.3, bf16[4096,768]{1,0:T(8,128)(2,1)} %get-tuple-element.123.o_ref.on_ref.oa_ref.rest_0_, bf16[1024,768]{1,0:T(8,128)(2,1)} %copy-done.2, bf16[2048,768]{1,0:T(8,128)(2,1)} %get-tuple-element.129.ob_ref.rest_2_, ...), custom_call_target="tpu_custom_call" | custom-call | flops 19327352832 | bytes 37748736 | tf_op jit(solution)/shard_map/pallas_call | solution.py:51
  597.0 55.1 %collective-permute-done.16.gc_ref.ga_ref.rest_4_ = bf16[4096,640]{1,0:T(8,128)(2,1)} collective-permute-done((bf16[4096,640]{1,0:T(8,128)(2,1)}, bf16[4096,640]{1,0:T(8,128)(2,1)}, u32[]{:S(2)}, u32[]{:S(2)}) %collective-permute-start.16) | collective-permute-done | bytes 5242912 | tf_op jit(solution)/shard_map/ppermute | solution.py:742
  652.1 58.8 %shard_map.185 = (f32[3072,3072]{1,0:T(8,128)}, f32[3072,1024]{1,0:T(8,128)}, f32[3072,1024]{1,0:T(8,128)}, f32[3072,1792]{1,0:T(8,128)}, f32[3072,3072]{1,0:T(8,128)}, /*index=5*/bf16[1024,640]{1,0:T(8,128)(2,1)}) custom-call(s32[4]{0:T(128)} %pad_add_fusion.9.s_ref, bf16[4096,3072]{1,0:T(8,128)(2,1)} %get-tuple-element.125.h_ref, ...), custom_call_target="tpu_custom_call", output_to_operand_aliasing={{4}: (6, {})} | custom-call | flops 45097156608 | bytes 88080384 | tf_op jit(solution)/shard_map/pallas_call | solution.py:51
  712.8 114.0 %collective-permute-done.17.gb_ref.rest_5_ = bf16[4096,640]{1,0:T(8,128)(2,1)} collective-permute-done((bf16[4096,640]{1,0:T(8,128)(2,1)}, bf16[4096,640]{1,0:T(8,128)(2,1)}, u32[]{:S(2)}, u32[]{:S(2)}) %collective-permute-start.17) | collective-permute-done | bytes 5242912 | tf_op jit(solution)/shard_map/ppermute | solution.py:742
  826.8 28.5 %shard_map.186 = (f32[3072,3072]{1,0:T(8,128)}, f32[3072,1024]{1,0:T(8,128)}, f32[3072,1024]{1,0:T(8,128)}, f32[3072,768]{1,0:T(8,128)}) custom-call(s32[1]{0:T(128)} %bitcast.2.s_ref, bf16[4096,3072]{1,0:T(8,128)(2,1)} %get-tuple-element.125.h_ref, ...), custom_call_target="tpu_custom_call", output_to_operand_aliasing={{0}: (4, {}), {1}: (5, {}), {2}: (6, {})} | custom-call | flops 19327352832 | bytes 37748736 | tf_op jit(solution)/shard_map/pallas_call | solution.py:51
  857.7 14.3 %collective-permute-done.20.rest_3_ = bf16[1024,640]{1,0:T(8,128)(2,1)S(1)} collective-permute-done((bf16[1024,640]{1,0:T(8,128)(2,1)}, bf16[1024,640]{1,0:T(8,128)(2,1)S(1)}, u32[]{:S(2)}, u32[]{:S(2)}) %collective-permute-start.20) | collective-permute-done | bytes 1310752 | tf_op jit(solution)/shard_map/ppermute | solution.py:745
  877.7 54.1 %shard_map.187 = (bf16[1024,3072]{1,0:T(8,128)(2,1)}, f32[8,3072]{1,0:T(8,128)}, f32[3072,3072]{1,0:T(8,128)}, f32[3072,1024]{1,0:T(8,128)}, f32[3072,1024]{1,0:T(8,128)}) custom-call(s32[4]{0:T(128)} %pad_add_fusion.9.s_ref, bf16[1024,3072]{1,0:T(8,128)(2,1)} %x_ref.3, ...), custom_call_target="tpu_custom_call", output_to_operand_aliasing={{2}: (26, {}), {3}: (27, {}), {4}: (28, {})} | custom-call | flops 32212254720 | bytes 62914560 | tf_op jit(solution)/shard_map/pallas_call | solution.py:51
  935.7 8.3 shard_map.188
  (96 shorter events, 76.2 us)
Async XLA Ops:
  0.7 11.0 %collective-permute-start.2 = (bf16[1024,3072]{1,0:T(8,128)(2,1)}, bf16[1024,3072]{1,0:T(8,128)(2,1)}, u32[]{:S(2)}, u32[]{:S(2)}) collective-permute-start(bf16[1024,3072]{1,0:T(8,128)(2,1)} %x_ref.3), channel_id=1, source_target_pairs={{0,1},{1,0},{2,3},{3,2},{4,5},{5,4},{6,7},{7,6}} | collective-permute-start | bytes 18874376 | tf_op jit(solution)/shard_map/ppermute | solution.py:745
  11.6 64.3 %collective-permute-start.6 = (bf16[1024,3072]{1,0:T(8,128)(2,1)}, bf16[1024,3072]{1,0:T(8,128)(2,1)}, u32[]{:S(2)}, u32[]{:S(2)}) collective-permute-start(bf16[1024,3072]{1,0:T(8,128)(2,1)} %dy_ref.1), channel_id=1, source_target_pairs={{0,1},{1,0},{2,3},{3,2},{4,5},{5,4},{6,7},{7,6}} | collective-permute-start | bytes 18874376 | tf_op jit(solution)/shard_map/ppermute | solution.py:745
  19.5 10.5 %collective-permute-start.3 = (s32[1024]{0:T(1024)S(1)}, s32[1024]{0:T(1024)S(1)}, u32[]{:S(2)}, u32[]{:S(2)}) collective-permute-start(s32[1024]{0:T(1024)S(1)} %copy-done.5), channel_id=1, source_target_pairs={{0,1},{1,0},{2,3},{3,2},{4,5},{5,4},{6,7},{7,6}} | collective-permute-start | bytes 12296 | tf_op jit(solution)/shard_map/ppermute | solution.py:745
  19.6 104.4 %collective-permute-start.1 = (bf16[768,3072]{1,0:T(8,128)(2,1)}, bf16[768,3072]{1,0:T(8,128)(2,1)}, u32[]{:S(2)}, u32[]{:S(2)}) collective-permute-start(bf16[768,3072]{1,0:T(8,128)(2,1)} %slice.22), channel_id=1, source_target_pairs={{0,2},{1,3},{2,0},{3,1},{4,6},{5,7},{6,4},{7,5}} | collective-permute-start | bytes 14155784 | tf_op jit(solution)/shard_map/ppermute | solution.py:742
  21.1 9.5 %collective-permute-start.5 = (s32[1024]{0:T(1024)S(1)}, s32[1024]{0:T(1024)S(1)}, u32[]{:S(2)}, u32[]{:S(2)}) collective-permute-start(s32[1024]{0:T(1024)S(1)} %collective-permute-done.4), channel_id=1, source_target_pairs={{0,1},{1,0},{2,3},{3,2},{4,5},{5,4},{6,7},{7,6}} | collective-permute-start | bytes 12296 | tf_op jit(solution)/shard_map/ppermute | solution.py:745
  124.0 8.3 collective-permute-start.7
  125.5 36.9 %collective-permute-start = (bf16[256,3072]{1,0:T(8,128)(2,1)S(1)}, bf16[256,3072]{1,0:T(8,128)(2,1)}, u32[]{:S(2)}, u32[]{:S(2)}) collective-permute-start(bf16[256,3072]{1,0:T(8,128)(2,1)S(1)} %slice.23), channel_id=1, source_target_pairs={{0,2},{1,3},{2,0},{3,1},{4,6},{5,7},{6,4},{7,5}} | collective-permute-start | bytes 4718600 | tf_op jit(solution)/shard_map/ppermute | solution.py:742
  162.5 104.5 %collective-permute-start.11 = (bf16[768,3072]{1,0:T(8,128)(2,1)}, bf16[768,3072]{1,0:T(8,128)(2,1)}, u32[]{:S(2)}, u32[]{:S(2)}) collective-permute-start(bf16[768,3072]{1,0:T(8,128)(2,1)} %slice.24), channel_id=1, source_target_pairs={{0,2},{1,3},{2,0},{3,1},{4,6},{5,7},{6,4},{7,5}} | collective-permute-start | bytes 14155784 | tf_op jit(solution)/shard_map/ppermute | solution.py:742
  267.0 38.6 %collective-permute-start.12 = (bf16[768,3072]{1,0:T(8,128)(2,1)}, bf16[768,3072]{1,0:T(8,128)(2,1)}, u32[]{:S(2)}, u32[]{:S(2)}) collective-permute-start(bf16[768,3072]{1,0:T(8,128)(2,1)} %collective-permute-done.11.da_ref), channel_id=1, source_target_pairs={{0,1},{1,0},{2,3},{3,2},{4,5},{5,4},{6,7},{7,6}} | collective-permute-start | bytes 14155784 | tf_op jit(solution)/shard_map/ppermute | solution.py:745
  267.0 37.0 %collective-permute-start.9 = (bf16[256,3072]{1,0:T(8,128)(2,1)}, bf16[256,3072]{1,0:T(8,128)(2,1)S(1)}, u32[]{:S(2)}, u32[]{:S(2)}) collective-permute-start(bf16[256,3072]{1,0:T(8,128)(2,1)} %slice.25), channel_id=1, source_target_pairs={{0,2},{1,3},{2,0},{3,1},{4,6},{5,7},{6,4},{7,5}} | collective-permute-start | bytes 4718600 | tf_op jit(solution)/shard_map/ppermute | solution.py:742
  304.0 16.8 %collective-permute-start.10 = (bf16[256,3072]{1,0:T(8,128)(2,1)S(1)}, bf16[256,3072]{1,0:T(8,128)(2,1)}, u32[]{:S(2)}, u32[]{:S(2)}) collective-permute-start(bf16[256,3072]{1,0:T(8,128)(2,1)S(1)} %collective-permute-done.9.da_ref), channel_id=1, source_target_pairs={{0,1},{1,0},{2,3},{3,2},{4,5},{5,4},{6,7},{7,6}} | collective-permute-start | bytes 4718600 | tf_op jit(solution)/shard_map/ppermute | solution.py:745
  305.3 177.2 %collective-permute-start.13 = (bf16[2048,768]{1,0:T(8,128)(2,1)}, bf16[2048,768]{1,0:T(8,128)(2,1)}, u32[]{:S(2)}, u32[]{:S(2)}) collective-permute-start(bf16[2048,768]{1,0:T(8,128)(2,1)} %get-tuple-element.143), channel_id=1, source_target_pairs={{0,2},{1,3},{2,0},{3,1},{4,6},{5,7},{6,4},{7,5}} | collective-permute-start | bytes 9437192 | tf_op jit(solution)/shard_map/ppermute | solution.py:742
  536.4 115.8 %collective-permute-start.18 = (f32[1536,3072]{1,0:T(8,128)}, f32[1536,3072]{1,0:T(8,128)}, u32[]{:S(2)}, u32[]{:S(2)}) collective-permute-start(f32[1536,3072]{1,0:T(8,128)} %get-tuple-element.146), channel_id=1, source_target_pairs={{0,1},{1,0},{2,3},{3,2},{4,5},{5,4},{6,7},{7,6}} | collective-permute-start | bytes 56623112 | tf_op jit(solution)/shard_map/ppermute | solution.py:745
  536.5 115.6 %collective-permute-start.16 = (bf16[4096,640]{1,0:T(8,128)(2,1)}, bf16[4096,640]{1,0:T(8,128)(2,1)}, u32[]{:S(2)}, u32[]{:S(2)}) collective-permute-start(bf16[4096,640]{1,0:T(8,128)(2,1)} %get-tuple-element.139.ga_ref.rest_0_), channel_id=1, source_target_pairs={{0,2},{1,3},{2,0},{3,1},{4,6},{5,7},{6,4},{7,5}} | collective-permute-start | bytes 15728648 | tf_op jit(solution)/shard_map/ppermute | solution.py:742
  538.2 28.7 %collective-permute-start.14 = (bf16[1024,768]{1,0:T(8,128)(2,1)}, bf16[1024,768]{1,0:T(8,128)(2,1)S(1)}, u32[]{:S(2)}, u32[]{:S(2)}) collective-permute-start(bf16[1024,768]{1,0:T(8,128)(2,1)} %get-tuple-element.148), channel_id=1, source_target_pairs={{0,1},{1,0},{2,3},{3,2},{4,5},{5,4},{6,7},{7,6}} | collective-permute-start | bytes 4718600 | tf_op jit(solution)/shard_map/ppermute | solution.py:745
  540.6 28.8 %collective-permute-start.15 = (bf16[1024,768]{1,0:T(8,128)(2,1)S(1)}, bf16[1024,768]{1,0:T(8,128)(2,1)}, u32[]{:S(2)}, u32[]{:S(2)}) collective-permute-start(bf16[1024,768]{1,0:T(8,128)(2,1)S(1)} %dynamic-slice_select_fusion), channel_id=1, source_target_pairs={{0,1},{1,0},{2,3},{3,2},{4,5},{5,4},{6,7},{7,6}} | collective-permute-start | bytes 4718600 | tf_op jit(solution)/shard_map/ppermute | solution.py:745
  711.0 166.8 %collective-permute-start.23 = (f32[3072,1792]{1,0:T(8,128)}, f32[3072,1792]{1,0:T(8,128)}, u32[]{:S(2)}, u32[]{:S(2)}) collective-permute-start(f32[3072,1792]{1,0:T(8,128)} %get-tuple-element.152), channel_id=1, source_target_pairs={{0,1},{1,0},{2,3},{3,2},{4,5},{5,4},{6,7},{7,6}} | collective-permute-start | bytes 66060296 | tf_op jit(solution)/shard_map/ppermute | solution.py:745
  711.0 115.8 %collective-permute-start.17 = (bf16[4096,640]{1,0:T(8,128)(2,1)}, bf16[4096,640]{1,0:T(8,128)(2,1)}, u32[]{:S(2)}, u32[]{:S(2)}) collective-permute-start(bf16[4096,640]{1,0:T(8,128)(2,1)} %get-tuple-element.141.gb_ref.rest_1_), channel_id=1, source_target_pairs={{0,2},{1,3},{2,0},{3,1},{4,6},{5,7},{6,4},{7,5}} | collective-permute-start | bytes 15728648 | tf_op jit(solution)/shard_map/ppermute | solution.py:742
  855.2 80.5 %collective-permute-start.24 = (f32[3072,768]{1,0:T(8,128)}, f32[3072,768]{1,0:T(8,128)}, u32[]{:S(2)}, u32[]{:S(2)}) collective-permute-start(f32[3072,768]{1,0:T(8,128)} %get-tuple-element.157), channel_id=1, source_target_pairs={{0,1},{1,0},{2,3},{3,2},{4,5},{5,4},{6,7},{7,6}} | collective-permute-start | bytes 28311560 | tf_op jit(solution)/shard_map/ppermute | solution.py:745
  855.2 16.7 %collective-permute-start.20 = (bf16[1024,640]{1,0:T(8,128)(2,1)}, bf16[1024,640]{1,0:T(8,128)(2,1)S(1)}, u32[]{:S(2)}, u32[]{:S(2)}) collective-permute-start(bf16[1024,640]{1,0:T(8,128)(2,1)} %get-tuple-element.161), channel_id=1, source_target_pairs={{0,1},{1,0},{2,3},{3,2},{4,5},{5,4},{6,7},{7,6}} | collective-permute-start | bytes 3932168 | tf_op jit(solution)/shard_map/ppermute | solution.py:745
  855.7 18.2 %collective-permute-start.19 = (bf16[1024,640]{1,0:T(8,128)(2,1)}, bf16[1024,640]{1,0:T(8,128)(2,1)}, u32[]{:S(2)}, u32[]{:S(2)}) collective-permute-start(bf16[1024,640]{1,0:T(8,128)(2,1)} %get-tuple-element.160), channel_id=1, source_target_pairs={{0,1},{1,0},{2,3},{3,2},{4,5},{5,4},{6,7},{7,6}} | collective-permute-start | bytes 3932168 | tf_op jit(solution)/shard_map/ppermute | solution.py:745
  857.2 18.7 %collective-permute-start.22 = (bf16[1024,640]{1,0:T(8,128)(2,1)S(1)}, bf16[1024,640]{1,0:T(8,128)(2,1)}, u32[]{:S(2)}, u32[]{:S(2)}) collective-permute-start(bf16[1024,640]{1,0:T(8,128)(2,1)S(1)} %constant_dynamic-slice_fusion), channel_id=1, source_target_pairs={{0,1},{1,0},{2,3},{3,2},{4,5},{5,4},{6,7},{7,6}} | collective-permute-start | bytes 3932168 | tf_op jit(solution)/shard_map/ppermute | solution.py:745
  872.0 5.8 collective-permute-start.21
  933.9 10.0 %collective-permute-start.26 = (f32[3072]{0:T(1024)S(1)}, f32[3072]{0:T(1024)S(1)}, u32[]{:S(2)}, u32[]{:S(2)}) collective-permute-start(f32[3072]{0:T(1024)S(1)} %add.49), channel_id=1, source_target_pairs={{0,2},{1,3},{2,0},{3,1},{4,6},{5,7},{6,4},{7,5}} | collective-permute-start | bytes 36872 | tf_op jit(solution)/shard_map/ppermute | solution.py:742
  (12 other events, 137.0 us)

commit v6 on v5

--- a/solution.py
+++ b/solution.py
@@ -67,6 +67,14 @@
     return lax.broadcasted_iota(jnp.int32, shape, 1)
 
 
+def loop(count, body):
+    def run(c, _):
+        body(c)
+        return 0
+
+    lax.fori_loop(0, count, run, 0)
+
+
 def one(h):
     return slice(h, h + 1)
 
@@ -116,23 +124,21 @@
     def norm(src):
         step = HEAD // 2
 
-        def stats(c, _):
+        def stats(c):
             sl = ds(c * step, step)
             xf = src[sl, :].astype(F32)
             inv = lax.rsqrt(jnp.mean(xf * xf, axis=-1, keepdims=True) + NORM_EPS)
             inv_ref[sl, :] = jnp.broadcast_to(inv, (step, HEAD))
-            return 0
-
-        def scale(c, _):
+
+        def scale(c):
             sl = ds(c * step, step)
             inv, gain = inv_ref[sl, :], gain_ref[...]
             for n in range(src.shape[1] // HEAD):
                 cols = head_cols(n)
                 h_ref[sl, cols] = (src[sl, cols].astype(F32) * inv * gain[:, cols]).astype(BF)
-            return 0
-
-        lax.fori_loop(0, src.shape[0] // step, stats, 0)
-        lax.fori_loop(0, src.shape[0] // step, scale, 0)
+
+        loop(src.shape[0] // step, stats)
+        loop(src.shape[0] // step, scale)
 
     @pl.when(pl.program_id(0) < half)
     def _():
@@ -240,7 +246,7 @@
         o_ref, lse_ref = rest[:2]
     seq = k_ref.shape[0]
 
-    def setup(c, _):
+    def setup(c):
         sl = ds(c * BLK, BLK)
         vt[:, sl] = v_ref[sl, :].T
         kk[sl, :HEAD] = k_ref[sl, :]
@@ -250,9 +256,8 @@
             hi = qf.astype(BF)
             qt[h, :HEAD, sl] = hi.T
             qt[h, HEAD:, sl] = (qf - hi.astype(F32)).astype(BF).T
-        return 0
-
-    lax.fori_loop(0, seq // BLK, setup, 0)
+
+    loop(seq // BLK, setup)
     acc[...] = jnp.zeros_like(acc)
     stat[...] = jnp.zeros_like(stat)
     cur, old, den_row = 0, 1, 2
@@ -267,12 +272,23 @@
 
     def stage_a(h, i, j, masked, init=None):
         row = one(h)
-        s = mm(kk[ds(j * BLK, BLK), :], qt[h, :, ds(i * BLK, BLK)])
-        if masked is not False:
-            keep = down(s.shape) <= across(s.shape)
-            s = jnp.where(keep if masked is True else jnp.logical_or(keep, jnp.logical_not(masked)), s, NEG_LARGE)
-        s_scr[h] = s
-        m_new = jnp.max(s, axis=0, keepdims=True)
+        if masked is True:
+            top = mm(kk[ds(j * BLK, HB), :], qt[h, :, ds(i * BLK, BLK)])
+            low = mm(kk[ds(j * BLK + HB, HB), :], qt[h, :, ds(i * BLK + HB, HB)])
+            top = jnp.where(down(top.shape) <= across(top.shape), top, NEG_LARGE)
+            low = jnp.where(down(low.shape) <= across(low.shape), low, NEG_LARGE)
+            s_scr[h, :HB, :] = top
+            s_scr[h, HB:, HB:] = low
+            m_new = jnp.max(top, axis=0, keepdims=True)
+            right = jnp.maximum(m_new[:, HB:], jnp.max(low, axis=0, keepdims=True))
+            m_new = jnp.concatenate([m_new[:, :HB], right], axis=1)
+        else:
+            s = mm(kk[ds(j * BLK, BLK), :], qt[h, :, ds(i * BLK, BLK)])
+            if masked is not False:
+                keep = down(s.shape) <= across(s.shape)
+                s = jnp.where(jnp.logical_or(keep, jnp.logical_not(masked)), s, NEG_LARGE)
+            s_scr[h] = s
+            m_new = jnp.max(s, axis=0, keepdims=True)
         if init is None:
             m_old = stat[cur, row]
         elif kind == "rest":
@@ -283,16 +299,31 @@
         stat[old, row] = jnp.exp2(m_old - m_new)
         stat[cur, row] = m_new
 
-    def stage_p(h):
+    def stage_p(h, diag=False):
         row = one(h)
-        p = jnp.exp2(s_scr[h] - stat[cur, row])
-        alpha = stat[old, row]
-        stat[den_row, row] = stat[den_row, row] * alpha + jnp.sum(p, axis=0, keepdims=True)
-        return p.astype(BF), alpha
-
-    def stage_v(h, j, held):
+        m, alpha = stat[cur, row], stat[old, row]
+        if diag:
+            top = jnp.exp2(s_scr[h, :HB, :] - m)
+            low = jnp.exp2(s_scr[h, HB:, HB:] - m[:, HB:])
+            total = jnp.sum(top, axis=0, keepdims=True)
+            right = total[:, HB:] + jnp.sum(low, axis=0, keepdims=True)
+            total = jnp.concatenate([total[:, :HB], right], axis=1)
+            top = top.astype(BF)
+            p = (top[:, :HB], jnp.concatenate([top[:, HB:], low.astype(BF)], axis=0))
+        else:
+            p = jnp.exp2(s_scr[h] - m)
+            total = jnp.sum(p, axis=0, keepdims=True)
+            p = p.astype(BF)
+        stat[den_row, row] = stat[den_row, row] * alpha + total
+        return p, alpha
+
+    def stage_v(h, j, held, diag=False):
         p, alpha = held
-        acc[h] = acc[h] * alpha + mm(vt[:, ds(j * BLK, BLK)], p)
+        if diag:
+            acc[h, :, :HB] = acc[h, :, :HB] * alpha[:, :HB] + mm(vt[:, ds(j * BLK, HB)], p[0])
+            acc[h, :, HB:] = acc[h, :, HB:] * alpha[:, HB:] + mm(vt[:, ds(j * BLK, BLK)], p[1])
+        else:
+            acc[h] = acc[h] * alpha + mm(vt[:, ds(j * BLK, BLK)], p)
 
     def finish(h, i, den, top):
         row = one(h)
@@ -313,46 +344,44 @@
     for h in range(GROUP):
         stage_a(h, i, 0, jnp.logical_and(steps == 1, diag == 1), init)
 
-    def row(t, _):
+    def row(t):
         i, steps, diag, _ = task(t)
 
-        def inner(j, _):
-            pipeline(i, j, False)
-            return 0
-
-        lax.fori_loop(0, steps - 2, inner, 0)
-
-        @pl.when(jnp.logical_and(steps > 1, diag == 1))
-        def _():
-            pipeline(i, steps - 2, True)
-
+        loop(steps - 2, lambda j: pipeline(i, j, False))
+
+        pl.when(jnp.logical_and(steps > 1, diag == 1))(lambda: pipeline(i, steps - 2, True))
         if kind == "rest":
-            @pl.when(diag == 0)
-            def _():
-                pipeline(i, steps - 2, False)
+            pl.when(diag == 0)(lambda: pipeline(i, steps - 2, False))
         i2, _, _, init2 = task(jnp.minimum(t + 1, count - 1))
-        for h in range(GROUP):
-            held = stage_p(h)
-            final = (stat[den_row, one(h)], stat[cur, one(h)])
-            stage_a(h, i2, 0, False, init2)
-            stage_v(h, steps - 1, held)
-            finish(h, i, *final)
-        if kind == "rest":
+
+        def last_step(on_diag):
+            for h in range(GROUP):
+                held = stage_p(h, on_diag)
+                final = (stat[den_row, one(h)], stat[cur, one(h)])
+                stage_a(h, i2, 0, False, init2)
+                stage_v(h, steps - 1, held, on_diag)
+                finish(h, i, *final)
+
+        if kind != "rest":
+            last_step(True)
+        else:
+            pl.when(diag == 1)(lambda: last_step(True))
+            pl.when(diag == 0)(lambda: last_step(False))
+
             @pl.when(init2 >= 0)
             def _():
                 stat[den_row] = jnp.ones(stat.shape[1:], F32)
                 for h in range(GROUP):
                     acc[h] = st_ref[0, h, :, ds(init2 * BLK, BLK)]
-        return 0
-
-    lax.fori_loop(0, count, row, 0)
+
+    loop(count, row)
     lse_ref[0, GROUP:, :] = jnp.zeros((8 - GROUP, seq), F32)
     if kind == "rest":
-        hi_ref[...] = o_ref[seq // 2:, :]
+        hi_ref[...] = o_ref[seq - hi_ref.shape[0]:, :]
         pair_ref[...] = o_ref[ds(s_ref[0] * pair_ref.shape[0], pair_ref.shape[0]), :]
 
 
-def attn_fwd(kind, idx, q, k, v, rows=0, local=()):
+def attn_fwd(kind, idx, q, k, v, extra=(), local=()):
     whole = q.shape[0]
     seq = whole if kind == "rest" else whole // (2 if kind == "local" else 1)
     nkv = k.shape[1] // HEAD
@@ -376,8 +405,8 @@
         out_specs.append(state)
     if kind == "rest":
         specs = [pl.BlockSpec((seq // 2, GW), col_map), pl.BlockSpec((1, 8, seq // 2), head_map), state]
-        outs += [sds(r, q.shape[1]) for r in (seq // 2, rows)]
-        out_specs += [pl.BlockSpec((r, GW), col_map) for r in (seq // 2, rows)]
+        outs += [sds(r, q.shape[1]) for r in extra]
+        out_specs += [pl.BlockSpec((r, GW), col_map) for r in extra]
     kspec = pl.BlockSpec((seq, HEAD), at)
     return call(lambda *refs: fwd_body(kind, *refs), (nkv,), [pl.BlockSpec((seq, GW), at), kspec, kspec] + specs,
                 out_specs, outs, [idx, q, k, v, *local], nkv * GROUP * seq * seq * PAIR,
@@ -425,15 +454,14 @@
         dkt[...] = jnp.zeros_like(dkt)
         dvt[...] = jnp.zeros_like(dvt)
 
-        def setup(c, _):
+        def setup(c):
             sl = ds(c * BLK, BLK)
             third = across((BLK, HEAD)) // 3
             for n, (src, dst) in enumerate(((k_ref, ka), (v_ref, va))):
                 dst[sl, :HEAD] = src[sl, :]
                 dst[sl, HEAD:] = jnp.where(third == n, -1.0, 0.0).astype(BF)
-            return 0
-
-        lax.fori_loop(0, seq // BLK, setup, 0)
+
+        loop(seq // BLK, setup)
         prepare(q_ref, do_ref, o_ref, lse_ref, sets[0])
 
     def run(mine, other, tail_width):
@@ -455,11 +483,10 @@
             dkt[:, sl] += mm(q3t[:, rows], dsv)
             dq3[rows, :] += mm(dsv, ka[sl, :HEAD])
 
-        def body(t, _):
+        def body(t):
             step(slice(0, 2 * m3), t * 2 * BLK, 2 * BLK, False)
-            return 0
-
-        lax.fori_loop(0, i // 2, body, 0)
+
+        loop(i // 2, body)
         start = (i // 2) * 2 * BLK
         step(slice(0, m3), start, tail_width - HB, True)
         prepare(qn_ref, don_ref, on_ref, lsen_ref, other)
@@ -478,13 +505,12 @@
 
     @pl.when(i == last)
     def _():
-        def fin(c, _):
+        def fin(c):
             sl = ds(c * BLK, BLK)
             out_ref[sl, GW:QK] = rotate(dkt[:, sl].T * SCALE, cos_ref[sl, :], -sin_ref[sl, :]).astype(BF)
             out_ref[sl, QK:] = dvt[:, sl].T.astype(BF)
-            return 0
-
-        lax.fori_loop(0, seq // BLK, fin, 0)
+
+        loop(seq // BLK, fin)
         pair_ref[...] = out_ref[ds(s_ref[0] * pair_ref.shape[0], pair_ref.shape[0]), :]
 
 
@@ -506,41 +532,36 @@
 
 
 def out_body(s_ref, x_ref, *rest):
-    ops, weights, out_ref = rest[:5], rest[5:9], rest[9]
-    o0, o1, oc, orv, o3 = [r[...] for r in ops]
-    lhs = jnp.concatenate([o0, o1, jnp.where(s_ref[4] == 0, oc, orv), o3], axis=1)
+    ops, weights, out_ref = rest[:4], rest[4:8], rest[8]
+    lhs = jnp.concatenate([r[...] for r in ops], axis=1)
     rhs = jnp.concatenate([r[...] for r in weights], axis=0)
     out_ref[...] = (x_ref[...].astype(F32) + mm(lhs, rhs)).astype(BF)
 
 
 def out_proj(idx, x, pieces, w_o):
-    def first_map(n, s):
+    def chip_map(n, s):
         return (s[0] % 2, 0)
 
     rows, d = x.shape
     hw = pieces[0].shape[1]
     return call(out_body, (d // BLK,),
                 [pl.BlockSpec((rows, BLK), col_map)]
-                + [pl.BlockSpec((rows, hw), m) for m in (own_map, first_row, first_map, first_map, first_row)]
+                + [pl.BlockSpec((rows, hw), m) for m in (own_map, first_row, chip_map, first_row)]
                 + [pl.BlockSpec((hw, BLK), lambda n, s, p=p: (s[p], n)) for p in range(4)],
                 pl.BlockSpec((rows, BLK), col_map), sds(rows, d), [idx, x, *pieces] + [w_o] * 4,
                 2 * rows * d * d)
 
 
 def dwo_body(s_ref, oa_ref, ob_ref, oc_ref, dy_ref, fin, snd, ot):
-    half, hw = ob_ref.shape
+    first, hw = ob_ref.shape
 
     @pl.when(jnp.logical_and(pl.program_id(0) == 0, pl.program_id(1) == 0))
     def _():
-        def tr(c, _):
-            sl, up = ds(c * BLK, BLK), ds(c * BLK + half, BLK)
-            ot[:hw, sl] = oa_ref[sl, :].T
-            ot[:hw, up] = oa_ref[up, :].T
-            ot[hw:, sl] = ob_ref[sl, :].T
-            ot[hw:, up] = oc_ref[sl, :].T
-            return 0
-
-        lax.fori_loop(0, half // BLK, tr, 0)
+        for src, rows, base in ((oa_ref, slice(0, hw), 0), (ob_ref, slice(hw, 2 * hw), 0), (oc_ref, slice(hw, 2 * hw), first)):
+            def tr(c):
+                ot[rows, ds(c * BLK + base, BLK)] = src[ds(c * BLK, BLK), :].T
+
+            loop(src.shape[0] // BLK, tr)
 
     val = mm(ot[ds(pl.program_id(1) * hw, hw), :], dy_ref[...])
     fin[...] = val
@@ -693,23 +714,21 @@
     def _():
         step = HEAD // 2
 
-        def stats(r, _):
+        def stats(r):
             sl = ds(r * step, step)
             inv = inv_ref[sl, :]
             tot[sl, :] = jnp.broadcast_to(jnp.sum(tot[sl, :], axis=-1, keepdims=True) / d, (step, HEAD)) * inv * inv * inv
-            return 0
-
-        lax.fori_loop(0, rows // step, stats, 0)
-
-        def epi(r, _):
+
+        loop(rows // step, stats)
+
+        def epi(r):
             sl = ds(r * step, step)
             coef = tot[sl, :]
             for c in range(d // HEAD):
                 cols = head_cols(c)
                 dx_ref[sl, cols] = (acc[sl, cols] - xs[sl, cols].astype(F32) * coef).astype(BF)
-            return 0
-
-        lax.fori_loop(0, rows // step, epi, 0)
+
+        loop(rows // step, epi)
 
     for copy in copies:
         copy.wait()
@@ -790,6 +809,7 @@
 
         chip, nh = j // 2, seq // BLK // 2
         tri = row_tasks(0, nh)
+        first = seq // 2 - BLK
         square = [(i + nh, nh, 0, i) for i in range(nh)]
 
         def table(head, tasks):
@@ -808,13 +828,13 @@
         x3b = near(x2b)
         bufs = project(vec((j2 + 1) * hpr - 1, (j3 + 1) * hpr - 1, j), x2b, x3b, gain_f, ws, tabs, bufs, seq)
         h_all, q, k, v, inv = bufs
-        o, lse, o_hi, o_pair = attn_fwd("rest", rest_tasks, q, k, v, rows, local)
+        o, lse, o_hi, o_pair = attn_fwd("rest", rest_tasks, q, k, v, (seq - first, rows), local)
         orv = over(o_hi)
         o1 = near(o_pair)
-        qc, kc, vc = project_first(vec(j2, dep=(o,)), h_all, ws, tabs, seq // 2)
+        qc, kc, vc = project_first(vec(j2, dep=(o,)), h_all, ws, tabs, first)
         dy2a = after(dy2a, qc)
         dy3a = near(dy2a)
-        oc = attn_fwd("first", table((j1, 0), tri), qc, kc, vc)[0]
+        oc = attn_fwd("first", table((j1, 0), tri[:-1]), qc, kc, vc)[0]
 
         dy2b = after(dy2b, oc)
         dy3b = near(dy2b)
@@ -830,10 +850,11 @@
         gb1 = near(gb_pair)
 
         orv = after(orv, gb)
-        o3 = near(jnp.where(chip == 0, rows_of(oc, j1 % 2), rows_of(orv, j1 % 2)))
+        ox = jnp.where(chip == 0, jnp.concatenate([oc, orv[:BLK]]), orv[BLK:])
+        o3 = near(rows_of(ox, j1 % 2))
         wo_fin, wo_snd = dw_o(vec(j, j2, dep=(gb,)), o, oc, orv, dy_all)
         wo_rcv = near(wo_snd)
-        result = out_proj(vec(*dev, chip, dep=(wo_snd,)), x, (o, o1, oc, orv, o3), w_o)
+        result = out_proj(vec(*dev, dep=(wo_snd,)), x, (o, o1, ox, o3), w_o)
         ga2 = after(ga2, wo_snd)
         fq, fk, fv, snd, wo_fin, g3 = dw_own(vec(*dev, dep=(result,)), h_all, ga, gb, ga2, wo_rcv, wo_fin)
         rcv = near(snd)

time: 955 us -> 956 us (level)
  Pallas kernels: 639 us -> 624 us
  waiting for transfers between devices: 254 us -> 266 us
    pallas_call x18, Pallas kernels: 639 us -> 624 us  [call(): pl.pallas_call(body, grid_spec=pltpu.PrefetchScalarGridSpec(num_scalar_pr...]
    ppermute x9, waiting for transfers between devices: 188 us -> 203 us  [over(): return lax.ppermute(val, 'sp', cross)]
  transfers between devices with their start and end apart: 27 -> 27, of which waited for: 17 -> 17; matrix products, arithmetic and copies ran while one was open for 4% -> 4% of each run, Pallas kernels for 56% -> 54%
where the time goes in v6:
time: 956 us; the launch traced here: 946 us
  Pallas kernels  624 us (65%)
  waiting for transfers between devices  266 us (28%)
  other arithmetic  22.1 us (2%)
  local copies, waits for them, and re-layouts  20.4 us (2%)
  starting transfers between devices  12.7 us (1%)
    pallas_call x18, Pallas kernels, call(): pl.pallas_call(body, grid_spec=pltpu.PrefetchScalarGridSpec(num_scalar_pr...  624 us
    ppermute x9, waiting for transfers between devices, over(): return lax.ppermute(val, 'sp', cross)  203 us
    ppermute x18, waiting for transfers between devices, near(): return lax.ppermute(val, 'sp', pair)  62.9 us
  transfers between devices with their start and end apart: 27, of which 17 were waited for; matrix products, arithmetic and copies ran while one was open for 4% of the time, Pallas kernels for 54%

profile of v6, /device:TPU:0, one launch (start us, length us, event | category | flops | bytes accessed | tf_op | source)
XLA Modules:
  0.0 946.0 jit_solution(6083973795206934636)
XLA Ops:
  1.5 10.1 %collective-permute-done.2.xb_ref = bf16[1024,3072]{1,0:T(8,128)(2,1)} collective-permute-done((bf16[1024,3072]{1,0:T(8,128)(2,1)}, bf16[1024,3072]{1,0:T(8,128)(2,1)}, u32[]{:S(2)}, u32[]{:S(2)}) %collective-permute-start.2) | collective-permute-done | bytes 6291488 | tf_op jit(solution)/shard_map/ppermute | solution.py:764
  41.5 34.5 %shard_map.171 = (bf16[4096,3072]{1,0:T(8,128)(2,1)}, bf16[4096,768]{1,0:T(8,128)(2,1)}, bf16[4096,256]{1,0:T(8,128)(2,1)}, bf16[4096,256]{1,0:T(8,128)(2,1)}, f32[4096,128]{1,0:T(8,128)}) custom-call(s32[3]{0:T(128)} %add_add_fusion.2.s_ref, bf16[1024,3072]{1,0:T(8,128)(2,1)} %x_ref.3, bf16[1024,3072]{1,0:T(8,128)(2,1)} %collective-permute-done.2.xb_ref, ...), custom_call_target="tpu_custom_call" | custom-call | flops 16106127360 | bytes 31457280 | tf_op jit(solution)/shard_map/pallas_call | solution.py:51
  76.0 17.7 %shard_map.172 = (bf16[4096,3072]{1,0:T(8,128)(2,1)}, bf16[4096,768]{1,0:T(8,128)(2,1)}) custom-call(s32[3]{0:T(128)} %add_add_fusion.2.s_ref, bf16[1024,3072]{1,0:T(8,128)(2,1)} %dy_ref.1, bf16[1024,3072]{1,0:T(8,128)(2,1)} %collective-permute-done.6.db_ref, bf16[3072,3072]{1,0:T(8,128)(2,1)} %rest_7_.1), custom_call_target="tpu_custom_call" | custom-call | flops 9663676416 | bytes 18874368 | tf_op jit(solution)/shard_map/pallas_call | solution.py:51
  93.7 27.0 %shard_map.173 = (bf16[2048,768]{1,0:T(8,128)(2,1)}, f32[2,8,2048]{2,1,0:T(8,128)}, f32[2,3,128,2048]{3,2,1,0:T(8,128)}) custom-call(s32[19]{0:T(128)} %pad_add_fusion.6.refs_0_, bf16[4096,768]{1,0:T(8,128)(2,1)} %get-tuple-element.100.refs_1_.rest_1_, bf16[4096,256]{1,0:T(8,128)(2,1)} %get-tuple-element.105.refs_2_.rest_2_, ...), custom_call_target="tpu_custom_call" | custom-call | flops 6442450944 | bytes 12582912 | tf_op jit(solution)/shard_map/pallas_call | solution.py:51
  132.3 27.4 %shard_map.174 = (bf16[4096,3072]{1,0:T(8,128)(2,1)}, bf16[4096,768]{1,0:T(8,128)(2,1)}, bf16[4096,256]{1,0:T(8,128)(2,1)}, bf16[4096,256]{1,0:T(8,128)(2,1)}, f32[4096,128]{1,0:T(8,128)}) custom-call(s32[3]{0:T(128)} %add_add_fusion.1.s_ref, ...), custom_call_target="tpu_custom_call", output_to_operand_aliasing={{0}: (9, {}), {1}: (10, {}), {2}: (11, {}), {3}: (12, {}), ... | custom-call | flops 12079595520 | bytes 23592960 | tf_op jit(solution)/shard_map/pallas_call | solution.py:51
  167.2 13.1 %shard_map.175 = (bf16[4096,3072]{1,0:T(8,128)(2,1)}, bf16[4096,768]{1,0:T(8,128)(2,1)}, bf16[4096,256]{1,0:T(8,128)(2,1)}, bf16[4096,256]{1,0:T(8,128)(2,1)}, f32[4096,128]{1,0:T(8,128)}) custom-call(s32[3]{0:T(128)} %add_add_fusion.s_ref, ...), custom_call_target="tpu_custom_call", output_to_operand_aliasing={{0}: (9, {}), {1}: (10, {}), {2}: (11, {}), {3}: (12, {}), ... | custom-call | flops 4026531840 | bytes 7864320 | tf_op jit(solution)/shard_map/pallas_call | solution.py:51
  180.4 60.6 %shard_map.176 = (bf16[4096,768]{1,0:T(8,128)(2,1)}, f32[2,8,4096]{2,1,0:T(8,128)}, bf16[2560,768]{1,0:T(8,128)(2,1)}, bf16[1024,768]{1,0:T(8,128)(2,1)}) custom-call(s32[35]{0:T(128)} %broadcast_select_fusion.refs_0_, bf16[4096,768]{1,0:T(8,128)(2,1)} %get-tuple-element.117.refs_1_.q_ref.qn_ref, bf16[4096,256]{1,0:T(8,128)(2,1)} %get-tuple-element.119.refs_2_.k_ref, ...), custom_call_target="tpu_custom_call" | custom-call | flops 25769803776 | bytes 50331648 | tf_op jit(solution)/shard_map/pallas_call | solution.py:51
  241.0 18.4 %shard_map.177 = (bf16[1536,768]{1,0:T(8,128)(2,1)}, bf16[1536,256]{1,0:T(8,128)(2,1)}, bf16[1536,256]{1,0:T(8,128)(2,1)}) custom-call(s32[1]{0:T(128)} %bitcast.2.s_ref, bf16[4096,3072]{1,0:T(8,128)(2,1)} %get-tuple-element.125.h_ref, bf16[3072,3072]{1,0:T(8,128)(2,1)} %rest_17_.1, bf16[3072,1024]{1,0:T(8,128)(2,1)} %rest_18_.1, ...), custom_call_target="tpu_custom_call" | custom-call | flops 12079595520 | bytes 23592960 | tf_op jit(solution)/shard_map/pallas_call | solution.py:51
  267.9 17.0 %shard_map.178 = (bf16[1536,768]{1,0:T(8,128)(2,1)}, f32[2,8,1536]{2,1,0:T(8,128)}) custom-call(s32[15]{0:T(128)} %pad_add_fusion.7.refs_0_, bf16[1536,768]{1,0:T(8,128)(2,1)} %get-tuple-element.126.refs_1_, bf16[1536,256]{1,0:T(8,128)(2,1)} %get-tuple-element.127.refs_2_, bf16[1536,256]{1,0:T(8,128)(2,1)} %get-tuple-element.128.refs_3_), custom_call_target="tpu_custom_call" | custom-call | flops 3623878656 | bytes 7077888 | tf_op jit(solution)/shard_map/pallas_call | solution.py:51
  285.0 19.0 %collective-permute-done.9.da_ref = bf16[256,3072]{1,0:T(8,128)(2,1)S(1)} collective-permute-done((bf16[256,3072]{1,0:T(8,128)(2,1)}, bf16[256,3072]{1,0:T(8,128)(2,1)S(1)}, u32[]{:S(2)}, u32[]{:S(2)}) %collective-permute-start.9) | collective-permute-done | bytes 1572896 | tf_op jit(solution)/shard_map/ppermute | solution.py:761
  306.2 15.2 %shard_map.179 = (bf16[4096,3072]{1,0:T(8,128)(2,1)}, bf16[4096,768]{1,0:T(8,128)(2,1)}) custom-call(s32[3]{0:T(128)} %add_add_fusion.1.s_ref, bf16[768,3072]{1,0:T(8,128)(2,1)} %collective-permute-done.11.da_ref, bf16[768,3072]{1,0:T(8,128)(2,1)} %collective-permute-done.12.db_ref, ...), custom_call_target="tpu_custom_call", output_to_operand_aliasing={{0}: (4, {}), {1}: (5, {})} | custom-call | flops 7247757312 | bytes 14155776 | tf_op jit(solution)/shard_map/pallas_call | solution.py:51
  321.4 7.8 shard_map.180
  329.2 76.8 %shard_map.181 = (bf16[4096,640]{1,0:T(8,128)(2,1)}, bf16[1024,640]{1,0:T(8,128)(2,1)}) custom-call(s32[2]{0:T(128)} %pad_add_fusion.5.s_ref, bf16[4096,768]{1,0:T(8,128)(2,1)} %get-tuple-element.117.refs_1_.q_ref.qn_ref, bf16[4096,768]{1,0:T(8,128)(2,1)} %get-tuple-element.137.do_ref.don_ref, ...), custom_call_target="tpu_custom_call" | custom-call | flops 36238786560 | bytes 70778880 | tf_op jit(solution)/shard_map/pallas_call | solution.py:51
  406.1 77.1 %shard_map.182 = (bf16[4096,640]{1,0:T(8,128)(2,1)}, bf16[1024,640]{1,0:T(8,128)(2,1)}) custom-call(s32[2]{0:T(128)} %pad_add_fusion.4.s_ref, bf16[4096,768]{1,0:T(8,128)(2,1)} %get-tuple-element.117.refs_1_.q_ref.qn_ref, bf16[4096,768]{1,0:T(8,128)(2,1)} %get-tuple-element.137.do_ref.don_ref, ...), custom_call_target="tpu_custom_call" | custom-call | flops 36238786560 | bytes 70778880 | tf_op jit(solution)/shard_map/pallas_call | solution.py:51
  483.2 54.4 %shard_map.183 = (f32[3072,3072]{1,0:T(8,128)}, f32[1536,3072]{1,0:T(8,128)}) custom-call(s32[2]{0:T(128)} %pad_add_fusion.3.s_ref, bf16[4096,768]{1,0:T(8,128)(2,1)} %get-tuple-element.123.o_ref.on_ref.oa_ref.rest_0_, bf16[1536,768]{1,0:T(8,128)(2,1)} %get-tuple-element.129.ob_ref, bf16[2560,768]{1,0:T(8,128)(2,1)} %collective-permute-done.13.oc_ref, ...), custom_call_target="tpu_custom_call" | custom-call | flops 38654705664 | bytes 75497472 | tf_op jit(solution)/shard_map/pallas_call | solution.py:51
  546.6 21.6 %collective-permute-done.14.rest_1_ = bf16[1024,768]{1,0:T(8,128)(2,1)S(1)} collective-permute-done((bf16[1024,768]{1,0:T(8,128)(2,1)}, bf16[1024,768]{1,0:T(8,128)(2,1)S(1)}, u32[]{:S(2)}, u32[]{:S(2)}) %collective-permute-start.14) | collective-permute-done | bytes 1572896 | tf_op jit(solution)/shard_map/ppermute | solution.py:764
  570.6 27.1 %shard_map.184 = bf16[1024,3072]{1,0:T(8,128)(2,1)} custom-call(s32[4]{0:T(128)} %pad_add_fusion.2.s_ref, bf16[1024,3072]{1,0:T(8,128)(2,1)} %x_ref.3, bf16[4096,768]{1,0:T(8,128)(2,1)} %get-tuple-element.123.o_ref.on_ref.oa_ref.rest_0_, bf16[1024,768]{1,0:T(8,128)(2,1)} %copy-done.3, bf16[2048,768]{1,0:T(8,128)(2,1)} %copy-done, ...), custom_call_target="tpu_custom_call" | custom-call | flops 19327352832 | bytes 37748736 | tf_op jit(solution)/shard_map/pallas_call | solution.py:51
  597.8 55.6 %collective-permute-done.16.gc_ref.ga_ref.rest_4_ = bf16[4096,640]{1,0:T(8,128)(2,1)} collective-permute-done((bf16[4096,640]{1,0:T(8,128)(2,1)}, bf16[4096,640]{1,0:T(8,128)(2,1)}, u32[]{:S(2)}, u32[]{:S(2)}) %collective-permute-start.16) | collective-permute-done | bytes 5242912 | tf_op jit(solution)/shard_map/ppermute | solution.py:761
  653.4 58.8 %shard_map.185 = (f32[3072,3072]{1,0:T(8,128)}, f32[3072,1024]{1,0:T(8,128)}, f32[3072,1024]{1,0:T(8,128)}, f32[3072,1792]{1,0:T(8,128)}, f32[3072,3072]{1,0:T(8,128)}, /*index=5*/bf16[1024,640]{1,0:T(8,128)(2,1)}) custom-call(s32[4]{0:T(128)} %pad_add_fusion.2.s_ref, bf16[4096,3072]{1,0:T(8,128)(2,1)} %get-tuple-element.125.h_ref, ...), custom_call_target="tpu_custom_call", output_to_operand_aliasing={{4}: (6, {})} | custom-call | flops 45097156608 | bytes 88080384 | tf_op jit(solution)/shard_map/pallas_call | solution.py:51
  714.0 114.0 %collective-permute-done.17.gb_ref.rest_5_ = bf16[4096,640]{1,0:T(8,128)(2,1)} collective-permute-done((bf16[4096,640]{1,0:T(8,128)(2,1)}, bf16[4096,640]{1,0:T(8,128)(2,1)}, u32[]{:S(2)}, u32[]{:S(2)}) %collective-permute-start.17) | collective-permute-done | bytes 5242912 | tf_op jit(solution)/shard_map/ppermute | solution.py:761
  828.0 28.5 %shard_map.186 = (f32[3072,3072]{1,0:T(8,128)}, f32[3072,1024]{1,0:T(8,128)}, f32[3072,1024]{1,0:T(8,128)}, f32[3072,768]{1,0:T(8,128)}) custom-call(s32[1]{0:T(128)} %bitcast.2.s_ref, bf16[4096,3072]{1,0:T(8,128)(2,1)} %get-tuple-element.125.h_ref, ...), custom_call_target="tpu_custom_call", output_to_operand_aliasing={{0}: (4, {}), {1}: (5, {}), {2}: (6, {})} | custom-call | flops 19327352832 | bytes 37748736 | tf_op jit(solution)/shard_map/pallas_call | solution.py:51
  859.0 14.3 %collective-permute-done.20.rest_3_ = bf16[1024,640]{1,0:T(8,128)(2,1)S(1)} collective-permute-done((bf16[1024,640]{1,0:T(8,128)(2,1)}, bf16[1024,640]{1,0:T(8,128)(2,1)S(1)}, u32[]{:S(2)}, u32[]{:S(2)}) %collective-permute-start.20) | collective-permute-done | bytes 1310752 | tf_op jit(solution)/shard_map/ppermute | solution.py:764
  879.0 53.8 %shard_map.187 = (bf16[1024,3072]{1,0:T(8,128)(2,1)}, f32[8,3072]{1,0:T(8,128)}, f32[3072,3072]{1,0:T(8,128)}, f32[3072,1024]{1,0:T(8,128)}, f32[3072,1024]{1,0:T(8,128)}) custom-call(s32[4]{0:T(128)} %pad_add_fusion.2.s_ref, bf16[1024,3072]{1,0:T(8,128)(2,1)} %x_ref.3, ...), custom_call_target="tpu_custom_call", output_to_operand_aliasing={{2}: (26, {}), {3}: (27, {}), {4}: (28, {})} | custom-call | flops 32212254720 | bytes 62914560 | tf_op jit(solution)/shard_map/pallas_call | solution.py:51
  936.7 8.3 shard_map.188
  (103 shorter events, 86.4 us)
Async XLA Ops:
  0.7 11.0 %collective-permute-start.2 = (bf16[1024,3072]{1,0:T(8,128)(2,1)}, bf16[1024,3072]{1,0:T(8,128)(2,1)}, u32[]{:S(2)}, u32[]{:S(2)}) collective-permute-start(bf16[1024,3072]{1,0:T(8,128)(2,1)} %x_ref.3), channel_id=1, source_target_pairs={{0,1},{1,0},{2,3},{3,2},{4,5},{5,4},{6,7},{7,6}} | collective-permute-start | bytes 18874376 | tf_op jit(solution)/shard_map/ppermute | solution.py:764
  11.6 64.4 %collective-permute-start.6 = (bf16[1024,3072]{1,0:T(8,128)(2,1)}, bf16[1024,3072]{1,0:T(8,128)(2,1)}, u32[]{:S(2)}, u32[]{:S(2)}) collective-permute-start(bf16[1024,3072]{1,0:T(8,128)(2,1)} %dy_ref.1), channel_id=1, source_target_pairs={{0,1},{1,0},{2,3},{3,2},{4,5},{5,4},{6,7},{7,6}} | collective-permute-start | bytes 18874376 | tf_op jit(solution)/shard_map/ppermute | solution.py:764
  19.5 10.5 %collective-permute-start.3 = (s32[1024]{0:T(1024)S(1)}, s32[1024]{0:T(1024)S(1)}, u32[]{:S(2)}, u32[]{:S(2)}) collective-permute-start(s32[1024]{0:T(1024)S(1)} %copy-done.6), channel_id=1, source_target_pairs={{0,1},{1,0},{2,3},{3,2},{4,5},{5,4},{6,7},{7,6}} | collective-permute-start | bytes 12296 | tf_op jit(solution)/shard_map/ppermute | solution.py:764
  19.6 104.4 %collective-permute-start.1 = (bf16[768,3072]{1,0:T(8,128)(2,1)}, bf16[768,3072]{1,0:T(8,128)(2,1)}, u32[]{:S(2)}, u32[]{:S(2)}) collective-permute-start(bf16[768,3072]{1,0:T(8,128)(2,1)} %slice.28), channel_id=1, source_target_pairs={{0,2},{1,3},{2,0},{3,1},{4,6},{5,7},{6,4},{7,5}} | collective-permute-start | bytes 14155784 | tf_op jit(solution)/shard_map/ppermute | solution.py:761
  21.1 9.5 %collective-permute-start.5 = (s32[1024]{0:T(1024)S(1)}, s32[1024]{0:T(1024)S(1)}, u32[]{:S(2)}, u32[]{:S(2)}) collective-permute-start(s32[1024]{0:T(1024)S(1)} %collective-permute-done.4), channel_id=1, source_target_pairs={{0,1},{1,0},{2,3},{3,2},{4,5},{5,4},{6,7},{7,6}} | collective-permute-start | bytes 12296 | tf_op jit(solution)/shard_map/ppermute | solution.py:764
  124.0 8.3 collective-permute-start.7
  125.5 36.9 %collective-permute-start = (bf16[256,3072]{1,0:T(8,128)(2,1)S(1)}, bf16[256,3072]{1,0:T(8,128)(2,1)}, u32[]{:S(2)}, u32[]{:S(2)}) collective-permute-start(bf16[256,3072]{1,0:T(8,128)(2,1)S(1)} %slice.29), channel_id=1, source_target_pairs={{0,2},{1,3},{2,0},{3,1},{4,6},{5,7},{6,4},{7,5}} | collective-permute-start | bytes 4718600 | tf_op jit(solution)/shard_map/ppermute | solution.py:761
  162.5 104.5 %collective-permute-start.11 = (bf16[768,3072]{1,0:T(8,128)(2,1)}, bf16[768,3072]{1,0:T(8,128)(2,1)}, u32[]{:S(2)}, u32[]{:S(2)}) collective-permute-start(bf16[768,3072]{1,0:T(8,128)(2,1)} %slice.30), channel_id=1, source_target_pairs={{0,2},{1,3},{2,0},{3,1},{4,6},{5,7},{6,4},{7,5}} | collective-permute-start | bytes 14155784 | tf_op jit(solution)/shard_map/ppermute | solution.py:761
  267.0 39.2 %collective-permute-start.12 = (bf16[768,3072]{1,0:T(8,128)(2,1)}, bf16[768,3072]{1,0:T(8,128)(2,1)}, u32[]{:S(2)}, u32[]{:S(2)}) collective-permute-start(bf16[768,3072]{1,0:T(8,128)(2,1)} %collective-permute-done.11.da_ref), channel_id=1, source_target_pairs={{0,1},{1,0},{2,3},{3,2},{4,5},{5,4},{6,7},{7,6}} | collective-permute-start | bytes 14155784 | tf_op jit(solution)/shard_map/ppermute | solution.py:764
  267.0 37.0 %collective-permute-start.9 = (bf16[256,3072]{1,0:T(8,128)(2,1)}, bf16[256,3072]{1,0:T(8,128)(2,1)S(1)}, u32[]{:S(2)}, u32[]{:S(2)}) collective-permute-start(bf16[256,3072]{1,0:T(8,128)(2,1)} %slice.31), channel_id=1, source_target_pairs={{0,2},{1,3},{2,0},{3,1},{4,6},{5,7},{6,4},{7,5}} | collective-permute-start | bytes 4718600 | tf_op jit(solution)/shard_map/ppermute | solution.py:761
  304.0 17.4 %collective-permute-start.10 = (bf16[256,3072]{1,0:T(8,128)(2,1)S(1)}, bf16[256,3072]{1,0:T(8,128)(2,1)}, u32[]{:S(2)}, u32[]{:S(2)}) collective-permute-start(bf16[256,3072]{1,0:T(8,128)(2,1)S(1)} %collective-permute-done.9.da_ref), channel_id=1, source_target_pairs={{0,1},{1,0},{2,3},{3,2},{4,5},{5,4},{6,7},{7,6}} | collective-permute-start | bytes 4718600 | tf_op jit(solution)/shard_map/ppermute | solution.py:764
  305.9 177.2 %collective-permute-start.13 = (bf16[2560,768]{1,0:T(8,128)(2,1)}, bf16[2560,768]{1,0:T(8,128)(2,1)}, u32[]{:S(2)}, u32[]{:S(2)}) collective-permute-start(bf16[2560,768]{1,0:T(8,128)(2,1)} %get-tuple-element.143), channel_id=1, source_target_pairs={{0,2},{1,3},{2,0},{3,1},{4,6},{5,7},{6,4},{7,5}} | collective-permute-start | bytes 11796488 | tf_op jit(solution)/shard_map/ppermute | solution.py:761
  537.6 115.8 %collective-permute-start.18 = (f32[1536,3072]{1,0:T(8,128)}, f32[1536,3072]{1,0:T(8,128)}, u32[]{:S(2)}, u32[]{:S(2)}) collective-permute-start(f32[1536,3072]{1,0:T(8,128)} %get-tuple-element.146), channel_id=1, source_target_pairs={{0,1},{1,0},{2,3},{3,2},{4,5},{5,4},{6,7},{7,6}} | collective-permute-start | bytes 56623112 | tf_op jit(solution)/shard_map/ppermute | solution.py:764
  537.8 115.6 %collective-permute-start.16 = (bf16[4096,640]{1,0:T(8,128)(2,1)}, bf16[4096,640]{1,0:T(8,128)(2,1)}, u32[]{:S(2)}, u32[]{:S(2)}) collective-permute-start(bf16[4096,640]{1,0:T(8,128)(2,1)} %get-tuple-element.139.ga_ref.rest_0_), channel_id=1, source_target_pairs={{0,2},{1,3},{2,0},{3,1},{4,6},{5,7},{6,4},{7,5}} | collective-permute-start | bytes 15728648 | tf_op jit(solution)/shard_map/ppermute | solution.py:761
  539.5 28.7 %collective-permute-start.14 = (bf16[1024,768]{1,0:T(8,128)(2,1)}, bf16[1024,768]{1,0:T(8,128)(2,1)S(1)}, u32[]{:S(2)}, u32[]{:S(2)}) collective-permute-start(bf16[1024,768]{1,0:T(8,128)(2,1)} %get-tuple-element.148), channel_id=1, source_target_pairs={{0,1},{1,0},{2,3},{3,2},{4,5},{5,4},{6,7},{7,6}} | collective-permute-start | bytes 4718600 | tf_op jit(solution)/shard_map/ppermute | solution.py:764
  545.6 25.0 %collective-permute-start.15 = (bf16[1024,768]{1,0:T(8,128)(2,1)S(1)}, bf16[1024,768]{1,0:T(8,128)(2,1)}, u32[]{:S(2)}, u32[]{:S(2)}) collective-permute-start(bf16[1024,768]{1,0:T(8,128)(2,1)S(1)} %constant_dynamic-slice_fusion.1), channel_id=1, source_target_pairs={{0,1},{1,0},{2,3},{3,2},{4,5},{5,4},{6,7},{7,6}} | collective-permute-start | bytes 4718600 | tf_op jit(solution)/shard_map/ppermute | solution.py:764
  712.2 166.8 %collective-permute-start.23 = (f32[3072,1792]{1,0:T(8,128)}, f32[3072,1792]{1,0:T(8,128)}, u32[]{:S(2)}, u32[]{:S(2)}) collective-permute-start(f32[3072,1792]{1,0:T(8,128)} %get-tuple-element.152), channel_id=1, source_target_pairs={{0,1},{1,0},{2,3},{3,2},{4,5},{5,4},{6,7},{7,6}} | collective-permute-start | bytes 66060296 | tf_op jit(solution)/shard_map/ppermute | solution.py:764
  712.3 115.8 %collective-permute-start.17 = (bf16[4096,640]{1,0:T(8,128)(2,1)}, bf16[4096,640]{1,0:T(8,128)(2,1)}, u32[]{:S(2)}, u32[]{:S(2)}) collective-permute-start(bf16[4096,640]{1,0:T(8,128)(2,1)} %get-tuple-element.141.gb_ref.rest_1_), channel_id=1, source_target_pairs={{0,2},{1,3},{2,0},{3,1},{4,6},{5,7},{6,4},{7,5}} | collective-permute-start | bytes 15728648 | tf_op jit(solution)/shard_map/ppermute | solution.py:761
  856.5 80.2 %collective-permute-start.24 = (f32[3072,768]{1,0:T(8,128)}, f32[3072,768]{1,0:T(8,128)}, u32[]{:S(2)}, u32[]{:S(2)}) collective-permute-start(f32[3072,768]{1,0:T(8,128)} %get-tuple-element.157), channel_id=1, source_target_pairs={{0,1},{1,0},{2,3},{3,2},{4,5},{5,4},{6,7},{7,6}} | collective-permute-start | bytes 28311560 | tf_op jit(solution)/shard_map/ppermute | solution.py:764
  856.5 16.7 %collective-permute-start.20 = (bf16[1024,640]{1,0:T(8,128)(2,1)}, bf16[1024,640]{1,0:T(8,128)(2,1)S(1)}, u32[]{:S(2)}, u32[]{:S(2)}) collective-permute-start(bf16[1024,640]{1,0:T(8,128)(2,1)} %get-tuple-element.161), channel_id=1, source_target_pairs={{0,1},{1,0},{2,3},{3,2},{4,5},{5,4},{6,7},{7,6}} | collective-permute-start | bytes 3932168 | tf_op jit(solution)/shard_map/ppermute | solution.py:764
  857.0 18.2 %collective-permute-start.19 = (bf16[1024,640]{1,0:T(8,128)(2,1)}, bf16[1024,640]{1,0:T(8,128)(2,1)}, u32[]{:S(2)}, u32[]{:S(2)}) collective-permute-start(bf16[1024,640]{1,0:T(8,128)(2,1)} %get-tuple-element.160), channel_id=1, source_target_pairs={{0,1},{1,0},{2,3},{3,2},{4,5},{5,4},{6,7},{7,6}} | collective-permute-start | bytes 3932168 | tf_op jit(solution)/shard_map/ppermute | solution.py:764
  858.5 18.7 %collective-permute-start.22 = (bf16[1024,640]{1,0:T(8,128)(2,1)S(1)}, bf16[1024,640]{1,0:T(8,128)(2,1)}, u32[]{:S(2)}, u32[]{:S(2)}) collective-permute-start(bf16[1024,640]{1,0:T(8,128)(2,1)S(1)} %constant_dynamic-slice_fusion), channel_id=1, source_target_pairs={{0,1},{1,0},{2,3},{3,2},{4,5},{5,4},{6,7},{7,6}} | collective-permute-start | bytes 3932168 | tf_op jit(solution)/shard_map/ppermute | solution.py:764
  873.2 5.8 collective-permute-start.21
  935.0 10.0 %collective-permute-start.26 = (f32[3072]{0:T(1024)S(1)}, f32[3072]{0:T(1024)S(1)}, u32[]{:S(2)}, u32[]{:S(2)}) collective-permute-start(f32[3072]{0:T(1024)S(1)} %add.47), channel_id=1, source_target_pairs={{0,2},{1,3},{2,0},{3,1},{4,6},{5,7},{6,4},{7,5}} | collective-permute-start | bytes 36872 | tf_op jit(solution)/shard_map/ppermute | solution.py:761
  (14 other events, 166.8 us)

commit v7 on v6

--- a/solution.py
+++ b/solution.py
@@ -122,7 +122,7 @@
     half = pl.num_programs(0) // 2
 
     def norm(src):
-        step = HEAD // 2
+        step = HEAD
 
         def stats(c):
             sl = ds(c * step, step)
@@ -415,13 +415,14 @@
                          pltpu.VMEM((GROUP, HEAD, BLK), F32), pltpu.VMEM((GROUP, 8, BLK), F32)])
 
 
-def bwd_body(s_ref, q_ref, do_ref, o_ref, lse_ref, qn_ref, don_ref, on_ref, lsen_ref, k_ref, v_ref, cos_ref, sin_ref,
-             out_ref, pair_ref, ka, va, dkt, dvt, *sets):
+def bwd_body(s_ref, q_ref, do_ref, o_ref, lse_ref, qn_ref, don_ref, on_ref, lsen_ref, k_ref, v_ref, cos_hbm, sin_hbm,
+             out_ref, pair_ref, ka, va, dkt, dvt, tab, tab_sem, *sets):
     i = pl.program_id(0)
     last = pl.num_programs(0) - 1
     seq = k_ref.shape[0]
     m3 = GROUP * HB
     sets = (sets[:5], sets[5:])
+    cos_ref, sin_ref = tab.at[0], tab.at[1]
 
     def spots():
         for b in range(2):
@@ -451,6 +452,9 @@
 
     @pl.when(i == 0)
     def _():
+        copies = [pltpu.make_async_copy(src, tab.at[n], tab_sem.at[n]) for n, src in enumerate((cos_hbm, sin_hbm))]
+        for copy in copies:
+            copy.start()
         dkt[...] = jnp.zeros_like(dkt)
         dvt[...] = jnp.zeros_like(dvt)
 
@@ -463,6 +467,8 @@
 
         loop(seq // BLK, setup)
         prepare(q_ref, do_ref, o_ref, lse_ref, sets[0])
+        for copy in copies:
+            copy.wait()
 
     def run(mine, other, tail_width):
         qa, da, q3t, do3t, dq3 = mine
@@ -506,11 +512,11 @@
     @pl.when(i == last)
     def _():
         def fin(c):
-            sl = ds(c * BLK, BLK)
+            sl = ds(c * 2 * BLK, 2 * BLK)
             out_ref[sl, GW:QK] = rotate(dkt[:, sl].T * SCALE, cos_ref[sl, :], -sin_ref[sl, :]).astype(BF)
             out_ref[sl, QK:] = dvt[:, sl].T.astype(BF)
 
-        loop(seq // BLK, fin)
+        loop(seq // BLK // 2, fin)
         pair_ref[...] = out_ref[ds(s_ref[0] * pair_ref.shape[0], pair_ref.shape[0]), :]
 
 
@@ -525,10 +531,11 @@
         row_specs += [pl.BlockSpec((1, 8, BLK), lambda i, s, a=ahead: (s[1], 0, jnp.minimum(i + a, nq - 1)))]
     one_set = [pltpu.VMEM((m3, PAIR), BF)] * 2 + [pltpu.VMEM((HEAD, m3), BF)] * 2 + [pltpu.VMEM((m3, HEAD), F32)]
     return call(bwd_body, (nq,),
-                row_specs + [kspec] * 2 + [pl.BlockSpec((seq, HEAD), first_row)] * 2,
+                row_specs + [kspec] * 2 + [ANY] * 2,
                 [pl.BlockSpec((r, PW), first_row) for r in (seq, rows)], [sds(r, PW) for r in (seq, rows)],
                 [idx] + [q, do, o, lse] * 2 + [k, v, *tabs], GROUP * nq * (nq + 1) * BLK * BLK * PW,
-                scratch=[pltpu.VMEM((seq, PAIR), BF)] * 2 + [pltpu.VMEM((HEAD, seq), F32)] * 2 + one_set * 2)
+                scratch=[pltpu.VMEM((seq, PAIR), BF)] * 2 + [pltpu.VMEM((HEAD, seq), F32)] * 2
+                + [pltpu.VMEM((2, seq, HEAD), F32), pltpu.SemaphoreType.DMA((2,))] + one_set * 2)
 
 
 def out_body(s_ref, x_ref, *rest):
@@ -836,9 +843,9 @@
         dy3a = near(dy2a)
         oc = attn_fwd("first", table((j1, 0), tri[:-1]), qc, kc, vc)[0]
 
-        dy2b = after(dy2b, oc)
+        dbufs = dout(vec(j2 * hpr, j3 * hpr, j, dep=(oc,)), dy2a, dy3a, w_o, dbufs, seq)
+        dy2b = after(dy2b, dbufs[1])
         dy3b = near(dy2b)
-        dbufs = dout(vec(j2 * hpr, j3 * hpr, j, dep=(oc,)), dy2a, dy3a, w_o, dbufs, seq)
         dbufs = dout(vec((j2 + 1) * hpr - 1, (j3 + 1) * hpr - 1, j), dy2b, dy3b, w_o, dbufs, seq)
         dy_all, do = dbufs
 

time: 956 us -> 943 us (0.986)
  waiting for transfers between devices: 266 us -> 246 us
    ppermute x9, waiting for transfers between devices: 203 us -> 182 us  [over(): return lax.ppermute(val, 'sp', cross)]
  transfers between devices with their start and end apart: 27 -> 27, of which waited for: 17 -> 17; matrix products, arithmetic and copies ran while one was open for 4% -> 4% of each run, Pallas kernels for 54% -> 55%
where the time goes in v7:
time: 943 us; the launch traced here: 933 us
  Pallas kernels  629 us (67%)
  waiting for transfers between devices  246 us (26%)
  other arithmetic  22.1 us (2%)
  local copies, waits for them, and re-layouts  21.6 us (2%)
  starting transfers between devices  12.9 us (1%)
    pallas_call x18, Pallas kernels, call(): pl.pallas_call(body, grid_spec=pltpu.PrefetchScalarGridSpec(num_scalar_pr...  629 us
    ppermute x9, waiting for transfers between devices, over(): return lax.ppermute(val, 'sp', cross)  182 us
    ppermute x18, waiting for transfers between devices, near(): return lax.ppermute(val, 'sp', pair)  63.7 us
  transfers between devices with their start and end apart: 27, of which 17 were waited for; matrix products, arithmetic and copies ran while one was open for 4% of the time, Pallas kernels for 55%

profile of v7, /device:TPU:0, one launch (start us, length us, event | category | flops | bytes accessed | tf_op | source)
XLA Modules:
  0.0 932.5 jit_solution(15015024443301482853)
XLA Ops:
  1.5 10.1 %collective-permute-done.2.xb_ref = bf16[1024,3072]{1,0:T(8,128)(2,1)} collective-permute-done((bf16[1024,3072]{1,0:T(8,128)(2,1)}, bf16[1024,3072]{1,0:T(8,128)(2,1)}, u32[]{:S(2)}, u32[]{:S(2)}) %collective-permute-start.2) | collective-permute-done | bytes 6291488 | tf_op jit(solution)/shard_map/ppermute | solution.py:771
  30.8 7.5 fusion
  41.5 33.5 %shard_map.171 = (bf16[4096,3072]{1,0:T(8,128)(2,1)}, bf16[4096,768]{1,0:T(8,128)(2,1)}, bf16[4096,256]{1,0:T(8,128)(2,1)}, bf16[4096,256]{1,0:T(8,128)(2,1)}, f32[4096,128]{1,0:T(8,128)}) custom-call(s32[3]{0:T(128)} %add_add_fusion.2.s_ref, bf16[1024,3072]{1,0:T(8,128)(2,1)} %x_ref.3, bf16[1024,3072]{1,0:T(8,128)(2,1)} %collective-permute-done.2.xb_ref, ...), custom_call_target="tpu_custom_call" | custom-call | flops 16106127360 | bytes 31457280 | tf_op jit(solution)/shard_map/pallas_call | solution.py:51
  75.0 17.7 %shard_map.172 = (bf16[4096,3072]{1,0:T(8,128)(2,1)}, bf16[4096,768]{1,0:T(8,128)(2,1)}) custom-call(s32[3]{0:T(128)} %add_add_fusion.2.s_ref, bf16[1024,3072]{1,0:T(8,128)(2,1)} %dy_ref.1, bf16[1024,3072]{1,0:T(8,128)(2,1)} %collective-permute-done.6.db_ref, bf16[3072,3072]{1,0:T(8,128)(2,1)} %rest_7_.1), custom_call_target="tpu_custom_call" | custom-call | flops 9663676416 | bytes 18874368 | tf_op jit(solution)/shard_map/pallas_call | solution.py:51
  92.7 26.7 %shard_map.173 = (bf16[2048,768]{1,0:T(8,128)(2,1)}, f32[2,8,2048]{2,1,0:T(8,128)}, f32[2,3,128,2048]{3,2,1,0:T(8,128)}) custom-call(s32[19]{0:T(128)} %pad_add_fusion.6.refs_0_, bf16[4096,768]{1,0:T(8,128)(2,1)} %get-tuple-element.100.refs_1_.rest_1_, bf16[4096,256]{1,0:T(8,128)(2,1)} %get-tuple-element.105.refs_2_.rest_2_, ...), custom_call_target="tpu_custom_call" | custom-call | flops 6442450944 | bytes 12582912 | tf_op jit(solution)/shard_map/pallas_call | solution.py:51
  132.3 26.7 %shard_map.174 = (bf16[4096,3072]{1,0:T(8,128)(2,1)}, bf16[4096,768]{1,0:T(8,128)(2,1)}, bf16[4096,256]{1,0:T(8,128)(2,1)}, bf16[4096,256]{1,0:T(8,128)(2,1)}, f32[4096,128]{1,0:T(8,128)}) custom-call(s32[3]{0:T(128)} %add_add_fusion.1.s_ref, ...), custom_call_target="tpu_custom_call", output_to_operand_aliasing={{0}: (9, {}), {1}: (10, {}), {2}: (11, {}), {3}: (12, {}), ... | custom-call | flops 12079595520 | bytes 23592960 | tf_op jit(solution)/shard_map/pallas_call | solution.py:51
  167.2 12.9 %shard_map.175 = (bf16[4096,3072]{1,0:T(8,128)(2,1)}, bf16[4096,768]{1,0:T(8,128)(2,1)}, bf16[4096,256]{1,0:T(8,128)(2,1)}, bf16[4096,256]{1,0:T(8,128)(2,1)}, f32[4096,128]{1,0:T(8,128)}) custom-call(s32[3]{0:T(128)} %add_add_fusion.s_ref, ...), custom_call_target="tpu_custom_call", output_to_operand_aliasing={{0}: (9, {}), {1}: (10, {}), {2}: (11, {}), {3}: (12, {}), ... | custom-call | flops 4026531840 | bytes 7864320 | tf_op jit(solution)/shard_map/pallas_call | solution.py:51
  180.1 70.8 %shard_map.176 = (bf16[4096,768]{1,0:T(8,128)(2,1)}, f32[2,8,4096]{2,1,0:T(8,128)}, bf16[2560,768]{1,0:T(8,128)(2,1)}, bf16[1024,768]{1,0:T(8,128)(2,1)}) custom-call(s32[35]{0:T(128)} %broadcast_select_fusion.refs_0_, bf16[4096,768]{1,0:T(8,128)(2,1)} %get-tuple-element.117.refs_1_.q_ref.qn_ref, bf16[4096,256]{1,0:T(8,128)(2,1)} %get-tuple-element.119.refs_2_.k_ref, ...), custom_call_target="tpu_custom_call" | custom-call | flops 25769803776 | bytes 50331648 | tf_op jit(solution)/shard_map/pallas_call | solution.py:51
  250.9 18.4 %shard_map.177 = (bf16[1536,768]{1,0:T(8,128)(2,1)}, bf16[1536,256]{1,0:T(8,128)(2,1)}, bf16[1536,256]{1,0:T(8,128)(2,1)}) custom-call(s32[1]{0:T(128)} %bitcast.2.s_ref, bf16[4096,3072]{1,0:T(8,128)(2,1)} %get-tuple-element.125.h_ref, bf16[3072,3072]{1,0:T(8,128)(2,1)} %rest_17_.1, bf16[3072,1024]{1,0:T(8,128)(2,1)} %rest_18_.1, ...), custom_call_target="tpu_custom_call" | custom-call | flops 12079595520 | bytes 23592960 | tf_op jit(solution)/shard_map/pallas_call | solution.py:51
  271.2 17.0 %shard_map.178 = (bf16[1536,768]{1,0:T(8,128)(2,1)}, f32[2,8,1536]{2,1,0:T(8,128)}) custom-call(s32[15]{0:T(128)} %pad_add_fusion.7.refs_0_, bf16[1536,768]{1,0:T(8,128)(2,1)} %get-tuple-element.126.refs_1_, bf16[1536,256]{1,0:T(8,128)(2,1)} %get-tuple-element.127.refs_2_, bf16[1536,256]{1,0:T(8,128)(2,1)} %get-tuple-element.128.refs_3_), custom_call_target="tpu_custom_call" | custom-call | flops 3623878656 | bytes 7077888 | tf_op jit(solution)/shard_map/pallas_call | solution.py:51
  288.2 15.2 %shard_map.179 = (bf16[4096,3072]{1,0:T(8,128)(2,1)}, bf16[4096,768]{1,0:T(8,128)(2,1)}) custom-call(s32[3]{0:T(128)} %add_add_fusion.1.s_ref, bf16[768,3072]{1,0:T(8,128)(2,1)} %collective-permute-done.10.da_ref, bf16[768,3072]{1,0:T(8,128)(2,1)} %collective-permute-done.11.db_ref, ...), custom_call_target="tpu_custom_call", output_to_operand_aliasing={{0}: (4, {}), {1}: (5, {})} | custom-call | flops 7247757312 | bytes 14155776 | tf_op jit(solution)/shard_map/pallas_call | solution.py:51
  310.9 7.8 shard_map.180
  318.8 75.6 %shard_map.181 = (bf16[4096,640]{1,0:T(8,128)(2,1)}, bf16[1024,640]{1,0:T(8,128)(2,1)}) custom-call(s32[2]{0:T(128)} %pad_add_fusion.5.s_ref, bf16[4096,768]{1,0:T(8,128)(2,1)} %get-tuple-element.117.refs_1_.q_ref.qn_ref, bf16[4096,768]{1,0:T(8,128)(2,1)} %get-tuple-element.137.do_ref.don_ref, ...), custom_call_target="tpu_custom_call" | custom-call | flops 36238786560 | bytes 70778880 | tf_op jit(solution)/shard_map/pallas_call | solution.py:51
  394.4 75.9 %shard_map.182 = (bf16[4096,640]{1,0:T(8,128)(2,1)}, bf16[1024,640]{1,0:T(8,128)(2,1)}) custom-call(s32[2]{0:T(128)} %pad_add_fusion.4.s_ref, bf16[4096,768]{1,0:T(8,128)(2,1)} %get-tuple-element.117.refs_1_.q_ref.qn_ref, bf16[4096,768]{1,0:T(8,128)(2,1)} %get-tuple-element.137.do_ref.don_ref, ...), custom_call_target="tpu_custom_call" | custom-call | flops 36238786560 | bytes 70778880 | tf_op jit(solution)/shard_map/pallas_call | solution.py:51
  470.3 54.4 %shard_map.183 = (f32[3072,3072]{1,0:T(8,128)}, f32[1536,3072]{1,0:T(8,128)}) custom-call(s32[2]{0:T(128)} %pad_add_fusion.3.s_ref, bf16[4096,768]{1,0:T(8,128)(2,1)} %get-tuple-element.123.o_ref.on_ref.oa_ref.rest_0_, bf16[1536,768]{1,0:T(8,128)(2,1)} %get-tuple-element.129.ob_ref, bf16[2560,768]{1,0:T(8,128)(2,1)} %collective-permute-done.13.oc_ref, ...), custom_call_target="tpu_custom_call" | custom-call | flops 38654705664 | bytes 75497472 | tf_op jit(solution)/shard_map/pallas_call | solution.py:51
  533.2 22.1 %collective-permute-done.14.rest_1_ = bf16[1024,768]{1,0:T(8,128)(2,1)S(1)} collective-permute-done((bf16[1024,768]{1,0:T(8,128)(2,1)}, bf16[1024,768]{1,0:T(8,128)(2,1)S(1)}, u32[]{:S(2)}, u32[]{:S(2)}) %collective-permute-start.14) | collective-permute-done | bytes 1572896 | tf_op jit(solution)/shard_map/ppermute | solution.py:771
  557.7 27.1 %shard_map.184 = bf16[1024,3072]{1,0:T(8,128)(2,1)} custom-call(s32[4]{0:T(128)} %pad_add_fusion.2.s_ref, bf16[1024,3072]{1,0:T(8,128)(2,1)} %x_ref.3, bf16[4096,768]{1,0:T(8,128)(2,1)} %get-tuple-element.123.o_ref.on_ref.oa_ref.rest_0_, bf16[1024,768]{1,0:T(8,128)(2,1)} %copy-done.4, bf16[2048,768]{1,0:T(8,128)(2,1)} %copy-done, ...), custom_call_target="tpu_custom_call" | custom-call | flops 19327352832 | bytes 37748736 | tf_op jit(solution)/shard_map/pallas_call | solution.py:51
  584.8 55.6 %collective-permute-done.16.gc_ref.ga_ref.rest_4_ = bf16[4096,640]{1,0:T(8,128)(2,1)} collective-permute-done((bf16[4096,640]{1,0:T(8,128)(2,1)}, bf16[4096,640]{1,0:T(8,128)(2,1)}, u32[]{:S(2)}, u32[]{:S(2)}) %collective-permute-start.16) | collective-permute-done | bytes 5242912 | tf_op jit(solution)/shard_map/ppermute | solution.py:768
  640.5 58.8 %shard_map.185 = (f32[3072,3072]{1,0:T(8,128)}, f32[3072,1024]{1,0:T(8,128)}, f32[3072,1024]{1,0:T(8,128)}, f32[3072,1792]{1,0:T(8,128)}, f32[3072,3072]{1,0:T(8,128)}, /*index=5*/bf16[1024,640]{1,0:T(8,128)(2,1)}) custom-call(s32[4]{0:T(128)} %pad_add_fusion.2.s_ref, bf16[4096,3072]{1,0:T(8,128)(2,1)} %get-tuple-element.125.h_ref, ...), custom_call_target="tpu_custom_call", output_to_operand_aliasing={{4}: (6, {})} | custom-call | flops 45097156608 | bytes 88080384 | tf_op jit(solution)/shard_map/pallas_call | solution.py:51
  700.6 114.5 %collective-permute-done.17.gb_ref.rest_5_ = bf16[4096,640]{1,0:T(8,128)(2,1)} collective-permute-done((bf16[4096,640]{1,0:T(8,128)(2,1)}, bf16[4096,640]{1,0:T(8,128)(2,1)}, u32[]{:S(2)}, u32[]{:S(2)}) %collective-permute-start.17) | collective-permute-done | bytes 5242912 | tf_op jit(solution)/shard_map/ppermute | solution.py:768
  815.1 28.5 %shard_map.186 = (f32[3072,3072]{1,0:T(8,128)}, f32[3072,1024]{1,0:T(8,128)}, f32[3072,1024]{1,0:T(8,128)}, f32[3072,768]{1,0:T(8,128)}) custom-call(s32[1]{0:T(128)} %bitcast.2.s_ref, bf16[4096,3072]{1,0:T(8,128)(2,1)} %get-tuple-element.125.h_ref, ...), custom_call_target="tpu_custom_call", output_to_operand_aliasing={{0}: (4, {}), {1}: (5, {}), {2}: (6, {})} | custom-call | flops 19327352832 | bytes 37748736 | tf_op jit(solution)/shard_map/pallas_call | solution.py:51
  846.1 14.3 %collective-permute-done.20.rest_3_ = bf16[1024,640]{1,0:T(8,128)(2,1)S(1)} collective-permute-done((bf16[1024,640]{1,0:T(8,128)(2,1)}, bf16[1024,640]{1,0:T(8,128)(2,1)S(1)}, u32[]{:S(2)}, u32[]{:S(2)}) %collective-permute-start.20) | collective-permute-done | bytes 1310752 | tf_op jit(solution)/shard_map/ppermute | solution.py:771
  866.1 53.8 %shard_map.187 = (bf16[1024,3072]{1,0:T(8,128)(2,1)}, f32[8,3072]{1,0:T(8,128)}, f32[3072,3072]{1,0:T(8,128)}, f32[3072,1024]{1,0:T(8,128)}, f32[3072,1024]{1,0:T(8,128)}) custom-call(s32[4]{0:T(128)} %pad_add_fusion.2.s_ref, bf16[1024,3072]{1,0:T(8,128)(2,1)} %x_ref.3, ...), custom_call_target="tpu_custom_call", output_to_operand_aliasing={{2}: (26, {}), {3}: (27, {}), {4}: (28, {})} | custom-call | flops 32212254720 | bytes 62914560 | tf_op jit(solution)/shard_map/pallas_call | solution.py:51
  923.3 8.3 shard_map.188
  (105 shorter events, 78.0 us)
Async XLA Ops:
  0.7 11.0 %collective-permute-start.2 = (bf16[1024,3072]{1,0:T(8,128)(2,1)}, bf16[1024,3072]{1,0:T(8,128)(2,1)}, u32[]{:S(2)}, u32[]{:S(2)}) collective-permute-start(bf16[1024,3072]{1,0:T(8,128)(2,1)} %x_ref.3), channel_id=1, source_target_pairs={{0,1},{1,0},{2,3},{3,2},{4,5},{5,4},{6,7},{7,6}} | collective-permute-start | bytes 18874376 | tf_op jit(solution)/shard_map/ppermute | solution.py:771
  11.6 63.4 %collective-permute-start.6 = (bf16[1024,3072]{1,0:T(8,128)(2,1)}, bf16[1024,3072]{1,0:T(8,128)(2,1)}, u32[]{:S(2)}, u32[]{:S(2)}) collective-permute-start(bf16[1024,3072]{1,0:T(8,128)(2,1)} %dy_ref.1), channel_id=1, source_target_pairs={{0,1},{1,0},{2,3},{3,2},{4,5},{5,4},{6,7},{7,6}} | collective-permute-start | bytes 18874376 | tf_op jit(solution)/shard_map/ppermute | solution.py:771
  16.9 4.2 collective-permute-start.4
  19.5 10.5 %collective-permute-start.3 = (s32[1024]{0:T(1024)S(1)}, s32[1024]{0:T(1024)S(1)}, u32[]{:S(2)}, u32[]{:S(2)}) collective-permute-start(s32[1024]{0:T(1024)S(1)} %copy-done.7), channel_id=1, source_target_pairs={{0,1},{1,0},{2,3},{3,2},{4,5},{5,4},{6,7},{7,6}} | collective-permute-start | bytes 12296 | tf_op jit(solution)/shard_map/ppermute | solution.py:771
  19.6 104.4 %collective-permute-start.1 = (bf16[768,3072]{1,0:T(8,128)(2,1)}, bf16[768,3072]{1,0:T(8,128)(2,1)}, u32[]{:S(2)}, u32[]{:S(2)}) collective-permute-start(bf16[768,3072]{1,0:T(8,128)(2,1)} %slice.28), channel_id=1, source_target_pairs={{0,2},{1,3},{2,0},{3,1},{4,6},{5,7},{6,4},{7,5}} | collective-permute-start | bytes 14155784 | tf_op jit(solution)/shard_map/ppermute | solution.py:768
  21.1 9.5 %collective-permute-start.5 = (s32[1024]{0:T(1024)S(1)}, s32[1024]{0:T(1024)S(1)}, u32[]{:S(2)}, u32[]{:S(2)}) collective-permute-start(s32[1024]{0:T(1024)S(1)} %collective-permute-done.4), channel_id=1, source_target_pairs={{0,1},{1,0},{2,3},{3,2},{4,5},{5,4},{6,7},{7,6}} | collective-permute-start | bytes 12296 | tf_op jit(solution)/shard_map/ppermute | solution.py:771
  124.0 8.3 collective-permute-start.7
  125.5 36.9 %collective-permute-start = (bf16[256,3072]{1,0:T(8,128)(2,1)S(1)}, bf16[256,3072]{1,0:T(8,128)(2,1)}, u32[]{:S(2)}, u32[]{:S(2)}) collective-permute-start(bf16[256,3072]{1,0:T(8,128)(2,1)S(1)} %slice.29), channel_id=1, source_target_pairs={{0,2},{1,3},{2,0},{3,1},{4,6},{5,7},{6,4},{7,5}} | collective-permute-start | bytes 4718600 | tf_op jit(solution)/shard_map/ppermute | solution.py:768
  162.5 106.9 %collective-permute-start.10 = (bf16[768,3072]{1,0:T(8,128)(2,1)}, bf16[768,3072]{1,0:T(8,128)(2,1)}, u32[]{:S(2)}, u32[]{:S(2)}) collective-permute-start(bf16[768,3072]{1,0:T(8,128)(2,1)} %slice.30), channel_id=1, source_target_pairs={{0,2},{1,3},{2,0},{3,1},{4,6},{5,7},{6,4},{7,5}} | collective-permute-start | bytes 14155784 | tf_op jit(solution)/shard_map/ppermute | solution.py:768
  269.3 18.9 %collective-permute-start.11 = (bf16[768,3072]{1,0:T(8,128)(2,1)}, bf16[768,3072]{1,0:T(8,128)(2,1)}, u32[]{:S(2)}, u32[]{:S(2)}) collective-permute-start(bf16[768,3072]{1,0:T(8,128)(2,1)} %collective-permute-done.10.da_ref), channel_id=1, source_target_pairs={{0,1},{1,0},{2,3},{3,2},{4,5},{5,4},{6,7},{7,6}} | collective-permute-start | bytes 14155784 | tf_op jit(solution)/shard_map/ppermute | solution.py:771
  269.4 37.0 %collective-permute-start.9 = (bf16[256,3072]{1,0:T(8,128)(2,1)}, bf16[256,3072]{1,0:T(8,128)(2,1)S(1)}, u32[]{:S(2)}, u32[]{:S(2)}) collective-permute-start(bf16[256,3072]{1,0:T(8,128)(2,1)} %slice.31), channel_id=1, source_target_pairs={{0,2},{1,3},{2,0},{3,1},{4,6},{5,7},{6,4},{7,5}} | collective-permute-start | bytes 4718600 | tf_op jit(solution)/shard_map/ppermute | solution.py:768
  308.3 162.0 %collective-permute-start.13 = (bf16[2560,768]{1,0:T(8,128)(2,1)}, bf16[2560,768]{1,0:T(8,128)(2,1)}, u32[]{:S(2)}, u32[]{:S(2)}) collective-permute-start(bf16[2560,768]{1,0:T(8,128)(2,1)} %get-tuple-element.143), channel_id=1, source_target_pairs={{0,2},{1,3},{2,0},{3,1},{4,6},{5,7},{6,4},{7,5}} | collective-permute-start | bytes 11796488 | tf_op jit(solution)/shard_map/ppermute | solution.py:768
  524.7 115.8 %collective-permute-start.18 = (f32[1536,3072]{1,0:T(8,128)}, f32[1536,3072]{1,0:T(8,128)}, u32[]{:S(2)}, u32[]{:S(2)}) collective-permute-start(f32[1536,3072]{1,0:T(8,128)} %get-tuple-element.146), channel_id=1, source_target_pairs={{0,1},{1,0},{2,3},{3,2},{4,5},{5,4},{6,7},{7,6}} | collective-permute-start | bytes 56623112 | tf_op jit(solution)/shard_map/ppermute | solution.py:771
  524.8 115.6 %collective-permute-start.16 = (bf16[4096,640]{1,0:T(8,128)(2,1)}, bf16[4096,640]{1,0:T(8,128)(2,1)}, u32[]{:S(2)}, u32[]{:S(2)}) collective-permute-start(bf16[4096,640]{1,0:T(8,128)(2,1)} %get-tuple-element.139.ga_ref.rest_0_), channel_id=1, source_target_pairs={{0,2},{1,3},{2,0},{3,1},{4,6},{5,7},{6,4},{7,5}} | collective-permute-start | bytes 15728648 | tf_op jit(solution)/shard_map/ppermute | solution.py:768
  526.0 29.3 %collective-permute-start.14 = (bf16[1024,768]{1,0:T(8,128)(2,1)}, bf16[1024,768]{1,0:T(8,128)(2,1)S(1)}, u32[]{:S(2)}, u32[]{:S(2)}) collective-permute-start(bf16[1024,768]{1,0:T(8,128)(2,1)} %get-tuple-element.148), channel_id=1, source_target_pairs={{0,1},{1,0},{2,3},{3,2},{4,5},{5,4},{6,7},{7,6}} | collective-permute-start | bytes 4718600 | tf_op jit(solution)/shard_map/ppermute | solution.py:771
  532.1 25.6 %collective-permute-start.15 = (bf16[1024,768]{1,0:T(8,128)(2,1)S(1)}, bf16[1024,768]{1,0:T(8,128)(2,1)}, u32[]{:S(2)}, u32[]{:S(2)}) collective-permute-start(bf16[1024,768]{1,0:T(8,128)(2,1)S(1)} %constant_dynamic-slice_fusion.1), channel_id=1, source_target_pairs={{0,1},{1,0},{2,3},{3,2},{4,5},{5,4},{6,7},{7,6}} | collective-permute-start | bytes 4718600 | tf_op jit(solution)/shard_map/ppermute | solution.py:771
  699.3 166.8 %collective-permute-start.23 = (f32[3072,1792]{1,0:T(8,128)}, f32[3072,1792]{1,0:T(8,128)}, u32[]{:S(2)}, u32[]{:S(2)}) collective-permute-start(f32[3072,1792]{1,0:T(8,128)} %get-tuple-element.152), channel_id=1, source_target_pairs={{0,1},{1,0},{2,3},{3,2},{4,5},{5,4},{6,7},{7,6}} | collective-permute-start | bytes 66060296 | tf_op jit(solution)/shard_map/ppermute | solution.py:771
  699.4 115.8 %collective-permute-start.17 = (bf16[4096,640]{1,0:T(8,128)(2,1)}, bf16[4096,640]{1,0:T(8,128)(2,1)}, u32[]{:S(2)}, u32[]{:S(2)}) collective-permute-start(bf16[4096,640]{1,0:T(8,128)(2,1)} %get-tuple-element.141.gb_ref.rest_1_), channel_id=1, source_target_pairs={{0,2},{1,3},{2,0},{3,1},{4,6},{5,7},{6,4},{7,5}} | collective-permute-start | bytes 15728648 | tf_op jit(solution)/shard_map/ppermute | solution.py:768
  843.6 79.7 %collective-permute-start.24 = (f32[3072,768]{1,0:T(8,128)}, f32[3072,768]{1,0:T(8,128)}, u32[]{:S(2)}, u32[]{:S(2)}) collective-permute-start(f32[3072,768]{1,0:T(8,128)} %get-tuple-element.157), channel_id=1, source_target_pairs={{0,1},{1,0},{2,3},{3,2},{4,5},{5,4},{6,7},{7,6}} | collective-permute-start | bytes 28311560 | tf_op jit(solution)/shard_map/ppermute | solution.py:771
  843.6 16.7 %collective-permute-start.20 = (bf16[1024,640]{1,0:T(8,128)(2,1)}, bf16[1024,640]{1,0:T(8,128)(2,1)S(1)}, u32[]{:S(2)}, u32[]{:S(2)}) collective-permute-start(bf16[1024,640]{1,0:T(8,128)(2,1)} %get-tuple-element.161), channel_id=1, source_target_pairs={{0,1},{1,0},{2,3},{3,2},{4,5},{5,4},{6,7},{7,6}} | collective-permute-start | bytes 3932168 | tf_op jit(solution)/shard_map/ppermute | solution.py:771
  844.1 18.2 %collective-permute-start.19 = (bf16[1024,640]{1,0:T(8,128)(2,1)}, bf16[1024,640]{1,0:T(8,128)(2,1)}, u32[]{:S(2)}, u32[]{:S(2)}) collective-permute-start(bf16[1024,640]{1,0:T(8,128)(2,1)} %get-tuple-element.160), channel_id=1, source_target_pairs={{0,1},{1,0},{2,3},{3,2},{4,5},{5,4},{6,7},{7,6}} | collective-permute-start | bytes 3932168 | tf_op jit(solution)/shard_map/ppermute | solution.py:771
  845.6 18.7 %collective-permute-start.22 = (bf16[1024,640]{1,0:T(8,128)(2,1)S(1)}, bf16[1024,640]{1,0:T(8,128)(2,1)}, u32[]{:S(2)}, u32[]{:S(2)}) collective-permute-start(bf16[1024,640]{1,0:T(8,128)(2,1)S(1)} %constant_dynamic-slice_fusion), channel_id=1, source_target_pairs={{0,1},{1,0},{2,3},{3,2},{4,5},{5,4},{6,7},{7,6}} | collective-permute-start | bytes 3932168 | tf_op jit(solution)/shard_map/ppermute | solution.py:771
  860.3 5.8 collective-permute-start.21
  922.1 9.5 %collective-permute-start.26 = (f32[3072]{0:T(1024)S(1)}, f32[3072]{0:T(1024)S(1)}, u32[]{:S(2)}, u32[]{:S(2)}) collective-permute-start(f32[3072]{0:T(1024)S(1)} %add.47), channel_id=1, source_target_pairs={{0,2},{1,3},{2,0},{3,1},{4,6},{5,7},{6,4},{7,5}} | collective-permute-start | bytes 36872 | tf_op jit(solution)/shard_map/ppermute | solution.py:768
  (15 other events, 147.8 us)

commit v8 on v7

--- a/solution.py
+++ b/solution.py
@@ -190,12 +190,12 @@
 
 
 def project_first(idx, h, ws, tabs, rows):
-    d = h.shape[1]
+    seq, d = h.shape
     widths = [w.shape[1] // 4 for w in ws]
     return call(projc_body, (rows // BLK,),
                 [pl.BlockSpec((BLK, d), row_map)] + [pl.BlockSpec((d, w), lambda i, s: (0, s[0])) for w in widths]
                 + [pl.BlockSpec((BLK, HEAD), row_map)] * 2,
-                [pl.BlockSpec((BLK, w), row_map) for w in widths], [sds(rows, w) for w in widths],
+                [pl.BlockSpec((BLK, w), row_map) for w in widths], [sds(seq, w) for w in widths],
                 [idx, h, *ws, *tabs], 2 * rows * d * sum(widths))
 
 
@@ -383,7 +383,7 @@
 
 def attn_fwd(kind, idx, q, k, v, extra=(), local=()):
     whole = q.shape[0]
-    seq = whole if kind == "rest" else whole // (2 if kind == "local" else 1)
+    seq = whole if kind == "rest" else whole // 2
     nkv = k.shape[1] // HEAD
 
     def half_map(g, s):
@@ -421,7 +421,6 @@
     last = pl.num_programs(0) - 1
     seq = k_ref.shape[0]
     m3 = GROUP * HB
-    sets = (sets[:5], sets[5:])
     cos_ref, sin_ref = tab.at[0], tab.at[1]
 
     def spots():
@@ -429,6 +428,9 @@
             for h in range(GROUP):
                 start = (b * GROUP + h) * HB
                 yield h, slice(b * HB, (b + 1) * HB), head_cols(h), slice(start, start + HB)
+
+    def pick(n):
+        return [ref.at[n] for ref in sets]
 
     def prepare(q_src, do_src, o_src, lse_src, dst):
         qa, da, q3t, do3t, dq3 = dst
@@ -466,48 +468,41 @@
                 dst[sl, HEAD:] = jnp.where(third == n, -1.0, 0.0).astype(BF)
 
         loop(seq // BLK, setup)
-        prepare(q_ref, do_ref, o_ref, lse_ref, sets[0])
+        prepare(q_ref, do_ref, o_ref, lse_ref, pick(0))
         for copy in copies:
             copy.wait()
 
-    def run(mine, other, tail_width):
+    def step(mine, rows, start, width, masked):
         qa, da, q3t, do3t, dq3 = mine
-
-        def step(rows, start, width, masked):
-            sl = pl.ds(pl.multiple_of(start, BLK), width)
-            s = mm_nt(qa[rows, :], ka[sl, :])
-            dp = mm_nt(da[rows, :], va[sl, :])
-            p = jnp.exp2(s * SCALE2)
-            if masked:
-                off = width - HB
-                tail = p[:, off:]
-                keep = down(tail.shape) % HB >= across(tail.shape)
-                tail = jnp.where(keep, tail, 0.0)
-                p = jnp.concatenate([p[:, :off], tail], axis=1) if off else tail
-            dvt[:, sl] += mm(do3t[:, rows], p.astype(BF))
-            dsv = (p * dp).astype(BF)
-            dkt[:, sl] += mm(q3t[:, rows], dsv)
-            dq3[rows, :] += mm(dsv, ka[sl, :HEAD])
-
-        def body(t):
-            step(slice(0, 2 * m3), t * 2 * BLK, 2 * BLK, False)
-
-        loop(i // 2, body)
-        start = (i // 2) * 2 * BLK
-        step(slice(0, m3), start, tail_width - HB, True)
-        prepare(qn_ref, don_ref, on_ref, lsen_ref, other)
-        step(slice(m3, 2 * m3), start, tail_width, True)
+        sl = pl.ds(pl.multiple_of(start, BLK), width)
+        s = mm_nt(qa[rows, :], ka[sl, :])
+        dp = mm_nt(da[rows, :], va[sl, :])
+        p = jnp.exp2(s * SCALE2)
+        if masked:
+            off = width - HB
+            tail = p[:, off:]
+            keep = down(tail.shape) % HB >= across(tail.shape)
+            tail = jnp.where(keep, tail, 0.0)
+            p = jnp.concatenate([p[:, :off], tail], axis=1) if off else tail
+        dvt[:, sl] += mm(do3t[:, rows], p.astype(BF))
+        dsv = (p * dp).astype(BF)
+        dkt[:, sl] += mm(q3t[:, rows], dsv)
+        dq3[rows, :] += mm(dsv, ka[sl, :HEAD])
+
+    par, start = i % 2, (i // 2) * 2 * BLK
+    loop(i // 2, lambda t: step(pick(par), slice(0, 2 * m3), t * 2 * BLK, 2 * BLK, False))
+
+    def tail_steps(n):
+        mine, width = pick(n), (n + 1) * BLK
+        step(mine, slice(0, m3), start, width - HB, True)
+        prepare(qn_ref, don_ref, on_ref, lsen_ref, pick(1 - n))
+        step(mine, slice(m3, 2 * m3), start, width, True)
         for h, src, cols, rows in spots():
             rsl = ds(i * BLK + src.start, HB)
-            out_ref[rsl, cols] = rotate(dq3[rows, :] * SCALE, cos_ref[rsl, :], -sin_ref[rsl, :]).astype(BF)
-
-    @pl.when(i % 2 == 0)
-    def _():
-        run(*sets, BLK)
-
-    @pl.when(i % 2 == 1)
-    def _():
-        run(*sets[::-1], 2 * BLK)
+            out_ref[rsl, cols] = rotate(mine[-1][rows, :] * SCALE, cos_ref[rsl, :], -sin_ref[rsl, :]).astype(BF)
+
+    pl.when(par == 0)(lambda: tail_steps(0))
+    pl.when(par == 1)(lambda: tail_steps(1))
 
     @pl.when(i == last)
     def _():
@@ -529,13 +524,13 @@
     for ahead in range(2):
         row_specs += [pl.BlockSpec((BLK, GW), lambda i, s, a=ahead: (jnp.minimum(i + a, nq - 1), s[1]))] * 3
         row_specs += [pl.BlockSpec((1, 8, BLK), lambda i, s, a=ahead: (s[1], 0, jnp.minimum(i + a, nq - 1)))]
-    one_set = [pltpu.VMEM((m3, PAIR), BF)] * 2 + [pltpu.VMEM((HEAD, m3), BF)] * 2 + [pltpu.VMEM((m3, HEAD), F32)]
+    two_sets = [pltpu.VMEM((2, m3, PAIR), BF)] * 2 + [pltpu.VMEM((2, HEAD, m3), BF)] * 2 + [pltpu.VMEM((2, m3, HEAD), F32)]
     return call(bwd_body, (nq,),
                 row_specs + [kspec] * 2 + [ANY] * 2,
                 [pl.BlockSpec((r, PW), first_row) for r in (seq, rows)], [sds(r, PW) for r in (seq, rows)],
                 [idx] + [q, do, o, lse] * 2 + [k, v, *tabs], GROUP * nq * (nq + 1) * BLK * BLK * PW,
                 scratch=[pltpu.VMEM((seq, PAIR), BF)] * 2 + [pltpu.VMEM((HEAD, seq), F32)] * 2
-                + [pltpu.VMEM((2, seq, HEAD), F32), pltpu.SemaphoreType.DMA((2,))] + one_set * 2)
+                + [pltpu.VMEM((2, seq, HEAD), F32), pltpu.SemaphoreType.DMA((2,))] + two_sets)
 
 
 def out_body(s_ref, x_ref, *rest):
@@ -578,7 +573,8 @@
 def dw_o(idx, oa, ob, oc, dy):
     seq, d = dy.shape
     hw = oa.shape[1]
-    o_specs = [pl.BlockSpec(o.shape, lambda i, p, s: (0, 0), pipeline_mode=pl.Buffered(1)) for o in (oa, ob, oc)]
+    o_specs = [pl.BlockSpec((r, hw), lambda i, p, s: (0, 0), pipeline_mode=pl.Buffered(1))
+               for r in (seq, seq - oc.shape[0], oc.shape[0])]
     return call(dwo_body, (d // BLK, 2),
                 o_specs + [pl.BlockSpec((seq, BLK), lambda i, p, s: (0, i))],
                 [pl.BlockSpec((hw, BLK), lambda i, p, s: (s[p], i)), pl.BlockSpec((hw, BLK), lambda i, p, s: (p, i))],
@@ -822,6 +818,7 @@
         def table(head, tasks):
             return jnp.concatenate([vec(*head, len(tasks)), jnp.asarray(tasks, jnp.int32).reshape(-1)])
 
+        c_tasks = table((j1, 0), tri).at[HEADER - 1].set(nh - 1)
         local = attn_fwd("local", after(table((j1, chip), tri), dbufs[1]), *bufs[1:4])
         rest_tasks = jnp.where(chip == 0, table((j1, 0), row_tasks(nh, 2 * nh) * 2).at[HEADER - 1].set(nh),
                                table((j1, 1), tri + square))
@@ -841,7 +838,7 @@
         qc, kc, vc = project_first(vec(j2, dep=(o,)), h_all, ws, tabs, first)
         dy2a = after(dy2a, qc)
         dy3a = near(dy2a)
-        oc = attn_fwd("first", table((j1, 0), tri[:-1]), qc, kc, vc)[0]
+        oc = attn_fwd("local", c_tasks, qc, kc, vc)[0]
 
         dbufs = dout(vec(j2 * hpr, j3 * hpr, j, dep=(oc,)), dy2a, dy3a, w_o, dbufs, seq)
         dy2b = after(dy2b, dbufs[1])
@@ -857,7 +854,7 @@
         gb1 = near(gb_pair)
 
         orv = after(orv, gb)
-        ox = jnp.where(chip == 0, jnp.concatenate([oc, orv[:BLK]]), orv[BLK:])
+        ox = jnp.where(chip == 0, jnp.concatenate([oc[:first], orv[:BLK]]), orv[BLK:])
         o3 = near(rows_of(ox, j1 % 2))
         wo_fin, wo_snd = dw_o(vec(j, j2, dep=(gb,)), o, oc, orv, dy_all)
         wo_rcv = near(wo_snd)

time: 943 us -> 940 us (level)
  transfers between devices with their start and end apart: 27 -> 27, of which waited for: 17 -> 18; matrix products, arithmetic and copies ran while one was open for 4% -> 4% of each run, Pallas kernels for 55% -> 55%
where the time goes in v8:
time: 940 us; the launch traced here: 929 us
  Pallas kernels  621 us (66%)
  waiting for transfers between devices  252 us (27%)
  local copies, waits for them, and re-layouts  23.9 us (3%)
  other arithmetic  20.9 us (2%)
  starting transfers between devices  9.52 us (1%)
    pallas_call x18, Pallas kernels, call(): pl.pallas_call(body, grid_spec=pltpu.PrefetchScalarGridSpec(num_scalar_pr...  621 us
    ppermute x9, waiting for transfers between devices, over(): return lax.ppermute(val, 'sp', cross)  189 us
    ppermute x18, waiting for transfers between devices, near(): return lax.ppermute(val, 'sp', pair)  63.6 us
  transfers between devices with their start and end apart: 27, of which 18 were waited for; matrix products, arithmetic and copies ran while one was open for 4% of the time, Pallas kernels for 55%

profile of v8, /device:TPU:0, one launch (start us, length us, event | category | flops | bytes accessed | tf_op | source)
XLA Modules:
  0.0 929.5 jit_solution(16722926082595106277)
XLA Ops:
  1.5 10.1 %collective-permute-done.2.xb_ref = bf16[1024,3072]{1,0:T(8,128)(2,1)} collective-permute-done((bf16[1024,3072]{1,0:T(8,128)(2,1)}, bf16[1024,3072]{1,0:T(8,128)(2,1)}, u32[]{:S(2)}, u32[]{:S(2)}) %collective-permute-start.2) | collective-permute-done | bytes 6291488 | tf_op jit(solution)/shard_map/ppermute | solution.py:767
  41.3 33.5 %shard_map.171 = (bf16[4096,3072]{1,0:T(8,128)(2,1)}, bf16[4096,768]{1,0:T(8,128)(2,1)}, bf16[4096,256]{1,0:T(8,128)(2,1)}, bf16[4096,256]{1,0:T(8,128)(2,1)}, f32[4096,128]{1,0:T(8,128)}) custom-call(s32[3]{0:T(128)} %add_add_fusion.2.s_ref, bf16[1024,3072]{1,0:T(8,128)(2,1)} %x_ref.3, bf16[1024,3072]{1,0:T(8,128)(2,1)} %collective-permute-done.2.xb_ref, ...), custom_call_target="tpu_custom_call" | custom-call | flops 16106127360 | bytes 31457280 | tf_op jit(solution)/shard_map/pallas_call | solution.py:51
  74.9 17.7 %shard_map.172 = (bf16[4096,3072]{1,0:T(8,128)(2,1)}, bf16[4096,768]{1,0:T(8,128)(2,1)}) custom-call(s32[3]{0:T(128)} %add_add_fusion.2.s_ref, bf16[1024,3072]{1,0:T(8,128)(2,1)} %dy_ref.1, bf16[1024,3072]{1,0:T(8,128)(2,1)} %collective-permute-done.6.db_ref, bf16[3072,3072]{1,0:T(8,128)(2,1)} %rest_7_.1), custom_call_target="tpu_custom_call" | custom-call | flops 9663676416 | bytes 18874368 | tf_op jit(solution)/shard_map/pallas_call | solution.py:51
  92.6 26.7 %shard_map.173 = (bf16[2048,768]{1,0:T(8,128)(2,1)}, f32[2,8,2048]{2,1,0:T(8,128)}, f32[2,3,128,2048]{3,2,1,0:T(8,128)}) custom-call(s32[19]{0:T(128)} %get-tuple-element.116.refs_0_, bf16[4096,768]{1,0:T(8,128)(2,1)} %get-tuple-element.112.refs_1_.rest_1_, bf16[4096,256]{1,0:T(8,128)(2,1)} %get-tuple-element.117.refs_2_.rest_2_, ...), custom_call_target="tpu_custom_call" | custom-call | flops 6442450944 | bytes 12582912 | tf_op jit(solution)/shard_map/pallas_call | solution.py:51
  132.3 26.7 %shard_map.174 = (bf16[4096,3072]{1,0:T(8,128)(2,1)}, bf16[4096,768]{1,0:T(8,128)(2,1)}, bf16[4096,256]{1,0:T(8,128)(2,1)}, bf16[4096,256]{1,0:T(8,128)(2,1)}, f32[4096,128]{1,0:T(8,128)}) custom-call(s32[3]{0:T(128)} %add_add_fusion.1.s_ref, ...), custom_call_target="tpu_custom_call", output_to_operand_aliasing={{0}: (9, {}), {1}: (10, {}), {2}: (11, {}), {3}: (12, {}), ... | custom-call | flops 12079595520 | bytes 23592960 | tf_op jit(solution)/shard_map/pallas_call | solution.py:51
  167.2 12.9 %shard_map.175 = (bf16[4096,3072]{1,0:T(8,128)(2,1)}, bf16[4096,768]{1,0:T(8,128)(2,1)}, bf16[4096,256]{1,0:T(8,128)(2,1)}, bf16[4096,256]{1,0:T(8,128)(2,1)}, f32[4096,128]{1,0:T(8,128)}) custom-call(s32[3]{0:T(128)} %add_add_fusion.s_ref, ...), custom_call_target="tpu_custom_call", output_to_operand_aliasing={{0}: (9, {}), {1}: (10, {}), {2}: (11, {}), {3}: (12, {}), ... | custom-call | flops 4026531840 | bytes 7864320 | tf_op jit(solution)/shard_map/pallas_call | solution.py:51
  180.1 60.9 %shard_map.176 = (bf16[4096,768]{1,0:T(8,128)(2,1)}, f32[2,8,4096]{2,1,0:T(8,128)}, bf16[2560,768]{1,0:T(8,128)(2,1)}, bf16[1024,768]{1,0:T(8,128)(2,1)}) custom-call(s32[35]{0:T(128)} %broadcast_select_fusion.refs_0_, bf16[4096,768]{1,0:T(8,128)(2,1)} %get-tuple-element.129.refs_1_.q_ref.qn_ref, bf16[4096,256]{1,0:T(8,128)(2,1)} %get-tuple-element.131.refs_2_.k_ref, ...), custom_call_target="tpu_custom_call" | custom-call | flops 25769803776 | bytes 50331648 | tf_op jit(solution)/shard_map/pallas_call | solution.py:51
  241.0 18.4 %shard_map.177 = (bf16[4096,768]{1,0:T(8,128)(2,1)}, bf16[4096,256]{1,0:T(8,128)(2,1)}, bf16[4096,256]{1,0:T(8,128)(2,1)}) custom-call(s32[1]{0:T(128)} %bitcast.2.s_ref, bf16[4096,3072]{1,0:T(8,128)(2,1)} %get-tuple-element.137.h_ref, bf16[3072,3072]{1,0:T(8,128)(2,1)} %rest_17_.1, bf16[3072,1024]{1,0:T(8,128)(2,1)} %rest_18_.1, ...), custom_call_target="tpu_custom_call" | custom-call | flops 12079595520 | bytes 23592960 | tf_op jit(solution)/shard_map/pallas_call | solution.py:51
  259.3 7.6 collective-permute-done.10.da_ref
  267.8 19.3 %shard_map.178 = (bf16[2048,768]{1,0:T(8,128)(2,1)}, f32[2,8,2048]{2,1,0:T(8,128)}, f32[2,3,128,2048]{3,2,1,0:T(8,128)}) custom-call(s32[19]{0:T(128)} %copy-done.10, bf16[4096,768]{1,0:T(8,128)(2,1)} %get-tuple-element.138.refs_1_, bf16[4096,256]{1,0:T(8,128)(2,1)} %get-tuple-element.139.refs_2_, bf16[4096,256]{1,0:T(8,128)(2,1)} %get-tuple-element.140.refs_3_), custom_call_target="tpu_custom_call" | custom-call | flops 6442450944 | bytes 12582912 | tf_op jit(solution)/shard_map/pallas_call | solution.py:51
  287.1 15.3 %shard_map.179 = (bf16[4096,3072]{1,0:T(8,128)(2,1)}, bf16[4096,768]{1,0:T(8,128)(2,1)}) custom-call(s32[3]{0:T(128)} %add_add_fusion.1.s_ref, bf16[768,3072]{1,0:T(8,128)(2,1)} %collective-permute-done.10.da_ref, bf16[768,3072]{1,0:T(8,128)(2,1)} %collective-permute-done.11.db_ref, ...), custom_call_target="tpu_custom_call", output_to_operand_aliasing={{0}: (4, {}), {1}: (5, {})} | custom-call | flops 7247757312 | bytes 14155776 | tf_op jit(solution)/shard_map/pallas_call | solution.py:51
  308.6 7.8 shard_map.180
  316.4 75.1 %shard_map.181 = (bf16[4096,640]{1,0:T(8,128)(2,1)}, bf16[1024,640]{1,0:T(8,128)(2,1)}) custom-call(s32[2]{0:T(128)} %pad_add_fusion.9.s_ref, bf16[4096,768]{1,0:T(8,128)(2,1)} %get-tuple-element.129.refs_1_.q_ref.qn_ref, bf16[4096,768]{1,0:T(8,128)(2,1)} %get-tuple-element.149.do_ref.don_ref, ...), custom_call_target="tpu_custom_call" | custom-call | flops 36238786560 | bytes 70778880 | tf_op jit(solution)/shard_map/pallas_call | solution.py:51
  391.6 75.6 %shard_map.182 = (bf16[4096,640]{1,0:T(8,128)(2,1)}, bf16[1024,640]{1,0:T(8,128)(2,1)}) custom-call(s32[2]{0:T(128)} %pad_add_fusion.8.s_ref, bf16[4096,768]{1,0:T(8,128)(2,1)} %get-tuple-element.129.refs_1_.q_ref.qn_ref, bf16[4096,768]{1,0:T(8,128)(2,1)} %get-tuple-element.149.do_ref.don_ref, ...), custom_call_target="tpu_custom_call" | custom-call | flops 36238786560 | bytes 70778880 | tf_op jit(solution)/shard_map/pallas_call | solution.py:51
  467.2 54.6 %shard_map.183 = (f32[3072,3072]{1,0:T(8,128)}, f32[1536,3072]{1,0:T(8,128)}) custom-call(s32[2]{0:T(128)} %pad_add_fusion.7.s_ref, bf16[4096,768]{1,0:T(8,128)(2,1)} %get-tuple-element.135.o_ref.on_ref.oa_ref.rest_0_, bf16[2048,768]{1,0:T(8,128)(2,1)} %get-tuple-element.141.ob_ref, bf16[2560,768]{1,0:T(8,128)(2,1)} %collective-permute-done.13.oc_ref, ...), custom_call_target="tpu_custom_call" | custom-call | flops 38654705664 | bytes 75497472 | tf_op jit(solution)/shard_map/pallas_call | solution.py:51
  530.9 21.5 %collective-permute-done.14.rest_1_ = bf16[1024,768]{1,0:T(8,128)(2,1)S(1)} collective-permute-done((bf16[1024,768]{1,0:T(8,128)(2,1)}, bf16[1024,768]{1,0:T(8,128)(2,1)S(1)}, u32[]{:S(2)}, u32[]{:S(2)}) %collective-permute-start.14) | collective-permute-done | bytes 1572896 | tf_op jit(solution)/shard_map/ppermute | solution.py:767
  554.8 27.1 %shard_map.184 = bf16[1024,3072]{1,0:T(8,128)(2,1)} custom-call(s32[4]{0:T(128)} %pad_add_fusion.6.s_ref, bf16[1024,3072]{1,0:T(8,128)(2,1)} %x_ref.3, bf16[4096,768]{1,0:T(8,128)(2,1)} %get-tuple-element.135.o_ref.on_ref.oa_ref.rest_0_, bf16[1024,768]{1,0:T(8,128)(2,1)} %copy-done.4, bf16[2048,768]{1,0:T(8,128)(2,1)} %copy-done, ...), custom_call_target="tpu_custom_call" | custom-call | flops 19327352832 | bytes 37748736 | tf_op jit(solution)/shard_map/pallas_call | solution.py:51
  581.9 55.6 %collective-permute-done.16.gc_ref.ga_ref.rest_4_ = bf16[4096,640]{1,0:T(8,128)(2,1)} collective-permute-done((bf16[4096,640]{1,0:T(8,128)(2,1)}, bf16[4096,640]{1,0:T(8,128)(2,1)}, u32[]{:S(2)}, u32[]{:S(2)}) %collective-permute-start.16) | collective-permute-done | bytes 5242912 | tf_op jit(solution)/shard_map/ppermute | solution.py:764
  637.6 58.8 %shard_map.185 = (f32[3072,3072]{1,0:T(8,128)}, f32[3072,1024]{1,0:T(8,128)}, f32[3072,1024]{1,0:T(8,128)}, f32[3072,1792]{1,0:T(8,128)}, f32[3072,3072]{1,0:T(8,128)}, /*index=5*/bf16[1024,640]{1,0:T(8,128)(2,1)}) custom-call(s32[4]{0:T(128)} %pad_add_fusion.6.s_ref, bf16[4096,3072]{1,0:T(8,128)(2,1)} %get-tuple-element.137.h_ref, ...), custom_call_target="tpu_custom_call", output_to_operand_aliasing={{4}: (6, {})} | custom-call | flops 45097156608 | bytes 88080384 | tf_op jit(solution)/shard_map/pallas_call | solution.py:51
  697.1 115.1 %collective-permute-done.17.gb_ref.rest_5_ = bf16[4096,640]{1,0:T(8,128)(2,1)} collective-permute-done((bf16[4096,640]{1,0:T(8,128)(2,1)}, bf16[4096,640]{1,0:T(8,128)(2,1)}, u32[]{:S(2)}, u32[]{:S(2)}) %collective-permute-start.17) | collective-permute-done | bytes 5242912 | tf_op jit(solution)/shard_map/ppermute | solution.py:764
  812.2 28.5 %shard_map.186 = (f32[3072,3072]{1,0:T(8,128)}, f32[3072,1024]{1,0:T(8,128)}, f32[3072,1024]{1,0:T(8,128)}, f32[3072,768]{1,0:T(8,128)}) custom-call(s32[1]{0:T(128)} %bitcast.2.s_ref, bf16[4096,3072]{1,0:T(8,128)(2,1)} %get-tuple-element.137.h_ref, ...), custom_call_target="tpu_custom_call", output_to_operand_aliasing={{0}: (4, {}), {1}: (5, {}), {2}: (6, {})} | custom-call | flops 19327352832 | bytes 37748736 | tf_op jit(solution)/shard_map/pallas_call | solution.py:51
  843.2 14.3 %collective-permute-done.20.rest_3_ = bf16[1024,640]{1,0:T(8,128)(2,1)S(1)} collective-permute-done((bf16[1024,640]{1,0:T(8,128)(2,1)}, bf16[1024,640]{1,0:T(8,128)(2,1)S(1)}, u32[]{:S(2)}, u32[]{:S(2)}) %collective-permute-start.20) | collective-permute-done | bytes 1310752 | tf_op jit(solution)/shard_map/ppermute | solution.py:767
  863.2 54.1 %shard_map.187 = (bf16[1024,3072]{1,0:T(8,128)(2,1)}, f32[8,3072]{1,0:T(8,128)}, f32[3072,3072]{1,0:T(8,128)}, f32[3072,1024]{1,0:T(8,128)}, f32[3072,1024]{1,0:T(8,128)}) custom-call(s32[4]{0:T(128)} %pad_add_fusion.6.s_ref, bf16[1024,3072]{1,0:T(8,128)(2,1)} %x_ref.3, ...), custom_call_target="tpu_custom_call", output_to_operand_aliasing={{2}: (26, {}), {3}: (27, {}), {4}: (28, {})} | custom-call | flops 32212254720 | bytes 62914560 | tf_op jit(solution)/shard_map/pallas_call | solution.py:51
  920.1 8.3 shard_map.188
  (106 shorter events, 82.4 us)
Async XLA Ops:
  0.7 11.0 %collective-permute-start.2 = (bf16[1024,3072]{1,0:T(8,128)(2,1)}, bf16[1024,3072]{1,0:T(8,128)(2,1)}, u32[]{:S(2)}, u32[]{:S(2)}) collective-permute-start(bf16[1024,3072]{1,0:T(8,128)(2,1)} %x_ref.3), channel_id=1, source_target_pairs={{0,1},{1,0},{2,3},{3,2},{4,5},{5,4},{6,7},{7,6}} | collective-permute-start | bytes 18874376 | tf_op jit(solution)/shard_map/ppermute | solution.py:767
  11.6 63.2 %collective-permute-start.6 = (bf16[1024,3072]{1,0:T(8,128)(2,1)}, bf16[1024,3072]{1,0:T(8,128)(2,1)}, u32[]{:S(2)}, u32[]{:S(2)}) collective-permute-start(bf16[1024,3072]{1,0:T(8,128)(2,1)} %dy_ref.1), channel_id=1, source_target_pairs={{0,1},{1,0},{2,3},{3,2},{4,5},{5,4},{6,7},{7,6}} | collective-permute-start | bytes 18874376 | tf_op jit(solution)/shard_map/ppermute | solution.py:767
  16.9 4.2 collective-permute-start.4
  19.5 10.5 %collective-permute-start.3 = (s32[1024]{0:T(1024)S(1)}, s32[1024]{0:T(1024)S(1)}, u32[]{:S(2)}, u32[]{:S(2)}) collective-permute-start(s32[1024]{0:T(1024)S(1)} %copy-done.7), channel_id=1, source_target_pairs={{0,1},{1,0},{2,3},{3,2},{4,5},{5,4},{6,7},{7,6}} | collective-permute-start | bytes 12296 | tf_op jit(solution)/shard_map/ppermute | solution.py:767
  19.6 104.4 %collective-permute-start.1 = (bf16[768,3072]{1,0:T(8,128)(2,1)}, bf16[768,3072]{1,0:T(8,128)(2,1)}, u32[]{:S(2)}, u32[]{:S(2)}) collective-permute-start(bf16[768,3072]{1,0:T(8,128)(2,1)} %slice.41), channel_id=1, source_target_pairs={{0,2},{1,3},{2,0},{3,1},{4,6},{5,7},{6,4},{7,5}} | collective-permute-start | bytes 14155784 | tf_op jit(solution)/shard_map/ppermute | solution.py:764
  21.1 9.4 %collective-permute-start.5 = (s32[1024]{0:T(1024)S(1)}, s32[1024]{0:T(1024)S(1)}, u32[]{:S(2)}, u32[]{:S(2)}) collective-permute-start(s32[1024]{0:T(1024)S(1)} %collective-permute-done.4), channel_id=1, source_target_pairs={{0,1},{1,0},{2,3},{3,2},{4,5},{5,4},{6,7},{7,6}} | collective-permute-start | bytes 12296 | tf_op jit(solution)/shard_map/ppermute | solution.py:767
  124.0 8.3 collective-permute-start.7
  125.5 36.9 %collective-permute-start = (bf16[256,3072]{1,0:T(8,128)(2,1)S(1)}, bf16[256,3072]{1,0:T(8,128)(2,1)}, u32[]{:S(2)}, u32[]{:S(2)}) collective-permute-start(bf16[256,3072]{1,0:T(8,128)(2,1)S(1)} %slice.42), channel_id=1, source_target_pairs={{0,2},{1,3},{2,0},{3,1},{4,6},{5,7},{6,4},{7,5}} | collective-permute-start | bytes 4718600 | tf_op jit(solution)/shard_map/ppermute | solution.py:764
  162.5 104.5 %collective-permute-start.10 = (bf16[768,3072]{1,0:T(8,128)(2,1)}, bf16[768,3072]{1,0:T(8,128)(2,1)}, u32[]{:S(2)}, u32[]{:S(2)}) collective-permute-start(bf16[768,3072]{1,0:T(8,128)(2,1)} %slice.43), channel_id=1, source_target_pairs={{0,2},{1,3},{2,0},{3,1},{4,6},{5,7},{6,4},{7,5}} | collective-permute-start | bytes 14155784 | tf_op jit(solution)/shard_map/ppermute | solution.py:764
  267.0 20.1 %collective-permute-start.11 = (bf16[768,3072]{1,0:T(8,128)(2,1)}, bf16[768,3072]{1,0:T(8,128)(2,1)}, u32[]{:S(2)}, u32[]{:S(2)}) collective-permute-start(bf16[768,3072]{1,0:T(8,128)(2,1)} %collective-permute-done.10.da_ref), channel_id=1, source_target_pairs={{0,1},{1,0},{2,3},{3,2},{4,5},{5,4},{6,7},{7,6}} | collective-permute-start | bytes 14155784 | tf_op jit(solution)/shard_map/ppermute | solution.py:767
  267.0 37.0 %collective-permute-start.9 = (bf16[256,3072]{1,0:T(8,128)(2,1)}, bf16[256,3072]{1,0:T(8,128)(2,1)S(1)}, u32[]{:S(2)}, u32[]{:S(2)}) collective-permute-start(bf16[256,3072]{1,0:T(8,128)(2,1)} %slice.44), channel_id=1, source_target_pairs={{0,2},{1,3},{2,0},{3,1},{4,6},{5,7},{6,4},{7,5}} | collective-permute-start | bytes 4718600 | tf_op jit(solution)/shard_map/ppermute | solution.py:764
  306.0 161.2 %collective-permute-start.13 = (bf16[2560,768]{1,0:T(8,128)(2,1)}, bf16[2560,768]{1,0:T(8,128)(2,1)}, u32[]{:S(2)}, u32[]{:S(2)}) collective-permute-start(bf16[2560,768]{1,0:T(8,128)(2,1)} %get-tuple-element.155), channel_id=1, source_target_pairs={{0,2},{1,3},{2,0},{3,1},{4,6},{5,7},{6,4},{7,5}} | collective-permute-start | bytes 11796488 | tf_op jit(solution)/shard_map/ppermute | solution.py:764
  521.8 115.8 %collective-permute-start.18 = (f32[1536,3072]{1,0:T(8,128)}, f32[1536,3072]{1,0:T(8,128)}, u32[]{:S(2)}, u32[]{:S(2)}) collective-permute-start(f32[1536,3072]{1,0:T(8,128)} %get-tuple-element.158), channel_id=1, source_target_pairs={{0,1},{1,0},{2,3},{3,2},{4,5},{5,4},{6,7},{7,6}} | collective-permute-start | bytes 56623112 | tf_op jit(solution)/shard_map/ppermute | solution.py:767
  521.9 115.7 %collective-permute-start.16 = (bf16[4096,640]{1,0:T(8,128)(2,1)}, bf16[4096,640]{1,0:T(8,128)(2,1)}, u32[]{:S(2)}, u32[]{:S(2)}) collective-permute-start(bf16[4096,640]{1,0:T(8,128)(2,1)} %get-tuple-element.151.ga_ref.rest_0_), channel_id=1, source_target_pairs={{0,2},{1,3},{2,0},{3,1},{4,6},{5,7},{6,4},{7,5}} | collective-permute-start | bytes 15728648 | tf_op jit(solution)/shard_map/ppermute | solution.py:764
  524.4 28.0 %collective-permute-start.14 = (bf16[1024,768]{1,0:T(8,128)(2,1)}, bf16[1024,768]{1,0:T(8,128)(2,1)S(1)}, u32[]{:S(2)}, u32[]{:S(2)}) collective-permute-start(bf16[1024,768]{1,0:T(8,128)(2,1)} %get-tuple-element.160), channel_id=1, source_target_pairs={{0,1},{1,0},{2,3},{3,2},{4,5},{5,4},{6,7},{7,6}} | collective-permute-start | bytes 4718600 | tf_op jit(solution)/shard_map/ppermute | solution.py:767
  529.8 25.0 %collective-permute-start.15 = (bf16[1024,768]{1,0:T(8,128)(2,1)S(1)}, bf16[1024,768]{1,0:T(8,128)(2,1)}, u32[]{:S(2)}, u32[]{:S(2)}) collective-permute-start(bf16[1024,768]{1,0:T(8,128)(2,1)S(1)} %constant_dynamic-slice_fusion.1), channel_id=1, source_target_pairs={{0,1},{1,0},{2,3},{3,2},{4,5},{5,4},{6,7},{7,6}} | collective-permute-start | bytes 4718600 | tf_op jit(solution)/shard_map/ppermute | solution.py:767
  696.4 166.8 %collective-permute-start.23 = (f32[3072,1792]{1,0:T(8,128)}, f32[3072,1792]{1,0:T(8,128)}, u32[]{:S(2)}, u32[]{:S(2)}) collective-permute-start(f32[3072,1792]{1,0:T(8,128)} %get-tuple-element.164), channel_id=1, source_target_pairs={{0,1},{1,0},{2,3},{3,2},{4,5},{5,4},{6,7},{7,6}} | collective-permute-start | bytes 66060296 | tf_op jit(solution)/shard_map/ppermute | solution.py:767
  696.5 115.8 %collective-permute-start.17 = (bf16[4096,640]{1,0:T(8,128)(2,1)}, bf16[4096,640]{1,0:T(8,128)(2,1)}, u32[]{:S(2)}, u32[]{:S(2)}) collective-permute-start(bf16[4096,640]{1,0:T(8,128)(2,1)} %get-tuple-element.153.gb_ref.rest_1_), channel_id=1, source_target_pairs={{0,2},{1,3},{2,0},{3,1},{4,6},{5,7},{6,4},{7,5}} | collective-permute-start | bytes 15728648 | tf_op jit(solution)/shard_map/ppermute | solution.py:764
  840.7 79.4 %collective-permute-start.24 = (f32[3072,768]{1,0:T(8,128)}, f32[3072,768]{1,0:T(8,128)}, u32[]{:S(2)}, u32[]{:S(2)}) collective-permute-start(f32[3072,768]{1,0:T(8,128)} %get-tuple-element.169), channel_id=1, source_target_pairs={{0,1},{1,0},{2,3},{3,2},{4,5},{5,4},{6,7},{7,6}} | collective-permute-start | bytes 28311560 | tf_op jit(solution)/shard_map/ppermute | solution.py:767
  840.7 16.7 %collective-permute-start.20 = (bf16[1024,640]{1,0:T(8,128)(2,1)}, bf16[1024,640]{1,0:T(8,128)(2,1)S(1)}, u32[]{:S(2)}, u32[]{:S(2)}) collective-permute-start(bf16[1024,640]{1,0:T(8,128)(2,1)} %get-tuple-element.173), channel_id=1, source_target_pairs={{0,1},{1,0},{2,3},{3,2},{4,5},{5,4},{6,7},{7,6}} | collective-permute-start | bytes 3932168 | tf_op jit(solution)/shard_map/ppermute | solution.py:767
  841.2 18.2 %collective-permute-start.19 = (bf16[1024,640]{1,0:T(8,128)(2,1)}, bf16[1024,640]{1,0:T(8,128)(2,1)}, u32[]{:S(2)}, u32[]{:S(2)}) collective-permute-start(bf16[1024,640]{1,0:T(8,128)(2,1)} %get-tuple-element.172), channel_id=1, source_target_pairs={{0,1},{1,0},{2,3},{3,2},{4,5},{5,4},{6,7},{7,6}} | collective-permute-start | bytes 3932168 | tf_op jit(solution)/shard_map/ppermute | solution.py:767
  842.6 18.7 %collective-permute-start.22 = (bf16[1024,640]{1,0:T(8,128)(2,1)S(1)}, bf16[1024,640]{1,0:T(8,128)(2,1)}, u32[]{:S(2)}, u32[]{:S(2)}) collective-permute-start(bf16[1024,640]{1,0:T(8,128)(2,1)S(1)} %constant_dynamic-slice_fusion), channel_id=1, source_target_pairs={{0,1},{1,0},{2,3},{3,2},{4,5},{5,4},{6,7},{7,6}} | collective-permute-start | bytes 3932168 | tf_op jit(solution)/shard_map/ppermute | solution.py:767
  857.4 5.8 collective-permute-start.21
  919.5 8.9 collective-permute-start.26
  (15 other events, 127.4 us)

commit v9 on v8

--- a/solution.py
+++ b/solution.py
@@ -23,7 +23,7 @@
 SCALE2 = SCALE * math.log2(math.e)
 BLK = 512
 HB = BLK // 2
-VMEM_LIMIT = 62 * 1024 * 1024
+VMEM_LIMIT = 65011712
 ANY = pl.BlockSpec(memory_space=pl.ANY)
 
 
@@ -261,6 +261,7 @@
     acc[...] = jnp.zeros_like(acc)
     stat[...] = jnp.zeros_like(stat)
     cur, old, den_row = 0, 1, 2
+    lse_ref[...] = jnp.zeros_like(lse_ref)
     if kind == "rest":
         @pl.when(s_ref[1] == 0)
         def _():
@@ -375,7 +376,6 @@
                     acc[h] = st_ref[0, h, :, ds(init2 * BLK, BLK)]
 
     loop(count, row)
-    lse_ref[0, GROUP:, :] = jnp.zeros((8 - GROUP, seq), F32)
     if kind == "rest":
         hi_ref[...] = o_ref[seq - hi_ref.shape[0]:, :]
         pair_ref[...] = o_ref[ds(s_ref[0] * pair_ref.shape[0], pair_ref.shape[0]), :]
@@ -534,9 +534,9 @@
 
 
 def out_body(s_ref, x_ref, *rest):
-    ops, weights, out_ref = rest[:4], rest[4:8], rest[8]
-    lhs = jnp.concatenate([r[...] for r in ops], axis=1)
-    rhs = jnp.concatenate([r[...] for r in weights], axis=0)
+    ops, out_ref = rest[:-1], rest[-1]
+    lhs = jnp.concatenate([r[...] for r in ops[:4]], axis=1)
+    rhs = jnp.concatenate([r[...] for r in ops[4:]], axis=0)
     out_ref[...] = (x_ref[...].astype(F32) + mm(lhs, rhs)).astype(BF)
 
 
@@ -641,7 +641,12 @@
 
 
 def dwgrp_body(s_ref, h_ref, ga_ref, gb_ref, *rest):
-    fq, fk, fv, snd, ht = rest[-5:]
+    fq, fk, fv, snd, g3, ht = rest[-6:]
+
+    @pl.when(pl.program_id(0) == 0)
+    def _():
+        g3[...] = gb_ref[ds(s_ref[1] * g3.shape[0], g3.shape[0]), :]
+
     ht[...] = h_ref[...].T
     lhs = ht[...]
     val = mm(lhs, gb_ref[:, :QK])
@@ -665,7 +670,8 @@
     return call(dwgrp_body, (d // HB,),
                 [pl.BlockSpec((seq, HB), col_map),
                  pl.BlockSpec((seq, HEAD), lambda i, s: (0, QK // HEAD), pipeline_mode=pl.Buffered(1)), gspec] + [ANY] * 3,
-                group_specs(HB) + [pl.BlockSpec((HB, sw), row_map)], [sds(*b.shape, F32) for b in bufs] + [sds(d, sw, F32)],
+                group_specs(HB) + [pl.BlockSpec((HB, sw), row_map), pl.BlockSpec((seq // 4, PW), first_row)],
+                [sds(*b.shape, F32) for b in bufs] + [sds(d, sw, F32), sds(seq // 4, PW)],
                 [idx, h, ga, gb, *bufs], 2 * seq * d * sw, scratch=[pltpu.VMEM((HB, seq), BF)],
                 aliases={4 + n: n for n in range(3)})
 
@@ -679,7 +685,7 @@
 
 def place(idx, rcv, bufs):
     d, w = rcv.shape
-    bm = 2 * BLK
+    bm = BLK
     return call(place_body, (d // bm,), [pl.BlockSpec((bm, w), row_map)] + [ANY] * 3, group_specs(bm),
                 [sds(*b.shape, F32) for b in bufs], [idx, rcv, *bufs], d * w, aliases={2 + n: n for n in range(3)})
 
@@ -766,6 +772,9 @@
     def near(val):
         return lax.ppermute(val, 'sp', pair)
 
+    def both(val):
+        return lax.ppermute(val, 'sp', [(a, a ^ 3) for a in range(sp)])
+
     def after(val, *deps):
         return lax.optimization_barrier((val,) + deps)[0]
 
@@ -808,7 +817,7 @@
 
         dya, dyb = dy[:cut], dy[cut:]
         bufs = project(vec(j * bpr, j1 * bpr, j, dep=(dya, dyb)), x, x1, gain_f, ws, tabs, None, seq)
-        dbufs = dout(vec(j * bpr, j1 * bpr, j, dep=(bufs[1],)), dy, dy1, w_o, None, seq)
+        dbufs = dout(vec(j * bpr, j1 * bpr, j, dep=bufs), dy, dy1, w_o, None, seq)
 
         chip, nh = j // 2, seq // BLK // 2
         tri = row_tasks(0, nh)
@@ -819,15 +828,15 @@
             return jnp.concatenate([vec(*head, len(tasks)), jnp.asarray(tasks, jnp.int32).reshape(-1)])
 
         c_tasks = table((j1, 0), tri).at[HEADER - 1].set(nh - 1)
-        local = attn_fwd("local", after(table((j1, chip), tri), dbufs[1]), *bufs[1:4])
+        local = attn_fwd("local", after(table((j1, chip), tri), *dbufs), *bufs[1:4])
         rest_tasks = jnp.where(chip == 0, table((j1, 0), row_tasks(nh, 2 * nh) * 2).at[HEADER - 1].set(nh),
                                table((j1, 1), tri + square))
 
-        x2a = after(x2a, local[0])
+        x2a = after(x2a, *local)
         dy2a = over(after(dya, x2a))
         x3a = near(x2a)
         bufs = project(vec(j2 * hpr, j3 * hpr, j), x2a, x3a, gain_f, ws, tabs, bufs, seq)
-        x2b = after(x2b, bufs[1])
+        x2b = after(x2b, *bufs)
         dy2b = over(after(dyb, x2b))
         x3b = near(x2b)
         bufs = project(vec((j2 + 1) * hpr - 1, (j3 + 1) * hpr - 1, j), x2b, x3b, gain_f, ws, tabs, bufs, seq)
@@ -841,7 +850,7 @@
         oc = attn_fwd("local", c_tasks, qc, kc, vc)[0]
 
         dbufs = dout(vec(j2 * hpr, j3 * hpr, j, dep=(oc,)), dy2a, dy3a, w_o, dbufs, seq)
-        dy2b = after(dy2b, dbufs[1])
+        dy2b = after(dy2b, *dbufs)
         dy3b = near(dy2b)
         dbufs = dout(vec((j2 + 1) * hpr - 1, (j3 + 1) * hpr - 1, j), dy2b, dy3b, w_o, dbufs, seq)
         dy_all, do = dbufs
@@ -854,7 +863,9 @@
         gb1 = near(gb_pair)
 
         orv = after(orv, gb)
-        ox = jnp.where(chip == 0, jnp.concatenate([oc[:first], orv[:BLK]]), orv[BLK:])
+        shifted = jnp.concatenate([orv[:first], orv[:BLK]])
+        upper = down(oc.shape) >= first
+        ox = jnp.where(chip == 0, jnp.where(upper, shifted, oc), orv[BLK:])
         o3 = near(rows_of(ox, j1 % 2))
         wo_fin, wo_snd = dw_o(vec(j, j2, dep=(gb,)), o, oc, orv, dy_all)
         wo_rcv = near(wo_snd)
@@ -865,14 +876,13 @@
         ga3 = near(g3)
 
         gb2 = after(gb2, snd)
-        gb3 = near(rows_of(gb2, j1))
-        fq, fk, fv, snd_b = dw_group(vec(j2), h_all, ga2, gb2, (fq, fk, fv))
+        fq, fk, fv, snd_b, g3b = dw_group(vec(j2, j1), h_all, ga2, gb2, (fq, fk, fv))
+        gb3 = near(g3b)
         rcv_b = near(snd_b)
         grad_x, dg, fq, fk, fv = dx_call(vec(*dev, dep=(snd_b,)), x, dy, gain_f, inv,
                                          (ga, gb, ga1, gb1, ga2, gb2, ga3, gb3), ws, rcv, (fq, fk, fv))
         dg = jnp.sum(dg, axis=0)
-        dg = dg + near(dg)
-        dg = dg + over(dg)
+        dg = (dg + near(dg)) + (over(dg) + both(dg))
         fq, fk, fv = place(vec(j3), rcv_b, (fq, fk, fv))
         return result, grad_x, fq, fk, fv, wo_fin, dg
 

time: 940 us -> 940 us (level)
  transfers between devices with their start and end apart: 27 -> 28, of which waited for: 18 -> 17; matrix products, arithmetic and copies ran while one was open for 4% -> 4% of each run, Pallas kernels for 55% -> 55%
where the time goes in v9:
time: 940 us; the launch traced here: 930 us
  Pallas kernels  622 us (66%)
  waiting for transfers between devices  251 us (27%)
  other arithmetic  22.7 us (2%)
  local copies, waits for them, and re-layouts  21.5 us (2%)
  starting transfers between devices  10.5 us (1%)
    pallas_call x18, Pallas kernels, call(): pl.pallas_call(body, grid_spec=pltpu.PrefetchScalarGridSpec(num_scalar_pr...  622 us
    ppermute x9, waiting for transfers between devices, over(): return lax.ppermute(val, 'sp', cross)  189 us
    ppermute x18, waiting for transfers between devices, near(): return lax.ppermute(val, 'sp', pair)  62.8 us
  transfers between devices with their start and end apart: 28, of which 17 were waited for; matrix products, arithmetic and copies ran while one was open for 4% of the time, Pallas kernels for 55%

profile of v9, /device:TPU:0, one launch (start us, length us, event | category | flops | bytes accessed | tf_op | source)
XLA Modules:
  0.0 929.5 jit_solution(4932800623199907637)
XLA Ops:
  1.5 10.1 %collective-permute-done.2.xb_ref = bf16[1024,3072]{1,0:T(8,128)(2,1)} collective-permute-done((bf16[1024,3072]{1,0:T(8,128)(2,1)}, bf16[1024,3072]{1,0:T(8,128)(2,1)}, u32[]{:S(2)}, u32[]{:S(2)}) %collective-permute-start.2) | collective-permute-done | bytes 6291488 | tf_op jit(solution)/shard_map/ppermute | solution.py:773
  41.3 33.5 %shard_map.171 = (bf16[4096,3072]{1,0:T(8,128)(2,1)}, bf16[4096,768]{1,0:T(8,128)(2,1)}, bf16[4096,256]{1,0:T(8,128)(2,1)}, bf16[4096,256]{1,0:T(8,128)(2,1)}, f32[4096,128]{1,0:T(8,128)}) custom-call(s32[3]{0:T(128)} %add_add_fusion.3.s_ref, bf16[1024,3072]{1,0:T(8,128)(2,1)} %x_ref.3, bf16[1024,3072]{1,0:T(8,128)(2,1)} %collective-permute-done.2.xb_ref, ...), custom_call_target="tpu_custom_call" | custom-call | flops 16106127360 | bytes 31457280 | tf_op jit(solution)/shard_map/pallas_call | solution.py:51
  74.9 17.7 %shard_map.172 = (bf16[4096,3072]{1,0:T(8,128)(2,1)}, bf16[4096,768]{1,0:T(8,128)(2,1)}) custom-call(s32[3]{0:T(128)} %add_add_fusion.3.s_ref, bf16[1024,3072]{1,0:T(8,128)(2,1)} %dy_ref.1, bf16[1024,3072]{1,0:T(8,128)(2,1)} %collective-permute-done.6.db_ref, bf16[3072,3072]{1,0:T(8,128)(2,1)} %rest_7_.1), custom_call_target="tpu_custom_call" | custom-call | flops 9663676416 | bytes 18874368 | tf_op jit(solution)/shard_map/pallas_call | solution.py:51
  92.6 26.9 %shard_map.173 = (bf16[2048,768]{1,0:T(8,128)(2,1)}, f32[2,8,2048]{2,1,0:T(8,128)}, f32[2,3,128,2048]{3,2,1,0:T(8,128)}) custom-call(s32[19]{0:T(128)} %get-tuple-element.122.refs_0_, bf16[4096,768]{1,0:T(8,128)(2,1)} %get-tuple-element.114.refs_1_.rest_1_, bf16[4096,256]{1,0:T(8,128)(2,1)} %get-tuple-element.115.refs_2_.rest_2_, ...), custom_call_target="tpu_custom_call" | custom-call | flops 6442450944 | bytes 12582912 | tf_op jit(solution)/shard_map/pallas_call | solution.py:51
  132.3 26.5 %shard_map.174 = (bf16[4096,3072]{1,0:T(8,128)(2,1)}, bf16[4096,768]{1,0:T(8,128)(2,1)}, bf16[4096,256]{1,0:T(8,128)(2,1)}, bf16[4096,256]{1,0:T(8,128)(2,1)}, f32[4096,128]{1,0:T(8,128)}) custom-call(s32[3]{0:T(128)} %add_add_fusion.2.s_ref, ...), custom_call_target="tpu_custom_call", output_to_operand_aliasing={{0}: (9, {}), {1}: (10, {}), {2}: (11, {}), {3}: (12, {}), ... | custom-call | flops 12079595520 | bytes 23592960 | tf_op jit(solution)/shard_map/pallas_call | solution.py:51
  167.2 12.9 %shard_map.175 = (bf16[4096,3072]{1,0:T(8,128)(2,1)}, bf16[4096,768]{1,0:T(8,128)(2,1)}, bf16[4096,256]{1,0:T(8,128)(2,1)}, bf16[4096,256]{1,0:T(8,128)(2,1)}, f32[4096,128]{1,0:T(8,128)}) custom-call(s32[3]{0:T(128)} %add_add_fusion.1.s_ref, ...), custom_call_target="tpu_custom_call", output_to_operand_aliasing={{0}: (9, {}), {1}: (10, {}), {2}: (11, {}), {3}: (12, {}), ... | custom-call | flops 4026531840 | bytes 7864320 | tf_op jit(solution)/shard_map/pallas_call | solution.py:51
  180.1 60.5 %shard_map.176 = (bf16[4096,768]{1,0:T(8,128)(2,1)}, f32[2,8,4096]{2,1,0:T(8,128)}, bf16[2560,768]{1,0:T(8,128)(2,1)}, bf16[1024,768]{1,0:T(8,128)(2,1)}) custom-call(s32[35]{0:T(128)} %broadcast_select_fusion.refs_0_, bf16[4096,768]{1,0:T(8,128)(2,1)} %get-tuple-element.133.refs_1_.q_ref.qn_ref, bf16[4096,256]{1,0:T(8,128)(2,1)} %get-tuple-element.135.refs_2_.k_ref, ...), custom_call_target="tpu_custom_call" | custom-call | flops 25769803776 | bytes 50331648 | tf_op jit(solution)/shard_map/pallas_call | solution.py:51
  240.7 18.3 %shard_map.177 = (bf16[4096,768]{1,0:T(8,128)(2,1)}, bf16[4096,256]{1,0:T(8,128)(2,1)}, bf16[4096,256]{1,0:T(8,128)(2,1)}) custom-call(s32[1]{0:T(128)} %bitcast.2.s_ref, bf16[4096,3072]{1,0:T(8,128)(2,1)} %get-tuple-element.139.h_ref, bf16[3072,3072]{1,0:T(8,128)(2,1)} %rest_17_.1, bf16[3072,1024]{1,0:T(8,128)(2,1)} %rest_18_.1, ...), custom_call_target="tpu_custom_call" | custom-call | flops 12079595520 | bytes 23592960 | tf_op jit(solution)/shard_map/pallas_call | solution.py:51
  259.0 8.0 collective-permute-done.10.da_ref
  267.9 19.3 %shard_map.178 = (bf16[2048,768]{1,0:T(8,128)(2,1)}, f32[2,8,2048]{2,1,0:T(8,128)}, f32[2,3,128,2048]{3,2,1,0:T(8,128)}) custom-call(s32[19]{0:T(128)} %copy-done.10, bf16[4096,768]{1,0:T(8,128)(2,1)} %get-tuple-element.140.refs_1_, bf16[4096,256]{1,0:T(8,128)(2,1)} %get-tuple-element.141.refs_2_, bf16[4096,256]{1,0:T(8,128)(2,1)} %get-tuple-element.142.refs_3_), custom_call_target="tpu_custom_call" | custom-call | flops 6442450944 | bytes 12582912 | tf_op jit(solution)/shard_map/pallas_call | solution.py:51
  287.2 15.4 %shard_map.179 = (bf16[4096,3072]{1,0:T(8,128)(2,1)}, bf16[4096,768]{1,0:T(8,128)(2,1)}) custom-call(s32[3]{0:T(128)} %add_add_fusion.2.s_ref, bf16[768,3072]{1,0:T(8,128)(2,1)} %collective-permute-done.10.da_ref, bf16[768,3072]{1,0:T(8,128)(2,1)} %collective-permute-done.11.db_ref, ...), custom_call_target="tpu_custom_call", output_to_operand_aliasing={{0}: (4, {}), {1}: (5, {})} | custom-call | flops 7247757312 | bytes 14155776 | tf_op jit(solution)/shard_map/pallas_call | solution.py:51
  307.6 7.9 shard_map.180
  315.4 75.1 %shard_map.181 = (bf16[4096,640]{1,0:T(8,128)(2,1)}, bf16[1024,640]{1,0:T(8,128)(2,1)}) custom-call(s32[2]{0:T(128)} %pad_add_fusion.9.s_ref, bf16[4096,768]{1,0:T(8,128)(2,1)} %get-tuple-element.133.refs_1_.q_ref.qn_ref, bf16[4096,768]{1,0:T(8,128)(2,1)} %get-tuple-element.150.do_ref.don_ref, ...), custom_call_target="tpu_custom_call" | custom-call | flops 36238786560 | bytes 70778880 | tf_op jit(solution)/shard_map/pallas_call | solution.py:51
  390.5 75.8 %shard_map.182 = (bf16[4096,640]{1,0:T(8,128)(2,1)}, bf16[1024,640]{1,0:T(8,128)(2,1)}) custom-call(s32[2]{0:T(128)} %pad_add_fusion.8.s_ref, bf16[4096,768]{1,0:T(8,128)(2,1)} %get-tuple-element.133.refs_1_.q_ref.qn_ref, bf16[4096,768]{1,0:T(8,128)(2,1)} %get-tuple-element.150.do_ref.don_ref, ...), custom_call_target="tpu_custom_call" | custom-call | flops 36238786560 | bytes 70778880 | tf_op jit(solution)/shard_map/pallas_call | solution.py:51
  466.4 54.6 %shard_map.183 = (f32[3072,3072]{1,0:T(8,128)}, f32[1536,3072]{1,0:T(8,128)}) custom-call(s32[2]{0:T(128)} %pad_add_fusion.7.s_ref, bf16[4096,768]{1,0:T(8,128)(2,1)} %get-tuple-element.137.o_ref.on_ref.oa_ref.rest_0_, bf16[2048,768]{1,0:T(8,128)(2,1)} %get-tuple-element.143.ob_ref, bf16[2560,768]{1,0:T(8,128)(2,1)} %collective-permute-done.13.oc_ref, ...), custom_call_target="tpu_custom_call" | custom-call | flops 38654705664 | bytes 75497472 | tf_op jit(solution)/shard_map/pallas_call | solution.py:51
  531.3 20.3 %collective-permute-done.14.rest_1_ = bf16[1024,768]{1,0:T(8,128)(2,1)S(1)} collective-permute-done((bf16[1024,768]{1,0:T(8,128)(2,1)}, bf16[1024,768]{1,0:T(8,128)(2,1)S(1)}, u32[]{:S(2)}, u32[]{:S(2)}) %collective-permute-start.14) | collective-permute-done | bytes 1572896 | tf_op jit(solution)/shard_map/ppermute | solution.py:773
  554.0 27.1 %shard_map.184 = bf16[1024,3072]{1,0:T(8,128)(2,1)} custom-call(s32[4]{0:T(128)} %pad_add_fusion.6.s_ref, bf16[1024,3072]{1,0:T(8,128)(2,1)} %x_ref.3, bf16[4096,768]{1,0:T(8,128)(2,1)} %get-tuple-element.137.o_ref.on_ref.oa_ref.rest_0_, bf16[1024,768]{1,0:T(8,128)(2,1)} %copy-done.4, bf16[2048,768]{1,0:T(8,128)(2,1)} %copy-done, ...), custom_call_target="tpu_custom_call" | custom-call | flops 19327352832 | bytes 37748736 | tf_op jit(solution)/shard_map/pallas_call | solution.py:51
  581.1 55.6 %collective-permute-done.16.gc_ref.ga_ref.rest_4_ = bf16[4096,640]{1,0:T(8,128)(2,1)} collective-permute-done((bf16[4096,640]{1,0:T(8,128)(2,1)}, bf16[4096,640]{1,0:T(8,128)(2,1)}, u32[]{:S(2)}, u32[]{:S(2)}) %collective-permute-start.16) | collective-permute-done | bytes 5242912 | tf_op jit(solution)/shard_map/ppermute | solution.py:770
  636.8 58.8 %shard_map.185 = (f32[3072,3072]{1,0:T(8,128)}, f32[3072,1024]{1,0:T(8,128)}, f32[3072,1024]{1,0:T(8,128)}, f32[3072,1792]{1,0:T(8,128)}, f32[3072,3072]{1,0:T(8,128)}, /*index=5*/bf16[1024,640]{1,0:T(8,128)(2,1)}) custom-call(s32[4]{0:T(128)} %pad_add_fusion.6.s_ref, bf16[4096,3072]{1,0:T(8,128)(2,1)} %get-tuple-element.139.h_ref, ...), custom_call_target="tpu_custom_call", output_to_operand_aliasing={{4}: (6, {})} | custom-call | flops 45097156608 | bytes 88080384 | tf_op jit(solution)/shard_map/pallas_call | solution.py:51
  696.8 114.6 %collective-permute-done.17.gb_ref.rest_5_ = bf16[4096,640]{1,0:T(8,128)(2,1)} collective-permute-done((bf16[4096,640]{1,0:T(8,128)(2,1)}, bf16[4096,640]{1,0:T(8,128)(2,1)}, u32[]{:S(2)}, u32[]{:S(2)}) %collective-permute-start.17) | collective-permute-done | bytes 5242912 | tf_op jit(solution)/shard_map/ppermute | solution.py:770
  811.4 29.3 %shard_map.186 = (f32[3072,3072]{1,0:T(8,128)}, f32[3072,1024]{1,0:T(8,128)}, f32[3072,1024]{1,0:T(8,128)}, f32[3072,768]{1,0:T(8,128)}, bf16[1024,640]{1,0:T(8,128)(2,1)}) custom-call(s32[2]{0:T(128)} %pad_add_fusion.10.s_ref, bf16[4096,3072]{1,0:T(8,128)(2,1)} %get-tuple-element.139.h_ref, ...), custom_call_target="tpu_custom_call", output_to_operand_aliasing={{0}: (4, {}), {1}: (5, {}), {2}: (6, {})} | custom-call | flops 19327352832 | bytes 37748736 | tf_op jit(solution)/shard_map/pallas_call | solution.py:51
  841.7 15.7 %collective-permute-done.20.rest_3_ = bf16[1024,640]{1,0:T(8,128)(2,1)S(1)} collective-permute-done((bf16[1024,640]{1,0:T(8,128)(2,1)}, bf16[1024,640]{1,0:T(8,128)(2,1)S(1)}, u32[]{:S(2)}, u32[]{:S(2)}) %collective-permute-start.20) | collective-permute-done | bytes 1310752 | tf_op jit(solution)/shard_map/ppermute | solution.py:773
  863.2 54.0 %shard_map.187 = (bf16[1024,3072]{1,0:T(8,128)(2,1)}, f32[8,3072]{1,0:T(8,128)}, f32[3072,3072]{1,0:T(8,128)}, f32[3072,1024]{1,0:T(8,128)}, f32[3072,1024]{1,0:T(8,128)}) custom-call(s32[4]{0:T(128)} %pad_add_fusion.6.s_ref, bf16[1024,3072]{1,0:T(8,128)(2,1)} %x_ref.3, ...), custom_call_target="tpu_custom_call", output_to_operand_aliasing={{2}: (26, {}), {3}: (27, {}), {4}: (28, {})} | custom-call | flops 32212254720 | bytes 62914560 | tf_op jit(solution)/shard_map/pallas_call | solution.py:51
  920.0 8.6 shard_map.188
  (108 shorter events, 81.6 us)
Async XLA Ops:
  0.7 11.0 %collective-permute-start.2 = (bf16[1024,3072]{1,0:T(8,128)(2,1)}, bf16[1024,3072]{1,0:T(8,128)(2,1)}, u32[]{:S(2)}, u32[]{:S(2)}) collective-permute-start(bf16[1024,3072]{1,0:T(8,128)(2,1)} %x_ref.3), channel_id=1, source_target_pairs={{0,1},{1,0},{2,3},{3,2},{4,5},{5,4},{6,7},{7,6}} | collective-permute-start | bytes 18874376 | tf_op jit(solution)/shard_map/ppermute | solution.py:773
  11.6 63.2 %collective-permute-start.6 = (bf16[1024,3072]{1,0:T(8,128)(2,1)}, bf16[1024,3072]{1,0:T(8,128)(2,1)}, u32[]{:S(2)}, u32[]{:S(2)}) collective-permute-start(bf16[1024,3072]{1,0:T(8,128)(2,1)} %dy_ref.1), channel_id=1, source_target_pairs={{0,1},{1,0},{2,3},{3,2},{4,5},{5,4},{6,7},{7,6}} | collective-permute-start | bytes 18874376 | tf_op jit(solution)/shard_map/ppermute | solution.py:773
  19.5 10.4 %collective-permute-start.3 = (s32[1024]{0:T(1024)S(1)}, s32[1024]{0:T(1024)S(1)}, u32[]{:S(2)}, u32[]{:S(2)}) collective-permute-start(s32[1024]{0:T(1024)S(1)} %copy-done.7), channel_id=1, source_target_pairs={{0,1},{1,0},{2,3},{3,2},{4,5},{5,4},{6,7},{7,6}} | collective-permute-start | bytes 12296 | tf_op jit(solution)/shard_map/ppermute | solution.py:773
  19.6 104.4 %collective-permute-start.1 = (bf16[768,3072]{1,0:T(8,128)(2,1)}, bf16[768,3072]{1,0:T(8,128)(2,1)}, u32[]{:S(2)}, u32[]{:S(2)}) collective-permute-start(bf16[768,3072]{1,0:T(8,128)(2,1)} %slice.41), channel_id=1, source_target_pairs={{0,2},{1,3},{2,0},{3,1},{4,6},{5,7},{6,4},{7,5}} | collective-permute-start | bytes 14155784 | tf_op jit(solution)/shard_map/ppermute | solution.py:770
  21.1 9.4 %collective-permute-start.5 = (s32[1024]{0:T(1024)S(1)}, s32[1024]{0:T(1024)S(1)}, u32[]{:S(2)}, u32[]{:S(2)}) collective-permute-start(s32[1024]{0:T(1024)S(1)} %collective-permute-done.4), channel_id=1, source_target_pairs={{0,1},{1,0},{2,3},{3,2},{4,5},{5,4},{6,7},{7,6}} | collective-permute-start | bytes 12296 | tf_op jit(solution)/shard_map/ppermute | solution.py:773
  124.0 8.3 collective-permute-start.7
  125.5 36.9 %collective-permute-start = (bf16[256,3072]{1,0:T(8,128)(2,1)S(1)}, bf16[256,3072]{1,0:T(8,128)(2,1)}, u32[]{:S(2)}, u32[]{:S(2)}) collective-permute-start(bf16[256,3072]{1,0:T(8,128)(2,1)S(1)} %slice.42), channel_id=1, source_target_pairs={{0,2},{1,3},{2,0},{3,1},{4,6},{5,7},{6,4},{7,5}} | collective-permute-start | bytes 4718600 | tf_op jit(solution)/shard_map/ppermute | solution.py:770
  162.5 104.5 %collective-permute-start.10 = (bf16[768,3072]{1,0:T(8,128)(2,1)}, bf16[768,3072]{1,0:T(8,128)(2,1)}, u32[]{:S(2)}, u32[]{:S(2)}) collective-permute-start(bf16[768,3072]{1,0:T(8,128)(2,1)} %slice.43), channel_id=1, source_target_pairs={{0,2},{1,3},{2,0},{3,1},{4,6},{5,7},{6,4},{7,5}} | collective-permute-start | bytes 14155784 | tf_op jit(solution)/shard_map/ppermute | solution.py:770
  267.0 20.2 %collective-permute-start.11 = (bf16[768,3072]{1,0:T(8,128)(2,1)}, bf16[768,3072]{1,0:T(8,128)(2,1)}, u32[]{:S(2)}, u32[]{:S(2)}) collective-permute-start(bf16[768,3072]{1,0:T(8,128)(2,1)} %collective-permute-done.10.da_ref), channel_id=1, source_target_pairs={{0,1},{1,0},{2,3},{3,2},{4,5},{5,4},{6,7},{7,6}} | collective-permute-start | bytes 14155784 | tf_op jit(solution)/shard_map/ppermute | solution.py:773
  267.0 37.0 %collective-permute-start.9 = (bf16[256,3072]{1,0:T(8,128)(2,1)}, bf16[256,3072]{1,0:T(8,128)(2,1)S(1)}, u32[]{:S(2)}, u32[]{:S(2)}) collective-permute-start(bf16[256,3072]{1,0:T(8,128)(2,1)} %slice.44), channel_id=1, source_target_pairs={{0,2},{1,3},{2,0},{3,1},{4,6},{5,7},{6,4},{7,5}} | collective-permute-start | bytes 4718600 | tf_op jit(solution)/shard_map/ppermute | solution.py:770
  306.0 160.4 %collective-permute-start.13 = (bf16[2560,768]{1,0:T(8,128)(2,1)}, bf16[2560,768]{1,0:T(8,128)(2,1)}, u32[]{:S(2)}, u32[]{:S(2)}) collective-permute-start(bf16[2560,768]{1,0:T(8,128)(2,1)} %get-tuple-element.156), channel_id=1, source_target_pairs={{0,2},{1,3},{2,0},{3,1},{4,6},{5,7},{6,4},{7,5}} | collective-permute-start | bytes 11796488 | tf_op jit(solution)/shard_map/ppermute | solution.py:770
  521.0 115.8 %collective-permute-start.18 = (f32[1536,3072]{1,0:T(8,128)}, f32[1536,3072]{1,0:T(8,128)}, u32[]{:S(2)}, u32[]{:S(2)}) collective-permute-start(f32[1536,3072]{1,0:T(8,128)} %get-tuple-element.159), channel_id=1, source_target_pairs={{0,1},{1,0},{2,3},{3,2},{4,5},{5,4},{6,7},{7,6}} | collective-permute-start | bytes 56623112 | tf_op jit(solution)/shard_map/ppermute | solution.py:773
  521.1 115.6 %collective-permute-start.16 = (bf16[4096,640]{1,0:T(8,128)(2,1)}, bf16[4096,640]{1,0:T(8,128)(2,1)}, u32[]{:S(2)}, u32[]{:S(2)}) collective-permute-start(bf16[4096,640]{1,0:T(8,128)(2,1)} %get-tuple-element.152.ga_ref.rest_0_), channel_id=1, source_target_pairs={{0,2},{1,3},{2,0},{3,1},{4,6},{5,7},{6,4},{7,5}} | collective-permute-start | bytes 15728648 | tf_op jit(solution)/shard_map/ppermute | solution.py:770
  521.6 30.0 %collective-permute-start.14 = (bf16[1024,768]{1,0:T(8,128)(2,1)}, bf16[1024,768]{1,0:T(8,128)(2,1)S(1)}, u32[]{:S(2)}, u32[]{:S(2)}) collective-permute-start(bf16[1024,768]{1,0:T(8,128)(2,1)} %get-tuple-element.161), channel_id=1, source_target_pairs={{0,1},{1,0},{2,3},{3,2},{4,5},{5,4},{6,7},{7,6}} | collective-permute-start | bytes 4718600 | tf_op jit(solution)/shard_map/ppermute | solution.py:773
  530.2 23.8 %collective-permute-start.15 = (bf16[1024,768]{1,0:T(8,128)(2,1)S(1)}, bf16[1024,768]{1,0:T(8,128)(2,1)}, u32[]{:S(2)}, u32[]{:S(2)}) collective-permute-start(bf16[1024,768]{1,0:T(8,128)(2,1)S(1)} %constant_dynamic-slice_fusion), channel_id=1, source_target_pairs={{0,1},{1,0},{2,3},{3,2},{4,5},{5,4},{6,7},{7,6}} | collective-permute-start | bytes 4718600 | tf_op jit(solution)/shard_map/ppermute | solution.py:773
  695.6 167.6 %collective-permute-start.23 = (f32[3072,1792]{1,0:T(8,128)}, f32[3072,1792]{1,0:T(8,128)}, u32[]{:S(2)}, u32[]{:S(2)}) collective-permute-start(f32[3072,1792]{1,0:T(8,128)} %get-tuple-element.165), channel_id=1, source_target_pairs={{0,1},{1,0},{2,3},{3,2},{4,5},{5,4},{6,7},{7,6}} | collective-permute-start | bytes 66060296 | tf_op jit(solution)/shard_map/ppermute | solution.py:773
  695.6 115.8 %collective-permute-start.17 = (bf16[4096,640]{1,0:T(8,128)(2,1)}, bf16[4096,640]{1,0:T(8,128)(2,1)}, u32[]{:S(2)}, u32[]{:S(2)}) collective-permute-start(bf16[4096,640]{1,0:T(8,128)(2,1)} %get-tuple-element.154.gb_ref.rest_1_), channel_id=1, source_target_pairs={{0,2},{1,3},{2,0},{3,1},{4,6},{5,7},{6,4},{7,5}} | collective-permute-start | bytes 15728648 | tf_op jit(solution)/shard_map/ppermute | solution.py:770
  840.7 79.4 %collective-permute-start.24 = (f32[3072,768]{1,0:T(8,128)}, f32[3072,768]{1,0:T(8,128)}, u32[]{:S(2)}, u32[]{:S(2)}) collective-permute-start(f32[3072,768]{1,0:T(8,128)} %get-tuple-element.170), channel_id=1, source_target_pairs={{0,1},{1,0},{2,3},{3,2},{4,5},{5,4},{6,7},{7,6}} | collective-permute-start | bytes 28311560 | tf_op jit(solution)/shard_map/ppermute | solution.py:773
  840.7 16.7 %collective-permute-start.20 = (bf16[1024,640]{1,0:T(8,128)(2,1)}, bf16[1024,640]{1,0:T(8,128)(2,1)S(1)}, u32[]{:S(2)}, u32[]{:S(2)}) collective-permute-start(bf16[1024,640]{1,0:T(8,128)(2,1)} %get-tuple-element.174), channel_id=1, source_target_pairs={{0,1},{1,0},{2,3},{3,2},{4,5},{5,4},{6,7},{7,6}} | collective-permute-start | bytes 3932168 | tf_op jit(solution)/shard_map/ppermute | solution.py:773
  841.2 18.2 %collective-permute-start.19 = (bf16[1024,640]{1,0:T(8,128)(2,1)}, bf16[1024,640]{1,0:T(8,128)(2,1)}, u32[]{:S(2)}, u32[]{:S(2)}) collective-permute-start(bf16[1024,640]{1,0:T(8,128)(2,1)} %get-tuple-element.173), channel_id=1, source_target_pairs={{0,1},{1,0},{2,3},{3,2},{4,5},{5,4},{6,7},{7,6}} | collective-permute-start | bytes 3932168 | tf_op jit(solution)/shard_map/ppermute | solution.py:773
  841.2 20.1 %collective-permute-start.22 = (bf16[1024,640]{1,0:T(8,128)(2,1)}, bf16[1024,640]{1,0:T(8,128)(2,1)}, u32[]{:S(2)}, u32[]{:S(2)}) collective-permute-start(bf16[1024,640]{1,0:T(8,128)(2,1)} %get-tuple-element.176), channel_id=1, source_target_pairs={{0,1},{1,0},{2,3},{3,2},{4,5},{5,4},{6,7},{7,6}} | collective-permute-start | bytes 3932168 | tf_op jit(solution)/shard_map/ppermute | solution.py:773
  918.2 10.5 %collective-permute-start.27 = (f32[3072]{0:T(1024)S(1)}, f32[3072]{0:T(1024)S(1)}, u32[]{:S(2)}, u32[]{:S(2)}) collective-permute-start(f32[3072]{0:T(1024)S(1)} %reduce_sum.9), channel_id=1, source_target_pairs={{0,3},{1,2},{2,1},{3,0},{4,7},{5,6},{6,5},{7,4}} | collective-permute-start | bytes 36872 | tf_op jit(solution)/shard_map/ppermute | solution.py:776
  918.4 10.3 %collective-permute-start.26 = (f32[3072]{0:T(1024)S(1)}, f32[3072]{0:T(1024)S(1)}, u32[]{:S(2)}, u32[]{:S(2)}) collective-permute-start(f32[3072]{0:T(1024)S(1)} %reduce_sum.9), channel_id=1, source_target_pairs={{0,2},{1,3},{2,0},{3,1},{4,6},{5,7},{6,4},{7,5}} | collective-permute-start | bytes 36872 | tf_op jit(solution)/shard_map/ppermute | solution.py:770
  920.0 8.7 collective-permute-start.25
  (16 other events, 149.0 us)
